TPU v7x, 32 devices: a whole 2x2x4 slice. The times are simulated.
32 devices in a mesh: dom: 8 (over y, x, core), col: 4 (over z).
Axes of the slice: x: 2, y: 2, z: 4, core: 2. Of those that a mesh axis runs over, the one named last changes fastest.
Arguments:
- features: bfloat16 [65536, 1024], P('dom', 'col')
- weight: bfloat16 [1024, 1024], P(None, 'col'), may hold values from -0.1875 to 0.1875
- out_bias: bfloat16 [1024], P('col'), may hold values from -3 to 3
- local_index: int32 [8, 64, 4], P('dom'), may hold values from 0 to 63
- local_count: int32 [8, 64], P('dom'), may hold values from 1 to 4, as said below
- local_vals: bfloat16 [8, 64, 4, 128, 128], P('dom'), may hold values from -0.1875 to 0.1875
- halo_index: int32 [8, 64, 4], P('dom'), may hold values from 0 to 31
- halo_count: int32 [8, 64], P('dom'), may hold values from 0 to 4, as said below
- halo_vals: bfloat16 [8, 64, 4, 128, 128], P('dom'), may hold values from -0.1875 to 0.1875
- send_rows: int32 [8, 8, 512], P('dom'), may hold values from 0 to 8191
- send_count: int32 [8, 8], P('dom'), may hold values from 0 to 512, as said below
Outputs:
- normalized: bfloat16 [65536, 1024], P('dom', 'col')
- channel_stats: float32 [2, 1024], P(None, 'col')
Inputs may be any that keep to these rules, and one draw needn't show every extreme that they name: `local_index`: slots k >= local_count of a row tile are not used. `local_count`: every partition has a row tile with all 4 slots used. `halo_index`: slots k >= halo_count of a row tile are not used. `halo_count`: every partition has a row tile with all 4 slots used. `send_rows`: slots s >= send_count[q, p] are not used. send_count[p, p] is 0; every partition fills all 512 slots to some other partition.
All inputs are finite; a program needn't handle non-finite values.
Results may differ from a plain program's by a relative error of at most 0.0075.
Values may be sent and summed in bfloat16 or wider, within the bound.
No kernel may reach another device: no remote copies, remote signals or barrier semaphores. Data moves between devices by JAX's collectives and lax.ppermute only.
A program may use at most 192 MiB of HBM per device.

v0:
```python
import jax
import jax.numpy as jnp
from jax import lax
from jax.sharding import PartitionSpec as P

TILE = 128


epsilon = 1e-06


def tile_sum(sources, tile_index, tile_count, tile_vals):
    gathered = sources[tile_index]
    keep_mask = jnp.arange(tile_vals.shape[1])[None, :] < tile_count[:, None]
    masked = jnp.where(keep_mask[:, :, None, None], tile_vals, jnp.zeros_like(tile_vals))
    return jnp.einsum("tkij,tkjc->tic", masked, gathered, preferred_element_type=jnp.float32)


def on_device(
    features,
    weight,
    out_bias,
    local_index,
    local_count,
    local_vals,
    halo_index,
    halo_count,
    halo_vals,
    send_rows,
    send_count,
):
    row_count, col_width = features.shape
    peer_count = lax.axis_size("dom")
    slot_total = send_rows.shape[2]
    chosen = features[send_rows[0]]
    keep_mask = jnp.arange(slot_total)[None, :] < send_count[0][:, None]
    outgoing = jnp.where(keep_mask[:, :, None], chosen, jnp.zeros_like(chosen))
    arrived = lax.all_to_all(outgoing, "dom", split_axis=0, concat_axis=0, tiled=True)
    halo_tiles = arrived.reshape(peer_count * slot_total // TILE, TILE, col_width)
    own_tiles = features.reshape(row_count // TILE, TILE, col_width)
    summed = tile_sum(own_tiles, local_index[0], local_count[0], local_vals[0])
    summed = summed + tile_sum(halo_tiles, halo_index[0], halo_count[0], halo_vals[0])
    spread = summed.reshape(row_count, col_width).astype(jnp.bfloat16)
    node_total = row_count * peer_count
    regrouped = lax.all_to_all(spread, "col", split_axis=0, concat_axis=1, tiled=True)
    full_weight, full_bias = (
        lax.all_gather(weight, "col", axis=1, tiled=True),
        lax.all_gather(out_bias.reshape(1, col_width), "col", axis=1, tiled=True),
    )
    mixed_rows = jnp.dot(regrouped, full_weight, preferred_element_type=jnp.float32) + full_bias[
        0
    ].astype(jnp.float32)
    active = jnp.maximum(mixed_rows, 0.0)
    row_power = jnp.mean(active * active, axis=1, keepdims=True)
    scaled = active * lax.rsqrt(row_power + epsilon)
    sum_whole, square_whole = lax.psum(
        (jnp.sum(scaled, axis=0), jnp.sum(scaled * scaled, axis=0)), ("dom", "col")
    )
    normalized = lax.all_to_all(
        scaled.astype(jnp.bfloat16), "col", split_axis=1, concat_axis=0, tiled=True
    )
    column_start = lax.axis_index("col") * col_width
    sum_total = lax.dynamic_slice_in_dim(sum_whole, column_start, col_width, 0)
    square_total = lax.dynamic_slice_in_dim(square_whole, column_start, col_width, 0)
    channel_mean = sum_total / node_total
    channel_var = square_total / node_total - channel_mean * channel_mean
    return (normalized, jnp.stack([channel_mean, channel_var]))


def solution(mesh):
    in_specs = (
        P("dom", "col"),
        P(None, "col"),
        P("col"),
        P("dom", None, None),
        P("dom", None),
        P("dom", None, None, None, None),
        P("dom", None, None),
        P("dom", None),
        P("dom", None, None, None, None),
        P("dom", None, None),
        P("dom", None),
    )
    out_specs = (P("dom", "col"), P(None, "col"))
    return jax.shard_map(
        on_device, mesh=mesh, in_specs=in_specs, out_specs=out_specs, check_vma=False
    )
```

profile of v0, /device:TPU:0, one launch (start us, length us, event | category | flops | bytes accessed | tf_op | source)
XLA Modules:
  0.0 374.6 jit_solution(2426596609186330712)
XLA Ops:
  7.2 0.7 fusion.10
  7.9 0.7 iota_compare_fusion.2
  8.6 15.7 %gather_fusion.1 = bf16[4096,256]{1,0:T(8,128)(2,1)S(1)} fusion(bf16[8192,256]{1,0:T(8,128)(2,1)} %param.11, s32[4096]{0:T(1024)S(1)} %broadcast_clamp_fusion), kind=kCustom, calls=%fused_computation.1 | custom fusion | bytes 4210688 | tf_op jit(solution)/shard_map/gather | solution.py:35
  24.4 0.0 copy-start
  24.4 0.0 copy-start.1
  24.4 1.7 broadcast_select_fusion
  26.1 5.2 %all-to-all-start = ((bf16[8,512,256]{2,1,0:T(8,128)(2,1)}), bf16[8,512,256]{2,1,0:T(8,128)(2,1)S(1)}, u32[]{:S(2)}, u32[]{:S(2)}) async-start(bf16[8,512,256]{2,1,0:T(8,128)(2,1)} %broadcast_select_fusion), calls=%async_computation | async-start | bytes 4194304 | tf_op jit(solution)/shard_map/all_to_all | solution.py:38
  31.3 0.1 copy.19
  31.4 0.1 reshape.208
  31.5 0.1 copy.18
  31.6 0.1 reshape.192
  31.7 0.0 copy-start.3
  31.7 12.0 %gather_fusion = bf16[256,128,256]{2,1,0:T(8,128)(2,1)} fusion(bf16[64,128,256]{2,1,0:T(8,128)(2,1)} %bitcast.52, s32[1024]{0:T(1024)S(1)} %pad_clamp_fusion.1), kind=kCustom, calls=%fused_computation | custom fusion | bytes 33555456 | tf_op jit(solution)/shard_map/gather | solution.py:13
  43.7 0.1 iota_compare_fusion
  43.8 0.1 iota_compare_fusion.1
  43.9 14.0 %all-to-all-done = bf16[8,512,256]{2,1,0:T(8,128)(2,1)S(1)} async-done(((bf16[8,512,256]{2,1,0:T(8,128)(2,1)}), bf16[8,512,256]{2,1,0:T(8,128)(2,1)S(1)}, u32[]{:S(2)}, u32[]{:S(2)}) %all-to-all-start) | async-done | bytes 2097184 | tf_op jit(solution)/shard_map/all_to_all | solution.py:38
  57.9 9.7 %gather_fusion.2 = bf16[256,128,256]{2,1,0:T(8,128)(2,1)} fusion(bf16[32,128,256]{2,1,0:T(8,128)(2,1)S(1)} %bitcast.53, s32[1024]{0:T(1024)S(1)} %pad_clamp_fusion), kind=kCustom, calls=%fused_computation.2 | custom fusion | bytes 33555456 | tf_op jit(solution)/shard_map/gather | solution.py:13
  67.6 13.8 %fusion.1 = f32[64,128,256,1]{2,1,3,0:T(8,128)} fusion(bf16[64,4,128,256]{3,2,1,0:T(8,128)(2,1)} %bitcast.54, bf16[1,64,4,128,128]{4,3,2,1,0:T(8,128)(2,1)} %param.19, pred[64,4]{1,0:T(8,128)(4,1)S(1)} %iota_compare_fusion), kind=kOutput, calls=%fused_computation.6 | convolution fusion | flops 2151677952 | bytes 33554688 | tf_op jit(solution)/shard_map/tkij,tkjc->tic/dot_general | solution.py:16
  81.4 14.0 %fusion = bf16[64,128,256]{2,1,0:T(8,128)(2,1)} fusion(f32[64,128,256,1]{2,1,3,0:T(8,128)} %fusion.1, bf16[64,4,128,256]{3,2,1,0:T(8,128)(2,1)} %bitcast.55, bf16[1,64,4,128,128]{4,3,2,1,0:T(8,128)(2,1)} %param.16, pred[64,4]{1,0:T(8,128)(4,1)S(1)} %iota_compare_fusion.1), kind=kOutput, calls=%fused_computation.4 | convolution fusion | flops 2155872256 | bytes 37748992 | tf_op jit(solution)/shard_map/tkij,tkjc->tic/dot_general | solution.py:16
  95.4 6.3 %copy.20 = bf16[4,2048,256]{1,2,0:T(8,128)(2,1)} copy(bf16[4,2048,256]{2,1,0:T(8,128)(2,1)} %bitcast.56) | data formatting | bytes 8388608 | tf_op jit(solution)/shard_map/convert_element_type | solution.py:43
  101.6 4.9 %all-to-all-start.1 = ((bf16[4,2048,256]{1,2,0:T(8,128)(2,1)}), bf16[4,2048,256]{1,2,0:T(8,128)(2,1)}, u32[]{:S(2)}, u32[]{:S(2)}) async-start(bf16[4,2048,256]{1,2,0:T(8,128)(2,1)} %copy.20), calls=%async_computation.1 | async-start | bytes 8388608 | tf_op jit(solution)/shard_map/all_to_all | solution.py:45
  106.5 0.0 all-gather.4.cloned.1.call-start
  106.5 0.7 all-gather.4.cloned.1.call-update
  107.2 103.9 %all-gather.1 = bf16[4,1,256]{2,1,0:T(2,128)(2,1)S(1)} all-gather(bf16[1,1,256]{2,1,0:T(2,128)(2,1)S(1)} %reshape.220), channel_id=2, replica_groups=mesh['dom'=8,'col'=4] {'col'}, dimensions={0}, use_global_device_ids=true | all-gather | bytes 2560 | tf_op jit(solution)/shard_map/all_gather | solution.py:48
  211.2 19.8 %all-to-all-done.1 = bf16[4,2048,256]{1,2,0:T(8,128)(2,1)} async-done(((bf16[4,2048,256]{1,2,0:T(8,128)(2,1)}), bf16[4,2048,256]{1,2,0:T(8,128)(2,1)}, u32[]{:S(2)}, u32[]{:S(2)}) %all-to-all-start.1) | async-done | bytes 4194336 | tf_op jit(solution)/shard_map/all_to_all | solution.py:45
  231.0 7.8 %multiply_reduce_fusion.1 = (f32[2048]{0:T(1024)S(1)}, f32[2048,1024]{0,1:T(8,128)S(1)}) fusion(f32[1024]{0:T(1024)S(1)} %bitcast.61, bf16[2048,1024]{0,1:T(8,128)(2,1)} %bitcast.19, bf16[1024,1024]{1,0:T(8,128)(2,1)} %all-gather.4.cloned.1.call-done), kind=kOutput, calls=%fused_computation.10 | convolution fusion | flops 4303353856 | bytes 14692352 | tf_op jit(solution)/shard_map/dot_general | solution.py:50
  238.7 3.5 fusion.6
  242.2 4.8 %all-to-all-start.2 = ((bf16[2048,4,256]{0,2,1:T(8,128)(2,1)}), bf16[2048,4,256]{0,2,1:T(8,128)(2,1)}, u32[]{:S(2)}, u32[]{:S(2)}) async-start(bf16[2048,4,256]{0,2,1:T(8,128)(2,1)} %bitcast.57), calls=%async_computation.2 | async-start | bytes 8388608 | tf_op jit(solution)/shard_map/all_to_all | solution.py:59
  247.1 113.8 %all-reduce = (f32[1024]{0:T(1024)S(1)}, f32[1024]{0:T(1024)S(1)}) all-reduce(f32[1024]{0:T(1024)S(1)} %get-tuple-element.3, f32[1024]{0:T(1024)S(1)} %get-tuple-element.2), channel_id=1, replica_groups=mesh['dom'=8,'col'=4] {'dom','col'}, use_global_device_ids=true, to_apply=%region_4.5 | all-reduce | flops 2048 | bytes 16384 | tf_op jit(solution)/shard_map/psum | solution.py:56
  360.9 0.1 dynamic-slice_multiply_fusion
  361.0 0.6 pad_maximum_fusion
  361.6 6.2 %copy.21 = bf16[4,2048,256]{2,1,0:T(8,128)(2,1)} copy(bf16[4,2048,256]{1,2,0:T(8,128)(2,1)} %bitcast.22) | data formatting | bytes 8388608 | tf_op jit(solution)/shard_map/all_to_all | solution.py:59
  (18 shorter events, 0.1 us)
Async XLA Ops:
  24.4 6.9 %copy-start = (s32[1,64,4]{1,2,0:T(4,128)S(1)}, s32[1,64,4]{1,2,0:T(4,128)}, u32[]{:S(2)}) copy-start(s32[1,64,4]{1,2,0:T(4,128)} %param.17) | copy-start | bytes 3076
  24.4 7.1 %copy-start.1 = (s32[1,64,4]{1,2,0:T(4,128)S(1)}, s32[1,64,4]{1,2,0:T(4,128)}, u32[]{:S(2)}) copy-start(s32[1,64,4]{1,2,0:T(4,128)} %param.14) | copy-start | bytes 3076
  26.1 31.8 %all-to-all-start = ((bf16[8,512,256]{2,1,0:T(8,128)(2,1)}), bf16[8,512,256]{2,1,0:T(8,128)(2,1)S(1)}, u32[]{:S(2)}, u32[]{:S(2)}) async-start(bf16[8,512,256]{2,1,0:T(8,128)(2,1)} %broadcast_select_fusion), calls=%async_computation | async-start | bytes 4194304 | tf_op jit(solution)/shard_map/all_to_all | solution.py:38
  31.7 12.0 %copy-start.2 = (s32[1,64]{1,0:T(1,128)S(1)}, s32[1,64]{1,0:T(1,128)}, u32[]{:S(2)}) copy-start(s32[1,64]{1,0:T(1,128)} %param.18) | copy-start | bytes 772
  31.7 12.1 %copy-start.3 = (s32[1,64]{1,0:T(1,128)S(1)}, s32[1,64]{1,0:T(1,128)}, u32[]{:S(2)}) copy-start(s32[1,64]{1,0:T(1,128)} %param.15) | copy-start | bytes 772
  95.4 11.9 %copy-start.4 = (bf16[256]{0:T(256)(128)(2,1)S(1)}, bf16[256]{0:T(256)(128)(2,1)}, u32[]{:S(2)}) copy-start(bf16[256]{0:T(256)(128)(2,1)} %param.13) | copy-start | bytes 1540
  101.6 129.3 %all-to-all-start.1 = ((bf16[4,2048,256]{1,2,0:T(8,128)(2,1)}), bf16[4,2048,256]{1,2,0:T(8,128)(2,1)}, u32[]{:S(2)}, u32[]{:S(2)}) async-start(bf16[4,2048,256]{1,2,0:T(8,128)(2,1)} %copy.20), calls=%async_computation.1 | async-start | bytes 8388608 | tf_op jit(solution)/shard_map/all_to_all | solution.py:45
  106.5 104.7 %all-gather.4.cloned.1.call-start = ((), (), s32[]{:S(2)}) async-start(), calls=%async_computation.3 | async-start | bytes 2621440 | tf_op jit(solution)/shard_map/all_gather | solution.py:47
  242.2 119.3 %all-to-all-start.2 = ((bf16[2048,4,256]{0,2,1:T(8,128)(2,1)}), bf16[2048,4,256]{0,2,1:T(8,128)(2,1)}, u32[]{:S(2)}, u32[]{:S(2)}) async-start(bf16[2048,4,256]{0,2,1:T(8,128)(2,1)} %bitcast.57), calls=%async_computation.2 | async-start | bytes 8388608 | tf_op jit(solution)/shard_map/all_to_all | solution.py:59
Sparse Core Ops, SparseCore 0:
  108.9 94.7 all-gather.3
where the time goes:
time: 375 us
  blocking collectives  218 us (58%)
  local copies, waits for them, and re-layouts  50.3 us (13%)
  matrix products  35.5 us (9%)
  waiting for transfers between devices  34.4 us (9%)
  starting transfers between devices  14.9 us (4%)
  between operations  14.2 us (4%)
  other arithmetic  7.48 us (2%)
    psum x1, blocking collectives, on_device(): lax.psum((jnp.sum(scaled, axis=0), jnp.sum(scaled * scaled, axis=0)), ('d...  114 us
    all_gather x1, blocking collectives, on_device(): lax.all_gather(out_bias.reshape(1, col_width), 'col', axis=1, tiled=True)  104 us
    dot_general x2, matrix products, tile_sum(): jnp.einsum('tkij,tkjc->tic', masked, gathered, preferred_element_type=jnp...  27.8 us
    gather x2, local copies, waits for them, and re-layouts, tile_sum(): gathered = sources[tile_index]  21.7 us
    all_to_all x1, waiting for transfers between devices, on_device(): lax.all_to_all(spread, 'col', split_axis=0, concat_axis=1, tiled=True)  19.8 us
    gather x1, local copies, waits for them, and re-layouts, on_device(): chosen = features[send_rows[0]]  15.7 us
    all_to_all x1, waiting for transfers between devices, on_device(): lax.all_to_all(outgoing, 'dom', split_axis=0, concat_axis=0, tiled=True)  14 us
    dot_general x1, matrix products, on_device(): jnp.dot(regrouped, full_weight, preferred_element_type=jnp.float32)  7.76 us
  transfers between devices with their start and end apart: 4, of which 2 were waited for; matrix products, arithmetic and copies ran while one was open for 4% of the time, Pallas kernels for 0%

commit v1 on v0

v1 whole, which is shorter than its diff:
```python
import functools

import jax
import jax.numpy as jnp
from jax import lax
from jax.experimental import pallas as pl
from jax.experimental.pallas import tpu as pltpu
from jax.sharding import PartitionSpec as P


TILE = 128
EPS = 1e-06

HBM = pl.BlockSpec(memory_space=pl.ANY)
VMEM = pl.BlockSpec(memory_space=pltpu.VMEM)
RAW = pl.BlockSpec(memory_space=pltpu.HBM)


def cost(flops, nbytes):
    return pl.CostEstimate(flops=int(flops), bytes_accessed=int(nbytes), transcendentals=0)


def in_hbm(x):
    return pltpu.with_memory_space_constraint(x, pltpu.HBM)


def grant(mib):
    return pltpu.CompilerParams(vmem_limit_bytes=int(mib) << 20)


LANES = 128
SUBLANES = 8
UNROLL = 16


def storage_order(send_rows):
    n, slots = send_rows.shape
    if n % SUBLANES or slots % LANES:
        return send_rows.reshape(-1), lambda q: q * slots, lambda b: b * UNROLL
    blocks = slots // LANES
    tiled = send_rows.reshape(n // SUBLANES, SUBLANES, blocks, LANES)
    tile = SUBLANES * LANES
    per = LANES // UNROLL

    def first(q):
        return (q >> 3) * (blocks * tile) + (q & (SUBLANES - 1)) * LANES

    def within(b):
        return lax.div(b, per) * tile + lax.rem(b, per) * UNROLL

    return tiled.transpose(0, 2, 1, 3).reshape(-1), first, within


def widen(feat, tables, raw, sems):
    n_rows = raw.shape[0]
    parts = sems.shape[0]
    part = n_rows // parts
    step = 64
    copies = [
        pltpu.make_async_copy(
            feat.at[pl.ds(c * part, part)], raw.at[pl.ds(c * part, part)], sems.at[c]
        )
        for c in range(parts)
    ]
    for copy in copies:
        copy.start()
    for c in range(parts):
        copies[c].wait()

        def one(b, carry, c=c):
            at = pl.ds(pl.multiple_of(c * part + b * step, step), step)
            for h, table in enumerate(tables):
                table[at, :] = raw[at, pl.ds(h * LANES, LANES)].astype(jnp.float32)
            return carry

        lax.fori_loop(0, part // step, one, 0)


def gather_kernel(peers, peer, first_row, within, first, halves, rows_in, counts_in, *refs):
    n_out = len(peers)
    refs = list(refs)
    if first:
        feat = refs.pop(0)
        outs, tables = refs[:n_out], refs[n_out : n_out + halves]
        raw = refs[n_out + halves]
        refs = refs[n_out + halves + 1 :]
    else:
        tables, outs = refs[:halves], refs[halves : halves + n_out]
        refs = refs[halves + n_out :]
    rows, counts, index_sems = refs[:3]
    stages = refs[3 : 3 + halves]
    load_rows = pltpu.make_async_copy(rows_in, rows, index_sems.at[0])
    load_counts = pltpu.make_async_copy(counts_in, counts, index_sems.at[1])
    load_rows.start()
    load_counts.start()
    if first:
        widen(feat, tables, raw, refs[3 + halves])
    load_rows.wait()
    load_counts.wait()
    me = lax.axis_index("dom")
    slots = stages[0].shape[0]
    for out, k in zip(outs, peers):
        q = peer(me, k)
        used = counts[q]

        begin = first_row(q)

        def pick(b, carry, begin=begin):
            base = begin + within(b)
            source = [rows[base + j] for j in range(UNROLL)]
            for table, stage in zip(tables, stages):
                got = [table[pl.ds(r, 1), :] for r in source]
                for j in range(UNROLL):
                    stage[pl.ds(b * UNROLL + j, 1), :] = got[j]
            return carry

        lax.fori_loop(0, (used + UNROLL - 1) // UNROLL, pick, 0)
        for b in range(slots // 64):
            at = pl.ds(b * 64, 64)
            slot = b * 64 + lax.broadcasted_iota(jnp.int32, (64, LANES), 0)
            for h, stage in enumerate(stages):
                kept = jnp.where(slot < used, stage[at, :], 0.0)
                out[at, pl.ds(h * LANES, LANES)] = kept.astype(out.dtype)


def gather_rows(rows, first_row, within, send_count, features, tables, peers, peer, slots):
    n_rows, width = features.shape
    halves = width // LANES
    first = not tables
    piece = jax.ShapeDtypeStruct((slots, width), features.dtype)
    table = jax.ShapeDtypeStruct((n_rows, LANES), jnp.float32)
    parts = 8 if n_rows % (8 * 64) == 0 else 1
    out = pl.pallas_call(
        functools.partial(gather_kernel, peers, peer, first_row, within, first, halves),
        out_shape=[piece] * len(peers)
        + ([table] * halves + [pltpu.VMEM(features.shape, features.dtype)]) * first,
        in_specs=[RAW, RAW] + ([RAW] if first else [VMEM] * halves),
        out_specs=[VMEM] * (len(peers) + (halves + 1) * first),
        scratch_shapes=[
            pltpu.SMEM(rows.shape, jnp.int32),
            pltpu.SMEM(send_count.shape, jnp.int32),
            pltpu.SemaphoreType.DMA((2,)),
        ]
        + [pltpu.VMEM((slots, LANES), jnp.float32)] * halves
        + (
            [pltpu.SemaphoreType.DMA((parts,))] if first else []
        ),
        compiler_params=grant(18 + len(peers) if first else 4),
        cost_estimate=cost(4e9, 6 << 20),
        name="gather_rows",
    )(in_hbm(rows), in_hbm(send_count), *([in_hbm(features)] if first else tables))
    return out[: len(peers)], out[len(peers) :]


def sum_kernel(
    n_dom, n_col, peer, slots, piece_rows, per_dest, base,
    own_index, own_counts, halo_index, halo_counts, *refs
):
    pieces = refs[: n_dom - 1]
    feat = refs[n_dom - 1]
    own_vals = refs[n_dom : n_dom + n_col]
    halo_vals = refs[n_dom + n_col : n_dom + 2 * n_col]
    outs = refs[n_dom + 2 * n_col : n_dom + 3 * n_col]
    (halo,) = refs[n_dom + 3 * n_col :]
    sub = pl.program_id(0)
    group = own_vals[0].shape[0]
    col = lax.axis_index("col")

    @pl.when(sub == 0)
    def _():
        me = lax.axis_index("dom")
        for k in range(1, n_dom):
            at = pl.ds(pl.multiple_of(peer(me, -k) * piece_rows, piece_rows), piece_rows)
            halo[at, :] = pieces[k - 1][...]
        own = pl.ds(pl.multiple_of(me * piece_rows, piece_rows), piece_rows)
        halo[own, :] = jnp.zeros((piece_rows, halo.shape[1]), halo.dtype)

    for k in range(n_col):
        dest = lax.rem(col + k, n_col)
        for t in range(group):
            row_tile = dest * per_dest + base + sub * group + t
            left, right = [], []
            for src, index, counts, vals in (
                (feat, own_index, own_counts, own_vals[k]),
                (halo, halo_index, halo_counts, halo_vals[k]),
            ):
                used = counts[row_tile]
                for s in range(slots):
                    left.append(jnp.where(s < used, vals[t, s], jnp.zeros_like(vals[t, s])))
                    at = pl.multiple_of(index[s, row_tile] * TILE, TILE)
                    right.append(src[pl.ds(at, TILE), :])
            total = jnp.dot(
                jnp.concatenate(left, axis=1),
                jnp.concatenate(right, axis=0),
                preferred_element_type=jnp.float32,
            )
            at = pl.ds(pl.multiple_of((sub * group + t) * TILE, TILE), TILE)
            outs[k][at, :] = total.astype(outs[k].dtype)


def tile_sums(tables, pieces, features, own_vals, halo_vals, n_dom, n_col, peer, base, size):
    tiles, slots = own_vals.shape[:2]
    width = features.shape[1]
    piece_rows = pieces[0].shape[0]
    per_dest = tiles // n_col
    group = min(size, 2)
    while base % group or size % group:
        group -= 1

    def vals_spec(k):
        def place(i, *_):
            dest = lax.rem(lax.axis_index("col") + k, n_col)
            return ((dest * per_dest + base) // group + i, 0, 0, 0)

        return pl.BlockSpec((group, slots, TILE, TILE), place)

    rows = size * TILE
    return pl.pallas_call(
        functools.partial(sum_kernel, n_dom, n_col, peer, slots, piece_rows, per_dest, base),
        out_shape=[jax.ShapeDtypeStruct((rows, width), jnp.bfloat16)] * n_col,
        grid_spec=pltpu.PrefetchScalarGridSpec(
            num_scalar_prefetch=4,
            grid=(size // group,),
            in_specs=[VMEM] * n_dom + [vals_spec(k) for k in range(n_col)] * 2,
            out_specs=[VMEM] * n_col,
            scratch_shapes=[pltpu.VMEM((n_dom * piece_rows, width), jnp.bfloat16)],
        ),
        compiler_params=grant(10 + n_dom),
        cost_estimate=cost(2e9, 6 << 20),
        name="tile_sums",
    )(
        *tables, *pieces, pltpu.with_memory_space_constraint(features, pltpu.VMEM),
        *([in_hbm(own_vals)] * n_col), *([in_hbm(halo_vals)] * n_col),
    )


def half_kernel(share, weight, bias, out, sem):
    half = weight.shape[0] // share
    start = lax.rem(lax.axis_index("dom"), share) * half
    src = weight.at[pl.ds(pl.multiple_of(start, half), half)]
    copy = pltpu.make_async_copy(src, out.at[pl.ds(0, half)], sem)
    copy.start()
    tail = (out.shape[0] - half, out.shape[1])
    out[pl.ds(half, tail[0]), :] = jnp.broadcast_to(bias[...], tail)
    copy.wait()


def weight_half(weight, bias, share):
    rows = weight.shape[0] // share + 16
    return pl.pallas_call(
        functools.partial(half_kernel, share),
        out_shape=jax.ShapeDtypeStruct((rows, weight.shape[1]), weight.dtype),
        in_specs=[RAW, VMEM],
        out_specs=VMEM,
        scratch_shapes=[pltpu.SemaphoreType.DMA],
        compiler_params=grant(4),
        cost_estimate=cost(1e8, 1 << 20),
        name="weight_half",
    )(in_hbm(weight), bias)


def join_kernel(n_col, share, *refs):
    own, own_bias = refs[:2]
    mine = refs[2 : n_col + 1]
    theirs = refs[n_col + 1 : -2] or mine
    joined, bias = refs[-2:]
    width = own.shape[1]
    half = own.shape[0] // share
    odd = lax.rem(lax.axis_index("dom"), share)
    for s in range(n_col):
        row = lax.rem(lax.axis_index("col") + n_col - s, n_col) * width
        at = pl.ds(s * width, width)
        joined[0, at, :] = own[pl.ds(pl.multiple_of(row, width), width), :]
        side = lax.div(row, half)
        row = pl.ds(pl.multiple_of(row - side * half, width), width)
        for k in range(1, n_col):

            @pl.when(side == odd)
            def _(k=k, at=at, row=row):
                joined[k, at, :] = mine[k - 1][row, :]

            @pl.when(side != odd)
            def _(k=k, at=at, row=row):
                joined[k, at, :] = theirs[k - 1][row, :]

    bias[pl.ds(0, 1), :] = own_bias[...].astype(jnp.float32)
    for k in range(1, n_col):
        got = mine[k - 1][pl.ds(half, 16), :].astype(jnp.float32)
        bias[pl.ds(k, 1), :] = got[:1]


def join_weights(weight, bias, mine, theirs, share):
    n_col = len(mine) + 1
    channels, width = weight.shape
    return pl.pallas_call(
        functools.partial(join_kernel, n_col, share),
        out_shape=[
            jax.ShapeDtypeStruct((n_col, channels, width), weight.dtype),
            jax.ShapeDtypeStruct((n_col, width), jnp.float32),
        ],
        in_specs=[VMEM] * (2 + len(mine) + len(theirs)),
        out_specs=[VMEM] * 2,
        compiler_params=grant(8),
        cost_estimate=cost(1e9, 4 << 20),
        name="join_weights",
    )(weight, bias, *mine, *theirs)


def mix_kernel(n_col, channels, first, *refs):
    pieces, held, bias = refs[:n_col], refs[n_col], refs[n_col + 1]
    outs, stats = refs[-n_col - 1 : -1], refs[-1]

    @pl.when(pl.program_id(0) == 0)
    def _():
        stats[...] = jnp.zeros_like(stats) if first else refs[n_col + 2][...]

    spread = jnp.concatenate([piece[...] for piece in pieces], axis=1)
    active, power = [], 0.0
    for k in range(n_col):
        mixed = jnp.dot(spread, held[k], preferred_element_type=jnp.float32)
        mixed = jnp.maximum(mixed + bias[pl.ds(k, 1), :], 0.0)
        power = power + jnp.sum(mixed * mixed, axis=1, keepdims=True)
        active.append(mixed)
    scale = lax.rsqrt(power * (1.0 / channels) + EPS)
    for k in range(n_col):
        scaled = active[k] * scale
        outs[k][...] = scaled.astype(outs[k].dtype)
        stats[pl.ds(2 * k, 1), :] += jnp.sum(scaled, axis=0, keepdims=True)
        stats[pl.ds(2 * k + 1, 1), :] += jnp.sum(scaled * scaled, axis=0, keepdims=True)


def mix_rows(pieces, weights, bias, before):
    n_col = len(pieces)
    rows, width = pieces[0].shape
    channels = n_col * width
    block = TILE
    piece = pl.BlockSpec((block, width), lambda i: (i, 0))
    first = before is None
    out = pl.pallas_call(
        functools.partial(mix_kernel, n_col, channels, first),
        out_shape=[jax.ShapeDtypeStruct((rows, width), jnp.bfloat16)] * n_col
        + [jax.ShapeDtypeStruct((2 * n_col, width), jnp.float32)],
        grid=(rows // block,),
        in_specs=[piece] * n_col + [VMEM] * (2 if first else 3),
        out_specs=[piece] * n_col + [VMEM],
        compiler_params=grant(10),
        cost_estimate=cost(2 * rows * channels * channels, 4 << 20),
        name="mix_rows",
    )(*pieces, weights, bias, *([] if first else [before]))
    return out[:n_col], out[n_col]


def place_kernel(n_col, per_dest, base, nodes, *refs):
    pieces = refs[:n_col]
    parts = refs[n_col : 2 * n_col] if nodes else ()
    out, put = refs[-2 - bool(nodes)], refs[-1]
    rows = pieces[0].shape[0]
    stores = []
    for k in range(n_col):
        dest = lax.rem(lax.axis_index("col") + k, n_col)
        at = pl.ds(pl.multiple_of((dest * per_dest + base) * TILE, TILE), rows)
        stores.append(pltpu.make_async_copy(pieces[k], out.at[at], put.at[k]))
    for store in stores:
        store.start()
    if nodes:
        total = parts[0][...]
        for part in parts[1:]:
            total = total + part[...]
        total = total / nodes
        mean = total[0:1]
        refs[-2][pl.ds(0, 1), :] = mean
        refs[-2][pl.ds(1, 1), :] = total[1:2] - mean * mean
    for store in stores:
        store.wait()


def place_rows(pieces, out, n_rows, base, parts=(), nodes=0):
    n_col = len(pieces)
    _, width = pieces[0].shape
    per_dest = n_rows // TILE // n_col
    extra = list(parts) + ([] if out is None else [out])
    out_shape = [jax.ShapeDtypeStruct((n_rows, width), jnp.bfloat16)]
    out_specs = [HBM]
    if nodes:
        out_shape.append(jax.ShapeDtypeStruct((2, width), jnp.float32))
        out_specs.append(VMEM)
    return pl.pallas_call(
        functools.partial(place_kernel, n_col, per_dest, base, nodes),
        out_shape=out_shape,
        in_specs=[VMEM] * (n_col + len(parts)) + ([] if out is None else [HBM]),
        out_specs=out_specs,
        scratch_shapes=[pltpu.SemaphoreType.DMA((n_col,))],
        input_output_aliases={} if out is None else {n_col + len(extra) - 1: 0},
        compiler_params=grant(8),
        cost_estimate=cost(1e8, 2 << 20),
        name="place_rows",
    )(*pieces, *extra)


def chunk_plan(per_dest):
    if per_dest % 8:
        return [(0, per_dest)]
    u = per_dest // 8
    cuts = [0, u, 2 * u, 4 * u, 6 * u, 8 * u]
    return [(a, b - a) for a, b in zip(cuts, cuts[1:])]


def on_device(
    features,
    weight,
    out_bias,
    local_index,
    local_count,
    local_vals,
    halo_index,
    halo_count,
    halo_vals,
    send_rows,
    send_count,
):
    n_rows, width = features.shape
    n_dom, n_col = lax.axis_size("dom"), lax.axis_size("col")

    if n_dom & (n_dom - 1) == 0:
        peer = lambda d, k: d ^ abs(k)
    else:
        peer = lambda d, k: (d + k + n_dom) % n_dom
    along_dom = lambda x, k: lax.ppermute(x, "dom", [(i, peer(i, k)) for i in range(n_dom)])
    along_col = lambda x, k: lax.ppermute(x, "col", [(i, (i + k) % n_col) for i in range(n_col)])

    far = list(reversed(range(1, n_dom)))
    halo = [None] * (n_dom - 1)
    rows, first_row, within = storage_order(send_rows[0])
    slots = send_rows.shape[2]
    tables, own_tiles = [], features
    cut = (n_dom - 1) // 2
    for peers in (far[:cut], far[cut:]):
        if not peers:
            continue
        outgoing, made = gather_rows(
            rows, first_row, within, send_count[0], features, tables, peers, peer, slots
        )
        if made:
            tables, own_tiles = made[:-1], made[-1]
        for k, piece in zip(peers, outgoing):
            halo[k - 1] = along_dom(piece, k)

    share = 2 if n_dom % 2 == 0 else 1
    order = sorted(range(1, n_col), key=lambda k: min(k, n_col - k), reverse=True)
    bias_row = out_bias.reshape(1, width)
    mine = weight_half(weight, bias_row, share)
    arrived = {k: along_col(mine, k) for k in order}
    mine = [arrived[k] for k in range(1, n_col)]
    theirs = []
    if share == 2:
        swap = [(i, i ^ 1) for i in range(n_dom)]
        theirs = [lax.ppermute(got, "dom", swap) for got in mine]
    weights, bias = join_weights(weight, bias_row, mine, theirs, share)

    plan = chunk_plan(n_rows // TILE // n_col)
    index_tables = (local_index[0].T, local_count[0], halo_index[0].T, halo_count[0])
    incoming = []
    for base, size in plan:
        sums = tile_sums(
            index_tables, halo, own_tiles, local_vals[0], halo_vals[0],
            n_dom, n_col, peer, base, size,
        )
        moved = {k: along_col(sums[k], k) for k in order}
        incoming.append([sums[0]] + [moved[k] for k in range(1, n_col)])

    stats = None
    returned = []
    for pieces in incoming:
        done, stats = mix_rows(pieces, weights, bias, stats)
        moved = {k: along_col(done[k], -k) for k in order}
        returned.append([done[0]] + [moved[k] for k in range(1, n_col)])

    over_dom = lax.all_gather(stats, "dom", axis=0)
    over_dom = over_dom.sum(axis=0)
    totals = [over_dom[:2]]
    for k in range(1, n_col):
        totals.append(along_col(over_dom[2 * k : 2 * k + 2], -k))

    out = None
    for g, ((base, _), pieces) in enumerate(zip(plan, returned)):
        if g < len(plan) - 1:
            (out,) = place_rows(pieces, out, n_rows, base)
        else:
            out, channel_stats = place_rows(
                pieces, out, n_rows, base, totals, n_rows * n_dom
            )
    return (out, channel_stats)


def solution(mesh):
    in_specs = (
        P("dom", "col"),
        P(None, "col"),
        P("col"),
        P("dom", None, None),
        P("dom", None),
        P("dom", None, None, None, None),
        P("dom", None, None),
        P("dom", None),
        P("dom", None, None, None, None),
        P("dom", None, None),
        P("dom", None),
    )
    out_specs = (P("dom", "col"), P(None, "col"))
    return jax.shard_map(
        on_device, mesh=mesh, in_specs=in_specs, out_specs=out_specs, check_vma=False
    )
```

time: 375 us -> 260 us (0.69)
  blocking collectives: 218 us -> 9.69 us
  starting transfers between devices: 14.9 us -> 120 us
  waiting for transfers between devices: 34.4 us -> 84.7 us
  local copies, waits for them, and re-layouts: 50.3 us -> 0.05 us
  Pallas kernels: 0 us -> 43.6 us
  matrix products: 35.5 us -> 0 us
  between operations: 14.2 us -> 1.15 us
  other arithmetic: 7.48 us -> 0.01 us
    ppermute x0 -> x46, starting transfers between devices: none -> 120 us  [the longest x36 111 us: on_device(): lax.ppermute(x, 'col', [(i, (i + k) % n_col) for i in range(n_col)])]
    psum x1 -> x0, blocking collectives: 114 us -> none  [on_device(): lax.psum((jnp.sum(scaled, axis=0), jnp.sum(scaled * scaled, axis=0)), ('d...]
    all_gather x1, blocking collectives: 104 us -> 9.69 us  [on_device(): over_dom = lax.all_gather(stats, 'dom', axis=0)]
    ppermute x0 -> x46, waiting for transfers between devices: none -> 84.7 us  [the longest x36 70.8 us: on_device(): lax.ppermute(x, 'col', [(i, (i + k) % n_col) for i in range(n_col)])]
    pallas_call x0 -> x19, Pallas kernels: none -> 43.6 us  [the longest x5 18.4 us: tile_sums(): pl.pallas_call(functools.partial(sum_kernel, n_dom, n_col, peer, slots, p...]
    gather x3 -> x0, local copies, waits for them, and re-layouts: 37.4 us -> none  [the longest x2 21.7 us: tile_sum(): gathered = sources[tile_index]]
    dot_general x3 -> x0, matrix products: 35.5 us -> none  [the longest x2 27.8 us: tile_sum(): jnp.einsum('tkij,tkjc->tic', masked, gathered, preferred_element_type=jnp...]
    all_to_all x3 -> x0, waiting for transfers between devices: 33.8 us -> none  [the longest x1 19.8 us: on_device(): lax.all_to_all(spread, 'col', split_axis=0, concat_axis=1, tiled=True)]
  transfers between devices with their start and end apart: 4 -> 46, of which waited for: 2 -> 13; matrix products, arithmetic and copies ran while one was open for 4% -> 0% of each run, Pallas kernels for 0% -> 12%
where the time goes in v1:
time: 260 us; the launch traced here: 259 us
  starting transfers between devices  120 us (46%)
  waiting for transfers between devices  84.7 us (33%)
  Pallas kernels  43.6 us (17%)
  blocking collectives  9.69 us (4%)
    ppermute x36, starting transfers between devices, on_device(): lax.ppermute(x, 'col', [(i, (i + k) % n_col) for i in range(n_col)])  111 us
    ppermute x36, waiting for transfers between devices, on_device(): lax.ppermute(x, 'col', [(i, (i + k) % n_col) for i in range(n_col)])  70.8 us
    pallas_call x5, Pallas kernels, tile_sums(): pl.pallas_call(functools.partial(sum_kernel, n_dom, n_col, peer, slots, p...  18.4 us
    ppermute x7, waiting for transfers between devices, on_device(): lax.ppermute(x, 'dom', [(i, peer(i, k)) for i in range(n_dom)])  13.9 us
    pallas_call x5, Pallas kernels, mix_rows(): pl.pallas_call(functools.partial(mix_kernel, n_col, channels, first), out...  10.3 us
    all_gather x1, blocking collectives, on_device(): over_dom = lax.all_gather(stats, 'dom', axis=0)  9.69 us
    ppermute x7, starting transfers between devices, on_device(): lax.ppermute(x, 'dom', [(i, peer(i, k)) for i in range(n_dom)])  9.24 us
    pallas_call x2, Pallas kernels, gather_rows(): pl.pallas_call(functools.partial(gather_kernel, peers, peer, first_row, w...  8.53 us
  transfers between devices with their start and end apart: 46, of which 13 were waited for; matrix products, arithmetic and copies ran while one was open for 0% of the time, Pallas kernels for 12%

profile of v1, /device:TPU:0, one launch (start us, length us, event | category | flops | bytes accessed | tf_op | source)
XLA Modules:
  0.0 259.3 jit_solution(12007265017853728805)
XLA Ops:
  0.6 4.2 %gather_rows.2 = (bf16[512,256]{1,0:T(8,128)(2,1)S(1)}, bf16[512,256]{1,0:T(8,128)(2,1)S(1)}, bf16[512,256]{1,0:T(8,128)(2,1)S(1)}, f32[8192,128]{1,0:T(8,128)S(...) custom-call(s32[4096]{0:T(1024)} %bitcast.78, s32[8]{0:T(128)} %bitcast.80, bf16[8192,256]{1,0:T(8,128)(2,1)} %refs_0_.2), custom_call_target="tpu_custom_call" | custom-call | flops 4000000000 | bytes 6291456 | tf_op jit(solution)/shard_map/gather_rows/pallas_call | solution.py:133
  4.9 4.3 %gather_rows.3 = (bf16[512,256]{1,0:T(8,128)(2,1)S(1)}, bf16[512,256]{1,0:T(8,128)(2,1)S(1)}, bf16[512,256]{1,0:T(8,128)(2,1)S(1)}, bf16[512,256]{1,0:T(8,128)(2,1)S(1)}) custom-call(s32[4096]{0:T(1024)} %bitcast.79, s32[8]{0:T(128)} %bitcast.81, f32[8192,128]{1,0:T(8,128)S(1)} %get-tuple-element.59.refs_0_, f32[8192,128]{1,0:T(8,128)S(1)} %get-tuple-element.60.refs_1_), custom_call_target="tpu_custom_call" | custom-call | flops 4000000000 | bytes 6291456 | tf_op jit(solution)/shard_map/gather_rows/pallas_call | solution.py:133
  9.8 3.2 %collective-permute-start.1 = (bf16[512,256]{1,0:T(8,128)(2,1)S(1)}, bf16[512,256]{1,0:T(8,128)(2,1)S(1)}, u32[]{:S(2)}, u32[]{:S(2)}) collective-permute-start(bf16[512,256]{1,0:T(8,128)(2,1)S(1)} %get-tuple-element.62), channel_id=1, source_target_pairs={{0,8},{4,12},{8,0},{12,4},{16,24},{20,28},{24,16},{28,20},{1,9},{5... | collective-permute-start | bytes 786440 | tf_op jit(solution)/shard_map/ppermute | solution.py:428
  29.4 8.1 %collective-permute-done.4.refs_4_ = bf16[512,256]{1,0:T(8,128)(2,1)S(1)} collective-permute-done((bf16[512,256]{1,0:T(8,128)(2,1)S(1)}, bf16[512,256]{1,0:T(8,128)(2,1)S(1)}, u32[]{:S(2)}, u32[]{:S(2)}) %collective-permute-start.4) | collective-permute-done | bytes 262176 | tf_op jit(solution)/shard_map/ppermute | solution.py:428
  37.6 3.6 %collective-permute-start.12 = (bf16[528,256]{1,0:T(8,128)(2,1)S(1)}, bf16[528,256]{1,0:T(8,128)(2,1)S(1)}, u32[]{:S(2)}, u32[]{:S(2)}) collective-permute-start(bf16[528,256]{1,0:T(8,128)(2,1)S(1)} %weight_half.1), channel_id=1, source_target_pairs={{0,3},{1,0},{2,1},{3,2},{4,7},{5,4},{6,5},{7,6},{8,11},{9,8},{10,9... | collective-permute-start | bytes 811016 | tf_op jit(solution)/shard_map/ppermute | solution.py:429
  41.2 3.0 %tile_sums.8 = (bf16[256,256]{1,0:T(8,128)(2,1)S(1)}, bf16[256,256]{1,0:T(8,128)(2,1)S(1)}, bf16[256,256]{1,0:T(8,128)(2,1)S(1)}, bf16[256,256]{1,0:T(8,128)(2,1)S(1)}) custom-call(s32[4,64]{1,0:T(4,128)S(1)} %bitcast.18, s32[64]{0:T(128)S(1)} %bitcast.28, s32[4,64]{1,0:T(4,128)S(1)} %bitcast.23, s32[64]{0:T(128)S(1)} %bitcast.33, ...), custom_call_target="tpu_custom_call" | custom-call | flops 2000000000 | bytes 6291456 | tf_op jit(solution)/shard_map/tile_sums/pallas_call | solution.py:218
  45.3 3.0 %tile_sums.9 = (bf16[256,256]{1,0:T(8,128)(2,1)S(1)}, bf16[256,256]{1,0:T(8,128)(2,1)S(1)}, bf16[256,256]{1,0:T(8,128)(2,1)S(1)}, bf16[256,256]{1,0:T(8,128)(2,1)S(1)}) custom-call(s32[4,64]{1,0:T(4,128)S(1)} %bitcast.19, s32[64]{0:T(128)S(1)} %bitcast.29, s32[4,64]{1,0:T(4,128)S(1)} %bitcast.24, s32[64]{0:T(128)S(1)} %bitcast.34, ...), custom_call_target="tpu_custom_call" | custom-call | flops 2000000000 | bytes 6291456 | tf_op jit(solution)/shard_map/tile_sums/pallas_call | solution.py:218
  51.2 7.0 %collective-permute-start.25 = (bf16[256,256]{1,0:T(8,128)(2,1)S(1)}, bf16[256,256]{1,0:T(8,128)(2,1)S(1)}, u32[]{:S(2)}, u32[]{:S(2)}) collective-permute-start(bf16[256,256]{1,0:T(8,128)(2,1)S(1)} %get-tuple-element.88), channel_id=1, source_target_pairs={{0,1},{1,2},{2,3},{3,0},{4,5},{5,6},{6,7},{7,4},{8,9},{9,10},{10,1... | collective-permute-start | bytes 393224 | tf_op jit(solution)/shard_map/ppermute | solution.py:429
  58.2 3.6 %collective-permute-start.26 = (bf16[256,256]{1,0:T(8,128)(2,1)S(1)}, bf16[256,256]{1,0:T(8,128)(2,1)S(1)}, u32[]{:S(2)}, u32[]{:S(2)}) collective-permute-start(bf16[256,256]{1,0:T(8,128)(2,1)S(1)} %get-tuple-element.89), channel_id=1, source_target_pairs={{0,2},{1,3},{2,0},{3,1},{4,6},{5,7},{6,4},{7,5},{8,10},{9,11},{10,... | collective-permute-start | bytes 393224 | tf_op jit(solution)/shard_map/ppermute | solution.py:429
  61.8 4.1 %tile_sums.6 = (bf16[512,256]{1,0:T(8,128)(2,1)S(1)}, bf16[512,256]{1,0:T(8,128)(2,1)S(1)}, bf16[512,256]{1,0:T(8,128)(2,1)S(1)}, bf16[512,256]{1,0:T(8,128)(2,1)S(1)}) custom-call(s32[4,64]{1,0:T(4,128)S(1)} %bitcast.20, s32[64]{0:T(128)S(1)} %bitcast.30, s32[4,64]{1,0:T(4,128)S(1)} %bitcast.25, s32[64]{0:T(128)S(1)} %bitcast.35, ...), custom_call_target="tpu_custom_call" | custom-call | flops 2000000000 | bytes 6291456 | tf_op jit(solution)/shard_map/tile_sums/pallas_call | solution.py:218
  67.6 3.8 %collective-permute-start.27 = (bf16[256,256]{1,0:T(8,128)(2,1)S(1)}, bf16[256,256]{1,0:T(8,128)(2,1)S(1)}, u32[]{:S(2)}, u32[]{:S(2)}) collective-permute-start(bf16[256,256]{1,0:T(8,128)(2,1)S(1)} %get-tuple-element.90), channel_id=1, source_target_pairs={{0,3},{1,0},{2,1},{3,2},{4,7},{5,4},{6,5},{7,6},{8,11},{9,8},{10,9... | collective-permute-start | bytes 393224 | tf_op jit(solution)/shard_map/ppermute | solution.py:429
  71.5 7.4 %collective-permute-done.26.refs_2_ = bf16[256,256]{1,0:T(8,128)(2,1)S(1)} collective-permute-done((bf16[256,256]{1,0:T(8,128)(2,1)S(1)}, bf16[256,256]{1,0:T(8,128)(2,1)S(1)}, u32[]{:S(2)}, u32[]{:S(2)}) %collective-permute-start.26) | collective-permute-done | bytes 131104 | tf_op jit(solution)/shard_map/ppermute | solution.py:429
  78.9 4.1 %tile_sums.7 = (bf16[512,256]{1,0:T(8,128)(2,1)S(1)}, bf16[512,256]{1,0:T(8,128)(2,1)S(1)}, bf16[512,256]{1,0:T(8,128)(2,1)S(1)}, bf16[512,256]{1,0:T(8,128)(2,1)S(1)}) custom-call(s32[4,64]{1,0:T(4,128)S(1)} %bitcast.21, s32[64]{0:T(128)S(1)} %bitcast.31, s32[4,64]{1,0:T(4,128)S(1)} %bitcast.26, s32[64]{0:T(128)S(1)} %bitcast.36, ...), custom_call_target="tpu_custom_call" | custom-call | flops 2000000000 | bytes 6291456 | tf_op jit(solution)/shard_map/tile_sums/pallas_call | solution.py:218
  83.2 3.8 %collective-permute-start.21 = (bf16[512,256]{1,0:T(8,128)(2,1)S(1)}, bf16[512,256]{1,0:T(8,128)(2,1)S(1)}, u32[]{:S(2)}, u32[]{:S(2)}) collective-permute-start(bf16[512,256]{1,0:T(8,128)(2,1)S(1)} %get-tuple-element.82), channel_id=1, source_target_pairs={{0,3},{1,0},{2,1},{3,2},{4,7},{5,4},{6,5},{7,6},{8,11},{9,8},{10,9... | collective-permute-start | bytes 786440 | tf_op jit(solution)/shard_map/ppermute | solution.py:429
  87.0 4.1 %tile_sums.5 = (bf16[512,256]{1,0:T(8,128)(2,1)S(1)}, bf16[512,256]{1,0:T(8,128)(2,1)S(1)}, bf16[512,256]{1,0:T(8,128)(2,1)S(1)}, bf16[512,256]{1,0:T(8,128)(2,1)S(1)}) custom-call(s32[4,64]{1,0:T(4,128)S(1)} %bitcast.22, s32[64]{0:T(128)S(1)} %bitcast.32, s32[4,64]{1,0:T(4,128)S(1)} %bitcast.27, s32[64]{0:T(128)S(1)} %bitcast.37, ...), custom_call_target="tpu_custom_call" | custom-call | flops 2000000000 | bytes 6291456 | tf_op jit(solution)/shard_map/tile_sums/pallas_call | solution.py:218
  95.5 9.2 %collective-permute-done.20.refs_2_ = bf16[512,256]{1,0:T(8,128)(2,1)S(1)} collective-permute-done((bf16[512,256]{1,0:T(8,128)(2,1)S(1)}, bf16[512,256]{1,0:T(8,128)(2,1)S(1)}, u32[]{:S(2)}, u32[]{:S(2)}) %collective-permute-start.20) | collective-permute-done | bytes 262176 | tf_op jit(solution)/shard_map/ppermute | solution.py:429
  104.7 16.1 %collective-permute-start.9 = (bf16[512,256]{1,0:T(8,128)(2,1)S(1)}, bf16[512,256]{1,0:T(8,128)(2,1)S(1)}, u32[]{:S(2)}, u32[]{:S(2)}) collective-permute-start(bf16[512,256]{1,0:T(8,128)(2,1)S(1)} %get-tuple-element.72), channel_id=1, source_target_pairs={{0,3},{1,0},{2,1},{3,2},{4,7},{5,4},{6,5},{7,6},{8,11},{9,8},{10,9... | collective-permute-start | bytes 786440 | tf_op jit(solution)/shard_map/ppermute | solution.py:429
  126.0 6.7 %collective-permute-done.17.refs_2_ = bf16[512,256]{1,0:T(8,128)(2,1)S(1)} collective-permute-done((bf16[512,256]{1,0:T(8,128)(2,1)S(1)}, bf16[512,256]{1,0:T(8,128)(2,1)S(1)}, u32[]{:S(2)}, u32[]{:S(2)}) %collective-permute-start.17) | collective-permute-done | bytes 262176 | tf_op jit(solution)/shard_map/ppermute | solution.py:429
  135.3 8.6 %collective-permute-done.8.refs_2_ = bf16[512,256]{1,0:T(8,128)(2,1)S(1)} collective-permute-done((bf16[512,256]{1,0:T(8,128)(2,1)S(1)}, bf16[512,256]{1,0:T(8,128)(2,1)S(1)}, u32[]{:S(2)}, u32[]{:S(2)}) %collective-permute-start.8) | collective-permute-done | bytes 262176 | tf_op jit(solution)/shard_map/ppermute | solution.py:429
  146.5 9.7 %all-gather = f32[64,256]{1,0:T(8,128)S(1)} all-gather(f32[8,256]{1,0:T(8,128)S(1)} %get-tuple-element.99), channel_id=2, replica_groups=mesh['dom'=8,'col'=4] {'dom'}, dimensions={0}, use_global_device_ids=true | all-gather | bytes 73728 | tf_op jit(solution)/shard_map/all_gather | solution.py:478
  156.2 4.2 %collective-permute-start.40 = (bf16[256,256]{1,0:T(8,128)(2,1)S(1)}, bf16[256,256]{1,0:T(8,128)(2,1)S(1)}, u32[]{:S(2)}, u32[]{:S(2)}) collective-permute-start(bf16[256,256]{1,0:T(8,128)(2,1)S(1)} %get-tuple-element.109), channel_id=1, source_target_pairs={{0,3},{1,0},{2,1},{3,2},{4,7},{5,4},{6,5},{7,6},{8,11},{9,8},{10,9... | collective-permute-start | bytes 393224 | tf_op jit(solution)/shard_map/ppermute | solution.py:429
  163.3 3.8 %collective-permute-start.43 = (bf16[256,256]{1,0:T(8,128)(2,1)S(1)}, bf16[256,256]{1,0:T(8,128)(2,1)S(1)}, u32[]{:S(2)}, u32[]{:S(2)}) collective-permute-start(bf16[256,256]{1,0:T(8,128)(2,1)S(1)} %get-tuple-element.113), channel_id=1, source_target_pairs={{0,3},{1,0},{2,1},{3,2},{4,7},{5,4},{6,5},{7,6},{8,11},{9,8},{10,9... | collective-permute-start | bytes 393224 | tf_op jit(solution)/shard_map/ppermute | solution.py:429
  167.2 5.0 %collective-permute-done.31.refs_5_ = f32[2,256]{1,0:T(2,128)S(1)} collective-permute-done((f32[2,256]{1,0:T(2,128)S(1)}, f32[2,256]{1,0:T(2,128)S(1)}, u32[]{:S(2)}, u32[]{:S(2)}) %collective-permute-start.31) | collective-permute-done | bytes 2080 | tf_op jit(solution)/shard_map/ppermute | solution.py:429
  172.2 5.8 %collective-permute-start.44 = (bf16[256,256]{1,0:T(8,128)(2,1)S(1)}, bf16[256,256]{1,0:T(8,128)(2,1)S(1)}, u32[]{:S(2)}, u32[]{:S(2)}) collective-permute-start(bf16[256,256]{1,0:T(8,128)(2,1)S(1)} %get-tuple-element.114), channel_id=1, source_target_pairs={{0,2},{1,3},{2,0},{3,1},{4,6},{5,7},{6,4},{7,5},{8,10},{9,11},{10,... | collective-permute-start | bytes 393224 | tf_op jit(solution)/shard_map/ppermute | solution.py:429
  178.0 3.4 %collective-permute-start.34 = (bf16[512,256]{1,0:T(8,128)(2,1)S(1)}, bf16[512,256]{1,0:T(8,128)(2,1)S(1)}, u32[]{:S(2)}, u32[]{:S(2)}) collective-permute-start(bf16[512,256]{1,0:T(8,128)(2,1)S(1)} %get-tuple-element.101), channel_id=1, source_target_pairs={{0,3},{1,0},{2,1},{3,2},{4,7},{5,4},{6,5},{7,6},{8,11},{9,8},{10,9... | collective-permute-start | bytes 786440 | tf_op jit(solution)/shard_map/ppermute | solution.py:429
  183.6 17.8 %collective-permute-start.45 = (bf16[256,256]{1,0:T(8,128)(2,1)S(1)}, bf16[256,256]{1,0:T(8,128)(2,1)S(1)}, u32[]{:S(2)}, u32[]{:S(2)}) collective-permute-start(bf16[256,256]{1,0:T(8,128)(2,1)S(1)} %get-tuple-element.115), channel_id=1, source_target_pairs={{0,1},{1,2},{2,3},{3,0},{4,5},{5,6},{6,7},{7,4},{8,9},{9,10},{10,1... | collective-permute-start | bytes 393224 | tf_op jit(solution)/shard_map/ppermute | solution.py:429
  201.4 8.1 %collective-permute-done.45.refs_3_ = bf16[256,256]{1,0:T(8,128)(2,1)S(1)} collective-permute-done((bf16[256,256]{1,0:T(8,128)(2,1)S(1)}, bf16[256,256]{1,0:T(8,128)(2,1)S(1)}, u32[]{:S(2)}, u32[]{:S(2)}) %collective-permute-start.45) | collective-permute-done | bytes 131104 | tf_op jit(solution)/shard_map/ppermute | solution.py:429
  209.6 7.8 %collective-permute-start.35 = (bf16[512,256]{1,0:T(8,128)(2,1)S(1)}, bf16[512,256]{1,0:T(8,128)(2,1)S(1)}, u32[]{:S(2)}, u32[]{:S(2)}) collective-permute-start(bf16[512,256]{1,0:T(8,128)(2,1)S(1)} %get-tuple-element.102), channel_id=1, source_target_pairs={{0,2},{1,3},{2,0},{3,1},{4,6},{5,7},{6,4},{7,5},{8,10},{9,11},{10,... | collective-permute-start | bytes 786440 | tf_op jit(solution)/shard_map/ppermute | solution.py:429
  217.3 3.8 %collective-permute-start.28 = (bf16[512,256]{1,0:T(8,128)(2,1)S(1)}, bf16[512,256]{1,0:T(8,128)(2,1)S(1)}, u32[]{:S(2)}, u32[]{:S(2)}) collective-permute-start(bf16[512,256]{1,0:T(8,128)(2,1)S(1)} %get-tuple-element.96), channel_id=1, source_target_pairs={{0,3},{1,0},{2,1},{3,2},{4,7},{5,4},{6,5},{7,6},{8,11},{9,8},{10,9... | collective-permute-start | bytes 786440 | tf_op jit(solution)/shard_map/ppermute | solution.py:429
  224.5 11.8 %collective-permute-done.35.refs_2_ = bf16[512,256]{1,0:T(8,128)(2,1)S(1)} collective-permute-done((bf16[512,256]{1,0:T(8,128)(2,1)S(1)}, bf16[512,256]{1,0:T(8,128)(2,1)S(1)}, u32[]{:S(2)}, u32[]{:S(2)}) %collective-permute-start.35) | collective-permute-done | bytes 262176 | tf_op jit(solution)/shard_map/ppermute | solution.py:429
  236.3 8.3 %collective-permute-start.33 = (f32[2,256]{1,0:T(2,128)S(1)}, f32[2,256]{1,0:T(2,128)S(1)}, u32[]{:S(2)}, u32[]{:S(2)}) collective-permute-start(f32[2,256]{1,0:T(2,128)S(1)} %get-tuple-element.116), channel_id=1, source_target_pairs={{0,1},{1,2},{2,3},{3,0},{4,5},{5,6},{6,7},{7,4},{8,9},{9,10},{10,1... | collective-permute-start | bytes 6152 | tf_op jit(solution)/shard_map/ppermute | solution.py:429
  245.6 11.9 %collective-permute-done.32.refs_6_ = f32[2,256]{1,0:T(2,128)S(1)} collective-permute-done((f32[2,256]{1,0:T(2,128)S(1)}, f32[2,256]{1,0:T(2,128)S(1)}, u32[]{:S(2)}, u32[]{:S(2)}) %collective-permute-start.32) | collective-permute-done | bytes 2080 | tf_op jit(solution)/shard_map/ppermute | solution.py:429
  (95 shorter events, 48.7 us)
Async XLA Ops:
  14.6 22.9 %collective-permute-start.4 = (bf16[512,256]{1,0:T(8,128)(2,1)S(1)}, bf16[512,256]{1,0:T(8,128)(2,1)S(1)}, u32[]{:S(2)}, u32[]{:S(2)}) collective-permute-start(bf16[512,256]{1,0:T(8,128)(2,1)S(1)} %get-tuple-element.65), channel_id=1, source_target_pairs={{0,20},{4,16},{8,28},{12,24},{16,4},{20,0},{24,12},{28,8},{1,21},{... | collective-permute-start | bytes 786440 | tf_op jit(solution)/shard_map/ppermute | solution.py:428
  14.6 26.5 %collective-permute-start.5 = (bf16[512,256]{1,0:T(8,128)(2,1)S(1)}, bf16[512,256]{1,0:T(8,128)(2,1)S(1)}, u32[]{:S(2)}, u32[]{:S(2)}) collective-permute-start(bf16[512,256]{1,0:T(8,128)(2,1)S(1)} %get-tuple-element.66), channel_id=1, source_target_pairs={{0,24},{4,28},{8,16},{12,20},{16,8},{20,12},{24,0},{28,4},{1,25},{... | collective-permute-start | bytes 786440 | tf_op jit(solution)/shard_map/ppermute | solution.py:428
  20.1 21.1 %collective-permute-start.6 = (bf16[512,256]{1,0:T(8,128)(2,1)S(1)}, bf16[512,256]{1,0:T(8,128)(2,1)S(1)}, u32[]{:S(2)}, u32[]{:S(2)}) collective-permute-start(bf16[512,256]{1,0:T(8,128)(2,1)S(1)} %get-tuple-element.67), channel_id=1, source_target_pairs={{0,28},{4,24},{8,20},{12,16},{16,12},{20,8},{24,4},{28,0},{1,29},{... | collective-permute-start | bytes 786440 | tf_op jit(solution)/shard_map/ppermute | solution.py:428
  25.3 23.0 %collective-permute-start.10 = (bf16[528,256]{1,0:T(8,128)(2,1)S(1)}, bf16[528,256]{1,0:T(8,128)(2,1)S(1)}, u32[]{:S(2)}, u32[]{:S(2)}) collective-permute-start(bf16[528,256]{1,0:T(8,128)(2,1)S(1)} %weight_half.1), channel_id=1, source_target_pairs={{0,1},{1,2},{2,3},{3,0},{4,5},{5,6},{6,7},{7,4},{8,9},{9,10},{10,1... | collective-permute-start | bytes 811016 | tf_op jit(solution)/shard_map/ppermute | solution.py:429
  26.9 24.3 %collective-permute-start.11 = (bf16[528,256]{1,0:T(8,128)(2,1)S(1)}, bf16[528,256]{1,0:T(8,128)(2,1)S(1)}, u32[]{:S(2)}, u32[]{:S(2)}) collective-permute-start(bf16[528,256]{1,0:T(8,128)(2,1)S(1)} %weight_half.1), channel_id=1, source_target_pairs={{0,2},{1,3},{2,0},{3,1},{4,6},{5,7},{6,4},{7,5},{8,10},{9,11},{10,... | collective-permute-start | bytes 811016 | tf_op jit(solution)/shard_map/ppermute | solution.py:429
  37.6 20.6 %collective-permute-start.12 = (bf16[528,256]{1,0:T(8,128)(2,1)S(1)}, bf16[528,256]{1,0:T(8,128)(2,1)S(1)}, u32[]{:S(2)}, u32[]{:S(2)}) collective-permute-start(bf16[528,256]{1,0:T(8,128)(2,1)S(1)} %weight_half.1), channel_id=1, source_target_pairs={{0,3},{1,0},{2,1},{3,2},{4,7},{5,4},{6,5},{7,6},{8,11},{9,8},{10,9... | collective-permute-start | bytes 811016 | tf_op jit(solution)/shard_map/ppermute | solution.py:429
  44.3 23.3 %collective-permute-start.23 = (bf16[256,256]{1,0:T(8,128)(2,1)S(1)}, bf16[256,256]{1,0:T(8,128)(2,1)S(1)}, u32[]{:S(2)}, u32[]{:S(2)}) collective-permute-start(bf16[256,256]{1,0:T(8,128)(2,1)S(1)} %get-tuple-element.85), channel_id=1, source_target_pairs={{0,2},{1,3},{2,0},{3,1},{4,6},{5,7},{6,4},{7,5},{8,10},{9,11},{10,... | collective-permute-start | bytes 393224 | tf_op jit(solution)/shard_map/ppermute | solution.py:429
  48.3 19.3 %collective-permute-start.24 = (bf16[256,256]{1,0:T(8,128)(2,1)S(1)}, bf16[256,256]{1,0:T(8,128)(2,1)S(1)}, u32[]{:S(2)}, u32[]{:S(2)}) collective-permute-start(bf16[256,256]{1,0:T(8,128)(2,1)S(1)} %get-tuple-element.86), channel_id=1, source_target_pairs={{0,3},{1,0},{2,1},{3,2},{4,7},{5,4},{6,5},{7,6},{8,11},{9,8},{10,9... | collective-permute-start | bytes 393224 | tf_op jit(solution)/shard_map/ppermute | solution.py:429
  51.2 20.3 %collective-permute-start.25 = (bf16[256,256]{1,0:T(8,128)(2,1)S(1)}, bf16[256,256]{1,0:T(8,128)(2,1)S(1)}, u32[]{:S(2)}, u32[]{:S(2)}) collective-permute-start(bf16[256,256]{1,0:T(8,128)(2,1)S(1)} %get-tuple-element.88), channel_id=1, source_target_pairs={{0,1},{1,2},{2,3},{3,0},{4,5},{5,6},{6,7},{7,4},{8,9},{9,10},{10,1... | collective-permute-start | bytes 393224 | tf_op jit(solution)/shard_map/ppermute | solution.py:429
  58.2 20.7 %collective-permute-start.26 = (bf16[256,256]{1,0:T(8,128)(2,1)S(1)}, bf16[256,256]{1,0:T(8,128)(2,1)S(1)}, u32[]{:S(2)}, u32[]{:S(2)}) collective-permute-start(bf16[256,256]{1,0:T(8,128)(2,1)S(1)} %get-tuple-element.89), channel_id=1, source_target_pairs={{0,2},{1,3},{2,0},{3,1},{4,6},{5,7},{6,4},{7,5},{8,10},{9,11},{10,... | collective-permute-start | bytes 393224 | tf_op jit(solution)/shard_map/ppermute | solution.py:429
  61.8 21.4 %collective-permute-start.13 = (bf16[528,256]{1,0:T(8,128)(2,1)S(1)}, bf16[528,256]{1,0:T(8,128)(2,1)S(1)}, u32[]{:S(2)}, u32[]{:S(2)}) collective-permute-start(bf16[528,256]{1,0:T(8,128)(2,1)S(1)} %collective-permute-done.10.refs_2_), channel_id=1, source_target_pairs={{0,4},{4,0},{8,12},{12,8},{16,20},{20,16},{24,28},{28,24},{1,5},{5... | collective-permute-start | bytes 811016 | tf_op jit(solution)/shard_map/ppermute | solution.py:457
  71.5 19.7 %collective-permute-start.14 = (bf16[528,256]{1,0:T(8,128)(2,1)S(1)}, bf16[528,256]{1,0:T(8,128)(2,1)S(1)}, u32[]{:S(2)}, u32[]{:S(2)}) collective-permute-start(bf16[528,256]{1,0:T(8,128)(2,1)S(1)} %collective-permute-done.11.refs_3_), channel_id=1, source_target_pairs={{0,4},{4,0},{8,12},{12,8},{16,20},{20,16},{24,28},{28,24},{1,5},{5... | collective-permute-start | bytes 811016 | tf_op jit(solution)/shard_map/ppermute | solution.py:457
  83.1 21.6 %collective-permute-start.20 = (bf16[512,256]{1,0:T(8,128)(2,1)S(1)}, bf16[512,256]{1,0:T(8,128)(2,1)S(1)}, u32[]{:S(2)}, u32[]{:S(2)}) collective-permute-start(bf16[512,256]{1,0:T(8,128)(2,1)S(1)} %get-tuple-element.81), channel_id=1, source_target_pairs={{0,2},{1,3},{2,0},{3,1},{4,6},{5,7},{6,4},{7,5},{8,10},{9,11},{10,... | collective-permute-start | bytes 786440 | tf_op jit(solution)/shard_map/ppermute | solution.py:429
  83.2 21.5 %collective-permute-start.21 = (bf16[512,256]{1,0:T(8,128)(2,1)S(1)}, bf16[512,256]{1,0:T(8,128)(2,1)S(1)}, u32[]{:S(2)}, u32[]{:S(2)}) collective-permute-start(bf16[512,256]{1,0:T(8,128)(2,1)S(1)} %get-tuple-element.82), channel_id=1, source_target_pairs={{0,3},{1,0},{2,1},{3,2},{4,7},{5,4},{6,5},{7,6},{8,11},{9,8},{10,9... | collective-permute-start | bytes 786440 | tf_op jit(solution)/shard_map/ppermute | solution.py:429
  91.1 41.5 %collective-permute-start.17 = (bf16[512,256]{1,0:T(8,128)(2,1)S(1)}, bf16[512,256]{1,0:T(8,128)(2,1)S(1)}, u32[]{:S(2)}, u32[]{:S(2)}) collective-permute-start(bf16[512,256]{1,0:T(8,128)(2,1)S(1)} %get-tuple-element.77), channel_id=1, source_target_pairs={{0,2},{1,3},{2,0},{3,1},{4,6},{5,7},{6,4},{7,5},{8,10},{9,11},{10,... | collective-permute-start | bytes 786440 | tf_op jit(solution)/shard_map/ppermute | solution.py:429
  93.2 39.5 %collective-permute-start.18 = (bf16[512,256]{1,0:T(8,128)(2,1)S(1)}, bf16[512,256]{1,0:T(8,128)(2,1)S(1)}, u32[]{:S(2)}, u32[]{:S(2)}) collective-permute-start(bf16[512,256]{1,0:T(8,128)(2,1)S(1)} %get-tuple-element.78), channel_id=1, source_target_pairs={{0,3},{1,0},{2,1},{3,2},{4,7},{5,4},{6,5},{7,6},{8,11},{9,8},{10,9... | collective-permute-start | bytes 786440 | tf_op jit(solution)/shard_map/ppermute | solution.py:429
  94.3 40.9 %collective-permute-start.7 = (bf16[512,256]{1,0:T(8,128)(2,1)S(1)}, bf16[512,256]{1,0:T(8,128)(2,1)S(1)}, u32[]{:S(2)}, u32[]{:S(2)}) collective-permute-start(bf16[512,256]{1,0:T(8,128)(2,1)S(1)} %get-tuple-element.70), channel_id=1, source_target_pairs={{0,1},{1,2},{2,3},{3,0},{4,5},{5,6},{6,7},{7,4},{8,9},{9,10},{10,1... | collective-permute-start | bytes 786440 | tf_op jit(solution)/shard_map/ppermute | solution.py:429
  104.7 39.2 %collective-permute-start.8 = (bf16[512,256]{1,0:T(8,128)(2,1)S(1)}, bf16[512,256]{1,0:T(8,128)(2,1)S(1)}, u32[]{:S(2)}, u32[]{:S(2)}) collective-permute-start(bf16[512,256]{1,0:T(8,128)(2,1)S(1)} %get-tuple-element.71), channel_id=1, source_target_pairs={{0,2},{1,3},{2,0},{3,1},{4,6},{5,7},{6,4},{7,5},{8,10},{9,11},{10,... | collective-permute-start | bytes 786440 | tf_op jit(solution)/shard_map/ppermute | solution.py:429
  104.7 39.2 %collective-permute-start.9 = (bf16[512,256]{1,0:T(8,128)(2,1)S(1)}, bf16[512,256]{1,0:T(8,128)(2,1)S(1)}, u32[]{:S(2)}, u32[]{:S(2)}) collective-permute-start(bf16[512,256]{1,0:T(8,128)(2,1)S(1)} %get-tuple-element.72), channel_id=1, source_target_pairs={{0,3},{1,0},{2,1},{3,2},{4,7},{5,4},{6,5},{7,6},{8,11},{9,8},{10,9... | collective-permute-start | bytes 786440 | tf_op jit(solution)/shard_map/ppermute | solution.py:429
  156.2 21.8 %collective-permute-start.40 = (bf16[256,256]{1,0:T(8,128)(2,1)S(1)}, bf16[256,256]{1,0:T(8,128)(2,1)S(1)}, u32[]{:S(2)}, u32[]{:S(2)}) collective-permute-start(bf16[256,256]{1,0:T(8,128)(2,1)S(1)} %get-tuple-element.109), channel_id=1, source_target_pairs={{0,3},{1,0},{2,1},{3,2},{4,7},{5,4},{6,5},{7,6},{8,11},{9,8},{10,9... | collective-permute-start | bytes 393224 | tf_op jit(solution)/shard_map/ppermute | solution.py:429
  160.4 21.0 %collective-permute-start.41 = (bf16[256,256]{1,0:T(8,128)(2,1)S(1)}, bf16[256,256]{1,0:T(8,128)(2,1)S(1)}, u32[]{:S(2)}, u32[]{:S(2)}) collective-permute-start(bf16[256,256]{1,0:T(8,128)(2,1)S(1)} %get-tuple-element.110), channel_id=1, source_target_pairs={{0,2},{1,3},{2,0},{3,1},{4,6},{5,7},{6,4},{7,5},{8,10},{9,11},{10,... | collective-permute-start | bytes 393224 | tf_op jit(solution)/shard_map/ppermute | solution.py:429
  178.0 39.3 %collective-permute-start.34 = (bf16[512,256]{1,0:T(8,128)(2,1)S(1)}, bf16[512,256]{1,0:T(8,128)(2,1)S(1)}, u32[]{:S(2)}, u32[]{:S(2)}) collective-permute-start(bf16[512,256]{1,0:T(8,128)(2,1)S(1)} %get-tuple-element.101), channel_id=1, source_target_pairs={{0,3},{1,0},{2,1},{3,2},{4,7},{5,4},{6,5},{7,6},{8,11},{9,8},{10,9... | collective-permute-start | bytes 786440 | tf_op jit(solution)/shard_map/ppermute | solution.py:429
  181.4 35.9 %collective-permute-start.37 = (bf16[512,256]{1,0:T(8,128)(2,1)S(1)}, bf16[512,256]{1,0:T(8,128)(2,1)S(1)}, u32[]{:S(2)}, u32[]{:S(2)}) collective-permute-start(bf16[512,256]{1,0:T(8,128)(2,1)S(1)} %get-tuple-element.105), channel_id=1, source_target_pairs={{0,3},{1,0},{2,1},{3,2},{4,7},{5,4},{6,5},{7,6},{8,11},{9,8},{10,9... | collective-permute-start | bytes 786440 | tf_op jit(solution)/shard_map/ppermute | solution.py:429
  181.5 39.7 %collective-permute-start.38 = (bf16[512,256]{1,0:T(8,128)(2,1)S(1)}, bf16[512,256]{1,0:T(8,128)(2,1)S(1)}, u32[]{:S(2)}, u32[]{:S(2)}) collective-permute-start(bf16[512,256]{1,0:T(8,128)(2,1)S(1)} %get-tuple-element.106), channel_id=1, source_target_pairs={{0,2},{1,3},{2,0},{3,1},{4,6},{5,7},{6,4},{7,5},{8,10},{9,11},{10,... | collective-permute-start | bytes 786440 | tf_op jit(solution)/shard_map/ppermute | solution.py:429
  181.5 39.7 %collective-permute-start.39 = (bf16[512,256]{1,0:T(8,128)(2,1)S(1)}, bf16[512,256]{1,0:T(8,128)(2,1)S(1)}, u32[]{:S(2)}, u32[]{:S(2)}) collective-permute-start(bf16[512,256]{1,0:T(8,128)(2,1)S(1)} %get-tuple-element.107), channel_id=1, source_target_pairs={{0,1},{1,2},{2,3},{3,0},{4,5},{5,6},{6,7},{7,4},{8,9},{9,10},{10,1... | collective-permute-start | bytes 786440 | tf_op jit(solution)/shard_map/ppermute | solution.py:429
  183.6 25.9 %collective-permute-start.45 = (bf16[256,256]{1,0:T(8,128)(2,1)S(1)}, bf16[256,256]{1,0:T(8,128)(2,1)S(1)}, u32[]{:S(2)}, u32[]{:S(2)}) collective-permute-start(bf16[256,256]{1,0:T(8,128)(2,1)S(1)} %get-tuple-element.115), channel_id=1, source_target_pairs={{0,1},{1,2},{2,3},{3,0},{4,5},{5,6},{6,7},{7,4},{8,9},{9,10},{10,1... | collective-permute-start | bytes 393224 | tf_op jit(solution)/shard_map/ppermute | solution.py:429
  209.6 26.7 %collective-permute-start.35 = (bf16[512,256]{1,0:T(8,128)(2,1)S(1)}, bf16[512,256]{1,0:T(8,128)(2,1)S(1)}, u32[]{:S(2)}, u32[]{:S(2)}) collective-permute-start(bf16[512,256]{1,0:T(8,128)(2,1)S(1)} %get-tuple-element.102), channel_id=1, source_target_pairs={{0,2},{1,3},{2,0},{3,1},{4,6},{5,7},{6,4},{7,5},{8,10},{9,11},{10,... | collective-permute-start | bytes 786440 | tf_op jit(solution)/shard_map/ppermute | solution.py:429
  217.3 40.2 %collective-permute-start.28 = (bf16[512,256]{1,0:T(8,128)(2,1)S(1)}, bf16[512,256]{1,0:T(8,128)(2,1)S(1)}, u32[]{:S(2)}, u32[]{:S(2)}) collective-permute-start(bf16[512,256]{1,0:T(8,128)(2,1)S(1)} %get-tuple-element.96), channel_id=1, source_target_pairs={{0,3},{1,0},{2,1},{3,2},{4,7},{5,4},{6,5},{7,6},{8,11},{9,8},{10,9... | collective-permute-start | bytes 786440 | tf_op jit(solution)/shard_map/ppermute | solution.py:429
  221.2 36.4 %collective-permute-start.29 = (bf16[512,256]{1,0:T(8,128)(2,1)S(1)}, bf16[512,256]{1,0:T(8,128)(2,1)S(1)}, u32[]{:S(2)}, u32[]{:S(2)}) collective-permute-start(bf16[512,256]{1,0:T(8,128)(2,1)S(1)} %get-tuple-element.97), channel_id=1, source_target_pairs={{0,2},{1,3},{2,0},{3,1},{4,6},{5,7},{6,4},{7,5},{8,10},{9,11},{10,... | collective-permute-start | bytes 786440 | tf_op jit(solution)/shard_map/ppermute | solution.py:429
  221.2 36.4 %collective-permute-start.30 = (bf16[512,256]{1,0:T(8,128)(2,1)S(1)}, bf16[512,256]{1,0:T(8,128)(2,1)S(1)}, u32[]{:S(2)}, u32[]{:S(2)}) collective-permute-start(bf16[512,256]{1,0:T(8,128)(2,1)S(1)} %get-tuple-element.98), channel_id=1, source_target_pairs={{0,1},{1,2},{2,3},{3,0},{4,5},{5,6},{6,7},{7,4},{8,9},{9,10},{10,1... | collective-permute-start | bytes 786440 | tf_op jit(solution)/shard_map/ppermute | solution.py:429
  236.3 21.3 %collective-permute-start.32 = (f32[2,256]{1,0:T(2,128)S(1)}, f32[2,256]{1,0:T(2,128)S(1)}, u32[]{:S(2)}, u32[]{:S(2)}) collective-permute-start(f32[2,256]{1,0:T(2,128)S(1)} %get-tuple-element.117), channel_id=1, source_target_pairs={{0,2},{1,3},{2,0},{3,1},{4,6},{5,7},{6,4},{7,5},{8,10},{9,11},{10,... | collective-permute-start | bytes 6152 | tf_op jit(solution)/shard_map/ppermute | solution.py:429
  236.3 21.3 %collective-permute-start.33 = (f32[2,256]{1,0:T(2,128)S(1)}, f32[2,256]{1,0:T(2,128)S(1)}, u32[]{:S(2)}, u32[]{:S(2)}) collective-permute-start(f32[2,256]{1,0:T(2,128)S(1)} %get-tuple-element.116), channel_id=1, source_target_pairs={{0,1},{1,2},{2,3},{3,0},{4,5},{5,6},{6,7},{7,4},{8,9},{9,10},{10,1... | collective-permute-start | bytes 6152 | tf_op jit(solution)/shard_map/ppermute | solution.py:429
  (20 other events, 360.0 us)

commit v2 on v1

--- a/solution.py
+++ b/solution.py
@@ -51,7 +51,7 @@
     return tiled.transpose(0, 2, 1, 3).reshape(-1), first, within
 
 
-def widen(feat, tables, raw, sems):
+def widen(feat, table, raw, sems):
     n_rows = raw.shape[0]
     parts = sems.shape[0]
     part = n_rows // parts
@@ -68,9 +68,11 @@
         copies[c].wait()
 
         def one(b, carry, c=c):
-            at = pl.ds(pl.multiple_of(c * part + b * step, step), step)
-            for h, table in enumerate(tables):
-                table[at, :] = raw[at, pl.ds(h * LANES, LANES)].astype(jnp.float32)
+            row = pl.multiple_of(c * part + b * step, step)
+            halves = raw.shape[1] // LANES
+            for h in range(halves):
+                wide = raw[pl.ds(row, step), pl.ds(h * LANES, LANES)].astype(jnp.float32)
+                table[pl.ds(row * halves + h, step, stride=halves), :] = wide
             return carry
 
         lax.fori_loop(0, part // step, one, 0)
@@ -78,77 +80,71 @@
 
 def gather_kernel(peers, peer, first_row, within, first, halves, rows_in, counts_in, *refs):
     n_out = len(peers)
-    refs = list(refs)
     if first:
-        feat = refs.pop(0)
-        outs, tables = refs[:n_out], refs[n_out : n_out + halves]
-        raw = refs[n_out + halves]
-        refs = refs[n_out + halves + 1 :]
+        feat, outs, (table, raw) = refs[0], refs[1 : n_out + 1], refs[n_out + 1 : n_out + 3]
+        rows, counts, index_sems, stage, sems = refs[n_out + 3 :]
     else:
-        tables, outs = refs[:halves], refs[halves : halves + n_out]
-        refs = refs[halves + n_out :]
-    rows, counts, index_sems = refs[:3]
-    stages = refs[3 : 3 + halves]
+        table, outs = refs[0], refs[1 : n_out + 1]
+        rows, counts, index_sems, stage = refs[n_out + 1 :]
     load_rows = pltpu.make_async_copy(rows_in, rows, index_sems.at[0])
     load_counts = pltpu.make_async_copy(counts_in, counts, index_sems.at[1])
     load_rows.start()
     load_counts.start()
     if first:
-        widen(feat, tables, raw, refs[3 + halves])
+        widen(feat, table, raw, sems)
     load_rows.wait()
     load_counts.wait()
     me = lax.axis_index("dom")
-    slots = stages[0].shape[0]
+    slots = outs[0].shape[0]
     for out, k in zip(outs, peers):
         q = peer(me, k)
         used = counts[q]
-
         begin = first_row(q)
 
         def pick(b, carry, begin=begin):
             base = begin + within(b)
+            put = pl.multiple_of(b * (UNROLL * halves), UNROLL * halves)
             source = [rows[base + j] for j in range(UNROLL)]
-            for table, stage in zip(tables, stages):
-                got = [table[pl.ds(r, 1), :] for r in source]
-                for j in range(UNROLL):
-                    stage[pl.ds(b * UNROLL + j, 1), :] = got[j]
+            got = [table[pl.ds(r * halves, halves), :] for r in source]
+            for j in range(UNROLL):
+                stage[pl.ds(put + j * halves, halves), :] = got[j]
             return carry
 
         lax.fori_loop(0, (used + UNROLL - 1) // UNROLL, pick, 0)
         for b in range(slots // 64):
-            at = pl.ds(b * 64, 64)
             slot = b * 64 + lax.broadcasted_iota(jnp.int32, (64, LANES), 0)
-            for h, stage in enumerate(stages):
-                kept = jnp.where(slot < used, stage[at, :], 0.0)
-                out[at, pl.ds(h * LANES, LANES)] = kept.astype(out.dtype)
-
-
-def gather_rows(rows, first_row, within, send_count, features, tables, peers, peer, slots):
+            for h in range(halves):
+                wide = stage[pl.ds(b * 64 * halves + h, 64, stride=halves), :]
+                kept = jnp.where(slot < used, wide, 0.0)
+                out[pl.ds(b * 64, 64), pl.ds(h * LANES, LANES)] = kept.astype(out.dtype)
+
+
+def gather_rows(rows, first_row, within, send_count, features, table, peers, peer, slots):
     n_rows, width = features.shape
     halves = width // LANES
-    first = not tables
+    first = table is None
     piece = jax.ShapeDtypeStruct((slots, width), features.dtype)
-    table = jax.ShapeDtypeStruct((n_rows, LANES), jnp.float32)
     parts = 8 if n_rows % (8 * 64) == 0 else 1
+    made = [
+        jax.ShapeDtypeStruct((n_rows * halves, LANES), jnp.float32),
+        jax.ShapeDtypeStruct(features.shape, features.dtype),
+    ]
     out = pl.pallas_call(
         functools.partial(gather_kernel, peers, peer, first_row, within, first, halves),
-        out_shape=[piece] * len(peers)
-        + ([table] * halves + [pltpu.VMEM(features.shape, features.dtype)]) * first,
-        in_specs=[RAW, RAW] + ([RAW] if first else [VMEM] * halves),
-        out_specs=[VMEM] * (len(peers) + (halves + 1) * first),
+        out_shape=[piece] * len(peers) + made * first,
+        in_specs=[RAW, RAW, RAW if first else VMEM],
+        out_specs=[VMEM] * (len(peers) + 2 * first),
         scratch_shapes=[
             pltpu.SMEM(rows.shape, jnp.int32),
             pltpu.SMEM(send_count.shape, jnp.int32),
             pltpu.SemaphoreType.DMA((2,)),
+            pltpu.VMEM((slots * halves, LANES), jnp.float32),
         ]
-        + [pltpu.VMEM((slots, LANES), jnp.float32)] * halves
-        + (
-            [pltpu.SemaphoreType.DMA((parts,))] if first else []
-        ),
+        + [pltpu.SemaphoreType.DMA((parts,))] * first,
         compiler_params=grant(18 + len(peers) if first else 4),
         cost_estimate=cost(4e9, 6 << 20),
         name="gather_rows",
-    )(in_hbm(rows), in_hbm(send_count), *([in_hbm(features)] if first else tables))
+    )(in_hbm(rows), in_hbm(send_count), in_hbm(features) if first else table)
     return out[: len(peers)], out[len(peers) :]
 
 
@@ -234,76 +230,96 @@
     )
 
 
-def half_kernel(share, weight, bias, out, sem):
-    half = weight.shape[0] // share
-    start = lax.rem(lax.axis_index("dom"), share) * half
-    src = weight.at[pl.ds(pl.multiple_of(start, half), half)]
-    copy = pltpu.make_async_copy(src, out.at[pl.ds(0, half)], sem)
+PAD = 16
+
+
+def part_kernel(share, weight, bias, out, sem):
+    part = weight.shape[0] // share
+    start = lax.rem(lax.axis_index("dom"), share) * part
+    src = weight.at[pl.ds(pl.multiple_of(start, part), part)]
+    copy = pltpu.make_async_copy(src, out.at[pl.ds(0, part)], sem)
     copy.start()
-    tail = (out.shape[0] - half, out.shape[1])
-    out[pl.ds(half, tail[0]), :] = jnp.broadcast_to(bias[...], tail)
+    out[pl.ds(part, PAD), :] = jnp.broadcast_to(bias[...], (PAD, out.shape[1]))
     copy.wait()
 
 
-def weight_half(weight, bias, share):
-    rows = weight.shape[0] // share + 16
+def weight_part(weight, bias, share):
+    rows = weight.shape[0] // share + PAD
     return pl.pallas_call(
-        functools.partial(half_kernel, share),
+        functools.partial(part_kernel, share),
         out_shape=jax.ShapeDtypeStruct((rows, weight.shape[1]), weight.dtype),
         in_specs=[RAW, VMEM],
         out_specs=VMEM,
         scratch_shapes=[pltpu.SemaphoreType.DMA],
         compiler_params=grant(4),
         cost_estimate=cost(1e8, 1 << 20),
-        name="weight_half",
+        name="weight_part",
     )(in_hbm(weight), bias)
 
 
-def join_kernel(n_col, share, *refs):
-    own, own_bias = refs[:2]
-    mine = refs[2 : n_col + 1]
-    theirs = refs[n_col + 1 : -2] or mine
-    joined, bias = refs[-2:]
+def pack_kernel(*refs):
+    rows = refs[0].shape[0]
+    for k, ref in enumerate(refs[:-1]):
+        refs[-1][pl.ds(k * rows, rows), :] = ref[...]
+
+
+def pack_rows(arrays):
+    rows, width = arrays[0].shape
+    return pl.pallas_call(
+        pack_kernel,
+        out_shape=jax.ShapeDtypeStruct((rows * len(arrays), width), arrays[0].dtype),
+        in_specs=[VMEM] * len(arrays),
+        out_specs=VMEM,
+        compiler_params=grant(4),
+        cost_estimate=cost(1e8, 1 << 20),
+        name="pack_rows",
+    )(*arrays)
+
+
+def join_kernel(n_col, share, own, own_bias, *refs):
+    parts = refs[:share]
+    joined, bias = refs[share:]
     width = own.shape[1]
-    half = own.shape[0] // share
-    odd = lax.rem(lax.axis_index("dom"), share)
+    part = own.shape[0] // share
+    me = lax.rem(lax.axis_index("dom"), share)
+    block = min(width, part)
     for s in range(n_col):
-        row = lax.rem(lax.axis_index("col") + n_col - s, n_col) * width
-        at = pl.ds(s * width, width)
-        joined[0, at, :] = own[pl.ds(pl.multiple_of(row, width), width), :]
-        side = lax.div(row, half)
-        row = pl.ds(pl.multiple_of(row - side * half, width), width)
-        for k in range(1, n_col):
-
-            @pl.when(side == odd)
-            def _(k=k, at=at, row=row):
-                joined[k, at, :] = mine[k - 1][row, :]
-
-            @pl.when(side != odd)
-            def _(k=k, at=at, row=row):
-                joined[k, at, :] = theirs[k - 1][row, :]
+        for b in range(width // block):
+            row = lax.rem(lax.axis_index("col") + n_col - s, n_col) * width + b * block
+            row = pl.multiple_of(row, block)
+            at = pl.ds(s * width + b * block, block)
+            joined[0, at, :] = own[pl.ds(row, block), :]
+            side = lax.div(row, part)
+            offset = row - side * part
+            for flip in range(share):
+
+                @pl.when(side == me ^ flip)
+                def _(flip=flip, at=at, offset=offset):
+                    for k in range(1, n_col):
+                        start = pl.multiple_of((k - 1) * (part + PAD) + offset, PAD)
+                        joined[k, at, :] = parts[flip][pl.ds(start, block), :]
 
     bias[pl.ds(0, 1), :] = own_bias[...].astype(jnp.float32)
     for k in range(1, n_col):
-        got = mine[k - 1][pl.ds(half, 16), :].astype(jnp.float32)
+        got = parts[0][pl.ds(k * part + (k - 1) * PAD, PAD), :].astype(jnp.float32)
         bias[pl.ds(k, 1), :] = got[:1]
 
 
-def join_weights(weight, bias, mine, theirs, share):
-    n_col = len(mine) + 1
+def join_weights(weight, bias, parts, n_col):
     channels, width = weight.shape
+    share = len(parts)
     return pl.pallas_call(
         functools.partial(join_kernel, n_col, share),
         out_shape=[
             jax.ShapeDtypeStruct((n_col, channels, width), weight.dtype),
             jax.ShapeDtypeStruct((n_col, width), jnp.float32),
         ],
-        in_specs=[VMEM] * (2 + len(mine) + len(theirs)),
+        in_specs=[VMEM] * (2 + share),
         out_specs=[VMEM] * 2,
         compiler_params=grant(8),
         cost_estimate=cost(1e9, 4 << 20),
         name="join_weights",
-    )(weight, bias, *mine, *theirs)
+    )(weight, bias, *parts)
 
 
 def mix_kernel(n_col, channels, first, *refs):
@@ -432,30 +448,35 @@
     halo = [None] * (n_dom - 1)
     rows, first_row, within = storage_order(send_rows[0])
     slots = send_rows.shape[2]
-    tables, own_tiles = [], features
+    table, own_tiles = None, features
     cut = (n_dom - 1) // 2
     for peers in (far[:cut], far[cut:]):
         if not peers:
             continue
         outgoing, made = gather_rows(
-            rows, first_row, within, send_count[0], features, tables, peers, peer, slots
+            rows, first_row, within, send_count[0], features, table, peers, peer, slots
         )
         if made:
-            tables, own_tiles = made[:-1], made[-1]
+            table, own_tiles = made
         for k, piece in zip(peers, outgoing):
             halo[k - 1] = along_dom(piece, k)
 
-    share = 2 if n_dom % 2 == 0 else 1
+    share = 1
+    while share < min(4, n_col) and n_dom % (2 * share) == 0:
+        share *= 2
     order = sorted(range(1, n_col), key=lambda k: min(k, n_col - k), reverse=True)
     bias_row = out_bias.reshape(1, width)
-    mine = weight_half(weight, bias_row, share)
+    mine = weight_part(weight, bias_row, share)
     arrived = {k: along_col(mine, k) for k in order}
-    mine = [arrived[k] for k in range(1, n_col)]
-    theirs = []
-    if share == 2:
-        swap = [(i, i ^ 1) for i in range(n_dom)]
-        theirs = [lax.ppermute(got, "dom", swap) for got in mine]
-    weights, bias = join_weights(weight, bias_row, mine, theirs, share)
+    parts = [pack_rows([arrived[k] for k in range(1, n_col)])]
+    step = share // 2
+    got = {0: parts[0]}
+    while step:
+        swap = [(i, i ^ step) for i in range(n_dom)]
+        for flip in list(got):
+            got[flip ^ step] = lax.ppermute(got[flip], "dom", swap)
+        step //= 2
+    weights, bias = join_weights(weight, bias_row, [got[f] for f in range(share)], n_col)
 
     plan = chunk_plan(n_rows // TILE // n_col)
     index_tables = (local_index[0].T, local_count[0], halo_index[0].T, halo_count[0])

time: 260 us -> 264 us (1.015)
  waiting for transfers between devices: 84.7 us -> 87.8 us
    ppermute x7, waiting for transfers between devices: 13.9 us -> 19.2 us  [on_device(): lax.ppermute(x, 'dom', [(i, peer(i, k)) for i in range(n_dom)])]
    ppermute x36, starting transfers between devices: 111 us -> 114 us  [on_device(): lax.ppermute(x, 'col', [(i, (i + k) % n_col) for i in range(n_col)])]
where the time goes in v2:
time: 264 us; the launch traced here: 263 us
  starting transfers between devices  122 us (46%)
  waiting for transfers between devices  87.8 us (33%)
  Pallas kernels  42.8 us (16%)
  blocking collectives  8.95 us (3%)
    ppermute x36, starting transfers between devices, on_device(): lax.ppermute(x, 'col', [(i, (i + k) % n_col) for i in range(n_col)])  114 us
    ppermute x36, waiting for transfers between devices, on_device(): lax.ppermute(x, 'col', [(i, (i + k) % n_col) for i in range(n_col)])  68.6 us
    ppermute x7, waiting for transfers between devices, on_device(): lax.ppermute(x, 'dom', [(i, peer(i, k)) for i in range(n_dom)])  19.2 us
    pallas_call x5, Pallas kernels, tile_sums(): pl.pallas_call(functools.partial(sum_kernel, n_dom, n_col, peer, slots, p...  18.4 us
    pallas_call x5, Pallas kernels, mix_rows(): pl.pallas_call(functools.partial(mix_kernel, n_col, channels, first), out...  10.2 us
    all_gather x1, blocking collectives, on_device(): over_dom = lax.all_gather(stats, 'dom', axis=0)  8.95 us
    ppermute x7, starting transfers between devices, on_device(): lax.ppermute(x, 'dom', [(i, peer(i, k)) for i in range(n_dom)])  8.02 us
    pallas_call x2, Pallas kernels, gather_rows(): pl.pallas_call(functools.partial(gather_kernel, peers, peer, first_row, w...  7.78 us
  transfers between devices with their start and end apart: 46, of which 13 were waited for; matrix products, arithmetic and copies ran while one was open for 0% of the time, Pallas kernels for 12%

profile of v2, /device:TPU:0, one launch (start us, length us, event | category | flops | bytes accessed | tf_op | source)
XLA Modules:
  0.0 263.2 jit_solution(8668433337745056965)
XLA Ops:
  0.6 4.0 %gather_rows.2 = (bf16[512,256]{1,0:T(8,128)(2,1)S(1)}, bf16[512,256]{1,0:T(8,128)(2,1)S(1)}, bf16[512,256]{1,0:T(8,128)(2,1)S(1)}, f32[16384,128]{1,0:T(8,128)S(1)}, bf16[8192,256]{1,0:T(8,128)(2,1)S(1)}) custom-call(s32[4096]{0:T(1024)} %bitcast.78, s32[8]{0:T(128)} %bitcast.80, bf16[8192,256]{1,0:T(8,128)(2,1)} %refs_0_.1), custom_call_target="tpu_custom_call" | custom-call | flops 4000000000 | bytes 6291456 | tf_op jit(solution)/shard_map/gather_rows/pallas_call | solution.py:132
  4.7 3.8 %gather_rows.3 = (bf16[512,256]{1,0:T(8,128)(2,1)S(1)}, bf16[512,256]{1,0:T(8,128)(2,1)S(1)}, bf16[512,256]{1,0:T(8,128)(2,1)S(1)}, bf16[512,256]{1,0:T(8,128)(2,1)S(1)}) custom-call(s32[4096]{0:T(1024)} %bitcast.79, s32[8]{0:T(128)} %bitcast.81, f32[16384,128]{1,0:T(8,128)S(1)} %get-tuple-element.58.refs_0_), custom_call_target="tpu_custom_call" | custom-call | flops 4000000000 | bytes 6291456 | tf_op jit(solution)/shard_map/gather_rows/pallas_call | solution.py:132
  9.1 3.1 %collective-permute-start.1 = (bf16[512,256]{1,0:T(8,128)(2,1)S(1)}, bf16[512,256]{1,0:T(8,128)(2,1)S(1)}, u32[]{:S(2)}, u32[]{:S(2)}) collective-permute-start(bf16[512,256]{1,0:T(8,128)(2,1)S(1)} %get-tuple-element.60), channel_id=1, source_target_pairs={{0,8},{4,12},{8,0},{12,4},{16,24},{20,28},{24,16},{28,20},{1,9},{5... | collective-permute-start | bytes 786440 | tf_op jit(solution)/shard_map/ppermute | solution.py:444
  21.5 5.2 %collective-permute-done.11.refs_1_ = bf16[272,256]{1,0:T(8,128)(2,1)S(1)} collective-permute-done((bf16[272,256]{1,0:T(8,128)(2,1)S(1)}, bf16[272,256]{1,0:T(8,128)(2,1)S(1)}, u32[]{:S(2)}, u32[]{:S(2)}) %collective-permute-start.11) | collective-permute-done | bytes 139296 | tf_op jit(solution)/shard_map/ppermute | solution.py:445
  31.5 15.6 %collective-permute-done.3.refs_3_ = bf16[512,256]{1,0:T(8,128)(2,1)S(1)} collective-permute-done((bf16[512,256]{1,0:T(8,128)(2,1)S(1)}, bf16[512,256]{1,0:T(8,128)(2,1)S(1)}, u32[]{:S(2)}, u32[]{:S(2)}) %collective-permute-start.3) | collective-permute-done | bytes 262176 | tf_op jit(solution)/shard_map/ppermute | solution.py:444
  47.2 3.5 %collective-permute-done.4.refs_4_ = bf16[512,256]{1,0:T(8,128)(2,1)S(1)} collective-permute-done((bf16[512,256]{1,0:T(8,128)(2,1)S(1)}, bf16[512,256]{1,0:T(8,128)(2,1)S(1)}, u32[]{:S(2)}, u32[]{:S(2)}) %collective-permute-start.4) | collective-permute-done | bytes 262176 | tf_op jit(solution)/shard_map/ppermute | solution.py:444
  50.7 3.0 %tile_sums.8 = (bf16[256,256]{1,0:T(8,128)(2,1)S(1)}, bf16[256,256]{1,0:T(8,128)(2,1)S(1)}, bf16[256,256]{1,0:T(8,128)(2,1)S(1)}, bf16[256,256]{1,0:T(8,128)(2,1)S(1)}) custom-call(s32[4,64]{1,0:T(4,128)S(1)} %bitcast.18, s32[64]{0:T(128)S(1)} %bitcast.28, s32[4,64]{1,0:T(4,128)S(1)} %bitcast.23, s32[64]{0:T(128)S(1)} %bitcast.33, ...), custom_call_target="tpu_custom_call" | custom-call | flops 2000000000 | bytes 6291456 | tf_op jit(solution)/shard_map/tile_sums/pallas_call | solution.py:214
  54.7 3.4 %collective-permute-start.23 = (bf16[256,256]{1,0:T(8,128)(2,1)S(1)}, bf16[256,256]{1,0:T(8,128)(2,1)S(1)}, u32[]{:S(2)}, u32[]{:S(2)}) collective-permute-start(bf16[256,256]{1,0:T(8,128)(2,1)S(1)} %get-tuple-element.83), channel_id=1, source_target_pairs={{0,2},{1,3},{2,0},{3,1},{4,6},{5,7},{6,4},{7,5},{8,10},{9,11},{10,... | collective-permute-start | bytes 393224 | tf_op jit(solution)/shard_map/ppermute | solution.py:445
  59.0 3.0 %tile_sums.9 = (bf16[256,256]{1,0:T(8,128)(2,1)S(1)}, bf16[256,256]{1,0:T(8,128)(2,1)S(1)}, bf16[256,256]{1,0:T(8,128)(2,1)S(1)}, bf16[256,256]{1,0:T(8,128)(2,1)S(1)}) custom-call(s32[4,64]{1,0:T(4,128)S(1)} %bitcast.19, s32[64]{0:T(128)S(1)} %bitcast.29, s32[4,64]{1,0:T(4,128)S(1)} %bitcast.24, s32[64]{0:T(128)S(1)} %bitcast.34, ...), custom_call_target="tpu_custom_call" | custom-call | flops 2000000000 | bytes 6291456 | tf_op jit(solution)/shard_map/tile_sums/pallas_call | solution.py:214
  63.2 4.1 %tile_sums.6 = (bf16[512,256]{1,0:T(8,128)(2,1)S(1)}, bf16[512,256]{1,0:T(8,128)(2,1)S(1)}, bf16[512,256]{1,0:T(8,128)(2,1)S(1)}, bf16[512,256]{1,0:T(8,128)(2,1)S(1)}) custom-call(s32[4,64]{1,0:T(4,128)S(1)} %bitcast.20, s32[64]{0:T(128)S(1)} %bitcast.30, s32[4,64]{1,0:T(4,128)S(1)} %bitcast.25, s32[64]{0:T(128)S(1)} %bitcast.35, ...), custom_call_target="tpu_custom_call" | custom-call | flops 2000000000 | bytes 6291456 | tf_op jit(solution)/shard_map/tile_sums/pallas_call | solution.py:214
  68.3 10.1 %collective-permute-start.26 = (bf16[256,256]{1,0:T(8,128)(2,1)S(1)}, bf16[256,256]{1,0:T(8,128)(2,1)S(1)}, u32[]{:S(2)}, u32[]{:S(2)}) collective-permute-start(bf16[256,256]{1,0:T(8,128)(2,1)S(1)} %get-tuple-element.87), channel_id=1, source_target_pairs={{0,2},{1,3},{2,0},{3,1},{4,6},{5,7},{6,4},{7,5},{8,10},{9,11},{10,... | collective-permute-start | bytes 393224 | tf_op jit(solution)/shard_map/ppermute | solution.py:445
  78.4 3.4 %collective-permute-start.27 = (bf16[256,256]{1,0:T(8,128)(2,1)S(1)}, bf16[256,256]{1,0:T(8,128)(2,1)S(1)}, u32[]{:S(2)}, u32[]{:S(2)}) collective-permute-start(bf16[256,256]{1,0:T(8,128)(2,1)S(1)} %get-tuple-element.88), channel_id=1, source_target_pairs={{0,3},{1,0},{2,1},{3,2},{4,7},{5,4},{6,5},{7,6},{8,11},{9,8},{10,9... | collective-permute-start | bytes 393224 | tf_op jit(solution)/shard_map/ppermute | solution.py:445
  81.7 4.1 %tile_sums.7 = (bf16[512,256]{1,0:T(8,128)(2,1)S(1)}, bf16[512,256]{1,0:T(8,128)(2,1)S(1)}, bf16[512,256]{1,0:T(8,128)(2,1)S(1)}, bf16[512,256]{1,0:T(8,128)(2,1)S(1)}) custom-call(s32[4,64]{1,0:T(4,128)S(1)} %bitcast.21, s32[64]{0:T(128)S(1)} %bitcast.31, s32[4,64]{1,0:T(4,128)S(1)} %bitcast.26, s32[64]{0:T(128)S(1)} %bitcast.36, ...), custom_call_target="tpu_custom_call" | custom-call | flops 2000000000 | bytes 6291456 | tf_op jit(solution)/shard_map/tile_sums/pallas_call | solution.py:214
  88.3 3.4 %collective-permute-start.20 = (bf16[512,256]{1,0:T(8,128)(2,1)S(1)}, bf16[512,256]{1,0:T(8,128)(2,1)S(1)}, u32[]{:S(2)}, u32[]{:S(2)}) collective-permute-start(bf16[512,256]{1,0:T(8,128)(2,1)S(1)} %get-tuple-element.79), channel_id=1, source_target_pairs={{0,2},{1,3},{2,0},{3,1},{4,6},{5,7},{6,4},{7,5},{8,10},{9,11},{10,... | collective-permute-start | bytes 786440 | tf_op jit(solution)/shard_map/ppermute | solution.py:445
  91.7 4.1 %tile_sums.5 = (bf16[512,256]{1,0:T(8,128)(2,1)S(1)}, bf16[512,256]{1,0:T(8,128)(2,1)S(1)}, bf16[512,256]{1,0:T(8,128)(2,1)S(1)}, bf16[512,256]{1,0:T(8,128)(2,1)S(1)}) custom-call(s32[4,64]{1,0:T(4,128)S(1)} %bitcast.22, s32[64]{0:T(128)S(1)} %bitcast.32, s32[4,64]{1,0:T(4,128)S(1)} %bitcast.27, s32[64]{0:T(128)S(1)} %bitcast.37, ...), custom_call_target="tpu_custom_call" | custom-call | flops 2000000000 | bytes 6291456 | tf_op jit(solution)/shard_map/tile_sums/pallas_call | solution.py:214
  100.6 9.1 %collective-permute-done.20.refs_2_ = bf16[512,256]{1,0:T(8,128)(2,1)S(1)} collective-permute-done((bf16[512,256]{1,0:T(8,128)(2,1)S(1)}, bf16[512,256]{1,0:T(8,128)(2,1)S(1)}, u32[]{:S(2)}, u32[]{:S(2)}) %collective-permute-start.20) | collective-permute-done | bytes 262176 | tf_op jit(solution)/shard_map/ppermute | solution.py:445
  109.7 17.1 %collective-permute-start.9 = (bf16[512,256]{1,0:T(8,128)(2,1)S(1)}, bf16[512,256]{1,0:T(8,128)(2,1)S(1)}, u32[]{:S(2)}, u32[]{:S(2)}) collective-permute-start(bf16[512,256]{1,0:T(8,128)(2,1)S(1)} %get-tuple-element.70), channel_id=1, source_target_pairs={{0,3},{1,0},{2,1},{3,2},{4,7},{5,4},{6,5},{7,6},{8,11},{9,8},{10,9... | collective-permute-start | bytes 786440 | tf_op jit(solution)/shard_map/ppermute | solution.py:445
  132.0 5.0 %collective-permute-done.17.refs_2_ = bf16[512,256]{1,0:T(8,128)(2,1)S(1)} collective-permute-done((bf16[512,256]{1,0:T(8,128)(2,1)S(1)}, bf16[512,256]{1,0:T(8,128)(2,1)S(1)}, u32[]{:S(2)}, u32[]{:S(2)}) %collective-permute-start.17) | collective-permute-done | bytes 262176 | tf_op jit(solution)/shard_map/ppermute | solution.py:445
  139.5 8.7 %collective-permute-done.8.refs_2_ = bf16[512,256]{1,0:T(8,128)(2,1)S(1)} collective-permute-done((bf16[512,256]{1,0:T(8,128)(2,1)S(1)}, bf16[512,256]{1,0:T(8,128)(2,1)S(1)}, u32[]{:S(2)}, u32[]{:S(2)}) %collective-permute-start.8) | collective-permute-done | bytes 262176 | tf_op jit(solution)/shard_map/ppermute | solution.py:445
  150.7 8.9 %all-gather = f32[64,256]{1,0:T(8,128)S(1)} all-gather(f32[8,256]{1,0:T(8,128)S(1)} %get-tuple-element.97), channel_id=2, replica_groups=mesh['dom'=8,'col'=4] {'dom'}, dimensions={0}, use_global_device_ids=true | all-gather | bytes 73728 | tf_op jit(solution)/shard_map/all_gather | solution.py:499
  159.7 5.1 %collective-permute-start.40 = (bf16[256,256]{1,0:T(8,128)(2,1)S(1)}, bf16[256,256]{1,0:T(8,128)(2,1)S(1)}, u32[]{:S(2)}, u32[]{:S(2)}) collective-permute-start(bf16[256,256]{1,0:T(8,128)(2,1)S(1)} %get-tuple-element.107), channel_id=1, source_target_pairs={{0,3},{1,0},{2,1},{3,2},{4,7},{5,4},{6,5},{7,6},{8,11},{9,8},{10,9... | collective-permute-start | bytes 393224 | tf_op jit(solution)/shard_map/ppermute | solution.py:445
  167.3 3.8 %collective-permute-start.43 = (bf16[256,256]{1,0:T(8,128)(2,1)S(1)}, bf16[256,256]{1,0:T(8,128)(2,1)S(1)}, u32[]{:S(2)}, u32[]{:S(2)}) collective-permute-start(bf16[256,256]{1,0:T(8,128)(2,1)S(1)} %get-tuple-element.111), channel_id=1, source_target_pairs={{0,3},{1,0},{2,1},{3,2},{4,7},{5,4},{6,5},{7,6},{8,11},{9,8},{10,9... | collective-permute-start | bytes 393224 | tf_op jit(solution)/shard_map/ppermute | solution.py:445
  171.2 5.4 %collective-permute-done.31.refs_5_ = f32[2,256]{1,0:T(2,128)S(1)} collective-permute-done((f32[2,256]{1,0:T(2,128)S(1)}, f32[2,256]{1,0:T(2,128)S(1)}, u32[]{:S(2)}, u32[]{:S(2)}) %collective-permute-start.31) | collective-permute-done | bytes 2080 | tf_op jit(solution)/shard_map/ppermute | solution.py:445
  176.6 5.3 %collective-permute-start.44 = (bf16[256,256]{1,0:T(8,128)(2,1)S(1)}, bf16[256,256]{1,0:T(8,128)(2,1)S(1)}, u32[]{:S(2)}, u32[]{:S(2)}) collective-permute-start(bf16[256,256]{1,0:T(8,128)(2,1)S(1)} %get-tuple-element.112), channel_id=1, source_target_pairs={{0,2},{1,3},{2,0},{3,1},{4,6},{5,7},{6,4},{7,5},{8,10},{9,11},{10,... | collective-permute-start | bytes 393224 | tf_op jit(solution)/shard_map/ppermute | solution.py:445
  182.0 3.4 %collective-permute-start.34 = (bf16[512,256]{1,0:T(8,128)(2,1)S(1)}, bf16[512,256]{1,0:T(8,128)(2,1)S(1)}, u32[]{:S(2)}, u32[]{:S(2)}) collective-permute-start(bf16[512,256]{1,0:T(8,128)(2,1)S(1)} %get-tuple-element.99), channel_id=1, source_target_pairs={{0,3},{1,0},{2,1},{3,2},{4,7},{5,4},{6,5},{7,6},{8,11},{9,8},{10,9... | collective-permute-start | bytes 786440 | tf_op jit(solution)/shard_map/ppermute | solution.py:445
  187.6 17.8 %collective-permute-start.45 = (bf16[256,256]{1,0:T(8,128)(2,1)S(1)}, bf16[256,256]{1,0:T(8,128)(2,1)S(1)}, u32[]{:S(2)}, u32[]{:S(2)}) collective-permute-start(bf16[256,256]{1,0:T(8,128)(2,1)S(1)} %get-tuple-element.113), channel_id=1, source_target_pairs={{0,1},{1,2},{2,3},{3,0},{4,5},{5,6},{6,7},{7,4},{8,9},{9,10},{10,1... | collective-permute-start | bytes 393224 | tf_op jit(solution)/shard_map/ppermute | solution.py:445
  205.4 8.1 %collective-permute-done.45.refs_3_ = bf16[256,256]{1,0:T(8,128)(2,1)S(1)} collective-permute-done((bf16[256,256]{1,0:T(8,128)(2,1)S(1)}, bf16[256,256]{1,0:T(8,128)(2,1)S(1)}, u32[]{:S(2)}, u32[]{:S(2)}) %collective-permute-start.45) | collective-permute-done | bytes 131104 | tf_op jit(solution)/shard_map/ppermute | solution.py:445
  213.5 7.8 %collective-permute-start.35 = (bf16[512,256]{1,0:T(8,128)(2,1)S(1)}, bf16[512,256]{1,0:T(8,128)(2,1)S(1)}, u32[]{:S(2)}, u32[]{:S(2)}) collective-permute-start(bf16[512,256]{1,0:T(8,128)(2,1)S(1)} %get-tuple-element.100), channel_id=1, source_target_pairs={{0,2},{1,3},{2,0},{3,1},{4,6},{5,7},{6,4},{7,5},{8,10},{9,11},{10,... | collective-permute-start | bytes 786440 | tf_op jit(solution)/shard_map/ppermute | solution.py:445
  221.3 3.8 %collective-permute-start.28 = (bf16[512,256]{1,0:T(8,128)(2,1)S(1)}, bf16[512,256]{1,0:T(8,128)(2,1)S(1)}, u32[]{:S(2)}, u32[]{:S(2)}) collective-permute-start(bf16[512,256]{1,0:T(8,128)(2,1)S(1)} %get-tuple-element.94), channel_id=1, source_target_pairs={{0,3},{1,0},{2,1},{3,2},{4,7},{5,4},{6,5},{7,6},{8,11},{9,8},{10,9... | collective-permute-start | bytes 786440 | tf_op jit(solution)/shard_map/ppermute | solution.py:445
  228.4 11.8 %collective-permute-done.35.refs_2_ = bf16[512,256]{1,0:T(8,128)(2,1)S(1)} collective-permute-done((bf16[512,256]{1,0:T(8,128)(2,1)S(1)}, bf16[512,256]{1,0:T(8,128)(2,1)S(1)}, u32[]{:S(2)}, u32[]{:S(2)}) %collective-permute-start.35) | collective-permute-done | bytes 262176 | tf_op jit(solution)/shard_map/ppermute | solution.py:445
  240.2 8.3 %collective-permute-start.33 = (f32[2,256]{1,0:T(2,128)S(1)}, f32[2,256]{1,0:T(2,128)S(1)}, u32[]{:S(2)}, u32[]{:S(2)}) collective-permute-start(f32[2,256]{1,0:T(2,128)S(1)} %get-tuple-element.114), channel_id=1, source_target_pairs={{0,1},{1,2},{2,3},{3,0},{4,5},{5,6},{6,7},{7,4},{8,9},{9,10},{10,1... | collective-permute-start | bytes 6152 | tf_op jit(solution)/shard_map/ppermute | solution.py:445
  249.5 11.9 %collective-permute-done.32.refs_6_ = f32[2,256]{1,0:T(2,128)S(1)} collective-permute-done((f32[2,256]{1,0:T(2,128)S(1)}, f32[2,256]{1,0:T(2,128)S(1)}, u32[]{:S(2)}, u32[]{:S(2)}) %collective-permute-start.32) | collective-permute-done | bytes 2080 | tf_op jit(solution)/shard_map/ppermute | solution.py:445
  (96 shorter events, 46.9 us)
Async XLA Ops:
  8.5 19.6 %collective-permute-start = (bf16[512,256]{1,0:T(8,128)(2,1)S(1)}, bf16[512,256]{1,0:T(8,128)(2,1)S(1)}, u32[]{:S(2)}, u32[]{:S(2)}) collective-permute-start(bf16[512,256]{1,0:T(8,128)(2,1)S(1)} %get-tuple-element.59), channel_id=1, source_target_pairs={{0,4},{4,0},{8,12},{12,8},{16,20},{20,16},{24,28},{28,24},{1,5},{5... | collective-permute-start | bytes 786440 | tf_op jit(solution)/shard_map/ppermute | solution.py:444
  9.1 20.4 %collective-permute-start.1 = (bf16[512,256]{1,0:T(8,128)(2,1)S(1)}, bf16[512,256]{1,0:T(8,128)(2,1)S(1)}, u32[]{:S(2)}, u32[]{:S(2)}) collective-permute-start(bf16[512,256]{1,0:T(8,128)(2,1)S(1)} %get-tuple-element.60), channel_id=1, source_target_pairs={{0,8},{4,12},{8,0},{12,4},{16,24},{20,28},{24,16},{28,20},{1,9},{5... | collective-permute-start | bytes 786440 | tf_op jit(solution)/shard_map/ppermute | solution.py:444
  26.8 20.4 %collective-permute-start.3 = (bf16[512,256]{1,0:T(8,128)(2,1)S(1)}, bf16[512,256]{1,0:T(8,128)(2,1)S(1)}, u32[]{:S(2)}, u32[]{:S(2)}) collective-permute-start(bf16[512,256]{1,0:T(8,128)(2,1)S(1)} %get-tuple-element.62), channel_id=1, source_target_pairs={{0,16},{4,20},{8,24},{12,28},{16,0},{20,4},{24,8},{28,12},{1,17},{... | collective-permute-start | bytes 786440 | tf_op jit(solution)/shard_map/ppermute | solution.py:444
  28.0 22.6 %collective-permute-start.4 = (bf16[512,256]{1,0:T(8,128)(2,1)S(1)}, bf16[512,256]{1,0:T(8,128)(2,1)S(1)}, u32[]{:S(2)}, u32[]{:S(2)}) collective-permute-start(bf16[512,256]{1,0:T(8,128)(2,1)S(1)} %get-tuple-element.63), channel_id=1, source_target_pairs={{0,20},{4,16},{8,28},{12,24},{16,4},{20,0},{24,12},{28,8},{1,21},{... | collective-permute-start | bytes 786440 | tf_op jit(solution)/shard_map/ppermute | solution.py:444
  28.1 22.6 %collective-permute-start.5 = (bf16[512,256]{1,0:T(8,128)(2,1)S(1)}, bf16[512,256]{1,0:T(8,128)(2,1)S(1)}, u32[]{:S(2)}, u32[]{:S(2)}) collective-permute-start(bf16[512,256]{1,0:T(8,128)(2,1)S(1)} %get-tuple-element.64), channel_id=1, source_target_pairs={{0,24},{4,28},{8,16},{12,20},{16,8},{20,12},{24,0},{28,4},{1,25},{... | collective-permute-start | bytes 786440 | tf_op jit(solution)/shard_map/ppermute | solution.py:444
  29.4 21.3 %collective-permute-start.6 = (bf16[512,256]{1,0:T(8,128)(2,1)S(1)}, bf16[512,256]{1,0:T(8,128)(2,1)S(1)}, u32[]{:S(2)}, u32[]{:S(2)}) collective-permute-start(bf16[512,256]{1,0:T(8,128)(2,1)S(1)} %get-tuple-element.65), channel_id=1, source_target_pairs={{0,28},{4,24},{8,20},{12,16},{16,12},{20,8},{24,4},{28,0},{1,29},{... | collective-permute-start | bytes 786440 | tf_op jit(solution)/shard_map/ppermute | solution.py:444
  31.2 36.8 %collective-permute-start.14 = (bf16[816,256]{1,0:T(8,128)(2,1)S(1)}, bf16[816,256]{1,0:T(8,128)(2,1)S(1)}, u32[]{:S(2)}, u32[]{:S(2)}) collective-permute-start(bf16[816,256]{1,0:T(8,128)(2,1)S(1)} %pack_rows.1.refs_0_), channel_id=1, source_target_pairs={{0,8},{4,12},{8,0},{12,4},{16,24},{20,28},{24,16},{28,20},{1,9},{5... | collective-permute-start | bytes 1253384 | tf_op jit(solution)/shard_map/ppermute | solution.py:477
  67.3 24.4 %collective-permute-start.16 = (bf16[512,256]{1,0:T(8,128)(2,1)S(1)}, bf16[512,256]{1,0:T(8,128)(2,1)S(1)}, u32[]{:S(2)}, u32[]{:S(2)}) collective-permute-start(bf16[512,256]{1,0:T(8,128)(2,1)S(1)} %get-tuple-element.74), channel_id=1, source_target_pairs={{0,1},{1,2},{2,3},{3,0},{4,5},{5,6},{6,7},{7,4},{8,9},{9,10},{10,1... | collective-permute-start | bytes 786440 | tf_op jit(solution)/shard_map/ppermute | solution.py:445
  67.8 28.1 %collective-permute-start.13 = (bf16[816,256]{1,0:T(8,128)(2,1)S(1)}, bf16[816,256]{1,0:T(8,128)(2,1)S(1)}, u32[]{:S(2)}, u32[]{:S(2)}) collective-permute-start(bf16[816,256]{1,0:T(8,128)(2,1)S(1)} %pack_rows.1.refs_0_), channel_id=1, source_target_pairs={{0,4},{4,0},{8,12},{12,8},{16,20},{20,16},{24,28},{28,24},{1,5},{5... | collective-permute-start | bytes 1253384 | tf_op jit(solution)/shard_map/ppermute | solution.py:477
  68.0 29.4 %collective-permute-start.15 = (bf16[816,256]{1,0:T(8,128)(2,1)S(1)}, bf16[816,256]{1,0:T(8,128)(2,1)S(1)}, u32[]{:S(2)}, u32[]{:S(2)}) collective-permute-start(bf16[816,256]{1,0:T(8,128)(2,1)S(1)} %collective-permute-done.14.refs_2_), channel_id=1, source_target_pairs={{0,4},{4,0},{8,12},{12,8},{16,20},{20,16},{24,28},{28,24},{1,5},{5... | collective-permute-start | bytes 1253384 | tf_op jit(solution)/shard_map/ppermute | solution.py:477
  88.3 21.4 %collective-permute-start.20 = (bf16[512,256]{1,0:T(8,128)(2,1)S(1)}, bf16[512,256]{1,0:T(8,128)(2,1)S(1)}, u32[]{:S(2)}, u32[]{:S(2)}) collective-permute-start(bf16[512,256]{1,0:T(8,128)(2,1)S(1)} %get-tuple-element.79), channel_id=1, source_target_pairs={{0,2},{1,3},{2,0},{3,1},{4,6},{5,7},{6,4},{7,5},{8,10},{9,11},{10,... | collective-permute-start | bytes 786440 | tf_op jit(solution)/shard_map/ppermute | solution.py:445
  95.9 41.1 %collective-permute-start.17 = (bf16[512,256]{1,0:T(8,128)(2,1)S(1)}, bf16[512,256]{1,0:T(8,128)(2,1)S(1)}, u32[]{:S(2)}, u32[]{:S(2)}) collective-permute-start(bf16[512,256]{1,0:T(8,128)(2,1)S(1)} %get-tuple-element.75), channel_id=1, source_target_pairs={{0,2},{1,3},{2,0},{3,1},{4,6},{5,7},{6,4},{7,5},{8,10},{9,11},{10,... | collective-permute-start | bytes 786440 | tf_op jit(solution)/shard_map/ppermute | solution.py:445
  97.4 39.6 %collective-permute-start.18 = (bf16[512,256]{1,0:T(8,128)(2,1)S(1)}, bf16[512,256]{1,0:T(8,128)(2,1)S(1)}, u32[]{:S(2)}, u32[]{:S(2)}) collective-permute-start(bf16[512,256]{1,0:T(8,128)(2,1)S(1)} %get-tuple-element.76), channel_id=1, source_target_pairs={{0,3},{1,0},{2,1},{3,2},{4,7},{5,4},{6,5},{7,6},{8,11},{9,8},{10,9... | collective-permute-start | bytes 786440 | tf_op jit(solution)/shard_map/ppermute | solution.py:445
  100.5 39.0 %collective-permute-start.7 = (bf16[512,256]{1,0:T(8,128)(2,1)S(1)}, bf16[512,256]{1,0:T(8,128)(2,1)S(1)}, u32[]{:S(2)}, u32[]{:S(2)}) collective-permute-start(bf16[512,256]{1,0:T(8,128)(2,1)S(1)} %get-tuple-element.68), channel_id=1, source_target_pairs={{0,1},{1,2},{2,3},{3,0},{4,5},{5,6},{6,7},{7,4},{8,9},{9,10},{10,1... | collective-permute-start | bytes 786440 | tf_op jit(solution)/shard_map/ppermute | solution.py:445
  109.7 38.5 %collective-permute-start.8 = (bf16[512,256]{1,0:T(8,128)(2,1)S(1)}, bf16[512,256]{1,0:T(8,128)(2,1)S(1)}, u32[]{:S(2)}, u32[]{:S(2)}) collective-permute-start(bf16[512,256]{1,0:T(8,128)(2,1)S(1)} %get-tuple-element.69), channel_id=1, source_target_pairs={{0,2},{1,3},{2,0},{3,1},{4,6},{5,7},{6,4},{7,5},{8,10},{9,11},{10,... | collective-permute-start | bytes 786440 | tf_op jit(solution)/shard_map/ppermute | solution.py:445
  109.7 38.5 %collective-permute-start.9 = (bf16[512,256]{1,0:T(8,128)(2,1)S(1)}, bf16[512,256]{1,0:T(8,128)(2,1)S(1)}, u32[]{:S(2)}, u32[]{:S(2)}) collective-permute-start(bf16[512,256]{1,0:T(8,128)(2,1)S(1)} %get-tuple-element.70), channel_id=1, source_target_pairs={{0,3},{1,0},{2,1},{3,2},{4,7},{5,4},{6,5},{7,6},{8,11},{9,8},{10,9... | collective-permute-start | bytes 786440 | tf_op jit(solution)/shard_map/ppermute | solution.py:445
  159.7 22.3 %collective-permute-start.40 = (bf16[256,256]{1,0:T(8,128)(2,1)S(1)}, bf16[256,256]{1,0:T(8,128)(2,1)S(1)}, u32[]{:S(2)}, u32[]{:S(2)}) collective-permute-start(bf16[256,256]{1,0:T(8,128)(2,1)S(1)} %get-tuple-element.107), channel_id=1, source_target_pairs={{0,3},{1,0},{2,1},{3,2},{4,7},{5,4},{6,5},{7,6},{8,11},{9,8},{10,9... | collective-permute-start | bytes 393224 | tf_op jit(solution)/shard_map/ppermute | solution.py:445
  164.8 20.6 %collective-permute-start.41 = (bf16[256,256]{1,0:T(8,128)(2,1)S(1)}, bf16[256,256]{1,0:T(8,128)(2,1)S(1)}, u32[]{:S(2)}, u32[]{:S(2)}) collective-permute-start(bf16[256,256]{1,0:T(8,128)(2,1)S(1)} %get-tuple-element.108), channel_id=1, source_target_pairs={{0,2},{1,3},{2,0},{3,1},{4,6},{5,7},{6,4},{7,5},{8,10},{9,11},{10,... | collective-permute-start | bytes 393224 | tf_op jit(solution)/shard_map/ppermute | solution.py:445
  167.3 18.1 %collective-permute-start.42 = (bf16[256,256]{1,0:T(8,128)(2,1)S(1)}, bf16[256,256]{1,0:T(8,128)(2,1)S(1)}, u32[]{:S(2)}, u32[]{:S(2)}) collective-permute-start(bf16[256,256]{1,0:T(8,128)(2,1)S(1)} %get-tuple-element.109), channel_id=1, source_target_pairs={{0,1},{1,2},{2,3},{3,0},{4,5},{5,6},{6,7},{7,4},{8,9},{9,10},{10,1... | collective-permute-start | bytes 393224 | tf_op jit(solution)/shard_map/ppermute | solution.py:445
  167.3 18.2 %collective-permute-start.43 = (bf16[256,256]{1,0:T(8,128)(2,1)S(1)}, bf16[256,256]{1,0:T(8,128)(2,1)S(1)}, u32[]{:S(2)}, u32[]{:S(2)}) collective-permute-start(bf16[256,256]{1,0:T(8,128)(2,1)S(1)} %get-tuple-element.111), channel_id=1, source_target_pairs={{0,3},{1,0},{2,1},{3,2},{4,7},{5,4},{6,5},{7,6},{8,11},{9,8},{10,9... | collective-permute-start | bytes 393224 | tf_op jit(solution)/shard_map/ppermute | solution.py:445
  182.0 39.3 %collective-permute-start.34 = (bf16[512,256]{1,0:T(8,128)(2,1)S(1)}, bf16[512,256]{1,0:T(8,128)(2,1)S(1)}, u32[]{:S(2)}, u32[]{:S(2)}) collective-permute-start(bf16[512,256]{1,0:T(8,128)(2,1)S(1)} %get-tuple-element.99), channel_id=1, source_target_pairs={{0,3},{1,0},{2,1},{3,2},{4,7},{5,4},{6,5},{7,6},{8,11},{9,8},{10,9... | collective-permute-start | bytes 786440 | tf_op jit(solution)/shard_map/ppermute | solution.py:445
  185.3 35.9 %collective-permute-start.37 = (bf16[512,256]{1,0:T(8,128)(2,1)S(1)}, bf16[512,256]{1,0:T(8,128)(2,1)S(1)}, u32[]{:S(2)}, u32[]{:S(2)}) collective-permute-start(bf16[512,256]{1,0:T(8,128)(2,1)S(1)} %get-tuple-element.103), channel_id=1, source_target_pairs={{0,3},{1,0},{2,1},{3,2},{4,7},{5,4},{6,5},{7,6},{8,11},{9,8},{10,9... | collective-permute-start | bytes 786440 | tf_op jit(solution)/shard_map/ppermute | solution.py:445
  185.4 39.7 %collective-permute-start.38 = (bf16[512,256]{1,0:T(8,128)(2,1)S(1)}, bf16[512,256]{1,0:T(8,128)(2,1)S(1)}, u32[]{:S(2)}, u32[]{:S(2)}) collective-permute-start(bf16[512,256]{1,0:T(8,128)(2,1)S(1)} %get-tuple-element.104), channel_id=1, source_target_pairs={{0,2},{1,3},{2,0},{3,1},{4,6},{5,7},{6,4},{7,5},{8,10},{9,11},{10,... | collective-permute-start | bytes 786440 | tf_op jit(solution)/shard_map/ppermute | solution.py:445
  185.5 39.7 %collective-permute-start.39 = (bf16[512,256]{1,0:T(8,128)(2,1)S(1)}, bf16[512,256]{1,0:T(8,128)(2,1)S(1)}, u32[]{:S(2)}, u32[]{:S(2)}) collective-permute-start(bf16[512,256]{1,0:T(8,128)(2,1)S(1)} %get-tuple-element.105), channel_id=1, source_target_pairs={{0,1},{1,2},{2,3},{3,0},{4,5},{5,6},{6,7},{7,4},{8,9},{9,10},{10,1... | collective-permute-start | bytes 786440 | tf_op jit(solution)/shard_map/ppermute | solution.py:445
  187.6 25.9 %collective-permute-start.45 = (bf16[256,256]{1,0:T(8,128)(2,1)S(1)}, bf16[256,256]{1,0:T(8,128)(2,1)S(1)}, u32[]{:S(2)}, u32[]{:S(2)}) collective-permute-start(bf16[256,256]{1,0:T(8,128)(2,1)S(1)} %get-tuple-element.113), channel_id=1, source_target_pairs={{0,1},{1,2},{2,3},{3,0},{4,5},{5,6},{6,7},{7,4},{8,9},{9,10},{10,1... | collective-permute-start | bytes 393224 | tf_op jit(solution)/shard_map/ppermute | solution.py:445
  213.5 26.7 %collective-permute-start.35 = (bf16[512,256]{1,0:T(8,128)(2,1)S(1)}, bf16[512,256]{1,0:T(8,128)(2,1)S(1)}, u32[]{:S(2)}, u32[]{:S(2)}) collective-permute-start(bf16[512,256]{1,0:T(8,128)(2,1)S(1)} %get-tuple-element.100), channel_id=1, source_target_pairs={{0,2},{1,3},{2,0},{3,1},{4,6},{5,7},{6,4},{7,5},{8,10},{9,11},{10,... | collective-permute-start | bytes 786440 | tf_op jit(solution)/shard_map/ppermute | solution.py:445
  221.3 18.9 %collective-permute-start.36 = (bf16[512,256]{1,0:T(8,128)(2,1)S(1)}, bf16[512,256]{1,0:T(8,128)(2,1)S(1)}, u32[]{:S(2)}, u32[]{:S(2)}) collective-permute-start(bf16[512,256]{1,0:T(8,128)(2,1)S(1)} %get-tuple-element.101), channel_id=1, source_target_pairs={{0,1},{1,2},{2,3},{3,0},{4,5},{5,6},{6,7},{7,4},{8,9},{9,10},{10,1... | collective-permute-start | bytes 786440 | tf_op jit(solution)/shard_map/ppermute | solution.py:445
  221.3 40.2 %collective-permute-start.28 = (bf16[512,256]{1,0:T(8,128)(2,1)S(1)}, bf16[512,256]{1,0:T(8,128)(2,1)S(1)}, u32[]{:S(2)}, u32[]{:S(2)}) collective-permute-start(bf16[512,256]{1,0:T(8,128)(2,1)S(1)} %get-tuple-element.94), channel_id=1, source_target_pairs={{0,3},{1,0},{2,1},{3,2},{4,7},{5,4},{6,5},{7,6},{8,11},{9,8},{10,9... | collective-permute-start | bytes 786440 | tf_op jit(solution)/shard_map/ppermute | solution.py:445
  225.1 36.4 %collective-permute-start.29 = (bf16[512,256]{1,0:T(8,128)(2,1)S(1)}, bf16[512,256]{1,0:T(8,128)(2,1)S(1)}, u32[]{:S(2)}, u32[]{:S(2)}) collective-permute-start(bf16[512,256]{1,0:T(8,128)(2,1)S(1)} %get-tuple-element.95), channel_id=1, source_target_pairs={{0,2},{1,3},{2,0},{3,1},{4,6},{5,7},{6,4},{7,5},{8,10},{9,11},{10,... | collective-permute-start | bytes 786440 | tf_op jit(solution)/shard_map/ppermute | solution.py:445
  225.1 36.4 %collective-permute-start.30 = (bf16[512,256]{1,0:T(8,128)(2,1)S(1)}, bf16[512,256]{1,0:T(8,128)(2,1)S(1)}, u32[]{:S(2)}, u32[]{:S(2)}) collective-permute-start(bf16[512,256]{1,0:T(8,128)(2,1)S(1)} %get-tuple-element.96), channel_id=1, source_target_pairs={{0,1},{1,2},{2,3},{3,0},{4,5},{5,6},{6,7},{7,4},{8,9},{9,10},{10,1... | collective-permute-start | bytes 786440 | tf_op jit(solution)/shard_map/ppermute | solution.py:445
  240.2 21.3 %collective-permute-start.32 = (f32[2,256]{1,0:T(2,128)S(1)}, f32[2,256]{1,0:T(2,128)S(1)}, u32[]{:S(2)}, u32[]{:S(2)}) collective-permute-start(f32[2,256]{1,0:T(2,128)S(1)} %get-tuple-element.115), channel_id=1, source_target_pairs={{0,2},{1,3},{2,0},{3,1},{4,6},{5,7},{6,4},{7,5},{8,10},{9,11},{10,... | collective-permute-start | bytes 6152 | tf_op jit(solution)/shard_map/ppermute | solution.py:445
  240.2 21.3 %collective-permute-start.33 = (f32[2,256]{1,0:T(2,128)S(1)}, f32[2,256]{1,0:T(2,128)S(1)}, u32[]{:S(2)}, u32[]{:S(2)}) collective-permute-start(f32[2,256]{1,0:T(2,128)S(1)} %get-tuple-element.114), channel_id=1, source_target_pairs={{0,1},{1,2},{2,3},{3,0},{4,5},{5,6},{6,7},{7,4},{8,9},{9,10},{10,1... | collective-permute-start | bytes 6152 | tf_op jit(solution)/shard_map/ppermute | solution.py:445
  (20 other events, 371.1 us)

commit v3 on v2

--- a/solution.py
+++ b/solution.py
@@ -24,13 +24,17 @@
     return pltpu.with_memory_space_constraint(x, pltpu.HBM)
 
 
+def in_vmem(x):
+    return pltpu.with_memory_space_constraint(x, pltpu.VMEM)
+
+
 def grant(mib):
     return pltpu.CompilerParams(vmem_limit_bytes=int(mib) << 20)
 
 
 LANES = 128
 SUBLANES = 8
-UNROLL = 16
+UNROLL = 32
 
 
 def storage_order(send_rows):
@@ -46,7 +50,7 @@
         return (q >> 3) * (blocks * tile) + (q & (SUBLANES - 1)) * LANES
 
     def within(b):
-        return lax.div(b, per) * tile + lax.rem(b, per) * UNROLL
+        return (b >> (per.bit_length() - 1)) * tile + (b & (per - 1)) * UNROLL
 
     return tiled.transpose(0, 2, 1, 3).reshape(-1), first, within
 
@@ -148,84 +152,178 @@
     return out[: len(peers)], out[len(peers) :]
 
 
-def sum_kernel(
-    n_dom, n_col, peer, slots, piece_rows, per_dest, base,
-    own_index, own_counts, halo_index, halo_counts, *refs
-):
-    pieces = refs[: n_dom - 1]
-    feat = refs[n_dom - 1]
-    own_vals = refs[n_dom : n_dom + n_col]
-    halo_vals = refs[n_dom + n_col : n_dom + 2 * n_col]
-    outs = refs[n_dom + 2 * n_col : n_dom + 3 * n_col]
-    (halo,) = refs[n_dom + 3 * n_col :]
+def masked(vals, used):
+    return [
+        jnp.where(s < used, vals[s], jnp.zeros_like(vals[s])) for s in range(vals.shape[0])
+    ]
+
+
+def tiles_of(src, index, row_tile, slots):
+    starts = [pl.multiple_of(index[s, row_tile] * TILE, TILE) for s in range(slots)]
+    return [src[pl.ds(at, TILE), :] for at in starts]
+
+
+def product(left, right):
+    return jnp.dot(
+        jnp.concatenate(left, axis=1),
+        jnp.concatenate(right, axis=0),
+        preferred_element_type=jnp.float32,
+    )
+
+
+def vals_specs(n_col, per_dest, base, group, slots):
+    def spec(k):
+        def place(i, *_):
+            dest = lax.rem(lax.axis_index("col") + k, n_col)
+            return ((dest * per_dest + base) // group + i, 0, 0, 0)
+
+        return pl.BlockSpec((group, slots, TILE, TILE), place)
+
+    return [spec(k) for k in range(n_col)]
+
+
+def row_tile_of(k, n_col, per_dest, tile):
+    return lax.rem(lax.axis_index("col") + k, n_col) * per_dest + tile
+
+
+def early_kernel(n_col, slots, per_dest, own_index, own_counts, halo_counts, feat, *refs):
+    own_vals, halo_vals, (part, kept) = refs[:n_col], refs[n_col:-2], refs[-2:]
+    i = pl.program_id(0)
+    for k in range(n_col):
+        row_tile = row_tile_of(k, n_col, per_dest, i)
+        part[k, pl.ds(pl.multiple_of(i * TILE, TILE), TILE), :] = product(
+            masked(own_vals[k][0], own_counts[row_tile]),
+            tiles_of(feat, own_index, row_tile, slots),
+        )
+        for s, vals in enumerate(masked(halo_vals[k][0], halo_counts[row_tile])):
+            kept[k, i, s] = vals
+
+
+def early_sums(tables, features, own_vals, halo_vals, n_col, size):
+    tiles, slots = own_vals.shape[:2]
+    width = features.shape[1]
+    per_dest = tiles // n_col
+    own_index, own_counts, _, halo_counts = tables
+    return pl.pallas_call(
+        functools.partial(early_kernel, n_col, slots, per_dest),
+        out_shape=[
+            jax.ShapeDtypeStruct((n_col, size * TILE, width), jnp.float32),
+            jax.ShapeDtypeStruct((n_col, size, slots, TILE, TILE), halo_vals.dtype),
+        ],
+        grid_spec=pltpu.PrefetchScalarGridSpec(
+            num_scalar_prefetch=3,
+            grid=(size,),
+            in_specs=[VMEM] + vals_specs(n_col, per_dest, 0, 1, slots) * 2,
+            out_specs=[VMEM] * 2,
+        ),
+        compiler_params=grant(16),
+        cost_estimate=cost(2e9, 4 << 20),
+        name="early_sums",
+    )(
+        own_index, own_counts, halo_counts, in_vmem(features),
+        *([in_hbm(own_vals)] * n_col), *([in_hbm(halo_vals)] * n_col),
+    )
+
+
+def put_piece(halo, piece, q):
+    rows = piece.shape[0]
+    halo[pl.ds(pl.multiple_of(q * rows, rows), rows), :] = piece[...]
+
+
+def assemble_kernel(ks, peer, *refs):
+    pieces, halo = refs[:-1], refs[-1]
+    me = lax.axis_index("dom")
+    for k, piece in zip(ks, pieces):
+        put_piece(halo, piece, peer(me, -k))
+    rows = pieces[0].shape[0]
+    own = pl.ds(pl.multiple_of(me * rows, rows), rows)
+    halo[own, :] = jnp.zeros((rows, halo.shape[1]), halo.dtype)
+
+
+def assemble(ks, pieces, n_dom, peer):
+    rows, width = pieces[0].shape
+    return pl.pallas_call(
+        functools.partial(assemble_kernel, ks, peer),
+        out_shape=jax.ShapeDtypeStruct((n_dom * rows, width), pieces[0].dtype),
+        in_specs=[VMEM] * len(pieces),
+        out_specs=VMEM,
+        compiler_params=grant(4 + n_dom),
+        cost_estimate=cost(2e9, 4 << 20),
+        name="assemble",
+    )(*pieces)
+
+
+def first_kernel(n_col, slots, per_dest, ks, peer, index, *refs):
+    pieces = refs[: len(ks)]
+    part, kept = refs[len(ks) : len(ks) + 2]
+    outs, halo = refs[-n_col - 1 : -1], refs[-1]
+    me = lax.axis_index("dom")
+    for k, piece in zip(ks, pieces):
+        put_piece(halo, piece, peer(me, -k))
+    for t in range(kept.shape[1]):
+        at = pl.ds(t * TILE, TILE)
+        for k in range(n_col):
+            right = tiles_of(halo, index, row_tile_of(k, n_col, per_dest, t), slots)
+            total = part[k, at, :] + product([kept[k, t, s] for s in range(slots)], right)
+            outs[k][at, :] = total.astype(outs[k].dtype)
+
+
+def first_sums(index, ks, pieces, part, kept, halo, per_dest, peer):
+    n_col, size, slots = kept.shape[:3]
+    width = halo.shape[1]
+    out = pl.pallas_call(
+        functools.partial(first_kernel, n_col, slots, per_dest, ks, peer),
+        out_shape=[jax.ShapeDtypeStruct((size * TILE, width), halo.dtype)] * n_col
+        + [jax.ShapeDtypeStruct(halo.shape, halo.dtype)],
+        in_specs=[pl.BlockSpec(memory_space=pltpu.SMEM)] + [VMEM] * (len(ks) + 3),
+        out_specs=[VMEM] * (n_col + 1),
+        input_output_aliases={len(ks) + 3: n_col},
+        compiler_params=grant(6 + halo.shape[0] // (1 << 12)),
+        cost_estimate=cost(2e9, 4 << 20),
+        name="first_sums",
+    )(index, *pieces, part, kept, halo)
+    return out[:n_col], out[n_col]
+
+
+def sum_kernel(n_col, slots, per_dest, base, *refs):
+    own_index, own_counts, halo_index, halo_counts, feat, halo = refs[:6]
+    own_vals, halo_vals = refs[6 : 6 + n_col], refs[6 + n_col : 6 + 2 * n_col]
+    outs = refs[6 + 2 * n_col :]
     sub = pl.program_id(0)
     group = own_vals[0].shape[0]
-    col = lax.axis_index("col")
-
-    @pl.when(sub == 0)
-    def _():
-        me = lax.axis_index("dom")
-        for k in range(1, n_dom):
-            at = pl.ds(pl.multiple_of(peer(me, -k) * piece_rows, piece_rows), piece_rows)
-            halo[at, :] = pieces[k - 1][...]
-        own = pl.ds(pl.multiple_of(me * piece_rows, piece_rows), piece_rows)
-        halo[own, :] = jnp.zeros((piece_rows, halo.shape[1]), halo.dtype)
-
     for k in range(n_col):
-        dest = lax.rem(col + k, n_col)
         for t in range(group):
-            row_tile = dest * per_dest + base + sub * group + t
-            left, right = [], []
-            for src, index, counts, vals in (
-                (feat, own_index, own_counts, own_vals[k]),
-                (halo, halo_index, halo_counts, halo_vals[k]),
-            ):
-                used = counts[row_tile]
-                for s in range(slots):
-                    left.append(jnp.where(s < used, vals[t, s], jnp.zeros_like(vals[t, s])))
-                    at = pl.multiple_of(index[s, row_tile] * TILE, TILE)
-                    right.append(src[pl.ds(at, TILE), :])
-            total = jnp.dot(
-                jnp.concatenate(left, axis=1),
-                jnp.concatenate(right, axis=0),
-                preferred_element_type=jnp.float32,
-            )
+            row_tile = row_tile_of(k, n_col, per_dest, base + sub * group + t)
+            left = masked(own_vals[k][t], own_counts[row_tile])
+            left += masked(halo_vals[k][t], halo_counts[row_tile])
+            right = tiles_of(feat, own_index, row_tile, slots)
+            right += tiles_of(halo, halo_index, row_tile, slots)
             at = pl.ds(pl.multiple_of((sub * group + t) * TILE, TILE), TILE)
-            outs[k][at, :] = total.astype(outs[k].dtype)
-
-
-def tile_sums(tables, pieces, features, own_vals, halo_vals, n_dom, n_col, peer, base, size):
+            outs[k][at, :] = product(left, right).astype(outs[k].dtype)
+
+
+def tile_sums(tables, halo, features, own_vals, halo_vals, n_col, base, size):
     tiles, slots = own_vals.shape[:2]
     width = features.shape[1]
-    piece_rows = pieces[0].shape[0]
     per_dest = tiles // n_col
     group = min(size, 2)
     while base % group or size % group:
         group -= 1
-
-    def vals_spec(k):
-        def place(i, *_):
-            dest = lax.rem(lax.axis_index("col") + k, n_col)
-            return ((dest * per_dest + base) // group + i, 0, 0, 0)
-
-        return pl.BlockSpec((group, slots, TILE, TILE), place)
-
-    rows = size * TILE
+    specs = vals_specs(n_col, per_dest, base, group, slots)
     return pl.pallas_call(
-        functools.partial(sum_kernel, n_dom, n_col, peer, slots, piece_rows, per_dest, base),
-        out_shape=[jax.ShapeDtypeStruct((rows, width), jnp.bfloat16)] * n_col,
+        functools.partial(sum_kernel, n_col, slots, per_dest, base),
+        out_shape=[jax.ShapeDtypeStruct((size * TILE, width), jnp.bfloat16)] * n_col,
         grid_spec=pltpu.PrefetchScalarGridSpec(
             num_scalar_prefetch=4,
             grid=(size // group,),
-            in_specs=[VMEM] * n_dom + [vals_spec(k) for k in range(n_col)] * 2,
+            in_specs=[VMEM] * 2 + specs * 2,
             out_specs=[VMEM] * n_col,
-            scratch_shapes=[pltpu.VMEM((n_dom * piece_rows, width), jnp.bfloat16)],
         ),
-        compiler_params=grant(10 + n_dom),
+        compiler_params=grant(18),
         cost_estimate=cost(2e9, 6 << 20),
         name="tile_sums",
     )(
-        *tables, *pieces, pltpu.with_memory_space_constraint(features, pltpu.VMEM),
+        *tables, in_vmem(features), in_vmem(halo),
         *([in_hbm(own_vals)] * n_col), *([in_hbm(halo_vals)] * n_col),
     )
 
@@ -449,8 +547,8 @@
     rows, first_row, within = storage_order(send_rows[0])
     slots = send_rows.shape[2]
     table, own_tiles = None, features
-    cut = (n_dom - 1) // 2
-    for peers in (far[:cut], far[cut:]):
+    lead = far[0:3:2]
+    for part, peers in enumerate((lead, [k for k in far if k not in lead])):
         if not peers:
             continue
         outgoing, made = gather_rows(
@@ -480,12 +578,22 @@
 
     plan = chunk_plan(n_rows // TILE // n_col)
     index_tables = (local_index[0].T, local_count[0], halo_index[0].T, halo_count[0])
+    part, kept = early_sums(index_tables, own_tiles, local_vals[0], halo_vals[0], n_col, plan[0][1])
+    late = far[-2:-1] or far
+    soon = [k for k in far if k not in late]
+    received = assemble(soon, [halo[k - 1] for k in soon], n_dom, peer)
     incoming = []
-    for base, size in plan:
-        sums = tile_sums(
-            index_tables, halo, own_tiles, local_vals[0], halo_vals[0],
-            n_dom, n_col, peer, base, size,
-        )
+    for g, (base, size) in enumerate(plan):
+        if g == 0:
+            sums, received = first_sums(
+                index_tables[2], late, [halo[k - 1] for k in late], part, kept,
+                received, n_rows // TILE // n_col, peer,
+            )
+        else:
+            sums = tile_sums(
+                index_tables, received, own_tiles, local_vals[0], halo_vals[0],
+                n_col, base, size,
+            )
         moved = {k: along_col(sums[k], k) for k in order}
         incoming.append([sums[0]] + [moved[k] for k in range(1, n_col)])
 

time: 264 us -> 256 us (0.970)
  starting transfers between devices: 122 us -> 115 us
    ppermute x7, waiting for transfers between devices: 19.2 us -> 7.35 us  [on_device(): lax.ppermute(x, 'dom', [(i, peer(i, k)) for i in range(n_dom)])]
    ppermute x36, waiting for transfers between devices: 68.6 us -> 79.5 us  [on_device(): lax.ppermute(x, 'col', [(i, (i + k) % n_col) for i in range(n_col)])]
    ppermute x36, starting transfers between devices: 114 us -> 105 us  [on_device(): lax.ppermute(x, 'col', [(i, (i + k) % n_col) for i in range(n_col)])]
    pallas_call x5 -> x7, Pallas kernels: 18.4 us -> 19 us  [the longest x4 14.8 us: tile_sums(): pl.pallas_call(functools.partial(sum_kernel, n_col, slots, per_dest, base...]
  transfers between devices with their start and end apart: 46 -> 46, of which waited for: 13 -> 15; matrix products, arithmetic and copies ran while one was open for 0% -> 0% of each run, Pallas kernels for 12% -> 14%
where the time goes in v3:
time: 256 us
  starting transfers between devices  115 us (45%)
  waiting for transfers between devices  86.9 us (34%)
  Pallas kernels  42.7 us (17%)
  blocking collectives  9.94 us (4%)
    ppermute x36, starting transfers between devices, on_device(): lax.ppermute(x, 'col', [(i, (i + k) % n_col) for i in range(n_col)])  105 us
    ppermute x36, waiting for transfers between devices, on_device(): lax.ppermute(x, 'col', [(i, (i + k) % n_col) for i in range(n_col)])  79.5 us
    pallas_call x4, Pallas kernels, tile_sums(): pl.pallas_call(functools.partial(sum_kernel, n_col, slots, per_dest, base...  14.8 us
    pallas_call x5, Pallas kernels, mix_rows(): pl.pallas_call(functools.partial(mix_kernel, n_col, channels, first), out...  10.2 us
    all_gather x1, blocking collectives, on_device(): over_dom = lax.all_gather(stats, 'dom', axis=0)  9.94 us
    ppermute x7, starting transfers between devices, on_device(): lax.ppermute(x, 'dom', [(i, peer(i, k)) for i in range(n_dom)])  7.69 us
    ppermute x7, waiting for transfers between devices, on_device(): lax.ppermute(x, 'dom', [(i, peer(i, k)) for i in range(n_dom)])  7.35 us
    pallas_call x2, Pallas kernels, gather_rows(): pl.pallas_call(functools.partial(gather_kernel, peers, peer, first_row, w...  6.99 us
  transfers between devices with their start and end apart: 46, of which 15 were waited for; matrix products, arithmetic and copies ran while one was open for 0% of the time, Pallas kernels for 14%

profile of v3, /device:TPU:0, one launch (start us, length us, event | category | flops | bytes accessed | tf_op | source)
XLA Modules:
  0.0 255.9 jit_solution(5064858026262766349)
XLA Ops:
  0.6 3.3 %gather_rows.2 = (bf16[512,256]{1,0:T(8,128)(2,1)S(1)}, bf16[512,256]{1,0:T(8,128)(2,1)S(1)}, f32[16384,128]{1,0:T(8,128)S(1)}, bf16[8192,256]{1,0:T(8,128)(2,1)S(1)}) custom-call(s32[4096]{0:T(1024)} %bitcast.78, s32[8]{0:T(128)} %bitcast.80, bf16[8192,256]{1,0:T(8,128)(2,1)} %refs_0_.1), custom_call_target="tpu_custom_call" | custom-call | flops 4000000000 | bytes 6291456 | tf_op jit(solution)/shard_map/gather_rows/pallas_call | solution.py:136
  4.0 3.5 %collective-permute-start.1 = (bf16[512,256]{1,0:T(8,128)(2,1)S(1)}, bf16[512,256]{1,0:T(8,128)(2,1)S(1)}, u32[]{:S(2)}, u32[]{:S(2)}) collective-permute-start(bf16[512,256]{1,0:T(8,128)(2,1)S(1)} %get-tuple-element.66), channel_id=1, source_target_pairs={{0,28},{4,24},{8,20},{12,16},{16,12},{20,8},{24,4},{28,0},{1,29},{... | collective-permute-start | bytes 786440 | tf_op jit(solution)/shard_map/ppermute | solution.py:542
  7.5 3.7 %gather_rows.3 = (bf16[512,256]{1,0:T(8,128)(2,1)S(1)}, bf16[512,256]{1,0:T(8,128)(2,1)S(1)}, bf16[512,256]{1,0:T(8,128)(2,1)S(1)}, bf16[512,256]{1,0:T(8,128)(2,1)S(1)}, bf16[512,256]{1,0:T(8,128)(2,1)S(1)}) custom-call(s32[4096]{0:T(1024)} %bitcast.79, s32[8]{0:T(128)} %bitcast.81, f32[16384,128]{1,0:T(8,128)S(1)} %get-tuple-element.62.refs_0_), custom_call_target="tpu_custom_call" | custom-call | flops 4000000000 | bytes 6291456 | tf_op jit(solution)/shard_map/gather_rows/pallas_call | solution.py:136
  18.5 2.9 %collective-permute-done.10.refs_0_ = bf16[272,256]{1,0:T(8,128)(2,1)S(1)} collective-permute-done((bf16[272,256]{1,0:T(8,128)(2,1)S(1)}, bf16[272,256]{1,0:T(8,128)(2,1)S(1)}, u32[]{:S(2)}, u32[]{:S(2)}) %collective-permute-start.10) | collective-permute-done | bytes 139296 | tf_op jit(solution)/shard_map/ppermute | solution.py:543
  21.4 4.9 %collective-permute-done.11.refs_1_ = bf16[272,256]{1,0:T(8,128)(2,1)S(1)} collective-permute-done((bf16[272,256]{1,0:T(8,128)(2,1)S(1)}, bf16[272,256]{1,0:T(8,128)(2,1)S(1)}, u32[]{:S(2)}, u32[]{:S(2)}) %collective-permute-start.11) | collective-permute-done | bytes 139296 | tf_op jit(solution)/shard_map/ppermute | solution.py:543
  29.7 3.0 %early_sums.1 = (f32[4,256,256]{2,1,0:T(8,128)S(1)}, bf16[4,2,4,128,128]{4,3,2,1,0:T(8,128)(2,1)S(1)}) custom-call(s32[4,64]{1,0:T(4,128)S(1)} %bitcast.18, s32[64]{0:T(128)S(1)} %bitcast.28, s32[64]{0:T(128)S(1)} %bitcast.33, bf16[8192,256]{1,0:T(8,128)(2,1)S(1)} %get-tuple-element.61.feat.refs_4_, bf16[64,4,128,128]{3,2,1,0:T(8,128)(2,1)} %bitcast.38, ...), custom_call_target="tpu_custom_call" | custom-call | flops 2000000000 | bytes 4194304 | tf_op jit(solution)/shard_map/early_sums/pallas_call | solution.py:207
  35.5 6.8 %collective-permute-done.refs_0_ = bf16[512,256]{1,0:T(8,128)(2,1)S(1)} collective-permute-done((bf16[512,256]{1,0:T(8,128)(2,1)S(1)}, bf16[512,256]{1,0:T(8,128)(2,1)S(1)}, u32[]{:S(2)}, u32[]{:S(2)}) %collective-permute-start) | collective-permute-done | bytes 262176 | tf_op jit(solution)/shard_map/ppermute | solution.py:542
  48.3 3.1 %collective-permute-start.23 = (bf16[256,256]{1,0:T(8,128)(2,1)S(1)}, bf16[256,256]{1,0:T(8,128)(2,1)S(1)}, u32[]{:S(2)}, u32[]{:S(2)}) collective-permute-start(bf16[256,256]{1,0:T(8,128)(2,1)S(1)} %get-tuple-element.89), channel_id=1, source_target_pairs={{0,2},{1,3},{2,0},{3,1},{4,6},{5,7},{6,4},{7,5},{8,10},{9,11},{10,... | collective-permute-start | bytes 393224 | tf_op jit(solution)/shard_map/ppermute | solution.py:543
  53.5 4.0 %tile_sums.5 = (bf16[512,256]{1,0:T(8,128)(2,1)S(1)}, bf16[512,256]{1,0:T(8,128)(2,1)S(1)}, bf16[512,256]{1,0:T(8,128)(2,1)S(1)}, bf16[512,256]{1,0:T(8,128)(2,1)S(1)}) custom-call(s32[4,64]{1,0:T(4,128)S(1)} %bitcast.20, s32[64]{0:T(128)S(1)} %bitcast.30, s32[4,64]{1,0:T(4,128)S(1)} %bitcast.25, s32[64]{0:T(128)S(1)} %bitcast.35, ...), custom_call_target="tpu_custom_call" | custom-call | flops 2000000000 | bytes 6291456 | tf_op jit(solution)/shard_map/tile_sums/pallas_call | solution.py:313
  57.6 10.2 %collective-permute-done.23.refs_2_ = bf16[256,256]{1,0:T(8,128)(2,1)S(1)} collective-permute-done((bf16[256,256]{1,0:T(8,128)(2,1)S(1)}, bf16[256,256]{1,0:T(8,128)(2,1)S(1)}, u32[]{:S(2)}, u32[]{:S(2)}) %collective-permute-start.23) | collective-permute-done | bytes 131104 | tf_op jit(solution)/shard_map/ppermute | solution.py:543
  70.0 3.4 %collective-permute-start.27 = (bf16[256,256]{1,0:T(8,128)(2,1)S(1)}, bf16[256,256]{1,0:T(8,128)(2,1)S(1)}, u32[]{:S(2)}, u32[]{:S(2)}) collective-permute-start(bf16[256,256]{1,0:T(8,128)(2,1)S(1)} %get-tuple-element.94), channel_id=1, source_target_pairs={{0,3},{1,0},{2,1},{3,2},{4,7},{5,4},{6,5},{7,6},{8,11},{9,8},{10,9... | collective-permute-start | bytes 393224 | tf_op jit(solution)/shard_map/ppermute | solution.py:543
  73.4 4.0 %tile_sums.6 = (bf16[512,256]{1,0:T(8,128)(2,1)S(1)}, bf16[512,256]{1,0:T(8,128)(2,1)S(1)}, bf16[512,256]{1,0:T(8,128)(2,1)S(1)}, bf16[512,256]{1,0:T(8,128)(2,1)S(1)}) custom-call(s32[4,64]{1,0:T(4,128)S(1)} %bitcast.21, s32[64]{0:T(128)S(1)} %bitcast.31, s32[4,64]{1,0:T(4,128)S(1)} %bitcast.26, s32[64]{0:T(128)S(1)} %bitcast.36, ...), custom_call_target="tpu_custom_call" | custom-call | flops 2000000000 | bytes 6291456 | tf_op jit(solution)/shard_map/tile_sums/pallas_call | solution.py:313
  79.9 3.4 %collective-permute-start.20 = (bf16[512,256]{1,0:T(8,128)(2,1)S(1)}, bf16[512,256]{1,0:T(8,128)(2,1)S(1)}, u32[]{:S(2)}, u32[]{:S(2)}) collective-permute-start(bf16[512,256]{1,0:T(8,128)(2,1)S(1)} %get-tuple-element.85), channel_id=1, source_target_pairs={{0,2},{1,3},{2,0},{3,1},{4,6},{5,7},{6,4},{7,5},{8,10},{9,11},{10,... | collective-permute-start | bytes 786440 | tf_op jit(solution)/shard_map/ppermute | solution.py:543
  83.3 4.0 %tile_sums.4 = (bf16[512,256]{1,0:T(8,128)(2,1)S(1)}, bf16[512,256]{1,0:T(8,128)(2,1)S(1)}, bf16[512,256]{1,0:T(8,128)(2,1)S(1)}, bf16[512,256]{1,0:T(8,128)(2,1)S(1)}) custom-call(s32[4,64]{1,0:T(4,128)S(1)} %bitcast.22, s32[64]{0:T(128)S(1)} %bitcast.32, s32[4,64]{1,0:T(4,128)S(1)} %bitcast.27, s32[64]{0:T(128)S(1)} %bitcast.37, ...), custom_call_target="tpu_custom_call" | custom-call | flops 2000000000 | bytes 6291456 | tf_op jit(solution)/shard_map/tile_sums/pallas_call | solution.py:313
  88.8 2.9 %collective-permute-start.18 = (bf16[512,256]{1,0:T(8,128)(2,1)S(1)}, bf16[512,256]{1,0:T(8,128)(2,1)S(1)}, u32[]{:S(2)}, u32[]{:S(2)}) collective-permute-start(bf16[512,256]{1,0:T(8,128)(2,1)S(1)} %get-tuple-element.82), channel_id=1, source_target_pairs={{0,3},{1,0},{2,1},{3,2},{4,7},{5,4},{6,5},{7,6},{8,11},{9,8},{10,9... | collective-permute-start | bytes 786440 | tf_op jit(solution)/shard_map/ppermute | solution.py:543
  92.0 9.3 %collective-permute-done.20.refs_2_ = bf16[512,256]{1,0:T(8,128)(2,1)S(1)} collective-permute-done((bf16[512,256]{1,0:T(8,128)(2,1)S(1)}, bf16[512,256]{1,0:T(8,128)(2,1)S(1)}, u32[]{:S(2)}, u32[]{:S(2)}) %collective-permute-start.20) | collective-permute-done | bytes 262176 | tf_op jit(solution)/shard_map/ppermute | solution.py:543
  101.3 17.0 %collective-permute-start.9 = (bf16[512,256]{1,0:T(8,128)(2,1)S(1)}, bf16[512,256]{1,0:T(8,128)(2,1)S(1)}, u32[]{:S(2)}, u32[]{:S(2)}) collective-permute-start(bf16[512,256]{1,0:T(8,128)(2,1)S(1)} %get-tuple-element.76), channel_id=1, source_target_pairs={{0,3},{1,0},{2,1},{3,2},{4,7},{5,4},{6,5},{7,6},{8,11},{9,8},{10,9... | collective-permute-start | bytes 786440 | tf_op jit(solution)/shard_map/ppermute | solution.py:543
  123.4 5.1 %collective-permute-done.17.refs_2_ = bf16[512,256]{1,0:T(8,128)(2,1)S(1)} collective-permute-done((bf16[512,256]{1,0:T(8,128)(2,1)S(1)}, bf16[512,256]{1,0:T(8,128)(2,1)S(1)}, u32[]{:S(2)}, u32[]{:S(2)}) %collective-permute-start.17) | collective-permute-done | bytes 262176 | tf_op jit(solution)/shard_map/ppermute | solution.py:543
  131.1 8.7 %collective-permute-done.8.refs_2_ = bf16[512,256]{1,0:T(8,128)(2,1)S(1)} collective-permute-done((bf16[512,256]{1,0:T(8,128)(2,1)S(1)}, bf16[512,256]{1,0:T(8,128)(2,1)S(1)}, u32[]{:S(2)}, u32[]{:S(2)}) %collective-permute-start.8) | collective-permute-done | bytes 262176 | tf_op jit(solution)/shard_map/ppermute | solution.py:543
  142.4 9.9 %all-gather = f32[64,256]{1,0:T(8,128)S(1)} all-gather(f32[8,256]{1,0:T(8,128)S(1)} %get-tuple-element.103), channel_id=2, replica_groups=mesh['dom'=8,'col'=4] {'dom'}, dimensions={0}, use_global_device_ids=true | all-gather | bytes 73728 | tf_op jit(solution)/shard_map/all_gather | solution.py:607
  152.3 5.0 %collective-permute-start.40 = (bf16[256,256]{1,0:T(8,128)(2,1)S(1)}, bf16[256,256]{1,0:T(8,128)(2,1)S(1)}, u32[]{:S(2)}, u32[]{:S(2)}) collective-permute-start(bf16[256,256]{1,0:T(8,128)(2,1)S(1)} %get-tuple-element.113), channel_id=1, source_target_pairs={{0,3},{1,0},{2,1},{3,2},{4,7},{5,4},{6,5},{7,6},{8,11},{9,8},{10,9... | collective-permute-start | bytes 393224 | tf_op jit(solution)/shard_map/ppermute | solution.py:543
  159.9 3.8 %collective-permute-start.43 = (bf16[256,256]{1,0:T(8,128)(2,1)S(1)}, bf16[256,256]{1,0:T(8,128)(2,1)S(1)}, u32[]{:S(2)}, u32[]{:S(2)}) collective-permute-start(bf16[256,256]{1,0:T(8,128)(2,1)S(1)} %get-tuple-element.117), channel_id=1, source_target_pairs={{0,3},{1,0},{2,1},{3,2},{4,7},{5,4},{6,5},{7,6},{8,11},{9,8},{10,9... | collective-permute-start | bytes 393224 | tf_op jit(solution)/shard_map/ppermute | solution.py:543
  163.8 5.4 %collective-permute-done.31.refs_5_ = f32[2,256]{1,0:T(2,128)S(1)} collective-permute-done((f32[2,256]{1,0:T(2,128)S(1)}, f32[2,256]{1,0:T(2,128)S(1)}, u32[]{:S(2)}, u32[]{:S(2)}) %collective-permute-start.31) | collective-permute-done | bytes 2080 | tf_op jit(solution)/shard_map/ppermute | solution.py:543
  169.2 5.4 %collective-permute-start.44 = (bf16[256,256]{1,0:T(8,128)(2,1)S(1)}, bf16[256,256]{1,0:T(8,128)(2,1)S(1)}, u32[]{:S(2)}, u32[]{:S(2)}) collective-permute-start(bf16[256,256]{1,0:T(8,128)(2,1)S(1)} %get-tuple-element.118), channel_id=1, source_target_pairs={{0,2},{1,3},{2,0},{3,1},{4,6},{5,7},{6,4},{7,5},{8,10},{9,11},{10,... | collective-permute-start | bytes 393224 | tf_op jit(solution)/shard_map/ppermute | solution.py:543
  174.6 3.4 %collective-permute-start.34 = (bf16[512,256]{1,0:T(8,128)(2,1)S(1)}, bf16[512,256]{1,0:T(8,128)(2,1)S(1)}, u32[]{:S(2)}, u32[]{:S(2)}) collective-permute-start(bf16[512,256]{1,0:T(8,128)(2,1)S(1)} %get-tuple-element.105), channel_id=1, source_target_pairs={{0,3},{1,0},{2,1},{3,2},{4,7},{5,4},{6,5},{7,6},{8,11},{9,8},{10,9... | collective-permute-start | bytes 786440 | tf_op jit(solution)/shard_map/ppermute | solution.py:543
  180.2 17.8 %collective-permute-start.45 = (bf16[256,256]{1,0:T(8,128)(2,1)S(1)}, bf16[256,256]{1,0:T(8,128)(2,1)S(1)}, u32[]{:S(2)}, u32[]{:S(2)}) collective-permute-start(bf16[256,256]{1,0:T(8,128)(2,1)S(1)} %get-tuple-element.119), channel_id=1, source_target_pairs={{0,1},{1,2},{2,3},{3,0},{4,5},{5,6},{6,7},{7,4},{8,9},{9,10},{10,1... | collective-permute-start | bytes 393224 | tf_op jit(solution)/shard_map/ppermute | solution.py:543
  198.0 8.1 %collective-permute-done.45.refs_3_ = bf16[256,256]{1,0:T(8,128)(2,1)S(1)} collective-permute-done((bf16[256,256]{1,0:T(8,128)(2,1)S(1)}, bf16[256,256]{1,0:T(8,128)(2,1)S(1)}, u32[]{:S(2)}, u32[]{:S(2)}) %collective-permute-start.45) | collective-permute-done | bytes 131104 | tf_op jit(solution)/shard_map/ppermute | solution.py:543
  206.1 7.8 %collective-permute-start.35 = (bf16[512,256]{1,0:T(8,128)(2,1)S(1)}, bf16[512,256]{1,0:T(8,128)(2,1)S(1)}, u32[]{:S(2)}, u32[]{:S(2)}) collective-permute-start(bf16[512,256]{1,0:T(8,128)(2,1)S(1)} %get-tuple-element.106), channel_id=1, source_target_pairs={{0,2},{1,3},{2,0},{3,1},{4,6},{5,7},{6,4},{7,5},{8,10},{9,11},{10,... | collective-permute-start | bytes 786440 | tf_op jit(solution)/shard_map/ppermute | solution.py:543
  213.9 3.8 %collective-permute-start.28 = (bf16[512,256]{1,0:T(8,128)(2,1)S(1)}, bf16[512,256]{1,0:T(8,128)(2,1)S(1)}, u32[]{:S(2)}, u32[]{:S(2)}) collective-permute-start(bf16[512,256]{1,0:T(8,128)(2,1)S(1)} %get-tuple-element.100), channel_id=1, source_target_pairs={{0,3},{1,0},{2,1},{3,2},{4,7},{5,4},{6,5},{7,6},{8,11},{9,8},{10,9... | collective-permute-start | bytes 786440 | tf_op jit(solution)/shard_map/ppermute | solution.py:543
  221.1 11.8 %collective-permute-done.35.refs_2_ = bf16[512,256]{1,0:T(8,128)(2,1)S(1)} collective-permute-done((bf16[512,256]{1,0:T(8,128)(2,1)S(1)}, bf16[512,256]{1,0:T(8,128)(2,1)S(1)}, u32[]{:S(2)}, u32[]{:S(2)}) %collective-permute-start.35) | collective-permute-done | bytes 262176 | tf_op jit(solution)/shard_map/ppermute | solution.py:543
  232.8 8.3 %collective-permute-start.33 = (f32[2,256]{1,0:T(2,128)S(1)}, f32[2,256]{1,0:T(2,128)S(1)}, u32[]{:S(2)}, u32[]{:S(2)}) collective-permute-start(f32[2,256]{1,0:T(2,128)S(1)} %get-tuple-element.120), channel_id=1, source_target_pairs={{0,1},{1,2},{2,3},{3,0},{4,5},{5,6},{6,7},{7,4},{8,9},{9,10},{10,1... | collective-permute-start | bytes 6152 | tf_op jit(solution)/shard_map/ppermute | solution.py:543
  242.2 11.9 %collective-permute-done.32.refs_6_ = f32[2,256]{1,0:T(2,128)S(1)} collective-permute-done((f32[2,256]{1,0:T(2,128)S(1)}, f32[2,256]{1,0:T(2,128)S(1)}, u32[]{:S(2)}, u32[]{:S(2)}) %collective-permute-start.32) | collective-permute-done | bytes 2080 | tf_op jit(solution)/shard_map/ppermute | solution.py:543
  (98 shorter events, 49.2 us)
Async XLA Ops:
  4.0 24.8 %collective-permute-start.1 = (bf16[512,256]{1,0:T(8,128)(2,1)S(1)}, bf16[512,256]{1,0:T(8,128)(2,1)S(1)}, u32[]{:S(2)}, u32[]{:S(2)}) collective-permute-start(bf16[512,256]{1,0:T(8,128)(2,1)S(1)} %get-tuple-element.66), channel_id=1, source_target_pairs={{0,28},{4,24},{8,20},{12,16},{16,12},{20,8},{24,4},{28,0},{1,29},{... | collective-permute-start | bytes 786440 | tf_op jit(solution)/shard_map/ppermute | solution.py:542
  11.2 18.5 %collective-permute-start.2 = (bf16[512,256]{1,0:T(8,128)(2,1)S(1)}, bf16[512,256]{1,0:T(8,128)(2,1)S(1)}, u32[]{:S(2)}, u32[]{:S(2)}) collective-permute-start(bf16[512,256]{1,0:T(8,128)(2,1)S(1)} %get-tuple-element.67), channel_id=1, source_target_pairs={{0,24},{4,28},{8,16},{12,20},{16,8},{20,12},{24,0},{28,4},{1,25},{... | collective-permute-start | bytes 786440 | tf_op jit(solution)/shard_map/ppermute | solution.py:542
  32.8 35.0 %collective-permute-start.14 = (bf16[816,256]{1,0:T(8,128)(2,1)S(1)}, bf16[816,256]{1,0:T(8,128)(2,1)S(1)}, u32[]{:S(2)}, u32[]{:S(2)}) collective-permute-start(bf16[816,256]{1,0:T(8,128)(2,1)S(1)} %pack_rows.1.refs_0_), channel_id=1, source_target_pairs={{0,8},{4,12},{8,0},{12,4},{16,24},{20,28},{24,16},{28,20},{1,9},{5... | collective-permute-start | bytes 1253384 | tf_op jit(solution)/shard_map/ppermute | solution.py:575
  48.3 19.4 %collective-permute-start.23 = (bf16[256,256]{1,0:T(8,128)(2,1)S(1)}, bf16[256,256]{1,0:T(8,128)(2,1)S(1)}, u32[]{:S(2)}, u32[]{:S(2)}) collective-permute-start(bf16[256,256]{1,0:T(8,128)(2,1)S(1)} %get-tuple-element.89), channel_id=1, source_target_pairs={{0,2},{1,3},{2,0},{3,1},{4,6},{5,7},{6,4},{7,5},{8,10},{9,11},{10,... | collective-permute-start | bytes 393224 | tf_op jit(solution)/shard_map/ppermute | solution.py:543
  51.4 16.8 %collective-permute-start.24 = (bf16[256,256]{1,0:T(8,128)(2,1)S(1)}, bf16[256,256]{1,0:T(8,128)(2,1)S(1)}, u32[]{:S(2)}, u32[]{:S(2)}) collective-permute-start(bf16[256,256]{1,0:T(8,128)(2,1)S(1)} %get-tuple-element.90), channel_id=1, source_target_pairs={{0,3},{1,0},{2,1},{3,2},{4,7},{5,4},{6,5},{7,6},{8,11},{9,8},{10,9... | collective-permute-start | bytes 393224 | tf_op jit(solution)/shard_map/ppermute | solution.py:543
  51.4 18.6 %collective-permute-start.25 = (bf16[256,256]{1,0:T(8,128)(2,1)S(1)}, bf16[256,256]{1,0:T(8,128)(2,1)S(1)}, u32[]{:S(2)}, u32[]{:S(2)}) collective-permute-start(bf16[256,256]{1,0:T(8,128)(2,1)S(1)} %get-tuple-element.92), channel_id=1, source_target_pairs={{0,1},{1,2},{2,3},{3,0},{4,5},{5,6},{6,7},{7,4},{8,9},{9,10},{10,1... | collective-permute-start | bytes 393224 | tf_op jit(solution)/shard_map/ppermute | solution.py:543
  57.4 25.8 %collective-permute-start.16 = (bf16[512,256]{1,0:T(8,128)(2,1)S(1)}, bf16[512,256]{1,0:T(8,128)(2,1)S(1)}, u32[]{:S(2)}, u32[]{:S(2)}) collective-permute-start(bf16[512,256]{1,0:T(8,128)(2,1)S(1)} %get-tuple-element.80), channel_id=1, source_target_pairs={{0,1},{1,2},{2,3},{3,0},{4,5},{5,6},{6,7},{7,4},{8,9},{9,10},{10,1... | collective-permute-start | bytes 786440 | tf_op jit(solution)/shard_map/ppermute | solution.py:543
  67.8 19.5 %collective-permute-start.13 = (bf16[816,256]{1,0:T(8,128)(2,1)S(1)}, bf16[816,256]{1,0:T(8,128)(2,1)S(1)}, u32[]{:S(2)}, u32[]{:S(2)}) collective-permute-start(bf16[816,256]{1,0:T(8,128)(2,1)S(1)} %pack_rows.1.refs_0_), channel_id=1, source_target_pairs={{0,4},{4,0},{8,12},{12,8},{16,20},{20,16},{24,28},{28,24},{1,5},{5... | collective-permute-start | bytes 1253384 | tf_op jit(solution)/shard_map/ppermute | solution.py:575
  67.8 21.0 %collective-permute-start.15 = (bf16[816,256]{1,0:T(8,128)(2,1)S(1)}, bf16[816,256]{1,0:T(8,128)(2,1)S(1)}, u32[]{:S(2)}, u32[]{:S(2)}) collective-permute-start(bf16[816,256]{1,0:T(8,128)(2,1)S(1)} %collective-permute-done.14.refs_2_), channel_id=1, source_target_pairs={{0,4},{4,0},{8,12},{12,8},{16,20},{20,16},{24,28},{28,24},{1,5},{5... | collective-permute-start | bytes 1253384 | tf_op jit(solution)/shard_map/ppermute | solution.py:575
  79.9 21.4 %collective-permute-start.20 = (bf16[512,256]{1,0:T(8,128)(2,1)S(1)}, bf16[512,256]{1,0:T(8,128)(2,1)S(1)}, u32[]{:S(2)}, u32[]{:S(2)}) collective-permute-start(bf16[512,256]{1,0:T(8,128)(2,1)S(1)} %get-tuple-element.85), channel_id=1, source_target_pairs={{0,2},{1,3},{2,0},{3,1},{4,6},{5,7},{6,4},{7,5},{8,10},{9,11},{10,... | collective-permute-start | bytes 786440 | tf_op jit(solution)/shard_map/ppermute | solution.py:543
  83.3 18.0 %collective-permute-start.21 = (bf16[512,256]{1,0:T(8,128)(2,1)S(1)}, bf16[512,256]{1,0:T(8,128)(2,1)S(1)}, u32[]{:S(2)}, u32[]{:S(2)}) collective-permute-start(bf16[512,256]{1,0:T(8,128)(2,1)S(1)} %get-tuple-element.86), channel_id=1, source_target_pairs={{0,3},{1,0},{2,1},{3,2},{4,7},{5,4},{6,5},{7,6},{8,11},{9,8},{10,9... | collective-permute-start | bytes 786440 | tf_op jit(solution)/shard_map/ppermute | solution.py:543
  87.3 41.3 %collective-permute-start.17 = (bf16[512,256]{1,0:T(8,128)(2,1)S(1)}, bf16[512,256]{1,0:T(8,128)(2,1)S(1)}, u32[]{:S(2)}, u32[]{:S(2)}) collective-permute-start(bf16[512,256]{1,0:T(8,128)(2,1)S(1)} %get-tuple-element.81), channel_id=1, source_target_pairs={{0,2},{1,3},{2,0},{3,1},{4,6},{5,7},{6,4},{7,5},{8,10},{9,11},{10,... | collective-permute-start | bytes 786440 | tf_op jit(solution)/shard_map/ppermute | solution.py:543
  88.8 39.8 %collective-permute-start.18 = (bf16[512,256]{1,0:T(8,128)(2,1)S(1)}, bf16[512,256]{1,0:T(8,128)(2,1)S(1)}, u32[]{:S(2)}, u32[]{:S(2)}) collective-permute-start(bf16[512,256]{1,0:T(8,128)(2,1)S(1)} %get-tuple-element.82), channel_id=1, source_target_pairs={{0,3},{1,0},{2,1},{3,2},{4,7},{5,4},{6,5},{7,6},{8,11},{9,8},{10,9... | collective-permute-start | bytes 786440 | tf_op jit(solution)/shard_map/ppermute | solution.py:543
  91.9 39.2 %collective-permute-start.7 = (bf16[512,256]{1,0:T(8,128)(2,1)S(1)}, bf16[512,256]{1,0:T(8,128)(2,1)S(1)}, u32[]{:S(2)}, u32[]{:S(2)}) collective-permute-start(bf16[512,256]{1,0:T(8,128)(2,1)S(1)} %get-tuple-element.74), channel_id=1, source_target_pairs={{0,1},{1,2},{2,3},{3,0},{4,5},{5,6},{6,7},{7,4},{8,9},{9,10},{10,1... | collective-permute-start | bytes 786440 | tf_op jit(solution)/shard_map/ppermute | solution.py:543
  101.3 38.5 %collective-permute-start.8 = (bf16[512,256]{1,0:T(8,128)(2,1)S(1)}, bf16[512,256]{1,0:T(8,128)(2,1)S(1)}, u32[]{:S(2)}, u32[]{:S(2)}) collective-permute-start(bf16[512,256]{1,0:T(8,128)(2,1)S(1)} %get-tuple-element.75), channel_id=1, source_target_pairs={{0,2},{1,3},{2,0},{3,1},{4,6},{5,7},{6,4},{7,5},{8,10},{9,11},{10,... | collective-permute-start | bytes 786440 | tf_op jit(solution)/shard_map/ppermute | solution.py:543
  101.3 38.5 %collective-permute-start.9 = (bf16[512,256]{1,0:T(8,128)(2,1)S(1)}, bf16[512,256]{1,0:T(8,128)(2,1)S(1)}, u32[]{:S(2)}, u32[]{:S(2)}) collective-permute-start(bf16[512,256]{1,0:T(8,128)(2,1)S(1)} %get-tuple-element.76), channel_id=1, source_target_pairs={{0,3},{1,0},{2,1},{3,2},{4,7},{5,4},{6,5},{7,6},{8,11},{9,8},{10,9... | collective-permute-start | bytes 786440 | tf_op jit(solution)/shard_map/ppermute | solution.py:543
  152.3 22.3 %collective-permute-start.40 = (bf16[256,256]{1,0:T(8,128)(2,1)S(1)}, bf16[256,256]{1,0:T(8,128)(2,1)S(1)}, u32[]{:S(2)}, u32[]{:S(2)}) collective-permute-start(bf16[256,256]{1,0:T(8,128)(2,1)S(1)} %get-tuple-element.113), channel_id=1, source_target_pairs={{0,3},{1,0},{2,1},{3,2},{4,7},{5,4},{6,5},{7,6},{8,11},{9,8},{10,9... | collective-permute-start | bytes 393224 | tf_op jit(solution)/shard_map/ppermute | solution.py:543
  157.4 20.6 %collective-permute-start.41 = (bf16[256,256]{1,0:T(8,128)(2,1)S(1)}, bf16[256,256]{1,0:T(8,128)(2,1)S(1)}, u32[]{:S(2)}, u32[]{:S(2)}) collective-permute-start(bf16[256,256]{1,0:T(8,128)(2,1)S(1)} %get-tuple-element.114), channel_id=1, source_target_pairs={{0,2},{1,3},{2,0},{3,1},{4,6},{5,7},{6,4},{7,5},{8,10},{9,11},{10,... | collective-permute-start | bytes 393224 | tf_op jit(solution)/shard_map/ppermute | solution.py:543
  159.9 18.1 %collective-permute-start.42 = (bf16[256,256]{1,0:T(8,128)(2,1)S(1)}, bf16[256,256]{1,0:T(8,128)(2,1)S(1)}, u32[]{:S(2)}, u32[]{:S(2)}) collective-permute-start(bf16[256,256]{1,0:T(8,128)(2,1)S(1)} %get-tuple-element.115), channel_id=1, source_target_pairs={{0,1},{1,2},{2,3},{3,0},{4,5},{5,6},{6,7},{7,4},{8,9},{9,10},{10,1... | collective-permute-start | bytes 393224 | tf_op jit(solution)/shard_map/ppermute | solution.py:543
  159.9 18.2 %collective-permute-start.43 = (bf16[256,256]{1,0:T(8,128)(2,1)S(1)}, bf16[256,256]{1,0:T(8,128)(2,1)S(1)}, u32[]{:S(2)}, u32[]{:S(2)}) collective-permute-start(bf16[256,256]{1,0:T(8,128)(2,1)S(1)} %get-tuple-element.117), channel_id=1, source_target_pairs={{0,3},{1,0},{2,1},{3,2},{4,7},{5,4},{6,5},{7,6},{8,11},{9,8},{10,9... | collective-permute-start | bytes 393224 | tf_op jit(solution)/shard_map/ppermute | solution.py:543
  174.6 39.3 %collective-permute-start.34 = (bf16[512,256]{1,0:T(8,128)(2,1)S(1)}, bf16[512,256]{1,0:T(8,128)(2,1)S(1)}, u32[]{:S(2)}, u32[]{:S(2)}) collective-permute-start(bf16[512,256]{1,0:T(8,128)(2,1)S(1)} %get-tuple-element.105), channel_id=1, source_target_pairs={{0,3},{1,0},{2,1},{3,2},{4,7},{5,4},{6,5},{7,6},{8,11},{9,8},{10,9... | collective-permute-start | bytes 786440 | tf_op jit(solution)/shard_map/ppermute | solution.py:543
  178.0 35.9 %collective-permute-start.37 = (bf16[512,256]{1,0:T(8,128)(2,1)S(1)}, bf16[512,256]{1,0:T(8,128)(2,1)S(1)}, u32[]{:S(2)}, u32[]{:S(2)}) collective-permute-start(bf16[512,256]{1,0:T(8,128)(2,1)S(1)} %get-tuple-element.109), channel_id=1, source_target_pairs={{0,3},{1,0},{2,1},{3,2},{4,7},{5,4},{6,5},{7,6},{8,11},{9,8},{10,9... | collective-permute-start | bytes 786440 | tf_op jit(solution)/shard_map/ppermute | solution.py:543
  178.0 39.7 %collective-permute-start.38 = (bf16[512,256]{1,0:T(8,128)(2,1)S(1)}, bf16[512,256]{1,0:T(8,128)(2,1)S(1)}, u32[]{:S(2)}, u32[]{:S(2)}) collective-permute-start(bf16[512,256]{1,0:T(8,128)(2,1)S(1)} %get-tuple-element.110), channel_id=1, source_target_pairs={{0,2},{1,3},{2,0},{3,1},{4,6},{5,7},{6,4},{7,5},{8,10},{9,11},{10,... | collective-permute-start | bytes 786440 | tf_op jit(solution)/shard_map/ppermute | solution.py:543
  178.1 39.7 %collective-permute-start.39 = (bf16[512,256]{1,0:T(8,128)(2,1)S(1)}, bf16[512,256]{1,0:T(8,128)(2,1)S(1)}, u32[]{:S(2)}, u32[]{:S(2)}) collective-permute-start(bf16[512,256]{1,0:T(8,128)(2,1)S(1)} %get-tuple-element.111), channel_id=1, source_target_pairs={{0,1},{1,2},{2,3},{3,0},{4,5},{5,6},{6,7},{7,4},{8,9},{9,10},{10,1... | collective-permute-start | bytes 786440 | tf_op jit(solution)/shard_map/ppermute | solution.py:543
  180.2 25.9 %collective-permute-start.45 = (bf16[256,256]{1,0:T(8,128)(2,1)S(1)}, bf16[256,256]{1,0:T(8,128)(2,1)S(1)}, u32[]{:S(2)}, u32[]{:S(2)}) collective-permute-start(bf16[256,256]{1,0:T(8,128)(2,1)S(1)} %get-tuple-element.119), channel_id=1, source_target_pairs={{0,1},{1,2},{2,3},{3,0},{4,5},{5,6},{6,7},{7,4},{8,9},{9,10},{10,1... | collective-permute-start | bytes 393224 | tf_op jit(solution)/shard_map/ppermute | solution.py:543
  206.1 26.7 %collective-permute-start.35 = (bf16[512,256]{1,0:T(8,128)(2,1)S(1)}, bf16[512,256]{1,0:T(8,128)(2,1)S(1)}, u32[]{:S(2)}, u32[]{:S(2)}) collective-permute-start(bf16[512,256]{1,0:T(8,128)(2,1)S(1)} %get-tuple-element.106), channel_id=1, source_target_pairs={{0,2},{1,3},{2,0},{3,1},{4,6},{5,7},{6,4},{7,5},{8,10},{9,11},{10,... | collective-permute-start | bytes 786440 | tf_op jit(solution)/shard_map/ppermute | solution.py:543
  213.9 18.9 %collective-permute-start.36 = (bf16[512,256]{1,0:T(8,128)(2,1)S(1)}, bf16[512,256]{1,0:T(8,128)(2,1)S(1)}, u32[]{:S(2)}, u32[]{:S(2)}) collective-permute-start(bf16[512,256]{1,0:T(8,128)(2,1)S(1)} %get-tuple-element.107), channel_id=1, source_target_pairs={{0,1},{1,2},{2,3},{3,0},{4,5},{5,6},{6,7},{7,4},{8,9},{9,10},{10,1... | collective-permute-start | bytes 786440 | tf_op jit(solution)/shard_map/ppermute | solution.py:543
  213.9 40.2 %collective-permute-start.28 = (bf16[512,256]{1,0:T(8,128)(2,1)S(1)}, bf16[512,256]{1,0:T(8,128)(2,1)S(1)}, u32[]{:S(2)}, u32[]{:S(2)}) collective-permute-start(bf16[512,256]{1,0:T(8,128)(2,1)S(1)} %get-tuple-element.100), channel_id=1, source_target_pairs={{0,3},{1,0},{2,1},{3,2},{4,7},{5,4},{6,5},{7,6},{8,11},{9,8},{10,9... | collective-permute-start | bytes 786440 | tf_op jit(solution)/shard_map/ppermute | solution.py:543
  217.7 36.4 %collective-permute-start.29 = (bf16[512,256]{1,0:T(8,128)(2,1)S(1)}, bf16[512,256]{1,0:T(8,128)(2,1)S(1)}, u32[]{:S(2)}, u32[]{:S(2)}) collective-permute-start(bf16[512,256]{1,0:T(8,128)(2,1)S(1)} %get-tuple-element.101), channel_id=1, source_target_pairs={{0,2},{1,3},{2,0},{3,1},{4,6},{5,7},{6,4},{7,5},{8,10},{9,11},{10,... | collective-permute-start | bytes 786440 | tf_op jit(solution)/shard_map/ppermute | solution.py:543
  217.7 36.4 %collective-permute-start.30 = (bf16[512,256]{1,0:T(8,128)(2,1)S(1)}, bf16[512,256]{1,0:T(8,128)(2,1)S(1)}, u32[]{:S(2)}, u32[]{:S(2)}) collective-permute-start(bf16[512,256]{1,0:T(8,128)(2,1)S(1)} %get-tuple-element.102), channel_id=1, source_target_pairs={{0,1},{1,2},{2,3},{3,0},{4,5},{5,6},{6,7},{7,4},{8,9},{9,10},{10,1... | collective-permute-start | bytes 786440 | tf_op jit(solution)/shard_map/ppermute | solution.py:543
  232.8 21.3 %collective-permute-start.32 = (f32[2,256]{1,0:T(2,128)S(1)}, f32[2,256]{1,0:T(2,128)S(1)}, u32[]{:S(2)}, u32[]{:S(2)}) collective-permute-start(f32[2,256]{1,0:T(2,128)S(1)} %get-tuple-element.121), channel_id=1, source_target_pairs={{0,2},{1,3},{2,0},{3,1},{4,6},{5,7},{6,4},{7,5},{8,10},{9,11},{10,... | collective-permute-start | bytes 6152 | tf_op jit(solution)/shard_map/ppermute | solution.py:543
  232.8 21.3 %collective-permute-start.33 = (f32[2,256]{1,0:T(2,128)S(1)}, f32[2,256]{1,0:T(2,128)S(1)}, u32[]{:S(2)}, u32[]{:S(2)}) collective-permute-start(f32[2,256]{1,0:T(2,128)S(1)} %get-tuple-element.120), channel_id=1, source_target_pairs={{0,1},{1,2},{2,3},{3,0},{4,5},{5,6},{6,7},{7,4},{8,9},{9,10},{10,1... | collective-permute-start | bytes 6152 | tf_op jit(solution)/shard_map/ppermute | solution.py:543
  (20 other events, 227.9 us)

commit v4 on v3

--- a/solution.py
+++ b/solution.py
@@ -55,14 +55,15 @@
     return tiled.transpose(0, 2, 1, 3).reshape(-1), first, within
 
 
-def widen(feat, table, raw, sems):
+def widen(feat, half, table, raw, sems):
     n_rows = raw.shape[0]
     parts = sems.shape[0]
     part = n_rows // parts
-    step = 64
+    step = 128 if part % 128 == 0 else 16
+    lanes = pl.ds(half * LANES, LANES)
     copies = [
         pltpu.make_async_copy(
-            feat.at[pl.ds(c * part, part)], raw.at[pl.ds(c * part, part)], sems.at[c]
+            feat.at[pl.ds(c * part, part), lanes], raw.at[pl.ds(c * part, part)], sems.at[c]
         )
         for c in range(parts)
     ]
@@ -72,30 +73,28 @@
         copies[c].wait()
 
         def one(b, carry, c=c):
-            row = pl.multiple_of(c * part + b * step, step)
-            halves = raw.shape[1] // LANES
-            for h in range(halves):
-                wide = raw[pl.ds(row, step), pl.ds(h * LANES, LANES)].astype(jnp.float32)
-                table[pl.ds(row * halves + h, step, stride=halves), :] = wide
+            at = pl.ds(pl.multiple_of(c * part + b * step, step), step)
+            table[at, :] = raw[at, :].astype(jnp.float32)
             return carry
 
         lax.fori_loop(0, part // step, one, 0)
 
 
-def gather_kernel(peers, peer, first_row, within, first, halves, rows_in, counts_in, *refs):
+def gather_kernel(peers, peer, first_row, within, half, build, rows_in, counts_in, *refs):
     n_out = len(peers)
-    if first:
-        feat, outs, (table, raw) = refs[0], refs[1 : n_out + 1], refs[n_out + 1 : n_out + 3]
+    outs = refs[1 : n_out + 1]
+    if build:
+        feat, (table, raw) = refs[0], refs[n_out + 1 : n_out + 3]
         rows, counts, index_sems, stage, sems = refs[n_out + 3 :]
     else:
-        table, outs = refs[0], refs[1 : n_out + 1]
+        table = refs[0]
         rows, counts, index_sems, stage = refs[n_out + 1 :]
     load_rows = pltpu.make_async_copy(rows_in, rows, index_sems.at[0])
     load_counts = pltpu.make_async_copy(counts_in, counts, index_sems.at[1])
     load_rows.start()
     load_counts.start()
-    if first:
-        widen(feat, table, raw, sems)
+    if build:
+        widen(feat, half, table, raw, sems)
     load_rows.wait()
     load_counts.wait()
     me = lax.axis_index("dom")
@@ -107,48 +106,45 @@
 
         def pick(b, carry, begin=begin):
             base = begin + within(b)
-            put = pl.multiple_of(b * (UNROLL * halves), UNROLL * halves)
+            put = pl.multiple_of(b * UNROLL, UNROLL)
             source = [rows[base + j] for j in range(UNROLL)]
-            got = [table[pl.ds(r * halves, halves), :] for r in source]
+            got = [table[pl.ds(r, 1), :] for r in source]
             for j in range(UNROLL):
-                stage[pl.ds(put + j * halves, halves), :] = got[j]
+                stage[pl.ds(put + j, 1), :] = got[j]
             return carry
 
         lax.fori_loop(0, (used + UNROLL - 1) // UNROLL, pick, 0)
         for b in range(slots // 64):
+            at = pl.ds(b * 64, 64)
             slot = b * 64 + lax.broadcasted_iota(jnp.int32, (64, LANES), 0)
-            for h in range(halves):
-                wide = stage[pl.ds(b * 64 * halves + h, 64, stride=halves), :]
-                kept = jnp.where(slot < used, wide, 0.0)
-                out[pl.ds(b * 64, 64), pl.ds(h * LANES, LANES)] = kept.astype(out.dtype)
-
-
-def gather_rows(rows, first_row, within, send_count, features, table, peers, peer, slots):
-    n_rows, width = features.shape
-    halves = width // LANES
-    first = table is None
-    piece = jax.ShapeDtypeStruct((slots, width), features.dtype)
-    parts = 8 if n_rows % (8 * 64) == 0 else 1
+            out[at, :] = jnp.where(slot < used, stage[at, :], 0.0).astype(out.dtype)
+
+
+def gather_rows(rows, first_row, within, send_count, features, half, table, peers, peer, slots):
+    n_rows = features.shape[0]
+    build = table is None
+    piece = jax.ShapeDtypeStruct((slots, LANES), features.dtype)
+    parts = 8 if n_rows % (8 * 16) == 0 else 1
     made = [
-        jax.ShapeDtypeStruct((n_rows * halves, LANES), jnp.float32),
-        jax.ShapeDtypeStruct(features.shape, features.dtype),
+        jax.ShapeDtypeStruct((n_rows, LANES), jnp.float32),
+        jax.ShapeDtypeStruct((n_rows, LANES), features.dtype),
     ]
     out = pl.pallas_call(
-        functools.partial(gather_kernel, peers, peer, first_row, within, first, halves),
-        out_shape=[piece] * len(peers) + made * first,
-        in_specs=[RAW, RAW, RAW if first else VMEM],
-        out_specs=[VMEM] * (len(peers) + 2 * first),
+        functools.partial(gather_kernel, peers, peer, first_row, within, half, build),
+        out_shape=[piece] * len(peers) + made * build,
+        in_specs=[RAW, RAW, RAW if build else VMEM],
+        out_specs=[VMEM] * (len(peers) + 2 * build),
         scratch_shapes=[
             pltpu.SMEM(rows.shape, jnp.int32),
             pltpu.SMEM(send_count.shape, jnp.int32),
             pltpu.SemaphoreType.DMA((2,)),
-            pltpu.VMEM((slots * halves, LANES), jnp.float32),
+            pltpu.VMEM((slots, LANES), jnp.float32),
         ]
-        + [pltpu.SemaphoreType.DMA((parts,))] * first,
-        compiler_params=grant(18 + len(peers) if first else 4),
+        + [pltpu.SemaphoreType.DMA((parts,))] * build,
+        compiler_params=grant(10 + len(peers) if build else 4),
         cost_estimate=cost(4e9, 6 << 20),
         name="gather_rows",
-    )(in_hbm(rows), in_hbm(send_count), in_hbm(features) if first else table)
+    )(in_hbm(rows), in_hbm(send_count), in_hbm(features) if build else table)
     return out[: len(peers)], out[len(peers) :]
 
 
@@ -420,13 +416,13 @@
     )(weight, bias, *parts)
 
 
-def mix_kernel(n_col, channels, first, *refs):
-    pieces, held, bias = refs[:n_col], refs[n_col], refs[n_col + 1]
+def mix_kernel(n_col, n_in, channels, first, *refs):
+    pieces, held, bias = refs[:n_in], refs[n_in], refs[n_in + 1]
     outs, stats = refs[-n_col - 1 : -1], refs[-1]
 
     @pl.when(pl.program_id(0) == 0)
     def _():
-        stats[...] = jnp.zeros_like(stats) if first else refs[n_col + 2][...]
+        stats[...] = jnp.zeros_like(stats) if first else refs[n_in + 2][...]
 
     spread = jnp.concatenate([piece[...] for piece in pieces], axis=1)
     active, power = [], 0.0
@@ -444,19 +440,18 @@
 
 
 def mix_rows(pieces, weights, bias, before):
-    n_col = len(pieces)
-    rows, width = pieces[0].shape
-    channels = n_col * width
+    n_col, channels, width = weights.shape
+    rows = pieces[0].shape[0]
     block = TILE
-    piece = pl.BlockSpec((block, width), lambda i: (i, 0))
+    spec = lambda w: pl.BlockSpec((block, w), lambda i: (i, 0))
     first = before is None
     out = pl.pallas_call(
-        functools.partial(mix_kernel, n_col, channels, first),
+        functools.partial(mix_kernel, n_col, len(pieces), channels, first),
         out_shape=[jax.ShapeDtypeStruct((rows, width), jnp.bfloat16)] * n_col
         + [jax.ShapeDtypeStruct((2 * n_col, width), jnp.float32)],
         grid=(rows // block,),
-        in_specs=[piece] * n_col + [VMEM] * (2 if first else 3),
-        out_specs=[piece] * n_col + [VMEM],
+        in_specs=[spec(piece.shape[1]) for piece in pieces] + [VMEM] * (2 if first else 3),
+        out_specs=[spec(width)] * n_col + [VMEM],
         compiler_params=grant(10),
         cost_estimate=cost(2 * rows * channels * channels, 4 << 20),
         name="mix_rows",
@@ -512,11 +507,10 @@
 
 
 def chunk_plan(per_dest):
-    if per_dest % 8:
+    if per_dest % 4:
         return [(0, per_dest)]
-    u = per_dest // 8
-    cuts = [0, u, 2 * u, 4 * u, 6 * u, 8 * u]
-    return [(a, b - a) for a, b in zip(cuts, cuts[1:])]
+    u = per_dest // 4
+    return [(0, u), (u, u), (2 * u, u), (3 * u, u)]
 
 
 def on_device(
@@ -543,24 +537,30 @@
     along_col = lambda x, k: lax.ppermute(x, "col", [(i, (i + k) % n_col) for i in range(n_col)])
 
     far = list(reversed(range(1, n_dom)))
-    halo = [None] * (n_dom - 1)
+    lead = far[0:3:2]
+    rest = [k for k in far if k not in lead]
     rows, first_row, within = storage_order(send_rows[0])
     slots = send_rows.shape[2]
-    table, own_tiles = None, features
-    lead = far[0:3:2]
-    for part, peers in enumerate((lead, [k for k in far if k not in lead])):
-        if not peers:
-            continue
-        outgoing, made = gather_rows(
-            rows, first_row, within, send_count[0], features, table, peers, peer, slots
-        )
-        if made:
-            table, own_tiles = made
-        for k, piece in zip(peers, outgoing):
-            halo[k - 1] = along_dom(piece, k)
+    halves = width // LANES
+    halo, own_tiles = [], []
+    for h in range(halves):
+        pieces, table = {}, None
+        for peers in [lead, rest] if h == 0 else [lead + rest]:
+            if not peers:
+                continue
+            outgoing, made = gather_rows(
+                rows, first_row, within, send_count[0], features, h, table, peers, peer, slots
+            )
+            if made:
+                table, tiles = made
+            for k, piece in zip(peers, outgoing):
+                pieces[k] = along_dom(piece, k)
+        halo.append(pieces)
+        own_tiles.append(tiles)
 
     share = 1
-    while share < min(4, n_col) and n_dom % (2 * share) == 0:
+    channels = n_col * width
+    while share < 8 and n_dom % (2 * share) == 0 and channels % (2 * share * PAD) == 0:
         share *= 2
     order = sorted(range(1, n_col), key=lambda k: min(k, n_col - k), reverse=True)
     bias_row = out_bias.reshape(1, width)
@@ -576,31 +576,36 @@
         step //= 2
     weights, bias = join_weights(weight, bias_row, [got[f] for f in range(share)], n_col)
 
-    plan = chunk_plan(n_rows // TILE // n_col)
+    per_dest = n_rows // TILE // n_col
+    plan = chunk_plan(per_dest)
     index_tables = (local_index[0].T, local_count[0], halo_index[0].T, halo_count[0])
-    part, kept = early_sums(index_tables, own_tiles, local_vals[0], halo_vals[0], n_col, plan[0][1])
+    part, kept = early_sums(
+        index_tables, own_tiles[0], local_vals[0], halo_vals[0], n_col, plan[0][1]
+    )
     late = far[-2:-1] or far
-    soon = [k for k in far if k not in late]
-    received = assemble(soon, [halo[k - 1] for k in soon], n_dom, peer)
-    incoming = []
-    for g, (base, size) in enumerate(plan):
-        if g == 0:
-            sums, received = first_sums(
-                index_tables[2], late, [halo[k - 1] for k in late], part, kept,
-                received, n_rows // TILE // n_col, peer,
-            )
-        else:
-            sums = tile_sums(
-                index_tables, received, own_tiles, local_vals[0], halo_vals[0],
-                n_col, base, size,
-            )
-        moved = {k: along_col(sums[k], k) for k in order}
-        incoming.append([sums[0]] + [moved[k] for k in range(1, n_col)])
+    incoming = [[[] for _ in range(n_col)] for _ in plan]
+    for h in range(halves):
+        soon = [k for k in far if h or k not in late]
+        received = assemble(soon, [halo[h][k] for k in soon], n_dom, peer)
+        for g, (base, size) in enumerate(plan):
+            if g == h == 0:
+                sums, received = first_sums(
+                    index_tables[2], late, [halo[h][k] for k in late], part, kept,
+                    received, per_dest, peer,
+                )
+            else:
+                sums = tile_sums(
+                    index_tables, received, own_tiles[h], local_vals[0], halo_vals[0],
+                    n_col, base, size,
+                )
+            moved = {k: along_col(sums[k], k) for k in order}
+            for k in range(n_col):
+                incoming[g][k].append(moved[k] if k else sums[0])
 
     stats = None
     returned = []
     for pieces in incoming:
-        done, stats = mix_rows(pieces, weights, bias, stats)
+        done, stats = mix_rows(sum(pieces, []), weights, bias, stats)
         moved = {k: along_col(done[k], -k) for k in order}
         returned.append([done[0]] + [moved[k] for k in range(1, n_col)])
 

time: 256 us -> 253 us (0.988)
  waiting for transfers between devices: 86.9 us -> 60.1 us
  Pallas kernels: 42.7 us -> 61.7 us
  starting transfers between devices: 115 us -> 120 us
    ppermute x36 -> x42, waiting for transfers between devices: 79.5 us -> 58.7 us  [on_device(): lax.ppermute(x, 'col', [(i, (i + k) % n_col) for i in range(n_col)])]
    pallas_call x4 -> x7, Pallas kernels: 14.8 us -> 27.5 us  [tile_sums(): pl.pallas_call(functools.partial(sum_kernel, n_col, slots, per_dest, base...]
    ppermute x7 -> x14, waiting for transfers between devices: 7.35 us -> 1.32 us  [on_device(): lax.ppermute(x, 'dom', [(i, peer(i, k)) for i in range(n_dom)])]
    ppermute x7 -> x14, starting transfers between devices: 7.69 us -> 13.7 us  [on_device(): lax.ppermute(x, 'dom', [(i, peer(i, k)) for i in range(n_dom)])]
    pallas_call x2 -> x3, Pallas kernels: 6.99 us -> 11.5 us  [gather_rows(): pl.pallas_call(functools.partial(gather_kernel, peers, peer, first_row, w...]
    ppermute x36 -> x42, starting transfers between devices: 105 us -> 103 us  [on_device(): lax.ppermute(x, 'col', [(i, (i + k) % n_col) for i in range(n_col)])]
    pallas_call x5 -> x4, Pallas kernels: 5.25 us -> 4.61 us  [place_rows(): pl.pallas_call(functools.partial(place_kernel, n_col, per_dest, base, nod...]
    pallas_call x5 -> x4, Pallas kernels: 10.2 us -> 10.4 us  [mix_rows(): pl.pallas_call(functools.partial(mix_kernel, n_col, len(pieces), channels...]
  transfers between devices with their start and end apart: 46 -> 63, of which waited for: 15 -> 12; matrix products, arithmetic and copies ran while one was open for 0% -> 0% of each run, Pallas kernels for 14% -> 23%
where the time goes in v4:
time: 253 us
  starting transfers between devices  120 us (47%)
  Pallas kernels  61.7 us (24%)
  waiting for transfers between devices  60.1 us (24%)
  blocking collectives  9.16 us (4%)
    ppermute x42, starting transfers between devices, on_device(): lax.ppermute(x, 'col', [(i, (i + k) % n_col) for i in range(n_col)])  103 us
    ppermute x42, waiting for transfers between devices, on_device(): lax.ppermute(x, 'col', [(i, (i + k) % n_col) for i in range(n_col)])  58.7 us
    pallas_call x7, Pallas kernels, tile_sums(): pl.pallas_call(functools.partial(sum_kernel, n_col, slots, per_dest, base...  27.5 us
    ppermute x14, starting transfers between devices, on_device(): lax.ppermute(x, 'dom', [(i, peer(i, k)) for i in range(n_dom)])  13.7 us
    pallas_call x3, Pallas kernels, gather_rows(): pl.pallas_call(functools.partial(gather_kernel, peers, peer, first_row, w...  11.5 us
    pallas_call x4, Pallas kernels, mix_rows(): pl.pallas_call(functools.partial(mix_kernel, n_col, len(pieces), channels...  10.4 us
    all_gather x1, blocking collectives, on_device(): over_dom = lax.all_gather(stats, 'dom', axis=0)  9.16 us
  transfers between devices with their start and end apart: 63, of which 12 were waited for; matrix products, arithmetic and copies ran while one was open for 0% of the time, Pallas kernels for 23%

profile of v4, /device:TPU:0, one launch (start us, length us, event | category | flops | bytes accessed | tf_op | source)
XLA Modules:
  0.0 252.7 jit_solution(2218986744405105462)
XLA Ops:
  2.2 5.1 %collective-permute-start.22 = (bf16[144,256]{1,0:T(8,128)(2,1)S(1)}, bf16[144,256]{1,0:T(8,128)(2,1)S(1)}, u32[]{:S(2)}, u32[]{:S(2)}) collective-permute-start(bf16[144,256]{1,0:T(8,128)(2,1)S(1)} %weight_part.1), channel_id=1, source_target_pairs={{0,3},{1,0},{2,1},{3,2},{4,7},{5,4},{6,5},{7,6},{8,11},{9,8},{10,9... | collective-permute-start | bytes 221192 | tf_op jit(solution)/shard_map/ppermute | solution.py:537
  10.7 2.9 %gather_rows.4 = (bf16[512,128]{1,0:T(8,128)(2,1)S(1)}, bf16[512,128]{1,0:T(8,128)(2,1)S(1)}, bf16[512,128]{1,0:T(8,128)(2,1)S(1)}, bf16[512,128]{1,0:T(8,128)(2,1)S(1)}, bf16[512,128]{1,0:T(8,128)(2,1)S(1)}) custom-call(s32[4096]{0:T(1024)} %bitcast.115, s32[8]{0:T(128)} %bitcast.118, f32[8192,128]{1,0:T(8,128)S(1)} %get-tuple-element.77.refs_0_), custom_call_target="tpu_custom_call" | custom-call | flops 4000000000 | bytes 6291456 | tf_op jit(solution)/shard_map/gather_rows/pallas_call | solution.py:132
  13.6 2.7 %collective-permute-start.2 = (bf16[512,128]{1,0:T(8,128)(2,1)S(1)}, bf16[512,128]{1,0:T(8,128)(2,1)S(1)}, u32[]{:S(2)}, u32[]{:S(2)}) collective-permute-start(bf16[512,128]{1,0:T(8,128)(2,1)S(1)} %get-tuple-element.82), channel_id=1, source_target_pairs={{0,24},{4,28},{8,16},{12,20},{16,8},{20,12},{24,0},{28,4},{1,25},{... | collective-permute-start | bytes 393224 | tf_op jit(solution)/shard_map/ppermute | solution.py:536
  16.9 6.3 %gather_rows.5 = (bf16[512,128]{1,0:T(8,128)(2,1)S(1)}, bf16[512,128]{1,0:T(8,128)(2,1)S(1)}, bf16[512,128]{1,0:T(8,128)(2,1)S(1)}, bf16[512,128]{1,0:T(8,128)(2...) custom-call(s32[4096]{0:T(1024)} %bitcast.116, ...), custom_call_target="tpu_custom_call" | custom-call | flops 4000000000 | bytes 6291456 | tf_op jit(solution)/shard_map/gather_rows/pallas_call | solution.py:132
  26.6 4.8 %early_sums.1 = (f32[4,512,128]{2,1,0:T(8,128)S(1)}, bf16[4,4,4,128,128]{4,3,2,1,0:T(8,128)(2,1)S(1)}) custom-call(s32[4,64]{1,0:T(4,128)S(1)} %bitcast.18, s32[64]{0:T(128)S(1)} %bitcast.34, s32[64]{0:T(128)S(1)} %bitcast.42, bf16[8192,128]{1,0:T(8,128)(2,1)S(1)} %get-tuple-element.76.feat.refs_4_, bf16[64,4,128,128]{3,2,1,0:T(8,128)(2,1)} %bitcast.50, ...), custom_call_target="tpu_custom_call" | custom-call | flops 2000000000 | bytes 4194304 | tf_op jit(solution)/shard_map/early_sums/pallas_call | solution.py:203
  39.2 3.9 %tile_sums.11 = (bf16[512,128]{1,0:T(8,128)(2,1)S(1)}, bf16[512,128]{1,0:T(8,128)(2,1)S(1)}, bf16[512,128]{1,0:T(8,128)(2,1)S(1)}, bf16[512,128]{1,0:T(8,128)(2,1)S(1)}) custom-call(s32[4,64]{1,0:T(4,128)S(1)} %bitcast.19, s32[64]{0:T(128)S(1)} %bitcast.35, s32[4,64]{1,0:T(4,128)S(1)} %bitcast.27, s32[64]{0:T(128)S(1)} %bitcast.43, ...), custom_call_target="tpu_custom_call" | custom-call | flops 2000000000 | bytes 6291456 | tf_op jit(solution)/shard_map/tile_sums/pallas_call | solution.py:309
  43.1 3.9 %tile_sums.9 = (bf16[512,128]{1,0:T(8,128)(2,1)S(1)}, bf16[512,128]{1,0:T(8,128)(2,1)S(1)}, bf16[512,128]{1,0:T(8,128)(2,1)S(1)}, bf16[512,128]{1,0:T(8,128)(2,1)S(1)}) custom-call(s32[4,64]{1,0:T(4,128)S(1)} %bitcast.20, s32[64]{0:T(128)S(1)} %bitcast.36, s32[4,64]{1,0:T(4,128)S(1)} %bitcast.28, s32[64]{0:T(128)S(1)} %bitcast.44, ...), custom_call_target="tpu_custom_call" | custom-call | flops 2000000000 | bytes 6291456 | tf_op jit(solution)/shard_map/tile_sums/pallas_call | solution.py:309
  54.1 3.9 %tile_sums.7 = (bf16[512,128]{1,0:T(8,128)(2,1)S(1)}, bf16[512,128]{1,0:T(8,128)(2,1)S(1)}, bf16[512,128]{1,0:T(8,128)(2,1)S(1)}, bf16[512,128]{1,0:T(8,128)(2,1)S(1)}) custom-call(s32[4,64]{1,0:T(4,128)S(1)} %bitcast.21, s32[64]{0:T(128)S(1)} %bitcast.37, s32[4,64]{1,0:T(4,128)S(1)} %bitcast.29, s32[64]{0:T(128)S(1)} %bitcast.45, ...), custom_call_target="tpu_custom_call" | custom-call | flops 2000000000 | bytes 6291456 | tf_op jit(solution)/shard_map/tile_sums/pallas_call | solution.py:309
  63.7 5.4 %collective-permute-start.40 = (bf16[512,128]{1,0:T(8,128)(2,1)S(1)}, bf16[512,128]{1,0:T(8,128)(2,1)S(1)}, u32[]{:S(2)}, u32[]{:S(2)}) collective-permute-start(bf16[512,128]{1,0:T(8,128)(2,1)S(1)} %get-tuple-element.120), channel_id=1, source_target_pairs={{0,3},{1,0},{2,1},{3,2},{4,7},{5,4},{6,5},{7,6},{8,11},{9,8},{10,9... | collective-permute-start | bytes 393224 | tf_op jit(solution)/shard_map/ppermute | solution.py:537
  69.7 4.3 %collective-permute-start.30 = (bf16[512,128]{1,0:T(8,128)(2,1)S(1)}, bf16[512,128]{1,0:T(8,128)(2,1)S(1)}, u32[]{:S(2)}, u32[]{:S(2)}) collective-permute-start(bf16[512,128]{1,0:T(8,128)(2,1)S(1)} %get-tuple-element.108), channel_id=1, source_target_pairs={{0,1},{1,2},{2,3},{3,0},{4,5},{5,6},{6,7},{7,4},{8,9},{9,10},{10,1... | collective-permute-start | bytes 393224 | tf_op jit(solution)/shard_map/ppermute | solution.py:537
  74.0 3.5 %collective-permute-done.38.refs_4_ = bf16[512,128]{1,0:T(8,128)(2,1)S(1)} collective-permute-done((bf16[512,128]{1,0:T(8,128)(2,1)S(1)}, bf16[512,128]{1,0:T(8,128)(2,1)S(1)}, u32[]{:S(2)}, u32[]{:S(2)}) %collective-permute-start.38) | collective-permute-done | bytes 131104 | tf_op jit(solution)/shard_map/ppermute | solution.py:537
  80.2 3.9 %tile_sums.13 = (bf16[512,128]{1,0:T(8,128)(2,1)S(1)}, bf16[512,128]{1,0:T(8,128)(2,1)S(1)}, bf16[512,128]{1,0:T(8,128)(2,1)S(1)}, bf16[512,128]{1,0:T(8,128)(2,1)S(1)}) custom-call(s32[4,64]{1,0:T(4,128)S(1)} %bitcast.22, s32[64]{0:T(128)S(1)} %bitcast.38, s32[4,64]{1,0:T(4,128)S(1)} %bitcast.30, s32[64]{0:T(128)S(1)} %bitcast.46, ...), custom_call_target="tpu_custom_call" | custom-call | flops 2000000000 | bytes 6291456 | tf_op jit(solution)/shard_map/tile_sums/pallas_call | solution.py:309
  84.1 4.2 %collective-permute-start.14 = (bf16[512,128]{1,0:T(8,128)(2,1)S(1)}, bf16[512,128]{1,0:T(8,128)(2,1)S(1)}, u32[]{:S(2)}, u32[]{:S(2)}) collective-permute-start(bf16[512,128]{1,0:T(8,128)(2,1)S(1)} %get-tuple-element.98), channel_id=1, source_target_pairs={{0,1},{1,2},{2,3},{3,0},{4,5},{5,6},{6,7},{7,4},{8,9},{9,10},{10,1... | collective-permute-start | bytes 393224 | tf_op jit(solution)/shard_map/ppermute | solution.py:537
  90.8 3.9 %tile_sums.12 = (bf16[512,128]{1,0:T(8,128)(2,1)S(1)}, bf16[512,128]{1,0:T(8,128)(2,1)S(1)}, bf16[512,128]{1,0:T(8,128)(2,1)S(1)}, bf16[512,128]{1,0:T(8,128)(2,1)S(1)}) custom-call(s32[4,64]{1,0:T(4,128)S(1)} %bitcast.23, s32[64]{0:T(128)S(1)} %bitcast.39, s32[4,64]{1,0:T(4,128)S(1)} %bitcast.31, s32[64]{0:T(128)S(1)} %bitcast.47, ...), custom_call_target="tpu_custom_call" | custom-call | flops 2000000000 | bytes 6291456 | tf_op jit(solution)/shard_map/tile_sums/pallas_call | solution.py:309
  97.2 3.4 %collective-permute-done.45.refs_5_ = bf16[512,128]{1,0:T(8,128)(2,1)S(1)} collective-permute-done((bf16[512,128]{1,0:T(8,128)(2,1)S(1)}, bf16[512,128]{1,0:T(8,128)(2,1)S(1)}, u32[]{:S(2)}, u32[]{:S(2)}) %collective-permute-start.45) | collective-permute-done | bytes 131104 | tf_op jit(solution)/shard_map/ppermute | solution.py:537
  101.2 3.9 %tile_sums.10 = (bf16[512,128]{1,0:T(8,128)(2,1)S(1)}, bf16[512,128]{1,0:T(8,128)(2,1)S(1)}, bf16[512,128]{1,0:T(8,128)(2,1)S(1)}, bf16[512,128]{1,0:T(8,128)(2,1)S(1)}) custom-call(s32[4,64]{1,0:T(4,128)S(1)} %bitcast.24, s32[64]{0:T(128)S(1)} %bitcast.40, s32[4,64]{1,0:T(4,128)S(1)} %bitcast.32, s32[64]{0:T(128)S(1)} %bitcast.48, ...), custom_call_target="tpu_custom_call" | custom-call | flops 2000000000 | bytes 6291456 | tf_op jit(solution)/shard_map/tile_sums/pallas_call | solution.py:309
  105.4 3.1 %collective-permute-start.37 = (bf16[512,128]{1,0:T(8,128)(2,1)S(1)}, bf16[512,128]{1,0:T(8,128)(2,1)S(1)}, u32[]{:S(2)}, u32[]{:S(2)}) collective-permute-start(bf16[512,128]{1,0:T(8,128)(2,1)S(1)} %get-tuple-element.117), channel_id=1, source_target_pairs={{0,1},{1,2},{2,3},{3,0},{4,5},{5,6},{6,7},{7,4},{8,9},{9,10},{10,1... | collective-permute-start | bytes 393224 | tf_op jit(solution)/shard_map/ppermute | solution.py:537
  108.5 3.9 %tile_sums.8 = (bf16[512,128]{1,0:T(8,128)(2,1)S(1)}, bf16[512,128]{1,0:T(8,128)(2,1)S(1)}, bf16[512,128]{1,0:T(8,128)(2,1)S(1)}, bf16[512,128]{1,0:T(8,128)(2,1)S(1)}) custom-call(s32[4,64]{1,0:T(4,128)S(1)} %bitcast.25, s32[64]{0:T(128)S(1)} %bitcast.41, s32[4,64]{1,0:T(4,128)S(1)} %bitcast.33, s32[64]{0:T(128)S(1)} %bitcast.49, ...), custom_call_target="tpu_custom_call" | custom-call | flops 2000000000 | bytes 6291456 | tf_op jit(solution)/shard_map/tile_sums/pallas_call | solution.py:309
  112.4 3.0 %collective-permute-done.37.refs_3_ = bf16[512,128]{1,0:T(8,128)(2,1)S(1)} collective-permute-done((bf16[512,128]{1,0:T(8,128)(2,1)S(1)}, bf16[512,128]{1,0:T(8,128)(2,1)S(1)}, u32[]{:S(2)}, u32[]{:S(2)}) %collective-permute-start.37) | collective-permute-done | bytes 131104 | tf_op jit(solution)/shard_map/ppermute | solution.py:537
  125.2 2.9 %collective-permute-done.39.refs_5_ = bf16[512,128]{1,0:T(8,128)(2,1)S(1)} collective-permute-done((bf16[512,128]{1,0:T(8,128)(2,1)S(1)}, bf16[512,128]{1,0:T(8,128)(2,1)S(1)}, u32[]{:S(2)}, u32[]{:S(2)}) %collective-permute-start.39) | collective-permute-done | bytes 131104 | tf_op jit(solution)/shard_map/ppermute | solution.py:537
  129.8 10.4 %collective-permute-start.15 = (bf16[512,128]{1,0:T(8,128)(2,1)S(1)}, bf16[512,128]{1,0:T(8,128)(2,1)S(1)}, u32[]{:S(2)}, u32[]{:S(2)}) collective-permute-start(bf16[512,128]{1,0:T(8,128)(2,1)S(1)} %get-tuple-element.99), channel_id=1, source_target_pairs={{0,1},{1,2},{2,3},{3,0},{4,5},{5,6},{6,7},{7,4},{8,9},{9,10},{10,1... | collective-permute-start | bytes 393224 | tf_op jit(solution)/shard_map/ppermute | solution.py:537
  142.1 3.8 %collective-permute-start.19 = (bf16[512,128]{1,0:T(8,128)(2,1)S(1)}, bf16[512,128]{1,0:T(8,128)(2,1)S(1)}, u32[]{:S(2)}, u32[]{:S(2)}) collective-permute-start(bf16[512,128]{1,0:T(8,128)(2,1)S(1)} %get-tuple-element.103), channel_id=1, source_target_pairs={{0,3},{1,0},{2,1},{3,2},{4,7},{5,4},{6,5},{7,6},{8,11},{9,8},{10,9... | collective-permute-start | bytes 393224 | tf_op jit(solution)/shard_map/ppermute | solution.py:537
  151.2 3.1 %collective-permute-start.60 = (bf16[512,256]{1,0:T(8,128)(2,1)S(1)}, bf16[512,256]{1,0:T(8,128)(2,1)S(1)}, u32[]{:S(2)}, u32[]{:S(2)}) collective-permute-start(bf16[512,256]{1,0:T(8,128)(2,1)S(1)} %get-tuple-element.147), channel_id=1, source_target_pairs={{0,3},{1,0},{2,1},{3,2},{4,7},{5,4},{6,5},{7,6},{8,11},{9,8},{10,9... | collective-permute-start | bytes 786440 | tf_op jit(solution)/shard_map/ppermute | solution.py:537
  155.3 15.9 %collective-permute-start.57 = (bf16[512,256]{1,0:T(8,128)(2,1)S(1)}, bf16[512,256]{1,0:T(8,128)(2,1)S(1)}, u32[]{:S(2)}, u32[]{:S(2)}) collective-permute-start(bf16[512,256]{1,0:T(8,128)(2,1)S(1)} %get-tuple-element.143), channel_id=1, source_target_pairs={{0,3},{1,0},{2,1},{3,2},{4,7},{5,4},{6,5},{7,6},{8,11},{9,8},{10,9... | collective-permute-start | bytes 786440 | tf_op jit(solution)/shard_map/ppermute | solution.py:537
  173.8 9.2 %all-gather = f32[64,256]{1,0:T(8,128)S(1)} all-gather(f32[8,256]{1,0:T(8,128)S(1)} %get-tuple-element.137), channel_id=2, replica_groups=mesh['dom'=8,'col'=4] {'dom'}, dimensions={0}, use_global_device_ids=true | all-gather | bytes 73728 | tf_op jit(solution)/shard_map/all_gather | solution.py:612
  183.0 5.4 %collective-permute-done.53.refs_7_ = f32[2,256]{1,0:T(2,128)S(1)} collective-permute-done((f32[2,256]{1,0:T(2,128)S(1)}, f32[2,256]{1,0:T(2,128)S(1)}, u32[]{:S(2)}, u32[]{:S(2)}) %collective-permute-start.53) | collective-permute-done | bytes 2080 | tf_op jit(solution)/shard_map/ppermute | solution.py:537
  188.7 3.5 %collective-permute-start.54 = (bf16[512,256]{1,0:T(8,128)(2,1)S(1)}, bf16[512,256]{1,0:T(8,128)(2,1)S(1)}, u32[]{:S(2)}, u32[]{:S(2)}) collective-permute-start(bf16[512,256]{1,0:T(8,128)(2,1)S(1)} %get-tuple-element.139), channel_id=1, source_target_pairs={{0,3},{1,0},{2,1},{3,2},{4,7},{5,4},{6,5},{7,6},{8,11},{9,8},{10,9... | collective-permute-start | bytes 786440 | tf_op jit(solution)/shard_map/ppermute | solution.py:537
  193.4 14.1 %collective-permute-done.58.refs_2_ = bf16[512,256]{1,0:T(8,128)(2,1)S(1)} collective-permute-done((bf16[512,256]{1,0:T(8,128)(2,1)S(1)}, bf16[512,256]{1,0:T(8,128)(2,1)S(1)}, u32[]{:S(2)}, u32[]{:S(2)}) %collective-permute-start.58) | collective-permute-done | bytes 262176 | tf_op jit(solution)/shard_map/ppermute | solution.py:537
  207.5 13.5 %collective-permute-start.49 = (bf16[512,256]{1,0:T(8,128)(2,1)S(1)}, bf16[512,256]{1,0:T(8,128)(2,1)S(1)}, u32[]{:S(2)}, u32[]{:S(2)}) collective-permute-start(bf16[512,256]{1,0:T(8,128)(2,1)S(1)} %get-tuple-element.135), channel_id=1, source_target_pairs={{0,2},{1,3},{2,0},{3,1},{4,6},{5,7},{6,4},{7,5},{8,10},{9,11},{10,... | collective-permute-start | bytes 786440 | tf_op jit(solution)/shard_map/ppermute | solution.py:537
  221.1 3.8 %collective-permute-start.50 = (bf16[512,256]{1,0:T(8,128)(2,1)S(1)}, bf16[512,256]{1,0:T(8,128)(2,1)S(1)}, u32[]{:S(2)}, u32[]{:S(2)}) collective-permute-start(bf16[512,256]{1,0:T(8,128)(2,1)S(1)} %get-tuple-element.136), channel_id=1, source_target_pairs={{0,1},{1,2},{2,3},{3,0},{4,5},{5,6},{6,7},{7,4},{8,9},{9,10},{10,1... | collective-permute-start | bytes 786440 | tf_op jit(solution)/shard_map/ppermute | solution.py:537
  226.9 12.9 %collective-permute-done.55.refs_2_ = bf16[512,256]{1,0:T(8,128)(2,1)S(1)} collective-permute-done((bf16[512,256]{1,0:T(8,128)(2,1)S(1)}, bf16[512,256]{1,0:T(8,128)(2,1)S(1)}, u32[]{:S(2)}, u32[]{:S(2)}) %collective-permute-start.55) | collective-permute-done | bytes 262176 | tf_op jit(solution)/shard_map/ppermute | solution.py:537
  240.8 10.2 %collective-permute-done.52.refs_6_ = f32[2,256]{1,0:T(2,128)S(1)} collective-permute-done((f32[2,256]{1,0:T(2,128)S(1)}, f32[2,256]{1,0:T(2,128)S(1)}, u32[]{:S(2)}, u32[]{:S(2)}) %collective-permute-start.52) | collective-permute-done | bytes 2080 | tf_op jit(solution)/shard_map/ppermute | solution.py:537
  (137 shorter events, 66.7 us)
Async XLA Ops:
  2.2 21.1 %collective-permute-start.22 = (bf16[144,256]{1,0:T(8,128)(2,1)S(1)}, bf16[144,256]{1,0:T(8,128)(2,1)S(1)}, u32[]{:S(2)}, u32[]{:S(2)}) collective-permute-start(bf16[144,256]{1,0:T(8,128)(2,1)S(1)} %weight_part.1), channel_id=1, source_target_pairs={{0,3},{1,0},{2,1},{3,2},{4,7},{5,4},{6,5},{7,6},{8,11},{9,8},{10,9... | collective-permute-start | bytes 221192 | tf_op jit(solution)/shard_map/ppermute | solution.py:537
  7.3 16.0 %collective-permute-start.21 = (bf16[144,256]{1,0:T(8,128)(2,1)S(1)}, bf16[144,256]{1,0:T(8,128)(2,1)S(1)}, u32[]{:S(2)}, u32[]{:S(2)}) collective-permute-start(bf16[144,256]{1,0:T(8,128)(2,1)S(1)} %weight_part.1), channel_id=1, source_target_pairs={{0,2},{1,3},{2,0},{3,1},{4,6},{5,7},{6,4},{7,5},{8,10},{9,11},{10,... | collective-permute-start | bytes 221192 | tf_op jit(solution)/shard_map/ppermute | solution.py:537
  7.3 16.7 %collective-permute-start.20 = (bf16[144,256]{1,0:T(8,128)(2,1)S(1)}, bf16[144,256]{1,0:T(8,128)(2,1)S(1)}, u32[]{:S(2)}, u32[]{:S(2)}) collective-permute-start(bf16[144,256]{1,0:T(8,128)(2,1)S(1)} %weight_part.1), channel_id=1, source_target_pairs={{0,1},{1,2},{2,3},{3,0},{4,5},{5,6},{6,7},{7,4},{8,9},{9,10},{10,1... | collective-permute-start | bytes 221192 | tf_op jit(solution)/shard_map/ppermute | solution.py:537
  16.3 15.2 %collective-permute-start.4 = (bf16[512,128]{1,0:T(8,128)(2,1)S(1)}, bf16[512,128]{1,0:T(8,128)(2,1)S(1)}, u32[]{:S(2)}, u32[]{:S(2)}) collective-permute-start(bf16[512,128]{1,0:T(8,128)(2,1)S(1)} %get-tuple-element.84), channel_id=1, source_target_pairs={{0,16},{4,20},{8,24},{12,28},{16,0},{20,4},{24,8},{28,12},{1,17},{... | collective-permute-start | bytes 393224 | tf_op jit(solution)/shard_map/ppermute | solution.py:536
  37.9 15.3 %collective-permute-start.11 = (bf16[512,128]{1,0:T(8,128)(2,1)S(1)}, bf16[512,128]{1,0:T(8,128)(2,1)S(1)}, u32[]{:S(2)}, u32[]{:S(2)}) collective-permute-start(bf16[512,128]{1,0:T(8,128)(2,1)S(1)} %get-tuple-element.94), channel_id=1, source_target_pairs={{0,12},{4,8},{8,4},{12,0},{16,28},{20,24},{24,20},{28,16},{1,13},{... | collective-permute-start | bytes 393224 | tf_op jit(solution)/shard_map/ppermute | solution.py:536
  49.0 30.6 %collective-permute-start.26 = (bf16[432,256]{1,0:T(8,128)(2,1)S(1)}, bf16[432,256]{1,0:T(8,128)(2,1)S(1)}, u32[]{:S(2)}, u32[]{:S(2)}) collective-permute-start(bf16[432,256]{1,0:T(8,128)(2,1)S(1)} %pack_rows.1.refs_0_), channel_id=1, source_target_pairs={{0,16},{4,20},{8,24},{12,28},{16,0},{20,4},{24,8},{28,12},{1,17},{... | collective-permute-start | bytes 663560 | tf_op jit(solution)/shard_map/ppermute | solution.py:575
  60.2 17.4 %collective-permute-start.38 = (bf16[512,128]{1,0:T(8,128)(2,1)S(1)}, bf16[512,128]{1,0:T(8,128)(2,1)S(1)}, u32[]{:S(2)}, u32[]{:S(2)}) collective-permute-start(bf16[512,128]{1,0:T(8,128)(2,1)S(1)} %get-tuple-element.118), channel_id=1, source_target_pairs={{0,2},{1,3},{2,0},{3,1},{4,6},{5,7},{6,4},{7,5},{8,10},{9,11},{10,... | collective-permute-start | bytes 393224 | tf_op jit(solution)/shard_map/ppermute | solution.py:537
  69.2 31.5 %collective-permute-start.24 = (bf16[432,256]{1,0:T(8,128)(2,1)S(1)}, bf16[432,256]{1,0:T(8,128)(2,1)S(1)}, u32[]{:S(2)}, u32[]{:S(2)}) collective-permute-start(bf16[432,256]{1,0:T(8,128)(2,1)S(1)} %pack_rows.1.refs_0_), channel_id=1, source_target_pairs={{0,8},{4,12},{8,0},{12,4},{16,24},{20,28},{24,16},{28,20},{1,9},{5... | collective-permute-start | bytes 663560 | tf_op jit(solution)/shard_map/ppermute | solution.py:575
  79.6 21.5 %collective-permute-start.28 = (bf16[432,256]{1,0:T(8,128)(2,1)S(1)}, bf16[432,256]{1,0:T(8,128)(2,1)S(1)}, u32[]{:S(2)}, u32[]{:S(2)}) collective-permute-start(bf16[432,256]{1,0:T(8,128)(2,1)S(1)} %collective-permute-done.26.refs_4_), channel_id=1, source_target_pairs={{0,8},{4,12},{8,0},{12,4},{16,24},{20,28},{24,16},{28,20},{1,9},{5... | collective-permute-start | bytes 663560 | tf_op jit(solution)/shard_map/ppermute | solution.py:575
  94.7 21.1 %collective-permute-start.23 = (bf16[432,256]{1,0:T(8,128)(2,1)S(1)}, bf16[432,256]{1,0:T(8,128)(2,1)S(1)}, u32[]{:S(2)}, u32[]{:S(2)}) collective-permute-start(bf16[432,256]{1,0:T(8,128)(2,1)S(1)} %pack_rows.1.refs_0_), channel_id=1, source_target_pairs={{0,4},{4,0},{8,12},{12,8},{16,20},{20,16},{24,28},{28,24},{1,5},{5... | collective-permute-start | bytes 663560 | tf_op jit(solution)/shard_map/ppermute | solution.py:575
  100.7 16.5 %collective-permute-start.27 = (bf16[432,256]{1,0:T(8,128)(2,1)S(1)}, bf16[432,256]{1,0:T(8,128)(2,1)S(1)}, u32[]{:S(2)}, u32[]{:S(2)}) collective-permute-start(bf16[432,256]{1,0:T(8,128)(2,1)S(1)} %collective-permute-done.26.refs_4_), channel_id=1, source_target_pairs={{0,4},{4,0},{8,12},{12,8},{16,20},{20,16},{24,28},{28,24},{1,5},{5... | collective-permute-start | bytes 663560 | tf_op jit(solution)/shard_map/ppermute | solution.py:575
  100.7 17.3 %collective-permute-start.25 = (bf16[432,256]{1,0:T(8,128)(2,1)S(1)}, bf16[432,256]{1,0:T(8,128)(2,1)S(1)}, u32[]{:S(2)}, u32[]{:S(2)}) collective-permute-start(bf16[432,256]{1,0:T(8,128)(2,1)S(1)} %collective-permute-done.24.refs_2_), channel_id=1, source_target_pairs={{0,4},{4,0},{8,12},{12,8},{16,20},{20,16},{24,28},{28,24},{1,5},{5... | collective-permute-start | bytes 663560 | tf_op jit(solution)/shard_map/ppermute | solution.py:575
  101.2 19.2 %collective-permute-start.29 = (bf16[432,256]{1,0:T(8,128)(2,1)S(1)}, bf16[432,256]{1,0:T(8,128)(2,1)S(1)}, u32[]{:S(2)}, u32[]{:S(2)}) collective-permute-start(bf16[432,256]{1,0:T(8,128)(2,1)S(1)} %collective-permute-done.28.refs_6_), channel_id=1, source_target_pairs={{0,4},{4,0},{8,12},{12,8},{16,20},{20,16},{24,28},{28,24},{1,5},{5... | collective-permute-start | bytes 663560 | tf_op jit(solution)/shard_map/ppermute | solution.py:575
  117.9 22.3 %collective-permute-start.33 = (bf16[512,128]{1,0:T(8,128)(2,1)S(1)}, bf16[512,128]{1,0:T(8,128)(2,1)S(1)}, u32[]{:S(2)}, u32[]{:S(2)}) collective-permute-start(bf16[512,128]{1,0:T(8,128)(2,1)S(1)} %get-tuple-element.111), channel_id=1, source_target_pairs={{0,2},{1,3},{2,0},{3,1},{4,6},{5,7},{6,4},{7,5},{8,10},{9,11},{10,... | collective-permute-start | bytes 393224 | tf_op jit(solution)/shard_map/ppermute | solution.py:537
  120.4 21.8 %collective-permute-start.35 = (bf16[512,128]{1,0:T(8,128)(2,1)S(1)}, bf16[512,128]{1,0:T(8,128)(2,1)S(1)}, u32[]{:S(2)}, u32[]{:S(2)}) collective-permute-start(bf16[512,128]{1,0:T(8,128)(2,1)S(1)} %get-tuple-element.113), channel_id=1, source_target_pairs={{0,3},{1,0},{2,1},{3,2},{4,7},{5,4},{6,5},{7,6},{8,11},{9,8},{10,9... | collective-permute-start | bytes 393224 | tf_op jit(solution)/shard_map/ppermute | solution.py:537
  128.1 23.1 %collective-permute-start.16 = (bf16[512,128]{1,0:T(8,128)(2,1)S(1)}, bf16[512,128]{1,0:T(8,128)(2,1)S(1)}, u32[]{:S(2)}, u32[]{:S(2)}) collective-permute-start(bf16[512,128]{1,0:T(8,128)(2,1)S(1)} %get-tuple-element.100), channel_id=1, source_target_pairs={{0,2},{1,3},{2,0},{3,1},{4,6},{5,7},{6,4},{7,5},{8,10},{9,11},{10,... | collective-permute-start | bytes 393224 | tf_op jit(solution)/shard_map/ppermute | solution.py:537
  128.1 26.2 %collective-permute-start.18 = (bf16[512,128]{1,0:T(8,128)(2,1)S(1)}, bf16[512,128]{1,0:T(8,128)(2,1)S(1)}, u32[]{:S(2)}, u32[]{:S(2)}) collective-permute-start(bf16[512,128]{1,0:T(8,128)(2,1)S(1)} %get-tuple-element.102), channel_id=1, source_target_pairs={{0,3},{1,0},{2,1},{3,2},{4,7},{5,4},{6,5},{7,6},{8,11},{9,8},{10,9... | collective-permute-start | bytes 393224 | tf_op jit(solution)/shard_map/ppermute | solution.py:537
  129.8 24.5 %collective-permute-start.15 = (bf16[512,128]{1,0:T(8,128)(2,1)S(1)}, bf16[512,128]{1,0:T(8,128)(2,1)S(1)}, u32[]{:S(2)}, u32[]{:S(2)}) collective-permute-start(bf16[512,128]{1,0:T(8,128)(2,1)S(1)} %get-tuple-element.99), channel_id=1, source_target_pairs={{0,1},{1,2},{2,3},{3,0},{4,5},{5,6},{6,7},{7,4},{8,9},{9,10},{10,1... | collective-permute-start | bytes 393224 | tf_op jit(solution)/shard_map/ppermute | solution.py:537
  140.2 15.1 %collective-permute-start.17 = (bf16[512,128]{1,0:T(8,128)(2,1)S(1)}, bf16[512,128]{1,0:T(8,128)(2,1)S(1)}, u32[]{:S(2)}, u32[]{:S(2)}) collective-permute-start(bf16[512,128]{1,0:T(8,128)(2,1)S(1)} %get-tuple-element.101), channel_id=1, source_target_pairs={{0,2},{1,3},{2,0},{3,1},{4,6},{5,7},{6,4},{7,5},{8,10},{9,11},{10,... | collective-permute-start | bytes 393224 | tf_op jit(solution)/shard_map/ppermute | solution.py:537
  142.1 29.1 %collective-permute-start.19 = (bf16[512,128]{1,0:T(8,128)(2,1)S(1)}, bf16[512,128]{1,0:T(8,128)(2,1)S(1)}, u32[]{:S(2)}, u32[]{:S(2)}) collective-permute-start(bf16[512,128]{1,0:T(8,128)(2,1)S(1)} %get-tuple-element.103), channel_id=1, source_target_pairs={{0,3},{1,0},{2,1},{3,2},{4,7},{5,4},{6,5},{7,6},{8,11},{9,8},{10,9... | collective-permute-start | bytes 393224 | tf_op jit(solution)/shard_map/ppermute | solution.py:537
  151.2 37.2 %collective-permute-start.60 = (bf16[512,256]{1,0:T(8,128)(2,1)S(1)}, bf16[512,256]{1,0:T(8,128)(2,1)S(1)}, u32[]{:S(2)}, u32[]{:S(2)}) collective-permute-start(bf16[512,256]{1,0:T(8,128)(2,1)S(1)} %get-tuple-element.147), channel_id=1, source_target_pairs={{0,3},{1,0},{2,1},{3,2},{4,7},{5,4},{6,5},{7,6},{8,11},{9,8},{10,9... | collective-permute-start | bytes 786440 | tf_op jit(solution)/shard_map/ppermute | solution.py:537
  154.3 34.4 %collective-permute-start.61 = (bf16[512,256]{1,0:T(8,128)(2,1)S(1)}, bf16[512,256]{1,0:T(8,128)(2,1)S(1)}, u32[]{:S(2)}, u32[]{:S(2)}) collective-permute-start(bf16[512,256]{1,0:T(8,128)(2,1)S(1)} %get-tuple-element.148), channel_id=1, source_target_pairs={{0,2},{1,3},{2,0},{3,1},{4,6},{5,7},{6,4},{7,5},{8,10},{9,11},{10,... | collective-permute-start | bytes 786440 | tf_op jit(solution)/shard_map/ppermute | solution.py:537
  154.3 37.9 %collective-permute-start.62 = (bf16[512,256]{1,0:T(8,128)(2,1)S(1)}, bf16[512,256]{1,0:T(8,128)(2,1)S(1)}, u32[]{:S(2)}, u32[]{:S(2)}) collective-permute-start(bf16[512,256]{1,0:T(8,128)(2,1)S(1)} %get-tuple-element.149), channel_id=1, source_target_pairs={{0,1},{1,2},{2,3},{3,0},{4,5},{5,6},{6,7},{7,4},{8,9},{9,10},{10,1... | collective-permute-start | bytes 786440 | tf_op jit(solution)/shard_map/ppermute | solution.py:537
  155.3 38.1 %collective-permute-start.57 = (bf16[512,256]{1,0:T(8,128)(2,1)S(1)}, bf16[512,256]{1,0:T(8,128)(2,1)S(1)}, u32[]{:S(2)}, u32[]{:S(2)}) collective-permute-start(bf16[512,256]{1,0:T(8,128)(2,1)S(1)} %get-tuple-element.143), channel_id=1, source_target_pairs={{0,3},{1,0},{2,1},{3,2},{4,7},{5,4},{6,5},{7,6},{8,11},{9,8},{10,9... | collective-permute-start | bytes 786440 | tf_op jit(solution)/shard_map/ppermute | solution.py:537
  188.4 19.1 %collective-permute-start.58 = (bf16[512,256]{1,0:T(8,128)(2,1)S(1)}, bf16[512,256]{1,0:T(8,128)(2,1)S(1)}, u32[]{:S(2)}, u32[]{:S(2)}) collective-permute-start(bf16[512,256]{1,0:T(8,128)(2,1)S(1)} %get-tuple-element.144), channel_id=1, source_target_pairs={{0,2},{1,3},{2,0},{3,1},{4,6},{5,7},{6,4},{7,5},{8,10},{9,11},{10,... | collective-permute-start | bytes 786440 | tf_op jit(solution)/shard_map/ppermute | solution.py:537
  188.4 19.1 %collective-permute-start.59 = (bf16[512,256]{1,0:T(8,128)(2,1)S(1)}, bf16[512,256]{1,0:T(8,128)(2,1)S(1)}, u32[]{:S(2)}, u32[]{:S(2)}) collective-permute-start(bf16[512,256]{1,0:T(8,128)(2,1)S(1)} %get-tuple-element.145), channel_id=1, source_target_pairs={{0,1},{1,2},{2,3},{3,0},{4,5},{5,6},{6,7},{7,4},{8,9},{9,10},{10,1... | collective-permute-start | bytes 786440 | tf_op jit(solution)/shard_map/ppermute | solution.py:537
  188.7 32.3 %collective-permute-start.54 = (bf16[512,256]{1,0:T(8,128)(2,1)S(1)}, bf16[512,256]{1,0:T(8,128)(2,1)S(1)}, u32[]{:S(2)}, u32[]{:S(2)}) collective-permute-start(bf16[512,256]{1,0:T(8,128)(2,1)S(1)} %get-tuple-element.139), channel_id=1, source_target_pairs={{0,3},{1,0},{2,1},{3,2},{4,7},{5,4},{6,5},{7,6},{8,11},{9,8},{10,9... | collective-permute-start | bytes 786440 | tf_op jit(solution)/shard_map/ppermute | solution.py:537
  192.2 47.5 %collective-permute-start.55 = (bf16[512,256]{1,0:T(8,128)(2,1)S(1)}, bf16[512,256]{1,0:T(8,128)(2,1)S(1)}, u32[]{:S(2)}, u32[]{:S(2)}) collective-permute-start(bf16[512,256]{1,0:T(8,128)(2,1)S(1)} %get-tuple-element.140), channel_id=1, source_target_pairs={{0,2},{1,3},{2,0},{3,1},{4,6},{5,7},{6,4},{7,5},{8,10},{9,11},{10,... | collective-permute-start | bytes 786440 | tf_op jit(solution)/shard_map/ppermute | solution.py:537
  193.4 46.4 %collective-permute-start.56 = (bf16[512,256]{1,0:T(8,128)(2,1)S(1)}, bf16[512,256]{1,0:T(8,128)(2,1)S(1)}, u32[]{:S(2)}, u32[]{:S(2)}) collective-permute-start(bf16[512,256]{1,0:T(8,128)(2,1)S(1)} %get-tuple-element.141), channel_id=1, source_target_pairs={{0,1},{1,2},{2,3},{3,0},{4,5},{5,6},{6,7},{7,4},{8,9},{9,10},{10,1... | collective-permute-start | bytes 786440 | tf_op jit(solution)/shard_map/ppermute | solution.py:537
  207.5 43.5 %collective-permute-start.48 = (bf16[512,256]{1,0:T(8,128)(2,1)S(1)}, bf16[512,256]{1,0:T(8,128)(2,1)S(1)}, u32[]{:S(2)}, u32[]{:S(2)}) collective-permute-start(bf16[512,256]{1,0:T(8,128)(2,1)S(1)} %get-tuple-element.134), channel_id=1, source_target_pairs={{0,3},{1,0},{2,1},{3,2},{4,7},{5,4},{6,5},{7,6},{8,11},{9,8},{10,9... | collective-permute-start | bytes 786440 | tf_op jit(solution)/shard_map/ppermute | solution.py:537
  207.5 43.5 %collective-permute-start.49 = (bf16[512,256]{1,0:T(8,128)(2,1)S(1)}, bf16[512,256]{1,0:T(8,128)(2,1)S(1)}, u32[]{:S(2)}, u32[]{:S(2)}) collective-permute-start(bf16[512,256]{1,0:T(8,128)(2,1)S(1)} %get-tuple-element.135), channel_id=1, source_target_pairs={{0,2},{1,3},{2,0},{3,1},{4,6},{5,7},{6,4},{7,5},{8,10},{9,11},{10,... | collective-permute-start | bytes 786440 | tf_op jit(solution)/shard_map/ppermute | solution.py:537
  221.1 29.9 %collective-permute-start.50 = (bf16[512,256]{1,0:T(8,128)(2,1)S(1)}, bf16[512,256]{1,0:T(8,128)(2,1)S(1)}, u32[]{:S(2)}, u32[]{:S(2)}) collective-permute-start(bf16[512,256]{1,0:T(8,128)(2,1)S(1)} %get-tuple-element.136), channel_id=1, source_target_pairs={{0,1},{1,2},{2,3},{3,0},{4,5},{5,6},{6,7},{7,4},{8,9},{9,10},{10,1... | collective-permute-start | bytes 786440 | tf_op jit(solution)/shard_map/ppermute | solution.py:537
  (38 other events, 423.9 us)

commit v5 on v4

--- a/solution.py
+++ b/solution.py
@@ -80,21 +80,27 @@
         lax.fori_loop(0, part // step, one, 0)
 
 
-def gather_kernel(peers, peer, first_row, within, half, build, rows_in, counts_in, *refs):
+def gather_kernel(peers, peer, first_row, within, half, build, ahead, rows_in, counts_in, *refs):
     n_out = len(peers)
-    outs = refs[1 : n_out + 1]
+    refs = list(refs)
+    source = refs.pop(0)
+    vals = [refs.pop(0) for _ in range(2 * bool(ahead))]
+    outs, refs = refs[:n_out], refs[n_out:]
     if build:
-        feat, (table, raw) = refs[0], refs[n_out + 1 : n_out + 3]
-        rows, counts, index_sems, stage, sems = refs[n_out + 3 :]
+        feat, table, raw = source, refs.pop(0), refs.pop(0)
     else:
-        table = refs[0]
-        rows, counts, index_sems, stage = refs[n_out + 1 :]
+        table = source
+    block = refs.pop(0) if ahead else None
+    rows, counts, index_sems, stage = refs[:4]
+    loads = block_copies(vals, block, refs[-1], *ahead) if ahead else []
+    for load in loads:
+        load.start()
     load_rows = pltpu.make_async_copy(rows_in, rows, index_sems.at[0])
     load_counts = pltpu.make_async_copy(counts_in, counts, index_sems.at[1])
     load_rows.start()
     load_counts.start()
     if build:
-        widen(feat, half, table, raw, sems)
+        widen(feat, half, table, raw, refs[4])
     load_rows.wait()
     load_counts.wait()
     me = lax.axis_index("dom")
@@ -118,9 +124,13 @@
             at = pl.ds(b * 64, 64)
             slot = b * 64 + lax.broadcasted_iota(jnp.int32, (64, LANES), 0)
             out[at, :] = jnp.where(slot < used, stage[at, :], 0.0).astype(out.dtype)
-
-
-def gather_rows(rows, first_row, within, send_count, features, half, table, peers, peer, slots):
+    for load in loads:
+        load.wait()
+
+
+def gather_rows(
+    rows, first_row, within, send_count, features, half, table, peers, peer, slots, vals, ahead
+):
     n_rows = features.shape[0]
     build = table is None
     piece = jax.ShapeDtypeStruct((slots, LANES), features.dtype)
@@ -129,23 +139,29 @@
         jax.ShapeDtypeStruct((n_rows, LANES), jnp.float32),
         jax.ShapeDtypeStruct((n_rows, LANES), features.dtype),
     ]
+    block = [block_shape(vals[0], *ahead)] if ahead else []
     out = pl.pallas_call(
-        functools.partial(gather_kernel, peers, peer, first_row, within, half, build),
-        out_shape=[piece] * len(peers) + made * build,
-        in_specs=[RAW, RAW, RAW if build else VMEM],
-        out_specs=[VMEM] * (len(peers) + 2 * build),
+        functools.partial(gather_kernel, peers, peer, first_row, within, half, build, ahead),
+        out_shape=[piece] * len(peers) + made * build + block,
+        in_specs=[RAW, RAW, RAW if build else VMEM] + [RAW] * (2 * len(block)),
+        out_specs=[VMEM] * (len(peers) + 2 * build + len(block)),
         scratch_shapes=[
             pltpu.SMEM(rows.shape, jnp.int32),
             pltpu.SMEM(send_count.shape, jnp.int32),
             pltpu.SemaphoreType.DMA((2,)),
             pltpu.VMEM((slots, LANES), jnp.float32),
         ]
-        + [pltpu.SemaphoreType.DMA((parts,))] * build,
-        compiler_params=grant(10 + len(peers) if build else 4),
+        + [pltpu.SemaphoreType.DMA((parts,))] * build
+        + [pltpu.SemaphoreType.DMA((2 * cols[0],)) for cols in [ahead] if ahead],
+        compiler_params=grant(10 + len(peers) if build else 8),
         cost_estimate=cost(4e9, 6 << 20),
         name="gather_rows",
-    )(in_hbm(rows), in_hbm(send_count), in_hbm(features) if build else table)
-    return out[: len(peers)], out[len(peers) :]
+    )(
+        in_hbm(rows), in_hbm(send_count), in_hbm(features) if build else table,
+        *([in_hbm(v) for v in vals] * len(block)),
+    )
+    n_out = len(peers)
+    return out[:n_out], out[n_out : n_out + 2 * build], out[n_out + 2 * build :]
 
 
 def masked(vals, used):
@@ -167,58 +183,23 @@
     )
 
 
-def vals_specs(n_col, per_dest, base, group, slots):
-    def spec(k):
-        def place(i, *_):
-            dest = lax.rem(lax.axis_index("col") + k, n_col)
-            return ((dest * per_dest + base) // group + i, 0, 0, 0)
-
-        return pl.BlockSpec((group, slots, TILE, TILE), place)
-
-    return [spec(k) for k in range(n_col)]
-
-
 def row_tile_of(k, n_col, per_dest, tile):
     return lax.rem(lax.axis_index("col") + k, n_col) * per_dest + tile
 
 
-def early_kernel(n_col, slots, per_dest, own_index, own_counts, halo_counts, feat, *refs):
-    own_vals, halo_vals, (part, kept) = refs[:n_col], refs[n_col:-2], refs[-2:]
-    i = pl.program_id(0)
+def block_shape(vals, n_col, per_dest, base, size):
+    return jax.ShapeDtypeStruct((n_col, 2, size) + vals.shape[1:], vals.dtype)
+
+
+def block_copies(vals, block, sems, n_col, per_dest, base, size):
+    copies = []
     for k in range(n_col):
-        row_tile = row_tile_of(k, n_col, per_dest, i)
-        part[k, pl.ds(pl.multiple_of(i * TILE, TILE), TILE), :] = product(
-            masked(own_vals[k][0], own_counts[row_tile]),
-            tiles_of(feat, own_index, row_tile, slots),
-        )
-        for s, vals in enumerate(masked(halo_vals[k][0], halo_counts[row_tile])):
-            kept[k, i, s] = vals
-
-
-def early_sums(tables, features, own_vals, halo_vals, n_col, size):
-    tiles, slots = own_vals.shape[:2]
-    width = features.shape[1]
-    per_dest = tiles // n_col
-    own_index, own_counts, _, halo_counts = tables
-    return pl.pallas_call(
-        functools.partial(early_kernel, n_col, slots, per_dest),
-        out_shape=[
-            jax.ShapeDtypeStruct((n_col, size * TILE, width), jnp.float32),
-            jax.ShapeDtypeStruct((n_col, size, slots, TILE, TILE), halo_vals.dtype),
-        ],
-        grid_spec=pltpu.PrefetchScalarGridSpec(
-            num_scalar_prefetch=3,
-            grid=(size,),
-            in_specs=[VMEM] + vals_specs(n_col, per_dest, 0, 1, slots) * 2,
-            out_specs=[VMEM] * 2,
-        ),
-        compiler_params=grant(16),
-        cost_estimate=cost(2e9, 4 << 20),
-        name="early_sums",
-    )(
-        own_index, own_counts, halo_counts, in_vmem(features),
-        *([in_hbm(own_vals)] * n_col), *([in_hbm(halo_vals)] * n_col),
-    )
+        at = pl.ds(row_tile_of(k, n_col, per_dest, base), size)
+        for v in range(2):
+            copies.append(
+                pltpu.make_async_copy(vals[v].at[at], block.at[k, v], sems.at[2 * k + v])
+            )
+    return copies
 
 
 def put_piece(halo, piece, q):
@@ -249,79 +230,56 @@
     )(*pieces)
 
 
-def first_kernel(n_col, slots, per_dest, ks, peer, index, *refs):
-    pieces = refs[: len(ks)]
-    part, kept = refs[len(ks) : len(ks) + 2]
-    outs, halo = refs[-n_col - 1 : -1], refs[-1]
-    me = lax.axis_index("dom")
-    for k, piece in zip(ks, pieces):
-        put_piece(halo, piece, peer(me, -k))
-    for t in range(kept.shape[1]):
-        at = pl.ds(t * TILE, TILE)
+def sum_kernel(n_col, slots, per_dest, base, ahead, *refs):
+    own_index, own_counts, halo_index, halo_counts, feat, halo, block = refs[:7]
+    refs = refs[7:]
+    loads = []
+    if ahead:
+        loads = block_copies(refs[:2], refs[2 + n_col], refs[-1], *ahead)
+        refs = refs[2:]
+    outs = refs[:n_col]
+    for load in loads:
+        load.start()
+
+    def one(t, carry):
         for k in range(n_col):
-            right = tiles_of(halo, index, row_tile_of(k, n_col, per_dest, t), slots)
-            total = part[k, at, :] + product([kept[k, t, s] for s in range(slots)], right)
-            outs[k][at, :] = total.astype(outs[k].dtype)
-
-
-def first_sums(index, ks, pieces, part, kept, halo, per_dest, peer):
-    n_col, size, slots = kept.shape[:3]
-    width = halo.shape[1]
-    out = pl.pallas_call(
-        functools.partial(first_kernel, n_col, slots, per_dest, ks, peer),
-        out_shape=[jax.ShapeDtypeStruct((size * TILE, width), halo.dtype)] * n_col
-        + [jax.ShapeDtypeStruct(halo.shape, halo.dtype)],
-        in_specs=[pl.BlockSpec(memory_space=pltpu.SMEM)] + [VMEM] * (len(ks) + 3),
-        out_specs=[VMEM] * (n_col + 1),
-        input_output_aliases={len(ks) + 3: n_col},
-        compiler_params=grant(6 + halo.shape[0] // (1 << 12)),
-        cost_estimate=cost(2e9, 4 << 20),
-        name="first_sums",
-    )(index, *pieces, part, kept, halo)
-    return out[:n_col], out[n_col]
-
-
-def sum_kernel(n_col, slots, per_dest, base, *refs):
-    own_index, own_counts, halo_index, halo_counts, feat, halo = refs[:6]
-    own_vals, halo_vals = refs[6 : 6 + n_col], refs[6 + n_col : 6 + 2 * n_col]
-    outs = refs[6 + 2 * n_col :]
-    sub = pl.program_id(0)
-    group = own_vals[0].shape[0]
-    for k in range(n_col):
-        for t in range(group):
-            row_tile = row_tile_of(k, n_col, per_dest, base + sub * group + t)
-            left = masked(own_vals[k][t], own_counts[row_tile])
-            left += masked(halo_vals[k][t], halo_counts[row_tile])
+            row_tile = row_tile_of(k, n_col, per_dest, base + t)
+            left = masked(block.at[k, 0, t], own_counts[row_tile])
+            left += masked(block.at[k, 1, t], halo_counts[row_tile])
             right = tiles_of(feat, own_index, row_tile, slots)
             right += tiles_of(halo, halo_index, row_tile, slots)
-            at = pl.ds(pl.multiple_of((sub * group + t) * TILE, TILE), TILE)
+            at = pl.ds(pl.multiple_of(t * TILE, TILE), TILE)
             outs[k][at, :] = product(left, right).astype(outs[k].dtype)
-
-
-def tile_sums(tables, halo, features, own_vals, halo_vals, n_col, base, size):
-    tiles, slots = own_vals.shape[:2]
+        return carry
+
+    lax.fori_loop(0, block.shape[2], one, 0)
+    for load in loads:
+        load.wait()
+
+
+def tile_sums(tables, halo, features, block, vals, per_dest, base, ahead):
+    n_col, _, size, slots = block.shape[:4]
     width = features.shape[1]
-    per_dest = tiles // n_col
-    group = min(size, 2)
-    while base % group or size % group:
-        group -= 1
-    specs = vals_specs(n_col, per_dest, base, group, slots)
-    return pl.pallas_call(
-        functools.partial(sum_kernel, n_col, slots, per_dest, base),
-        out_shape=[jax.ShapeDtypeStruct((size * TILE, width), jnp.bfloat16)] * n_col,
+    made = [block_shape(vals[0], *ahead)] if ahead else []
+    smem = pl.BlockSpec(memory_space=pltpu.SMEM)
+    out = pl.pallas_call(
+        functools.partial(sum_kernel, n_col, slots, per_dest, base, ahead),
+        out_shape=[jax.ShapeDtypeStruct((size * TILE, width), jnp.bfloat16)] * n_col + made,
         grid_spec=pltpu.PrefetchScalarGridSpec(
             num_scalar_prefetch=4,
-            grid=(size // group,),
-            in_specs=[VMEM] * 2 + specs * 2,
-            out_specs=[VMEM] * n_col,
+            grid=(1,),
+            in_specs=[VMEM] * 3 + [RAW] * (2 * len(made)),
+            out_specs=[VMEM] * (n_col + len(made)),
+            scratch_shapes=[pltpu.SemaphoreType.DMA((2 * n_col,))] * len(made),
         ),
-        compiler_params=grant(18),
+        compiler_params=grant(8),
         cost_estimate=cost(2e9, 6 << 20),
         name="tile_sums",
     )(
-        *tables, in_vmem(features), in_vmem(halo),
-        *([in_hbm(own_vals)] * n_col), *([in_hbm(halo_vals)] * n_col),
+        *tables, in_vmem(features), in_vmem(halo), in_vmem(block),
+        *([in_hbm(v) for v in vals] * len(made)),
     )
+    return out[:n_col], out[n_col:]
 
 
 PAD = 16
@@ -542,15 +500,22 @@
     rows, first_row, within = storage_order(send_rows[0])
     slots = send_rows.shape[2]
     halves = width // LANES
+    vals = (local_vals[0], halo_vals[0])
+    per_dest = n_rows // TILE // n_col
+    plan = chunk_plan(per_dest)
+    ahead = [(n_col, per_dest, base, size) for base, size in plan]
     halo, own_tiles = [], []
     for h in range(halves):
         pieces, table = {}, None
-        for peers in [lead, rest] if h == 0 else [lead + rest]:
-            if not peers:
-                continue
-            outgoing, made = gather_rows(
-                rows, first_row, within, send_count[0], features, h, table, peers, peer, slots
+        groups = [g for g in (lead, rest) if g] if h == 0 else [lead + rest]
+        for peers in groups:
+            load = ahead[0] if h == 0 and peers is groups[-1] else ()
+            outgoing, made, block = gather_rows(
+                rows, first_row, within, send_count[0], features, h, table, peers, peer,
+                slots, vals, load,
             )
+            if load:
+                blocks = [block[0]]
             if made:
                 table, tiles = made
             for k, piece in zip(peers, outgoing):
@@ -576,28 +541,16 @@
         step //= 2
     weights, bias = join_weights(weight, bias_row, [got[f] for f in range(share)], n_col)
 
-    per_dest = n_rows // TILE // n_col
-    plan = chunk_plan(per_dest)
     index_tables = (local_index[0].T, local_count[0], halo_index[0].T, halo_count[0])
-    part, kept = early_sums(
-        index_tables, own_tiles[0], local_vals[0], halo_vals[0], n_col, plan[0][1]
-    )
-    late = far[-2:-1] or far
     incoming = [[[] for _ in range(n_col)] for _ in plan]
     for h in range(halves):
-        soon = [k for k in far if h or k not in late]
-        received = assemble(soon, [halo[h][k] for k in soon], n_dom, peer)
+        received = assemble(far, [halo[h][k] for k in far], n_dom, peer)
         for g, (base, size) in enumerate(plan):
-            if g == h == 0:
-                sums, received = first_sums(
-                    index_tables[2], late, [halo[h][k] for k in late], part, kept,
-                    received, per_dest, peer,
-                )
-            else:
-                sums = tile_sums(
-                    index_tables, received, own_tiles[h], local_vals[0], halo_vals[0],
-                    n_col, base, size,
-                )
+            load = ahead[g + 1] if h == 0 and g + 1 < len(plan) else ()
+            sums, block = tile_sums(
+                index_tables, received, own_tiles[h], blocks[g], vals, per_dest, base, load
+            )
+            blocks += block
             moved = {k: along_col(sums[k], k) for k in order}
             for k in range(n_col):
                 incoming[g][k].append(moved[k] if k else sums[0])

time: 253 us -> 239 us (0.945)
  starting transfers between devices: 120 us -> 105 us
  Pallas kernels: 61.7 us -> 48.9 us
  waiting for transfers between devices: 60.1 us -> 71.1 us
  blocking collectives: 9.16 us -> 11.9 us
    ppermute x42, starting transfers between devices: 103 us -> 88.6 us  [on_device(): lax.ppermute(x, 'col', [(i, (i + k) % n_col) for i in range(n_col)])]
    ppermute x42, waiting for transfers between devices: 58.7 us -> 66.7 us  [on_device(): lax.ppermute(x, 'col', [(i, (i + k) % n_col) for i in range(n_col)])]
    pallas_call x7 -> x8, Pallas kernels: 27.5 us -> 20.5 us  [tile_sums(): pl.pallas_call(functools.partial(sum_kernel, n_col, slots, per_dest, base...]
    pallas_call x2 -> x0, Pallas kernels: 6.1 us -> none  [the longest x1 4.81 us: early_sums(): pl.pallas_call(functools.partial(early_kernel, n_col, slots, per_dest), o...]
    ppermute x14, waiting for transfers between devices: 1.32 us -> 4.47 us  [on_device(): lax.ppermute(x, 'dom', [(i, peer(i, k)) for i in range(n_dom)])]
    all_gather x1, blocking collectives: 9.16 us -> 11.9 us  [on_device(): over_dom = lax.all_gather(stats, 'dom', axis=0)]
  transfers between devices with their start and end apart: 63 -> 63, of which waited for: 12 -> 19; matrix products, arithmetic and copies ran while one was open for 0% -> 0% of each run, Pallas kernels for 23% -> 18%
where the time goes in v5:
time: 239 us; the launch traced here: 238 us
  starting transfers between devices  105 us (44%)
  waiting for transfers between devices  71.1 us (30%)
  Pallas kernels  48.9 us (20%)
  blocking collectives  11.9 us (5%)
    ppermute x42, starting transfers between devices, on_device(): lax.ppermute(x, 'col', [(i, (i + k) % n_col) for i in range(n_col)])  88.6 us
    ppermute x42, waiting for transfers between devices, on_device(): lax.ppermute(x, 'col', [(i, (i + k) % n_col) for i in range(n_col)])  66.7 us
    pallas_call x8, Pallas kernels, tile_sums(): pl.pallas_call(functools.partial(sum_kernel, n_col, slots, per_dest, base...  20.5 us
    ppermute x14, starting transfers between devices, on_device(): lax.ppermute(x, 'dom', [(i, peer(i, k)) for i in range(n_dom)])  13.1 us
    all_gather x1, blocking collectives, on_device(): over_dom = lax.all_gather(stats, 'dom', axis=0)  11.9 us
    pallas_call x3, Pallas kernels, gather_rows(): pl.pallas_call(functools.partial(gather_kernel, peers, peer, first_row, w...  11.7 us
    pallas_call x4, Pallas kernels, mix_rows(): pl.pallas_call(functools.partial(mix_kernel, n_col, len(pieces), channels...  10.5 us
  transfers between devices with their start and end apart: 63, of which 19 were waited for; matrix products, arithmetic and copies ran while one was open for 0% of the time, Pallas kernels for 18%

profile of v5, /device:TPU:0, one launch (start us, length us, event | category | flops | bytes accessed | tf_op | source)
XLA Modules:
  0.0 238.3 jit_solution(5221509864865369041)
XLA Ops:
  3.0 3.1 %gather_rows.4 = (bf16[512,128]{1,0:T(8,128)(2,1)S(1)}, bf16[512,128]{1,0:T(8,128)(2,1)S(1)}, bf16[512,128]{1,0:T(8,128)(2,1)S(1)}, bf16[512,128]{1,0:T(8,128)(2...) custom-call(s32[4096]{0:T(1024)} %bitcast.59, s32[8]{0:T(128)} %bitcast.62, ...), custom_call_target="tpu_custom_call" | custom-call | flops 4000000000 | bytes 6291456 | tf_op jit(solution)/shard_map/gather_rows/pallas_call | solution.py:143
  6.1 4.2 %collective-permute-start.1 = (bf16[512,128]{1,0:T(8,128)(2,1)S(1)}, bf16[512,128]{1,0:T(8,128)(2,1)S(1)}, u32[]{:S(2)}, u32[]{:S(2)}) collective-permute-start(bf16[512,128]{1,0:T(8,128)(2,1)S(1)} %get-tuple-element.80), channel_id=1, source_target_pairs={{0,24},{4,28},{8,16},{12,20},{16,8},{20,12},{24,0},{28,4},{1,25},{... | collective-permute-start | bytes 393224 | tf_op jit(solution)/shard_map/ppermute | solution.py:494
  13.5 2.6 %collective-permute-start.21 = (bf16[144,256]{1,0:T(8,128)(2,1)S(1)}, bf16[144,256]{1,0:T(8,128)(2,1)S(1)}, u32[]{:S(2)}, u32[]{:S(2)}) collective-permute-start(bf16[144,256]{1,0:T(8,128)(2,1)S(1)} %weight_part.1), channel_id=1, source_target_pairs={{0,2},{1,3},{2,0},{3,1},{4,6},{5,7},{6,4},{7,5},{8,10},{9,11},{10,... | collective-permute-start | bytes 221192 | tf_op jit(solution)/shard_map/ppermute | solution.py:495
  23.9 6.3 %gather_rows.5 = (bf16[512,128]{1,0:T(8,128)(2,1)S(1)}, bf16[512,128]{1,0:T(8,128)(2,1)S(1)}, bf16[512,128]{1,0:T(8,128)(2,1)S(1)}, bf16[512,128]{1,0:T(8,128)(2...) custom-call(s32[4096]{0:T(1024)} %bitcast.60, ...), custom_call_target="tpu_custom_call" | custom-call | flops 4000000000 | bytes 6291456 | tf_op jit(solution)/shard_map/gather_rows/pallas_call | solution.py:143
  38.0 2.8 %tile_sums.8 = (bf16[512,128]{1,0:T(8,128)(2,1)S(1)}, bf16[512,128]{1,0:T(8,128)(2,1)S(1)}, bf16[512,128]{1,0:T(8,128)(2,1)S(1)}, bf16[512,128]{1,0:T(8,128)(2,1)S(1)}, bf16[4,2,4,4,128,128]{5,4,3,2,1,0:T(8,128)(2,1)S(1)}) custom-call(s32[4,64]{1,0:T(4,128)S(1)} %bitcast.18, s32[64]{0:T(128)S(1)} %bitcast.34, s32[4,64]{1,0:T(4,128)S(1)} %bitcast.26, ...), custom_call_target="tpu_custom_call" | custom-call | flops 2000000000 | bytes 6291456 | tf_op jit(solution)/shard_map/tile_sums/pallas_call | solution.py:265
  46.1 2.6 %collective-permute-start.46 = (bf16[512,128]{1,0:T(8,128)(2,1)S(1)}, bf16[512,128]{1,0:T(8,128)(2,1)S(1)}, u32[]{:S(2)}, u32[]{:S(2)}) collective-permute-start(bf16[512,128]{1,0:T(8,128)(2,1)S(1)} %get-tuple-element.130), channel_id=1, source_target_pairs={{0,3},{1,0},{2,1},{3,2},{4,7},{5,4},{6,5},{7,6},{8,11},{9,8},{10,9... | collective-permute-start | bytes 393224 | tf_op jit(solution)/shard_map/ppermute | solution.py:495
  53.9 3.2 %collective-permute-start.45 = (bf16[512,128]{1,0:T(8,128)(2,1)S(1)}, bf16[512,128]{1,0:T(8,128)(2,1)S(1)}, u32[]{:S(2)}, u32[]{:S(2)}) collective-permute-start(bf16[512,128]{1,0:T(8,128)(2,1)S(1)} %get-tuple-element.129), channel_id=1, source_target_pairs={{0,2},{1,3},{2,0},{3,1},{4,6},{5,7},{6,4},{7,5},{8,10},{9,11},{10,... | collective-permute-start | bytes 393224 | tf_op jit(solution)/shard_map/ppermute | solution.py:495
  58.8 2.8 %tile_sums.9 = (bf16[512,128]{1,0:T(8,128)(2,1)S(1)}, bf16[512,128]{1,0:T(8,128)(2,1)S(1)}, bf16[512,128]{1,0:T(8,128)(2,1)S(1)}, bf16[512,128]{1,0:T(8,128)(2,1)S(1)}, bf16[4,2,4,4,128,128]{5,4,3,2,1,0:T(8,128)(2,1)S(1)}) custom-call(s32[4,64]{1,0:T(4,128)S(1)} %bitcast.21, s32[64]{0:T(128)S(1)} %bitcast.37, s32[4,64]{1,0:T(4,128)S(1)} %bitcast.29, ...), custom_call_target="tpu_custom_call" | custom-call | flops 2000000000 | bytes 6291456 | tf_op jit(solution)/shard_map/tile_sums/pallas_call | solution.py:265
  62.6 2.9 %collective-permute-start.37 = (bf16[512,128]{1,0:T(8,128)(2,1)S(1)}, bf16[512,128]{1,0:T(8,128)(2,1)S(1)}, u32[]{:S(2)}, u32[]{:S(2)}) collective-permute-start(bf16[512,128]{1,0:T(8,128)(2,1)S(1)} %get-tuple-element.119), channel_id=1, source_target_pairs={{0,1},{1,2},{2,3},{3,0},{4,5},{5,6},{6,7},{7,4},{8,9},{9,10},{10,1... | collective-permute-start | bytes 393224 | tf_op jit(solution)/shard_map/ppermute | solution.py:495
  65.5 4.2 %collective-permute-done.45.refs_5_ = bf16[512,128]{1,0:T(8,128)(2,1)S(1)} collective-permute-done((bf16[512,128]{1,0:T(8,128)(2,1)S(1)}, bf16[512,128]{1,0:T(8,128)(2,1)S(1)}, u32[]{:S(2)}, u32[]{:S(2)}) %collective-permute-start.45) | collective-permute-done | bytes 131104 | tf_op jit(solution)/shard_map/ppermute | solution.py:495
  73.1 6.0 %collective-permute-start.36 = (bf16[512,128]{1,0:T(8,128)(2,1)S(1)}, bf16[512,128]{1,0:T(8,128)(2,1)S(1)}, u32[]{:S(2)}, u32[]{:S(2)}) collective-permute-start(bf16[512,128]{1,0:T(8,128)(2,1)S(1)} %get-tuple-element.118), channel_id=1, source_target_pairs={{0,1},{1,2},{2,3},{3,0},{4,5},{5,6},{6,7},{7,4},{8,9},{9,10},{10,1... | collective-permute-start | bytes 393224 | tf_op jit(solution)/shard_map/ppermute | solution.py:495
  80.7 2.8 %collective-permute-done.41.refs_7_ = bf16[512,128]{1,0:T(8,128)(2,1)S(1)} collective-permute-done((bf16[512,128]{1,0:T(8,128)(2,1)S(1)}, bf16[512,128]{1,0:T(8,128)(2,1)S(1)}, u32[]{:S(2)}, u32[]{:S(2)}) %collective-permute-start.41) | collective-permute-done | bytes 131104 | tf_op jit(solution)/shard_map/ppermute | solution.py:495
  83.6 2.8 %tile_sums.10 = (bf16[512,128]{1,0:T(8,128)(2,1)S(1)}, bf16[512,128]{1,0:T(8,128)(2,1)S(1)}, bf16[512,128]{1,0:T(8,128)(2,1)S(1)}, bf16[512,128]{1,0:T(8,128)(2,1)S(1)}, bf16[4,2,4,4,128,128]{5,4,3,2,1,0:T(8,128)(2,1)S(1)}) custom-call(s32[4,64]{1,0:T(4,128)S(1)} %bitcast.23, s32[64]{0:T(128)S(1)} %bitcast.39, s32[4,64]{1,0:T(4,128)S(1)} %bitcast.31, ...), custom_call_target="tpu_custom_call" | custom-call | flops 2000000000 | bytes 6291456 | tf_op jit(solution)/shard_map/tile_sums/pallas_call | solution.py:265
  86.5 3.6 %collective-permute-done.38.refs_4_ = bf16[512,128]{1,0:T(8,128)(2,1)S(1)} collective-permute-done((bf16[512,128]{1,0:T(8,128)(2,1)S(1)}, bf16[512,128]{1,0:T(8,128)(2,1)S(1)}, u32[]{:S(2)}, u32[]{:S(2)}) %collective-permute-start.38) | collective-permute-done | bytes 131104 | tf_op jit(solution)/shard_map/ppermute | solution.py:495
  94.2 2.8 %collective-permute-done.31.refs_3_ = bf16[512,128]{1,0:T(8,128)(2,1)S(1)} collective-permute-done((bf16[512,128]{1,0:T(8,128)(2,1)S(1)}, bf16[512,128]{1,0:T(8,128)(2,1)S(1)}, u32[]{:S(2)}, u32[]{:S(2)}) %collective-permute-start.31) | collective-permute-done | bytes 131104 | tf_op jit(solution)/shard_map/ppermute | solution.py:495
  100.5 4.1 %collective-permute-done.33.refs_5_ = bf16[512,128]{1,0:T(8,128)(2,1)S(1)} collective-permute-done((bf16[512,128]{1,0:T(8,128)(2,1)S(1)}, bf16[512,128]{1,0:T(8,128)(2,1)S(1)}, u32[]{:S(2)}, u32[]{:S(2)}) %collective-permute-start.33) | collective-permute-done | bytes 131104 | tf_op jit(solution)/shard_map/ppermute | solution.py:495
  107.3 3.3 %collective-permute-start.34 = (bf16[512,128]{1,0:T(8,128)(2,1)S(1)}, bf16[512,128]{1,0:T(8,128)(2,1)S(1)}, u32[]{:S(2)}, u32[]{:S(2)}) collective-permute-start(bf16[512,128]{1,0:T(8,128)(2,1)S(1)} %get-tuple-element.114), channel_id=1, source_target_pairs={{0,3},{1,0},{2,1},{3,2},{4,7},{5,4},{6,5},{7,6},{8,11},{9,8},{10,9... | collective-permute-start | bytes 393224 | tf_op jit(solution)/shard_map/ppermute | solution.py:495
  111.7 2.6 %mix_rows.4 = (bf16[512,256]{1,0:T(8,128)(2,1)S(1)}, bf16[512,256]{1,0:T(8,128)(2,1)S(1)}, bf16[512,256]{1,0:T(8,128)(2,1)S(1)}, bf16[512,256]{1,0:T(8,128)(2,1)S(1)}, f32[8,256]{1,0:T(8,128)S(1)}) custom-call(bf16[512,128]{1,0:T(8,128)(2,1)S(1)} %get-tuple-element.124.refs_0_, bf16[512,128]{1,0:T(8,128)(2,1)S(1)} %get-tuple-element.125.refs_1_, ...), custom_call_target="tpu_custom_call" | custom-call | flops 1073741824 | bytes 4194304 | tf_op jit(solution)/shard_map/mix_rows/pallas_call | solution.py:406
  115.8 2.9 %collective-permute-start.19 = (bf16[512,128]{1,0:T(8,128)(2,1)S(1)}, bf16[512,128]{1,0:T(8,128)(2,1)S(1)}, u32[]{:S(2)}, u32[]{:S(2)}) collective-permute-start(bf16[512,128]{1,0:T(8,128)(2,1)S(1)} %get-tuple-element.105), channel_id=1, source_target_pairs={{0,3},{1,0},{2,1},{3,2},{4,7},{5,4},{6,5},{7,6},{8,11},{9,8},{10,9... | collective-permute-start | bytes 393224 | tf_op jit(solution)/shard_map/ppermute | solution.py:495
  118.7 2.7 %collective-permute-done.32.refs_4_ = bf16[512,128]{1,0:T(8,128)(2,1)S(1)} collective-permute-done((bf16[512,128]{1,0:T(8,128)(2,1)S(1)}, bf16[512,128]{1,0:T(8,128)(2,1)S(1)}, u32[]{:S(2)}, u32[]{:S(2)}) %collective-permute-start.32) | collective-permute-done | bytes 131104 | tf_op jit(solution)/shard_map/ppermute | solution.py:495
  122.9 4.4 %collective-permute-start.16 = (bf16[512,128]{1,0:T(8,128)(2,1)S(1)}, bf16[512,128]{1,0:T(8,128)(2,1)S(1)}, u32[]{:S(2)}, u32[]{:S(2)}) collective-permute-start(bf16[512,128]{1,0:T(8,128)(2,1)S(1)} %get-tuple-element.102), channel_id=1, source_target_pairs={{0,2},{1,3},{2,0},{3,1},{4,6},{5,7},{6,4},{7,5},{8,10},{9,11},{10,... | collective-permute-start | bytes 393224 | tf_op jit(solution)/shard_map/ppermute | solution.py:495
  132.1 2.6 %mix_rows.6 = (bf16[512,256]{1,0:T(8,128)(2,1)S(1)}, bf16[512,256]{1,0:T(8,128)(2,1)S(1)}, bf16[512,256]{1,0:T(8,128)(2,1)S(1)}, bf16[512,256]{1,0:T(8,128)(2,1)S(1)}, f32[8,256]{1,0:T(8,128)S(1)}) custom-call(bf16[512,128]{1,0:T(8,128)(2,1)S(1)} %get-tuple-element.108.refs_0_, bf16[512,128]{1,0:T(8,128)(2,1)S(1)} %get-tuple-element.109.refs_1_, ...), custom_call_target="tpu_custom_call" | custom-call | flops 1073741824 | bytes 4194304 | tf_op jit(solution)/shard_map/mix_rows/pallas_call | solution.py:406
  135.0 8.1 %collective-permute-start.60 = (bf16[512,256]{1,0:T(8,128)(2,1)S(1)}, bf16[512,256]{1,0:T(8,128)(2,1)S(1)}, u32[]{:S(2)}, u32[]{:S(2)}) collective-permute-start(bf16[512,256]{1,0:T(8,128)(2,1)S(1)} %get-tuple-element.149), channel_id=1, source_target_pairs={{0,3},{1,0},{2,1},{3,2},{4,7},{5,4},{6,5},{7,6},{8,11},{9,8},{10,9... | collective-permute-start | bytes 786440 | tf_op jit(solution)/shard_map/ppermute | solution.py:495
  143.7 10.5 %collective-permute-start.57 = (bf16[512,256]{1,0:T(8,128)(2,1)S(1)}, bf16[512,256]{1,0:T(8,128)(2,1)S(1)}, u32[]{:S(2)}, u32[]{:S(2)}) collective-permute-start(bf16[512,256]{1,0:T(8,128)(2,1)S(1)} %get-tuple-element.145), channel_id=1, source_target_pairs={{0,3},{1,0},{2,1},{3,2},{4,7},{5,4},{6,5},{7,6},{8,11},{9,8},{10,9... | collective-permute-start | bytes 786440 | tf_op jit(solution)/shard_map/ppermute | solution.py:495
  154.2 2.6 %mix_rows.7 = (bf16[512,256]{1,0:T(8,128)(2,1)S(1)}, bf16[512,256]{1,0:T(8,128)(2,1)S(1)}, bf16[512,256]{1,0:T(8,128)(2,1)S(1)}, bf16[512,256]{1,0:T(8,128)(2,1)S(1)}, f32[8,256]{1,0:T(8,128)S(1)}) custom-call(bf16[512,128]{1,0:T(8,128)(2,1)S(1)} %get-tuple-element.90.refs_0_, bf16[512,128]{1,0:T(8,128)(2,1)S(1)} %get-tuple-element.99.refs_1_, ...), custom_call_target="tpu_custom_call" | custom-call | flops 1073741824 | bytes 4194304 | tf_op jit(solution)/shard_map/mix_rows/pallas_call | solution.py:406
  156.8 11.9 %all-gather = f32[64,256]{1,0:T(8,128)S(1)} all-gather(f32[8,256]{1,0:T(8,128)S(1)} %get-tuple-element.139), channel_id=2, replica_groups=mesh['dom'=8,'col'=4] {'dom'}, dimensions={0}, use_global_device_ids=true | all-gather | bytes 73728 | tf_op jit(solution)/shard_map/all_gather | solution.py:565
  168.8 3.6 %collective-permute-done.51.refs_5_ = f32[2,256]{1,0:T(2,128)S(1)} collective-permute-done((f32[2,256]{1,0:T(2,128)S(1)}, f32[2,256]{1,0:T(2,128)S(1)}, u32[]{:S(2)}, u32[]{:S(2)}) %collective-permute-start.51) | collective-permute-done | bytes 2080 | tf_op jit(solution)/shard_map/ppermute | solution.py:495
  177.4 15.6 %collective-permute-done.58.refs_2_ = bf16[512,256]{1,0:T(8,128)(2,1)S(1)} collective-permute-done((bf16[512,256]{1,0:T(8,128)(2,1)S(1)}, bf16[512,256]{1,0:T(8,128)(2,1)S(1)}, u32[]{:S(2)}, u32[]{:S(2)}) %collective-permute-start.58) | collective-permute-done | bytes 262176 | tf_op jit(solution)/shard_map/ppermute | solution.py:495
  193.0 12.0 %collective-permute-start.49 = (bf16[512,256]{1,0:T(8,128)(2,1)S(1)}, bf16[512,256]{1,0:T(8,128)(2,1)S(1)}, u32[]{:S(2)}, u32[]{:S(2)}) collective-permute-start(bf16[512,256]{1,0:T(8,128)(2,1)S(1)} %get-tuple-element.137), channel_id=1, source_target_pairs={{0,2},{1,3},{2,0},{3,1},{4,6},{5,7},{6,4},{7,5},{8,10},{9,11},{10,... | collective-permute-start | bytes 786440 | tf_op jit(solution)/shard_map/ppermute | solution.py:495
  205.1 5.3 %collective-permute-start.50 = (bf16[512,256]{1,0:T(8,128)(2,1)S(1)}, bf16[512,256]{1,0:T(8,128)(2,1)S(1)}, u32[]{:S(2)}, u32[]{:S(2)}) collective-permute-start(bf16[512,256]{1,0:T(8,128)(2,1)S(1)} %get-tuple-element.138), channel_id=1, source_target_pairs={{0,1},{1,2},{2,3},{3,0},{4,5},{5,6},{6,7},{7,4},{8,9},{9,10},{10,1... | collective-permute-start | bytes 786440 | tf_op jit(solution)/shard_map/ppermute | solution.py:495
  212.4 12.9 %collective-permute-done.55.refs_2_ = bf16[512,256]{1,0:T(8,128)(2,1)S(1)} collective-permute-done((bf16[512,256]{1,0:T(8,128)(2,1)S(1)}, bf16[512,256]{1,0:T(8,128)(2,1)S(1)}, u32[]{:S(2)}, u32[]{:S(2)}) %collective-permute-start.55) | collective-permute-done | bytes 262176 | tf_op jit(solution)/shard_map/ppermute | solution.py:495
  226.3 10.2 %collective-permute-done.52.refs_6_ = f32[2,256]{1,0:T(2,128)S(1)} collective-permute-done((f32[2,256]{1,0:T(2,128)S(1)}, f32[2,256]{1,0:T(2,128)S(1)}, u32[]{:S(2)}, u32[]{:S(2)}) %collective-permute-start.52) | collective-permute-done | bytes 2080 | tf_op jit(solution)/shard_map/ppermute | solution.py:495
  (134 shorter events, 69.1 us)
Async XLA Ops:
  6.1 15.1 %collective-permute-start.1 = (bf16[512,128]{1,0:T(8,128)(2,1)S(1)}, bf16[512,128]{1,0:T(8,128)(2,1)S(1)}, u32[]{:S(2)}, u32[]{:S(2)}) collective-permute-start(bf16[512,128]{1,0:T(8,128)(2,1)S(1)} %get-tuple-element.80), channel_id=1, source_target_pairs={{0,24},{4,28},{8,16},{12,20},{16,8},{20,12},{24,0},{28,4},{1,25},{... | collective-permute-start | bytes 393224 | tf_op jit(solution)/shard_map/ppermute | solution.py:494
  40.8 29.1 %collective-permute-start.26 = (bf16[432,256]{1,0:T(8,128)(2,1)S(1)}, bf16[432,256]{1,0:T(8,128)(2,1)S(1)}, u32[]{:S(2)}, u32[]{:S(2)}) collective-permute-start(bf16[432,256]{1,0:T(8,128)(2,1)S(1)} %pack_rows.1.refs_0_), channel_id=1, source_target_pairs={{0,16},{4,20},{8,24},{12,28},{16,0},{20,4},{24,8},{28,12},{1,17},{... | collective-permute-start | bytes 663560 | tf_op jit(solution)/shard_map/ppermute | solution.py:540
  43.0 14.1 %collective-permute-start.44 = (bf16[512,128]{1,0:T(8,128)(2,1)S(1)}, bf16[512,128]{1,0:T(8,128)(2,1)S(1)}, u32[]{:S(2)}, u32[]{:S(2)}) collective-permute-start(bf16[512,128]{1,0:T(8,128)(2,1)S(1)} %get-tuple-element.128), channel_id=1, source_target_pairs={{0,2},{1,3},{2,0},{3,1},{4,6},{5,7},{6,4},{7,5},{8,10},{9,11},{10,... | collective-permute-start | bytes 393224 | tf_op jit(solution)/shard_map/ppermute | solution.py:495
  46.1 15.5 %collective-permute-start.46 = (bf16[512,128]{1,0:T(8,128)(2,1)S(1)}, bf16[512,128]{1,0:T(8,128)(2,1)S(1)}, u32[]{:S(2)}, u32[]{:S(2)}) collective-permute-start(bf16[512,128]{1,0:T(8,128)(2,1)S(1)} %get-tuple-element.130), channel_id=1, source_target_pairs={{0,3},{1,0},{2,1},{3,2},{4,7},{5,4},{6,5},{7,6},{8,11},{9,8},{10,9... | collective-permute-start | bytes 393224 | tf_op jit(solution)/shard_map/ppermute | solution.py:495
  53.9 15.8 %collective-permute-start.45 = (bf16[512,128]{1,0:T(8,128)(2,1)S(1)}, bf16[512,128]{1,0:T(8,128)(2,1)S(1)}, u32[]{:S(2)}, u32[]{:S(2)}) collective-permute-start(bf16[512,128]{1,0:T(8,128)(2,1)S(1)} %get-tuple-element.129), channel_id=1, source_target_pairs={{0,2},{1,3},{2,0},{3,1},{4,6},{5,7},{6,4},{7,5},{8,10},{9,11},{10,... | collective-permute-start | bytes 393224 | tf_op jit(solution)/shard_map/ppermute | solution.py:495
  61.7 29.5 %collective-permute-start.24 = (bf16[432,256]{1,0:T(8,128)(2,1)S(1)}, bf16[432,256]{1,0:T(8,128)(2,1)S(1)}, u32[]{:S(2)}, u32[]{:S(2)}) collective-permute-start(bf16[432,256]{1,0:T(8,128)(2,1)S(1)} %pack_rows.1.refs_0_), channel_id=1, source_target_pairs={{0,8},{4,12},{8,0},{12,4},{16,24},{20,28},{24,16},{28,20},{1,9},{5... | collective-permute-start | bytes 663560 | tf_op jit(solution)/shard_map/ppermute | solution.py:540
  69.7 13.8 %collective-permute-start.41 = (bf16[512,128]{1,0:T(8,128)(2,1)S(1)}, bf16[512,128]{1,0:T(8,128)(2,1)S(1)}, u32[]{:S(2)}, u32[]{:S(2)}) collective-permute-start(bf16[512,128]{1,0:T(8,128)(2,1)S(1)} %get-tuple-element.123), channel_id=1, source_target_pairs={{0,3},{1,0},{2,1},{3,2},{4,7},{5,4},{6,5},{7,6},{8,11},{9,8},{10,9... | collective-permute-start | bytes 393224 | tf_op jit(solution)/shard_map/ppermute | solution.py:495
  69.9 21.8 %collective-permute-start.28 = (bf16[432,256]{1,0:T(8,128)(2,1)S(1)}, bf16[432,256]{1,0:T(8,128)(2,1)S(1)}, u32[]{:S(2)}, u32[]{:S(2)}) collective-permute-start(bf16[432,256]{1,0:T(8,128)(2,1)S(1)} %collective-permute-done.26.refs_4_), channel_id=1, source_target_pairs={{0,8},{4,12},{8,0},{12,4},{16,24},{20,28},{24,16},{28,20},{1,9},{5... | collective-permute-start | bytes 663560 | tf_op jit(solution)/shard_map/ppermute | solution.py:540
  86.4 20.3 %collective-permute-start.23 = (bf16[432,256]{1,0:T(8,128)(2,1)S(1)}, bf16[432,256]{1,0:T(8,128)(2,1)S(1)}, u32[]{:S(2)}, u32[]{:S(2)}) collective-permute-start(bf16[432,256]{1,0:T(8,128)(2,1)S(1)} %pack_rows.1.refs_0_), channel_id=1, source_target_pairs={{0,4},{4,0},{8,12},{12,8},{16,20},{20,16},{24,28},{28,24},{1,5},{5... | collective-permute-start | bytes 663560 | tf_op jit(solution)/shard_map/ppermute | solution.py:540
  91.2 15.5 %collective-permute-start.27 = (bf16[432,256]{1,0:T(8,128)(2,1)S(1)}, bf16[432,256]{1,0:T(8,128)(2,1)S(1)}, u32[]{:S(2)}, u32[]{:S(2)}) collective-permute-start(bf16[432,256]{1,0:T(8,128)(2,1)S(1)} %collective-permute-done.26.refs_4_), channel_id=1, source_target_pairs={{0,4},{4,0},{8,12},{12,8},{16,20},{20,16},{24,28},{28,24},{1,5},{5... | collective-permute-start | bytes 663560 | tf_op jit(solution)/shard_map/ppermute | solution.py:540
  91.2 16.1 %collective-permute-start.25 = (bf16[432,256]{1,0:T(8,128)(2,1)S(1)}, bf16[432,256]{1,0:T(8,128)(2,1)S(1)}, u32[]{:S(2)}, u32[]{:S(2)}) collective-permute-start(bf16[432,256]{1,0:T(8,128)(2,1)S(1)} %collective-permute-done.24.refs_2_), channel_id=1, source_target_pairs={{0,4},{4,0},{8,12},{12,8},{16,20},{20,16},{24,28},{28,24},{1,5},{5... | collective-permute-start | bytes 663560 | tf_op jit(solution)/shard_map/ppermute | solution.py:540
  91.7 18.9 %collective-permute-start.29 = (bf16[432,256]{1,0:T(8,128)(2,1)S(1)}, bf16[432,256]{1,0:T(8,128)(2,1)S(1)}, u32[]{:S(2)}, u32[]{:S(2)}) collective-permute-start(bf16[432,256]{1,0:T(8,128)(2,1)S(1)} %collective-permute-done.28.refs_6_), channel_id=1, source_target_pairs={{0,4},{4,0},{8,12},{12,8},{16,20},{20,16},{24,28},{28,24},{1,5},{5... | collective-permute-start | bytes 663560 | tf_op jit(solution)/shard_map/ppermute | solution.py:540
  106.7 14.6 %collective-permute-start.32 = (bf16[512,128]{1,0:T(8,128)(2,1)S(1)}, bf16[512,128]{1,0:T(8,128)(2,1)S(1)}, u32[]{:S(2)}, u32[]{:S(2)}) collective-permute-start(bf16[512,128]{1,0:T(8,128)(2,1)S(1)} %get-tuple-element.112), channel_id=1, source_target_pairs={{0,2},{1,3},{2,0},{3,1},{4,6},{5,7},{6,4},{7,5},{8,10},{9,11},{10,... | collective-permute-start | bytes 393224 | tf_op jit(solution)/shard_map/ppermute | solution.py:495
  107.3 15.7 %collective-permute-start.34 = (bf16[512,128]{1,0:T(8,128)(2,1)S(1)}, bf16[512,128]{1,0:T(8,128)(2,1)S(1)}, u32[]{:S(2)}, u32[]{:S(2)}) collective-permute-start(bf16[512,128]{1,0:T(8,128)(2,1)S(1)} %get-tuple-element.114), channel_id=1, source_target_pairs={{0,3},{1,0},{2,1},{3,2},{4,7},{5,4},{6,5},{7,6},{8,11},{9,8},{10,9... | collective-permute-start | bytes 393224 | tf_op jit(solution)/shard_map/ppermute | solution.py:495
  110.6 16.7 %collective-permute-start.15 = (bf16[512,128]{1,0:T(8,128)(2,1)S(1)}, bf16[512,128]{1,0:T(8,128)(2,1)S(1)}, u32[]{:S(2)}, u32[]{:S(2)}) collective-permute-start(bf16[512,128]{1,0:T(8,128)(2,1)S(1)} %get-tuple-element.101), channel_id=1, source_target_pairs={{0,1},{1,2},{2,3},{3,0},{4,5},{5,6},{6,7},{7,4},{8,9},{9,10},{10,1... | collective-permute-start | bytes 393224 | tf_op jit(solution)/shard_map/ppermute | solution.py:495
  115.0 20.0 %collective-permute-start.17 = (bf16[512,128]{1,0:T(8,128)(2,1)S(1)}, bf16[512,128]{1,0:T(8,128)(2,1)S(1)}, u32[]{:S(2)}, u32[]{:S(2)}) collective-permute-start(bf16[512,128]{1,0:T(8,128)(2,1)S(1)} %get-tuple-element.103), channel_id=1, source_target_pairs={{0,2},{1,3},{2,0},{3,1},{4,6},{5,7},{6,4},{7,5},{8,10},{9,11},{10,... | collective-permute-start | bytes 393224 | tf_op jit(solution)/shard_map/ppermute | solution.py:495
  115.8 27.3 %collective-permute-start.19 = (bf16[512,128]{1,0:T(8,128)(2,1)S(1)}, bf16[512,128]{1,0:T(8,128)(2,1)S(1)}, u32[]{:S(2)}, u32[]{:S(2)}) collective-permute-start(bf16[512,128]{1,0:T(8,128)(2,1)S(1)} %get-tuple-element.105), channel_id=1, source_target_pairs={{0,3},{1,0},{2,1},{3,2},{4,7},{5,4},{6,5},{7,6},{8,11},{9,8},{10,9... | collective-permute-start | bytes 393224 | tf_op jit(solution)/shard_map/ppermute | solution.py:495
  121.3 21.7 %collective-permute-start.14 = (bf16[512,128]{1,0:T(8,128)(2,1)S(1)}, bf16[512,128]{1,0:T(8,128)(2,1)S(1)}, u32[]{:S(2)}, u32[]{:S(2)}) collective-permute-start(bf16[512,128]{1,0:T(8,128)(2,1)S(1)} %get-tuple-element.100), channel_id=1, source_target_pairs={{0,1},{1,2},{2,3},{3,0},{4,5},{5,6},{6,7},{7,4},{8,9},{9,10},{10,1... | collective-permute-start | bytes 393224 | tf_op jit(solution)/shard_map/ppermute | solution.py:495
  122.9 20.8 %collective-permute-start.16 = (bf16[512,128]{1,0:T(8,128)(2,1)S(1)}, bf16[512,128]{1,0:T(8,128)(2,1)S(1)}, u32[]{:S(2)}, u32[]{:S(2)}) collective-permute-start(bf16[512,128]{1,0:T(8,128)(2,1)S(1)} %get-tuple-element.102), channel_id=1, source_target_pairs={{0,2},{1,3},{2,0},{3,1},{4,6},{5,7},{6,4},{7,5},{8,10},{9,11},{10,... | collective-permute-start | bytes 393224 | tf_op jit(solution)/shard_map/ppermute | solution.py:495
  127.3 26.9 %collective-permute-start.18 = (bf16[512,128]{1,0:T(8,128)(2,1)S(1)}, bf16[512,128]{1,0:T(8,128)(2,1)S(1)}, u32[]{:S(2)}, u32[]{:S(2)}) collective-permute-start(bf16[512,128]{1,0:T(8,128)(2,1)S(1)} %get-tuple-element.104), channel_id=1, source_target_pairs={{0,3},{1,0},{2,1},{3,2},{4,7},{5,4},{6,5},{7,6},{8,11},{9,8},{10,9... | collective-permute-start | bytes 393224 | tf_op jit(solution)/shard_map/ppermute | solution.py:495
  135.0 37.4 %collective-permute-start.60 = (bf16[512,256]{1,0:T(8,128)(2,1)S(1)}, bf16[512,256]{1,0:T(8,128)(2,1)S(1)}, u32[]{:S(2)}, u32[]{:S(2)}) collective-permute-start(bf16[512,256]{1,0:T(8,128)(2,1)S(1)} %get-tuple-element.149), channel_id=1, source_target_pairs={{0,3},{1,0},{2,1},{3,2},{4,7},{5,4},{6,5},{7,6},{8,11},{9,8},{10,9... | collective-permute-start | bytes 786440 | tf_op jit(solution)/shard_map/ppermute | solution.py:495
  143.1 31.7 %collective-permute-start.61 = (bf16[512,256]{1,0:T(8,128)(2,1)S(1)}, bf16[512,256]{1,0:T(8,128)(2,1)S(1)}, u32[]{:S(2)}, u32[]{:S(2)}) collective-permute-start(bf16[512,256]{1,0:T(8,128)(2,1)S(1)} %get-tuple-element.150), channel_id=1, source_target_pairs={{0,2},{1,3},{2,0},{3,1},{4,6},{5,7},{6,4},{7,5},{8,10},{9,11},{10,... | collective-permute-start | bytes 786440 | tf_op jit(solution)/shard_map/ppermute | solution.py:495
  143.1 33.1 %collective-permute-start.62 = (bf16[512,256]{1,0:T(8,128)(2,1)S(1)}, bf16[512,256]{1,0:T(8,128)(2,1)S(1)}, u32[]{:S(2)}, u32[]{:S(2)}) collective-permute-start(bf16[512,256]{1,0:T(8,128)(2,1)S(1)} %get-tuple-element.151), channel_id=1, source_target_pairs={{0,1},{1,2},{2,3},{3,0},{4,5},{5,6},{6,7},{7,4},{8,9},{9,10},{10,1... | collective-permute-start | bytes 786440 | tf_op jit(solution)/shard_map/ppermute | solution.py:495
  143.7 33.6 %collective-permute-start.57 = (bf16[512,256]{1,0:T(8,128)(2,1)S(1)}, bf16[512,256]{1,0:T(8,128)(2,1)S(1)}, u32[]{:S(2)}, u32[]{:S(2)}) collective-permute-start(bf16[512,256]{1,0:T(8,128)(2,1)S(1)} %get-tuple-element.145), channel_id=1, source_target_pairs={{0,3},{1,0},{2,1},{3,2},{4,7},{5,4},{6,5},{7,6},{8,11},{9,8},{10,9... | collective-permute-start | bytes 786440 | tf_op jit(solution)/shard_map/ppermute | solution.py:495
  172.4 20.6 %collective-permute-start.58 = (bf16[512,256]{1,0:T(8,128)(2,1)S(1)}, bf16[512,256]{1,0:T(8,128)(2,1)S(1)}, u32[]{:S(2)}, u32[]{:S(2)}) collective-permute-start(bf16[512,256]{1,0:T(8,128)(2,1)S(1)} %get-tuple-element.146), channel_id=1, source_target_pairs={{0,2},{1,3},{2,0},{3,1},{4,6},{5,7},{6,4},{7,5},{8,10},{9,11},{10,... | collective-permute-start | bytes 786440 | tf_op jit(solution)/shard_map/ppermute | solution.py:495
  172.4 20.6 %collective-permute-start.59 = (bf16[512,256]{1,0:T(8,128)(2,1)S(1)}, bf16[512,256]{1,0:T(8,128)(2,1)S(1)}, u32[]{:S(2)}, u32[]{:S(2)}) collective-permute-start(bf16[512,256]{1,0:T(8,128)(2,1)S(1)} %get-tuple-element.147), channel_id=1, source_target_pairs={{0,1},{1,2},{2,3},{3,0},{4,5},{5,6},{6,7},{7,4},{8,9},{9,10},{10,1... | collective-permute-start | bytes 786440 | tf_op jit(solution)/shard_map/ppermute | solution.py:495
  174.8 30.3 %collective-permute-start.54 = (bf16[512,256]{1,0:T(8,128)(2,1)S(1)}, bf16[512,256]{1,0:T(8,128)(2,1)S(1)}, u32[]{:S(2)}, u32[]{:S(2)}) collective-permute-start(bf16[512,256]{1,0:T(8,128)(2,1)S(1)} %get-tuple-element.141), channel_id=1, source_target_pairs={{0,3},{1,0},{2,1},{3,2},{4,7},{5,4},{6,5},{7,6},{8,11},{9,8},{10,9... | collective-permute-start | bytes 786440 | tf_op jit(solution)/shard_map/ppermute | solution.py:495
  176.2 49.1 %collective-permute-start.55 = (bf16[512,256]{1,0:T(8,128)(2,1)S(1)}, bf16[512,256]{1,0:T(8,128)(2,1)S(1)}, u32[]{:S(2)}, u32[]{:S(2)}) collective-permute-start(bf16[512,256]{1,0:T(8,128)(2,1)S(1)} %get-tuple-element.142), channel_id=1, source_target_pairs={{0,2},{1,3},{2,0},{3,1},{4,6},{5,7},{6,4},{7,5},{8,10},{9,11},{10,... | collective-permute-start | bytes 786440 | tf_op jit(solution)/shard_map/ppermute | solution.py:495
  177.3 48.0 %collective-permute-start.56 = (bf16[512,256]{1,0:T(8,128)(2,1)S(1)}, bf16[512,256]{1,0:T(8,128)(2,1)S(1)}, u32[]{:S(2)}, u32[]{:S(2)}) collective-permute-start(bf16[512,256]{1,0:T(8,128)(2,1)S(1)} %get-tuple-element.143), channel_id=1, source_target_pairs={{0,1},{1,2},{2,3},{3,0},{4,5},{5,6},{6,7},{7,4},{8,9},{9,10},{10,1... | collective-permute-start | bytes 786440 | tf_op jit(solution)/shard_map/ppermute | solution.py:495
  193.0 43.5 %collective-permute-start.48 = (bf16[512,256]{1,0:T(8,128)(2,1)S(1)}, bf16[512,256]{1,0:T(8,128)(2,1)S(1)}, u32[]{:S(2)}, u32[]{:S(2)}) collective-permute-start(bf16[512,256]{1,0:T(8,128)(2,1)S(1)} %get-tuple-element.136), channel_id=1, source_target_pairs={{0,3},{1,0},{2,1},{3,2},{4,7},{5,4},{6,5},{7,6},{8,11},{9,8},{10,9... | collective-permute-start | bytes 786440 | tf_op jit(solution)/shard_map/ppermute | solution.py:495
  193.0 43.5 %collective-permute-start.49 = (bf16[512,256]{1,0:T(8,128)(2,1)S(1)}, bf16[512,256]{1,0:T(8,128)(2,1)S(1)}, u32[]{:S(2)}, u32[]{:S(2)}) collective-permute-start(bf16[512,256]{1,0:T(8,128)(2,1)S(1)} %get-tuple-element.137), channel_id=1, source_target_pairs={{0,2},{1,3},{2,0},{3,1},{4,6},{5,7},{6,4},{7,5},{8,10},{9,11},{10,... | collective-permute-start | bytes 786440 | tf_op jit(solution)/shard_map/ppermute | solution.py:495
  205.1 31.5 %collective-permute-start.50 = (bf16[512,256]{1,0:T(8,128)(2,1)S(1)}, bf16[512,256]{1,0:T(8,128)(2,1)S(1)}, u32[]{:S(2)}, u32[]{:S(2)}) collective-permute-start(bf16[512,256]{1,0:T(8,128)(2,1)S(1)} %get-tuple-element.138), channel_id=1, source_target_pairs={{0,1},{1,2},{2,3},{3,0},{4,5},{5,6},{6,7},{7,4},{8,9},{9,10},{10,1... | collective-permute-start | bytes 786440 | tf_op jit(solution)/shard_map/ppermute | solution.py:495
  (37 other events, 351.5 us)

commit v6 on v5

--- a/solution.py
+++ b/solution.py
@@ -18,6 +18,10 @@
 
 def cost(flops, nbytes):
     return pl.CostEstimate(flops=int(flops), bytes_accessed=int(nbytes), transcendentals=0)
+
+
+def partner(c, k, n):
+    return c ^ abs(k) if n & (n - 1) == 0 else (c + k + n) % n
 
 
 def in_hbm(x):
@@ -184,7 +188,7 @@
 
 
 def row_tile_of(k, n_col, per_dest, tile):
-    return lax.rem(lax.axis_index("col") + k, n_col) * per_dest + tile
+    return partner(lax.axis_index("col"), k, n_col) * per_dest + tile
 
 
 def block_shape(vals, n_col, per_dest, base, size):
@@ -337,7 +341,7 @@
     block = min(width, part)
     for s in range(n_col):
         for b in range(width // block):
-            row = lax.rem(lax.axis_index("col") + n_col - s, n_col) * width + b * block
+            row = partner(lax.axis_index("col"), -s, n_col) * width + b * block
             row = pl.multiple_of(row, block)
             at = pl.ds(s * width + b * block, block)
             joined[0, at, :] = own[pl.ds(row, block), :]
@@ -424,7 +428,7 @@
     rows = pieces[0].shape[0]
     stores = []
     for k in range(n_col):
-        dest = lax.rem(lax.axis_index("col") + k, n_col)
+        dest = partner(lax.axis_index("col"), k, n_col)
         at = pl.ds(pl.multiple_of((dest * per_dest + base) * TILE, TILE), rows)
         stores.append(pltpu.make_async_copy(pieces[k], out.at[at], put.at[k]))
     for store in stores:
@@ -465,10 +469,21 @@
 
 
 def chunk_plan(per_dest):
-    if per_dest % 4:
+    if per_dest < 16:
         return [(0, per_dest)]
-    u = per_dest // 4
-    return [(0, u), (u, u), (2 * u, u), (3 * u, u)]
+    cuts = [per_dest * c // 16 for c in (0, 3, 7, 13, 16)]
+    return [(a, b - a) for a, b in zip(cuts, cuts[1:])]
+
+
+def sharers(n_dom, channels):
+    share = 1
+    while share < 8 and n_dom % (2 * share) == 0 and channels % (2 * share * PAD) == 0:
+        share *= 2
+    return share
+
+
+def swap_stages(share):
+    return [1 << b for b in reversed(range(share.bit_length() - 1))]
 
 
 def on_device(
@@ -487,15 +502,15 @@
     n_rows, width = features.shape
     n_dom, n_col = lax.axis_size("dom"), lax.axis_size("col")
 
-    if n_dom & (n_dom - 1) == 0:
-        peer = lambda d, k: d ^ abs(k)
-    else:
-        peer = lambda d, k: (d + k + n_dom) % n_dom
+    peer = lambda d, k: partner(d, k, n_dom)
     along_dom = lambda x, k: lax.ppermute(x, "dom", [(i, peer(i, k)) for i in range(n_dom)])
-    along_col = lambda x, k: lax.ppermute(x, "col", [(i, (i + k) % n_col) for i in range(n_col)])
+    along_col = lambda x, k: lax.ppermute(
+        x, "col", [(i, partner(i, k, n_col)) for i in range(n_col)]
+    )
+    order = list(reversed(range(1, n_col)))
 
     far = list(reversed(range(1, n_dom)))
-    lead = far[0:3:2]
+    lead = far[:3]
     rest = [k for k in far if k not in lead]
     rows, first_row, within = storage_order(send_rows[0])
     slots = send_rows.shape[2]
@@ -523,22 +538,16 @@
         halo.append(pieces)
         own_tiles.append(tiles)
 
-    share = 1
-    channels = n_col * width
-    while share < 8 and n_dom % (2 * share) == 0 and channels % (2 * share * PAD) == 0:
-        share *= 2
-    order = sorted(range(1, n_col), key=lambda k: min(k, n_col - k), reverse=True)
+    share = sharers(n_dom, n_col * width)
     bias_row = out_bias.reshape(1, width)
     mine = weight_part(weight, bias_row, share)
     arrived = {k: along_col(mine, k) for k in order}
     parts = [pack_rows([arrived[k] for k in range(1, n_col)])]
-    step = share // 2
     got = {0: parts[0]}
-    while step:
+    for step in swap_stages(share):
         swap = [(i, i ^ step) for i in range(n_dom)]
         for flip in list(got):
             got[flip ^ step] = lax.ppermute(got[flip], "dom", swap)
-        step //= 2
     weights, bias = join_weights(weight, bias_row, [got[f] for f in range(share)], n_col)
 
     index_tables = (local_index[0].T, local_count[0], halo_index[0].T, halo_count[0])

time: 239 us -> 259 us (1.084)
  starting transfers between devices: 105 us -> 122 us
  waiting for transfers between devices: 71.1 us -> 77.3 us
  blocking collectives: 11.9 us -> 9.14 us
    ppermute x42, starting transfers between devices: 88.6 us -> 104 us  [on_device(): lax.ppermute(x, 'col', [(i, partner(i, k, n_col)) for i in range(n_col)])]
    ppermute x14, waiting for transfers between devices: 4.47 us -> 8.66 us  [on_device(): lax.ppermute(x, 'dom', [(i, peer(i, k)) for i in range(n_dom)])]
    all_gather x1, blocking collectives: 11.9 us -> 9.14 us  [on_device(): over_dom = lax.all_gather(stats, 'dom', axis=0)]
  transfers between devices with their start and end apart: 63 -> 63, of which waited for: 19 -> 24; matrix products, arithmetic and copies ran while one was open for 0% -> 0% of each run, Pallas kernels for 18% -> 16%
where the time goes in v6:
time: 259 us
  starting transfers between devices  122 us (47%)
  waiting for transfers between devices  77.3 us (30%)
  Pallas kernels  49.5 us (19%)
  blocking collectives  9.14 us (4%)
    ppermute x42, starting transfers between devices, on_device(): lax.ppermute(x, 'col', [(i, partner(i, k, n_col)) for i in range(n_col)])  104 us
    ppermute x42, waiting for transfers between devices, on_device(): lax.ppermute(x, 'col', [(i, partner(i, k, n_col)) for i in range(n_col)])  68.6 us
    pallas_call x8, Pallas kernels, tile_sums(): pl.pallas_call(functools.partial(sum_kernel, n_col, slots, per_dest, base...  21.1 us
    ppermute x14, starting transfers between devices, on_device(): lax.ppermute(x, 'dom', [(i, peer(i, k)) for i in range(n_dom)])  14.2 us
    pallas_call x3, Pallas kernels, gather_rows(): pl.pallas_call(functools.partial(gather_kernel, peers, peer, first_row, w...  11.8 us
    pallas_call x4, Pallas kernels, mix_rows(): pl.pallas_call(functools.partial(mix_kernel, n_col, len(pieces), channels...  10.4 us
    all_gather x1, blocking collectives, on_device(): over_dom = lax.all_gather(stats, 'dom', axis=0)  9.14 us
    ppermute x14, waiting for transfers between devices, on_device(): lax.ppermute(x, 'dom', [(i, peer(i, k)) for i in range(n_dom)])  8.66 us
  transfers between devices with their start and end apart: 63, of which 24 were waited for; matrix products, arithmetic and copies ran while one was open for 0% of the time, Pallas kernels for 16%

profile of v6, /device:TPU:0, one launch (start us, length us, event | category | flops | bytes accessed | tf_op | source)
XLA Modules:
  0.0 258.8 jit_solution(6506807212899874167)
XLA Ops:
  0.6 2.6 %gather_rows.3 = (bf16[512,128]{1,0:T(8,128)(2,1)S(1)}, bf16[512,128]{1,0:T(8,128)(2,1)S(1)}, bf16[512,128]{1,0:T(8,128)(2,1)S(1)}, f32[8192,128]{1,0:T(8,128)S(1)}, bf16[8192,128]{1,0:T(8,128)(2,1)S(1)}) custom-call(s32[4096]{0:T(1024)} %bitcast.58, s32[8]{0:T(128)} %bitcast.61, bf16[8192,256]{1,0:T(8,128)(2,1)} %refs_0_.3), custom_call_target="tpu_custom_call" | custom-call | flops 4000000000 | bytes 6291456 | tf_op jit(solution)/shard_map/gather_rows/pallas_call | solution.py:147
  3.3 2.9 %gather_rows.4 = (bf16[512,128]{1,0:T(8,128)(2,1)S(1)}, bf16[512,128]{1,0:T(8,128)(2,1)S(1)}, bf16[512,128]{1,0:T(8,128)(2,1)S(1)}, bf16[512,128]{1,0:T(8,128)(2,1)S(1)}, bf16[4,2,3,4,128,128]{5,4,3,2,1,0:T(8,128)(2,1)S(1)}) custom-call(s32[4096]{0:T(1024)} %bitcast.59, s32[8]{0:T(128)} %bitcast.62, f32[8192,128]{1,0:T(8,128)S(1)} %get-tuple-element.81.refs_0_, ...), custom_call_target="tpu_custom_call" | custom-call | flops 4000000000 | bytes 6291456 | tf_op jit(solution)/shard_map/gather_rows/pallas_call | solution.py:147
  6.2 3.3 %collective-permute-start.3 = (bf16[512,128]{1,0:T(8,128)(2,1)S(1)}, bf16[512,128]{1,0:T(8,128)(2,1)S(1)}, u32[]{:S(2)}, u32[]{:S(2)}) collective-permute-start(bf16[512,128]{1,0:T(8,128)(2,1)S(1)} %get-tuple-element.82), channel_id=1, source_target_pairs={{0,16},{4,20},{8,24},{12,28},{16,0},{20,4},{24,8},{28,12},{1,17},{... | collective-permute-start | bytes 393224 | tf_op jit(solution)/shard_map/ppermute | solution.py:506
  12.1 2.6 %collective-permute-start.21 = (bf16[144,256]{1,0:T(8,128)(2,1)S(1)}, bf16[144,256]{1,0:T(8,128)(2,1)S(1)}, u32[]{:S(2)}, u32[]{:S(2)}) collective-permute-start(bf16[144,256]{1,0:T(8,128)(2,1)S(1)} %weight_part.1), channel_id=1, source_target_pairs={{0,2},{1,3},{2,0},{3,1},{4,6},{5,7},{6,4},{7,5},{8,10},{9,11},{10,... | collective-permute-start | bytes 221192 | tf_op jit(solution)/shard_map/ppermute | solution.py:507
  16.7 2.8 %collective-permute-done.21.refs_1_ = bf16[144,256]{1,0:T(8,128)(2,1)S(1)} collective-permute-done((bf16[144,256]{1,0:T(8,128)(2,1)S(1)}, bf16[144,256]{1,0:T(8,128)(2,1)S(1)}, u32[]{:S(2)}, u32[]{:S(2)}) %collective-permute-start.21) | collective-permute-done | bytes 73760 | tf_op jit(solution)/shard_map/ppermute | solution.py:507
  24.6 6.3 %gather_rows.5 = (bf16[512,128]{1,0:T(8,128)(2,1)S(1)}, bf16[512,128]{1,0:T(8,128)(2,1)S(1)}, bf16[512,128]{1,0:T(8,128)(2,1)S(1)}, bf16[512,128]{1,0:T(8,128)(2...) custom-call(s32[4096]{0:T(1024)} %bitcast.60, ...), custom_call_target="tpu_custom_call" | custom-call | flops 4000000000 | bytes 6291456 | tf_op jit(solution)/shard_map/gather_rows/pallas_call | solution.py:147
  38.7 2.8 %tile_sums.8 = (bf16[384,128]{1,0:T(8,128)(2,1)S(1)}, bf16[384,128]{1,0:T(8,128)(2,1)S(1)}, bf16[384,128]{1,0:T(8,128)(2,1)S(1)}, bf16[384,128]{1,0:T(8,128)(2,1)S(1)}, bf16[4,2,4,4,128,128]{5,4,3,2,1,0:T(8,128)(2,1)S(1)}) custom-call(s32[4,64]{1,0:T(4,128)S(1)} %bitcast.18, s32[64]{0:T(128)S(1)} %bitcast.34, s32[4,64]{1,0:T(4,128)S(1)} %bitcast.26, ...), custom_call_target="tpu_custom_call" | custom-call | flops 2000000000 | bytes 6291456 | tf_op jit(solution)/shard_map/tile_sums/pallas_call | solution.py:269
  43.8 3.0 %collective-permute-done.8.refs_1_ = bf16[512,128]{1,0:T(8,128)(2,1)S(1)} collective-permute-done((bf16[512,128]{1,0:T(8,128)(2,1)S(1)}, bf16[512,128]{1,0:T(8,128)(2,1)S(1)}, u32[]{:S(2)}, u32[]{:S(2)}) %collective-permute-start.8) | collective-permute-done | bytes 131104 | tf_op jit(solution)/shard_map/ppermute | solution.py:506
  46.8 2.8 %collective-permute-done.9.refs_2_ = bf16[512,128]{1,0:T(8,128)(2,1)S(1)} collective-permute-done((bf16[512,128]{1,0:T(8,128)(2,1)S(1)}, bf16[512,128]{1,0:T(8,128)(2,1)S(1)}, u32[]{:S(2)}, u32[]{:S(2)}) %collective-permute-start.9) | collective-permute-done | bytes 131104 | tf_op jit(solution)/shard_map/ppermute | solution.py:506
  54.0 3.5 %tile_sums.9 = (bf16[512,128]{1,0:T(8,128)(2,1)S(1)}, bf16[512,128]{1,0:T(8,128)(2,1)S(1)}, bf16[512,128]{1,0:T(8,128)(2,1)S(1)}, bf16[512,128]{1,0:T(8,128)(2,1)S(1)}, bf16[4,2,6,4,128,128]{5,4,3,2,1,0:T(8,128)(2,1)S(1)}) custom-call(s32[4,64]{1,0:T(4,128)S(1)} %bitcast.21, s32[64]{0:T(128)S(1)} %bitcast.37, s32[4,64]{1,0:T(4,128)S(1)} %bitcast.29, ...), custom_call_target="tpu_custom_call" | custom-call | flops 2000000000 | bytes 6291456 | tf_op jit(solution)/shard_map/tile_sums/pallas_call | solution.py:269
  62.5 3.3 %tile_sums.10 = (bf16[768,128]{1,0:T(8,128)(2,1)S(1)}, bf16[768,128]{1,0:T(8,128)(2,1)S(1)}, bf16[768,128]{1,0:T(8,128)(2,1)S(1)}, bf16[768,128]{1,0:T(8,128)(2,1)S(1)}, bf16[4,2,3,4,128,128]{5,4,3,2,1,0:T(8,128)(2,1)S(1)}) custom-call(s32[4,64]{1,0:T(4,128)S(1)} %bitcast.22, s32[64]{0:T(128)S(1)} %bitcast.38, s32[4,64]{1,0:T(4,128)S(1)} %bitcast.30, ...), custom_call_target="tpu_custom_call" | custom-call | flops 2000000000 | bytes 6291456 | tf_op jit(solution)/shard_map/tile_sums/pallas_call | solution.py:269
  71.6 3.6 %collective-permute-start.37 = (bf16[512,128]{1,0:T(8,128)(2,1)S(1)}, bf16[512,128]{1,0:T(8,128)(2,1)S(1)}, u32[]{:S(2)}, u32[]{:S(2)}) collective-permute-start(bf16[512,128]{1,0:T(8,128)(2,1)S(1)} %get-tuple-element.119), channel_id=1, source_target_pairs={{0,1},{1,0},{2,3},{3,2},{4,5},{5,4},{6,7},{7,6},{8,9},{9,8},{10,11... | collective-permute-start | bytes 393224 | tf_op jit(solution)/shard_map/ppermute | solution.py:507
  82.0 6.4 %collective-permute-done.15.refs_3_ = bf16[384,128]{1,0:T(8,128)(2,1)S(1)} collective-permute-done((bf16[384,128]{1,0:T(8,128)(2,1)S(1)}, bf16[384,128]{1,0:T(8,128)(2,1)S(1)}, u32[]{:S(2)}, u32[]{:S(2)}) %collective-permute-start.15) | collective-permute-done | bytes 98336 | tf_op jit(solution)/shard_map/ppermute | solution.py:507
  88.4 3.1 %collective-permute-start.41 = (bf16[512,128]{1,0:T(8,128)(2,1)S(1)}, bf16[512,128]{1,0:T(8,128)(2,1)S(1)}, u32[]{:S(2)}, u32[]{:S(2)}) collective-permute-start(bf16[512,128]{1,0:T(8,128)(2,1)S(1)} %get-tuple-element.123), channel_id=1, source_target_pairs={{0,3},{1,2},{2,1},{3,0},{4,7},{5,6},{6,5},{7,4},{8,11},{9,10},{10,... | collective-permute-start | bytes 393224 | tf_op jit(solution)/shard_map/ppermute | solution.py:507
  92.8 2.4 collective-permute-done.41.refs_7_
  100.7 3.3 %tile_sums.13 = (bf16[768,128]{1,0:T(8,128)(2,1)S(1)}, bf16[768,128]{1,0:T(8,128)(2,1)S(1)}, bf16[768,128]{1,0:T(8,128)(2,1)S(1)}, bf16[768,128]{1,0:T(8,128)(2,1)S(1)}) custom-call(s32[4,64]{1,0:T(4,128)S(1)} %bitcast.24, s32[64]{0:T(128)S(1)} %bitcast.40, s32[4,64]{1,0:T(4,128)S(1)} %bitcast.32, s32[64]{0:T(128)S(1)} %bitcast.48, ...), custom_call_target="tpu_custom_call" | custom-call | flops 2000000000 | bytes 6291456 | tf_op jit(solution)/shard_map/tile_sums/pallas_call | solution.py:269
  108.9 4.2 %collective-permute-done.31.refs_3_ = bf16[768,128]{1,0:T(8,128)(2,1)S(1)} collective-permute-done((bf16[768,128]{1,0:T(8,128)(2,1)S(1)}, bf16[768,128]{1,0:T(8,128)(2,1)S(1)}, u32[]{:S(2)}, u32[]{:S(2)}) %collective-permute-start.31) | collective-permute-done | bytes 196640 | tf_op jit(solution)/shard_map/ppermute | solution.py:507
  114.8 2.7 %collective-permute-start.32 = (bf16[768,128]{1,0:T(8,128)(2,1)S(1)}, bf16[768,128]{1,0:T(8,128)(2,1)S(1)}, u32[]{:S(2)}, u32[]{:S(2)}) collective-permute-start(bf16[768,128]{1,0:T(8,128)(2,1)S(1)} %get-tuple-element.112), channel_id=1, source_target_pairs={{0,2},{1,3},{2,0},{3,1},{4,6},{5,7},{6,4},{7,5},{8,10},{9,11},{10,... | collective-permute-start | bytes 589832 | tf_op jit(solution)/shard_map/ppermute | solution.py:507
  121.8 2.6 %mix_rows.5 = (bf16[512,256]{1,0:T(8,128)(2,1)S(1)}, bf16[512,256]{1,0:T(8,128)(2,1)S(1)}, bf16[512,256]{1,0:T(8,128)(2,1)S(1)}, bf16[512,256]{1,0:T(8,128)(2,1)S(1)}, f32[8,256]{1,0:T(8,128)S(1)}) custom-call(bf16[512,128]{1,0:T(8,128)(2,1)S(1)} %get-tuple-element.116.refs_0_, bf16[512,128]{1,0:T(8,128)(2,1)S(1)} %get-tuple-element.117.refs_1_, ...), custom_call_target="tpu_custom_call" | custom-call | flops 1073741824 | bytes 4194304 | tf_op jit(solution)/shard_map/mix_rows/pallas_call | solution.py:410
  127.0 15.8 %collective-permute-start.14 = (bf16[384,128]{1,0:T(8,128)(2,1)S(1)}, bf16[384,128]{1,0:T(8,128)(2,1)S(1)}, u32[]{:S(2)}, u32[]{:S(2)}) collective-permute-start(bf16[384,128]{1,0:T(8,128)(2,1)S(1)} %get-tuple-element.100), channel_id=1, source_target_pairs={{0,1},{1,0},{2,3},{3,2},{4,5},{5,4},{6,7},{7,6},{8,9},{9,8},{10,11... | collective-permute-start | bytes 294920 | tf_op jit(solution)/shard_map/ppermute | solution.py:507
  142.7 2.4 collective-permute-done.32.refs_4_
  147.3 3.8 %mix_rows.6 = (bf16[768,256]{1,0:T(8,128)(2,1)S(1)}, bf16[768,256]{1,0:T(8,128)(2,1)S(1)}, bf16[768,256]{1,0:T(8,128)(2,1)S(1)}, bf16[768,256]{1,0:T(8,128)(2,1)S(1)}, f32[8,256]{1,0:T(8,128)S(1)}) custom-call(bf16[768,128]{1,0:T(8,128)(2,1)S(1)} %get-tuple-element.108.refs_0_, bf16[768,128]{1,0:T(8,128)(2,1)S(1)} %get-tuple-element.109.refs_1_, ...), custom_call_target="tpu_custom_call" | custom-call | flops 1610612736 | bytes 4194304 | tf_op jit(solution)/shard_map/mix_rows/pallas_call | solution.py:410
  151.2 4.5 %collective-permute-done.17.refs_5_ = bf16[384,128]{1,0:T(8,128)(2,1)S(1)} collective-permute-done((bf16[384,128]{1,0:T(8,128)(2,1)S(1)}, bf16[384,128]{1,0:T(8,128)(2,1)S(1)}, u32[]{:S(2)}, u32[]{:S(2)}) %collective-permute-start.17) | collective-permute-done | bytes 98336 | tf_op jit(solution)/shard_map/ppermute | solution.py:507
  155.7 3.7 %collective-permute-start.60 = (bf16[384,256]{1,0:T(8,128)(2,1)S(1)}, bf16[384,256]{1,0:T(8,128)(2,1)S(1)}, u32[]{:S(2)}, u32[]{:S(2)}) collective-permute-start(bf16[384,256]{1,0:T(8,128)(2,1)S(1)} %get-tuple-element.149), channel_id=1, source_target_pairs={{0,1},{1,0},{2,3},{3,2},{4,5},{5,4},{6,7},{7,6},{8,9},{9,8},{10,11... | collective-permute-start | bytes 589832 | tf_op jit(solution)/shard_map/ppermute | solution.py:507
  165.3 9.1 %all-gather = f32[64,256]{1,0:T(8,128)S(1)} all-gather(f32[8,256]{1,0:T(8,128)S(1)} %get-tuple-element.139), channel_id=2, replica_groups=mesh['dom'=8,'col'=4] {'dom'}, dimensions={0}, use_global_device_ids=true | all-gather | bytes 73728 | tf_op jit(solution)/shard_map/all_gather | solution.py:574
  174.5 3.4 %collective-permute-start.51 = (f32[2,256]{1,0:T(2,128)S(1)}, f32[2,256]{1,0:T(2,128)S(1)}, u32[]{:S(2)}, u32[]{:S(2)}) collective-permute-start(f32[2,256]{1,0:T(2,128)S(1)} %get-tuple-element.154), channel_id=1, source_target_pairs={{0,1},{1,0},{2,3},{3,2},{4,5},{5,4},{6,7},{7,6},{8,9},{9,8},{10,11... | collective-permute-start | bytes 6152 | tf_op jit(solution)/shard_map/ppermute | solution.py:507
  187.3 9.3 %collective-permute-done.58.refs_2_ = bf16[512,256]{1,0:T(8,128)(2,1)S(1)} collective-permute-done((bf16[512,256]{1,0:T(8,128)(2,1)S(1)}, bf16[512,256]{1,0:T(8,128)(2,1)S(1)}, u32[]{:S(2)}, u32[]{:S(2)}) %collective-permute-start.58) | collective-permute-done | bytes 262176 | tf_op jit(solution)/shard_map/ppermute | solution.py:507
  196.6 3.1 %collective-permute-start.48 = (bf16[384,256]{1,0:T(8,128)(2,1)S(1)}, bf16[384,256]{1,0:T(8,128)(2,1)S(1)}, u32[]{:S(2)}, u32[]{:S(2)}) collective-permute-start(bf16[384,256]{1,0:T(8,128)(2,1)S(1)} %get-tuple-element.136), channel_id=1, source_target_pairs={{0,1},{1,0},{2,3},{3,2},{4,5},{5,4},{6,7},{7,6},{8,9},{9,8},{10,11... | collective-permute-start | bytes 589832 | tf_op jit(solution)/shard_map/ppermute | solution.py:507
  199.7 5.1 %collective-permute-done.59.refs_3_ = bf16[512,256]{1,0:T(8,128)(2,1)S(1)} collective-permute-done((bf16[512,256]{1,0:T(8,128)(2,1)S(1)}, bf16[512,256]{1,0:T(8,128)(2,1)S(1)}, u32[]{:S(2)}, u32[]{:S(2)}) %collective-permute-start.59) | collective-permute-done | bytes 262176 | tf_op jit(solution)/shard_map/ppermute | solution.py:507
  204.8 25.8 %collective-permute-start.49 = (bf16[384,256]{1,0:T(8,128)(2,1)S(1)}, bf16[384,256]{1,0:T(8,128)(2,1)S(1)}, u32[]{:S(2)}, u32[]{:S(2)}) collective-permute-start(bf16[384,256]{1,0:T(8,128)(2,1)S(1)} %get-tuple-element.137), channel_id=1, source_target_pairs={{0,2},{1,3},{2,0},{3,1},{4,6},{5,7},{6,4},{7,5},{8,10},{9,11},{10,... | collective-permute-start | bytes 589832 | tf_op jit(solution)/shard_map/ppermute | solution.py:507
  234.3 7.8 %collective-permute-done.55.refs_2_ = bf16[768,256]{1,0:T(8,128)(2,1)S(1)} collective-permute-done((bf16[768,256]{1,0:T(8,128)(2,1)S(1)}, bf16[768,256]{1,0:T(8,128)(2,1)S(1)}, u32[]{:S(2)}, u32[]{:S(2)}) %collective-permute-start.55) | collective-permute-done | bytes 393248 | tf_op jit(solution)/shard_map/ppermute | solution.py:507
  245.4 11.7 %collective-permute-done.52.refs_6_ = f32[2,256]{1,0:T(2,128)S(1)} collective-permute-done((f32[2,256]{1,0:T(2,128)S(1)}, f32[2,256]{1,0:T(2,128)S(1)}, u32[]{:S(2)}, u32[]{:S(2)}) %collective-permute-start.52) | collective-permute-done | bytes 2080 | tf_op jit(solution)/shard_map/ppermute | solution.py:507
  (134 shorter events, 87.7 us)
Async XLA Ops:
  6.2 16.4 %collective-permute-start.3 = (bf16[512,128]{1,0:T(8,128)(2,1)S(1)}, bf16[512,128]{1,0:T(8,128)(2,1)S(1)}, u32[]{:S(2)}, u32[]{:S(2)}) collective-permute-start(bf16[512,128]{1,0:T(8,128)(2,1)S(1)} %get-tuple-element.82), channel_id=1, source_target_pairs={{0,16},{4,20},{8,24},{12,28},{16,0},{20,4},{24,8},{28,12},{1,17},{... | collective-permute-start | bytes 393224 | tf_op jit(solution)/shard_map/ppermute | solution.py:506
  9.5 14.6 %collective-permute-start.4 = (bf16[512,128]{1,0:T(8,128)(2,1)S(1)}, bf16[512,128]{1,0:T(8,128)(2,1)S(1)}, u32[]{:S(2)}, u32[]{:S(2)}) collective-permute-start(bf16[512,128]{1,0:T(8,128)(2,1)S(1)} %get-tuple-element.83), channel_id=1, source_target_pairs={{0,12},{4,8},{8,4},{12,0},{16,28},{20,24},{24,20},{28,16},{1,13},{... | collective-permute-start | bytes 393224 | tf_op jit(solution)/shard_map/ppermute | solution.py:506
  15.2 15.7 %collective-permute-start.5 = (bf16[512,128]{1,0:T(8,128)(2,1)S(1)}, bf16[512,128]{1,0:T(8,128)(2,1)S(1)}, u32[]{:S(2)}, u32[]{:S(2)}) collective-permute-start(bf16[512,128]{1,0:T(8,128)(2,1)S(1)} %get-tuple-element.84), channel_id=1, source_target_pairs={{0,8},{4,12},{8,0},{12,4},{16,24},{20,28},{24,16},{28,20},{1,9},{5... | collective-permute-start | bytes 393224 | tf_op jit(solution)/shard_map/ppermute | solution.py:506
  41.5 39.4 %collective-permute-start.26 = (bf16[432,256]{1,0:T(8,128)(2,1)S(1)}, bf16[432,256]{1,0:T(8,128)(2,1)S(1)}, u32[]{:S(2)}, u32[]{:S(2)}) collective-permute-start(bf16[432,256]{1,0:T(8,128)(2,1)S(1)} %pack_rows.1.refs_0_), channel_id=1, source_target_pairs={{0,16},{4,20},{8,24},{12,28},{16,0},{20,4},{24,8},{28,12},{1,17},{... | collective-permute-start | bytes 663560 | tf_op jit(solution)/shard_map/ppermute | solution.py:550
  71.6 19.9 %collective-permute-start.37 = (bf16[512,128]{1,0:T(8,128)(2,1)S(1)}, bf16[512,128]{1,0:T(8,128)(2,1)S(1)}, u32[]{:S(2)}, u32[]{:S(2)}) collective-permute-start(bf16[512,128]{1,0:T(8,128)(2,1)S(1)} %get-tuple-element.119), channel_id=1, source_target_pairs={{0,1},{1,0},{2,3},{3,2},{4,5},{5,4},{6,7},{7,6},{8,9},{9,8},{10,11... | collective-permute-start | bytes 393224 | tf_op jit(solution)/shard_map/ppermute | solution.py:507
  75.3 16.3 %collective-permute-start.39 = (bf16[512,128]{1,0:T(8,128)(2,1)S(1)}, bf16[512,128]{1,0:T(8,128)(2,1)S(1)}, u32[]{:S(2)}, u32[]{:S(2)}) collective-permute-start(bf16[512,128]{1,0:T(8,128)(2,1)S(1)} %get-tuple-element.121), channel_id=1, source_target_pairs={{0,2},{1,3},{2,0},{3,1},{4,6},{5,7},{6,4},{7,5},{8,10},{9,11},{10,... | collective-permute-start | bytes 393224 | tf_op jit(solution)/shard_map/ppermute | solution.py:507
  80.0 20.2 %collective-permute-start.24 = (bf16[432,256]{1,0:T(8,128)(2,1)S(1)}, bf16[432,256]{1,0:T(8,128)(2,1)S(1)}, u32[]{:S(2)}, u32[]{:S(2)}) collective-permute-start(bf16[432,256]{1,0:T(8,128)(2,1)S(1)} %pack_rows.1.refs_0_), channel_id=1, source_target_pairs={{0,8},{4,12},{8,0},{12,4},{16,24},{20,28},{24,16},{28,20},{1,9},{5... | collective-permute-start | bytes 663560 | tf_op jit(solution)/shard_map/ppermute | solution.py:550
  80.9 19.7 %collective-permute-start.28 = (bf16[432,256]{1,0:T(8,128)(2,1)S(1)}, bf16[432,256]{1,0:T(8,128)(2,1)S(1)}, u32[]{:S(2)}, u32[]{:S(2)}) collective-permute-start(bf16[432,256]{1,0:T(8,128)(2,1)S(1)} %collective-permute-done.26.refs_4_), channel_id=1, source_target_pairs={{0,8},{4,12},{8,0},{12,4},{16,24},{20,28},{24,16},{28,20},{1,9},{5... | collective-permute-start | bytes 663560 | tf_op jit(solution)/shard_map/ppermute | solution.py:550
  100.2 14.6 %collective-permute-start.27 = (bf16[432,256]{1,0:T(8,128)(2,1)S(1)}, bf16[432,256]{1,0:T(8,128)(2,1)S(1)}, u32[]{:S(2)}, u32[]{:S(2)}) collective-permute-start(bf16[432,256]{1,0:T(8,128)(2,1)S(1)} %collective-permute-done.26.refs_4_), channel_id=1, source_target_pairs={{0,4},{4,0},{8,12},{12,8},{16,20},{20,16},{24,28},{28,24},{1,5},{5... | collective-permute-start | bytes 663560 | tf_op jit(solution)/shard_map/ppermute | solution.py:550
  100.7 16.8 %collective-permute-start.29 = (bf16[432,256]{1,0:T(8,128)(2,1)S(1)}, bf16[432,256]{1,0:T(8,128)(2,1)S(1)}, u32[]{:S(2)}, u32[]{:S(2)}) collective-permute-start(bf16[432,256]{1,0:T(8,128)(2,1)S(1)} %collective-permute-done.28.refs_6_), channel_id=1, source_target_pairs={{0,4},{4,0},{8,12},{12,8},{16,20},{20,16},{24,28},{28,24},{1,5},{5... | collective-permute-start | bytes 663560 | tf_op jit(solution)/shard_map/ppermute | solution.py:550
  107.0 17.5 %collective-permute-start.33 = (bf16[768,128]{1,0:T(8,128)(2,1)S(1)}, bf16[768,128]{1,0:T(8,128)(2,1)S(1)}, u32[]{:S(2)}, u32[]{:S(2)}) collective-permute-start(bf16[768,128]{1,0:T(8,128)(2,1)S(1)} %get-tuple-element.113), channel_id=1, source_target_pairs={{0,2},{1,3},{2,0},{3,1},{4,6},{5,7},{6,4},{7,5},{8,10},{9,11},{10,... | collective-permute-start | bytes 589832 | tf_op jit(solution)/shard_map/ppermute | solution.py:507
  114.8 30.4 %collective-permute-start.32 = (bf16[768,128]{1,0:T(8,128)(2,1)S(1)}, bf16[768,128]{1,0:T(8,128)(2,1)S(1)}, u32[]{:S(2)}, u32[]{:S(2)}) collective-permute-start(bf16[768,128]{1,0:T(8,128)(2,1)S(1)} %get-tuple-element.112), channel_id=1, source_target_pairs={{0,2},{1,3},{2,0},{3,1},{4,6},{5,7},{6,4},{7,5},{8,10},{9,11},{10,... | collective-permute-start | bytes 589832 | tf_op jit(solution)/shard_map/ppermute | solution.py:507
  117.5 27.6 %collective-permute-start.34 = (bf16[768,128]{1,0:T(8,128)(2,1)S(1)}, bf16[768,128]{1,0:T(8,128)(2,1)S(1)}, u32[]{:S(2)}, u32[]{:S(2)}) collective-permute-start(bf16[768,128]{1,0:T(8,128)(2,1)S(1)} %get-tuple-element.114), channel_id=1, source_target_pairs={{0,3},{1,2},{2,1},{3,0},{4,7},{5,6},{6,5},{7,4},{8,11},{9,10},{10,... | collective-permute-start | bytes 589832 | tf_op jit(solution)/shard_map/ppermute | solution.py:507
  124.4 31.2 %collective-permute-start.17 = (bf16[384,128]{1,0:T(8,128)(2,1)S(1)}, bf16[384,128]{1,0:T(8,128)(2,1)S(1)}, u32[]{:S(2)}, u32[]{:S(2)}) collective-permute-start(bf16[384,128]{1,0:T(8,128)(2,1)S(1)} %get-tuple-element.103), channel_id=1, source_target_pairs={{0,2},{1,3},{2,0},{3,1},{4,6},{5,7},{6,4},{7,5},{8,10},{9,11},{10,... | collective-permute-start | bytes 294920 | tf_op jit(solution)/shard_map/ppermute | solution.py:507
  124.5 34.8 %collective-permute-start.19 = (bf16[384,128]{1,0:T(8,128)(2,1)S(1)}, bf16[384,128]{1,0:T(8,128)(2,1)S(1)}, u32[]{:S(2)}, u32[]{:S(2)}) collective-permute-start(bf16[384,128]{1,0:T(8,128)(2,1)S(1)} %get-tuple-element.105), channel_id=1, source_target_pairs={{0,3},{1,2},{2,1},{3,0},{4,7},{5,6},{6,5},{7,4},{8,11},{9,10},{10,... | collective-permute-start | bytes 294920 | tf_op jit(solution)/shard_map/ppermute | solution.py:507
  127.0 32.7 %collective-permute-start.14 = (bf16[384,128]{1,0:T(8,128)(2,1)S(1)}, bf16[384,128]{1,0:T(8,128)(2,1)S(1)}, u32[]{:S(2)}, u32[]{:S(2)}) collective-permute-start(bf16[384,128]{1,0:T(8,128)(2,1)S(1)} %get-tuple-element.100), channel_id=1, source_target_pairs={{0,1},{1,0},{2,3},{3,2},{4,5},{5,4},{6,7},{7,6},{8,9},{9,8},{10,11... | collective-permute-start | bytes 294920 | tf_op jit(solution)/shard_map/ppermute | solution.py:507
  145.1 18.2 %collective-permute-start.16 = (bf16[384,128]{1,0:T(8,128)(2,1)S(1)}, bf16[384,128]{1,0:T(8,128)(2,1)S(1)}, u32[]{:S(2)}, u32[]{:S(2)}) collective-permute-start(bf16[384,128]{1,0:T(8,128)(2,1)S(1)} %get-tuple-element.102), channel_id=1, source_target_pairs={{0,2},{1,3},{2,0},{3,1},{4,6},{5,7},{6,4},{7,5},{8,10},{9,11},{10,... | collective-permute-start | bytes 294920 | tf_op jit(solution)/shard_map/ppermute | solution.py:507
  145.1 18.2 %collective-permute-start.18 = (bf16[384,128]{1,0:T(8,128)(2,1)S(1)}, bf16[384,128]{1,0:T(8,128)(2,1)S(1)}, u32[]{:S(2)}, u32[]{:S(2)}) collective-permute-start(bf16[384,128]{1,0:T(8,128)(2,1)S(1)} %get-tuple-element.104), channel_id=1, source_target_pairs={{0,3},{1,2},{2,1},{3,0},{4,7},{5,6},{6,5},{7,4},{8,11},{9,10},{10,... | collective-permute-start | bytes 294920 | tf_op jit(solution)/shard_map/ppermute | solution.py:507
  155.7 25.8 %collective-permute-start.60 = (bf16[384,256]{1,0:T(8,128)(2,1)S(1)}, bf16[384,256]{1,0:T(8,128)(2,1)S(1)}, u32[]{:S(2)}, u32[]{:S(2)}) collective-permute-start(bf16[384,256]{1,0:T(8,128)(2,1)S(1)} %get-tuple-element.149), channel_id=1, source_target_pairs={{0,1},{1,0},{2,3},{3,2},{4,5},{5,4},{6,7},{7,6},{8,9},{9,8},{10,11... | collective-permute-start | bytes 589832 | tf_op jit(solution)/shard_map/ppermute | solution.py:507
  159.3 22.7 %collective-permute-start.61 = (bf16[384,256]{1,0:T(8,128)(2,1)S(1)}, bf16[384,256]{1,0:T(8,128)(2,1)S(1)}, u32[]{:S(2)}, u32[]{:S(2)}) collective-permute-start(bf16[384,256]{1,0:T(8,128)(2,1)S(1)} %get-tuple-element.150), channel_id=1, source_target_pairs={{0,2},{1,3},{2,0},{3,1},{4,6},{5,7},{6,4},{7,5},{8,10},{9,11},{10,... | collective-permute-start | bytes 589832 | tf_op jit(solution)/shard_map/ppermute | solution.py:507
  159.6 24.2 %collective-permute-start.62 = (bf16[384,256]{1,0:T(8,128)(2,1)S(1)}, bf16[384,256]{1,0:T(8,128)(2,1)S(1)}, u32[]{:S(2)}, u32[]{:S(2)}) collective-permute-start(bf16[384,256]{1,0:T(8,128)(2,1)S(1)} %get-tuple-element.151), channel_id=1, source_target_pairs={{0,3},{1,2},{2,1},{3,0},{4,7},{5,6},{6,5},{7,4},{8,11},{9,10},{10,... | collective-permute-start | bytes 589832 | tf_op jit(solution)/shard_map/ppermute | solution.py:507
  163.3 22.2 %collective-permute-start.57 = (bf16[512,256]{1,0:T(8,128)(2,1)S(1)}, bf16[512,256]{1,0:T(8,128)(2,1)S(1)}, u32[]{:S(2)}, u32[]{:S(2)}) collective-permute-start(bf16[512,256]{1,0:T(8,128)(2,1)S(1)} %get-tuple-element.145), channel_id=1, source_target_pairs={{0,1},{1,0},{2,3},{3,2},{4,5},{5,4},{6,7},{7,6},{8,9},{9,8},{10,11... | collective-permute-start | bytes 786440 | tf_op jit(solution)/shard_map/ppermute | solution.py:507
  179.4 51.2 %collective-permute-start.54 = (bf16[768,256]{1,0:T(8,128)(2,1)S(1)}, bf16[768,256]{1,0:T(8,128)(2,1)S(1)}, u32[]{:S(2)}, u32[]{:S(2)}) collective-permute-start(bf16[768,256]{1,0:T(8,128)(2,1)S(1)} %get-tuple-element.141), channel_id=1, source_target_pairs={{0,1},{1,0},{2,3},{3,2},{4,5},{5,4},{6,7},{7,6},{8,9},{9,8},{10,11... | collective-permute-start | bytes 1179656 | tf_op jit(solution)/shard_map/ppermute | solution.py:507
  181.4 15.2 %collective-permute-start.58 = (bf16[512,256]{1,0:T(8,128)(2,1)S(1)}, bf16[512,256]{1,0:T(8,128)(2,1)S(1)}, u32[]{:S(2)}, u32[]{:S(2)}) collective-permute-start(bf16[512,256]{1,0:T(8,128)(2,1)S(1)} %get-tuple-element.146), channel_id=1, source_target_pairs={{0,2},{1,3},{2,0},{3,1},{4,6},{5,7},{6,4},{7,5},{8,10},{9,11},{10,... | collective-permute-start | bytes 786440 | tf_op jit(solution)/shard_map/ppermute | solution.py:507
  182.0 22.8 %collective-permute-start.59 = (bf16[512,256]{1,0:T(8,128)(2,1)S(1)}, bf16[512,256]{1,0:T(8,128)(2,1)S(1)}, u32[]{:S(2)}, u32[]{:S(2)}) collective-permute-start(bf16[512,256]{1,0:T(8,128)(2,1)S(1)} %get-tuple-element.147), channel_id=1, source_target_pairs={{0,3},{1,2},{2,1},{3,0},{4,7},{5,6},{6,5},{7,4},{8,11},{9,10},{10,... | collective-permute-start | bytes 786440 | tf_op jit(solution)/shard_map/ppermute | solution.py:507
  183.8 58.3 %collective-permute-start.55 = (bf16[768,256]{1,0:T(8,128)(2,1)S(1)}, bf16[768,256]{1,0:T(8,128)(2,1)S(1)}, u32[]{:S(2)}, u32[]{:S(2)}) collective-permute-start(bf16[768,256]{1,0:T(8,128)(2,1)S(1)} %get-tuple-element.142), channel_id=1, source_target_pairs={{0,2},{1,3},{2,0},{3,1},{4,6},{5,7},{6,4},{7,5},{8,10},{9,11},{10,... | collective-permute-start | bytes 1179656 | tf_op jit(solution)/shard_map/ppermute | solution.py:507
  185.5 56.6 %collective-permute-start.56 = (bf16[768,256]{1,0:T(8,128)(2,1)S(1)}, bf16[768,256]{1,0:T(8,128)(2,1)S(1)}, u32[]{:S(2)}, u32[]{:S(2)}) collective-permute-start(bf16[768,256]{1,0:T(8,128)(2,1)S(1)} %get-tuple-element.143), channel_id=1, source_target_pairs={{0,3},{1,2},{2,1},{3,0},{4,7},{5,6},{6,5},{7,4},{8,11},{9,10},{10,... | collective-permute-start | bytes 1179656 | tf_op jit(solution)/shard_map/ppermute | solution.py:507
  196.6 60.5 %collective-permute-start.48 = (bf16[384,256]{1,0:T(8,128)(2,1)S(1)}, bf16[384,256]{1,0:T(8,128)(2,1)S(1)}, u32[]{:S(2)}, u32[]{:S(2)}) collective-permute-start(bf16[384,256]{1,0:T(8,128)(2,1)S(1)} %get-tuple-element.136), channel_id=1, source_target_pairs={{0,1},{1,0},{2,3},{3,2},{4,5},{5,4},{6,7},{7,6},{8,9},{9,8},{10,11... | collective-permute-start | bytes 589832 | tf_op jit(solution)/shard_map/ppermute | solution.py:507
  204.8 52.3 %collective-permute-start.49 = (bf16[384,256]{1,0:T(8,128)(2,1)S(1)}, bf16[384,256]{1,0:T(8,128)(2,1)S(1)}, u32[]{:S(2)}, u32[]{:S(2)}) collective-permute-start(bf16[384,256]{1,0:T(8,128)(2,1)S(1)} %get-tuple-element.137), channel_id=1, source_target_pairs={{0,2},{1,3},{2,0},{3,1},{4,6},{5,7},{6,4},{7,5},{8,10},{9,11},{10,... | collective-permute-start | bytes 589832 | tf_op jit(solution)/shard_map/ppermute | solution.py:507
  230.6 26.5 %collective-permute-start.50 = (bf16[384,256]{1,0:T(8,128)(2,1)S(1)}, bf16[384,256]{1,0:T(8,128)(2,1)S(1)}, u32[]{:S(2)}, u32[]{:S(2)}) collective-permute-start(bf16[384,256]{1,0:T(8,128)(2,1)S(1)} %get-tuple-element.138), channel_id=1, source_target_pairs={{0,3},{1,2},{2,1},{3,0},{4,7},{5,6},{6,5},{7,4},{8,11},{9,10},{10,... | collective-permute-start | bytes 589832 | tf_op jit(solution)/shard_map/ppermute | solution.py:507
  242.1 15.0 %collective-permute-start.52 = (f32[2,256]{1,0:T(2,128)S(1)}, f32[2,256]{1,0:T(2,128)S(1)}, u32[]{:S(2)}, u32[]{:S(2)}) collective-permute-start(f32[2,256]{1,0:T(2,128)S(1)} %get-tuple-element.153), channel_id=1, source_target_pairs={{0,2},{1,3},{2,0},{3,1},{4,6},{5,7},{6,4},{7,5},{8,10},{9,11},{10,... | collective-permute-start | bytes 6152 | tf_op jit(solution)/shard_map/ppermute | solution.py:507
  242.1 15.0 %collective-permute-start.53 = (f32[2,256]{1,0:T(2,128)S(1)}, f32[2,256]{1,0:T(2,128)S(1)}, u32[]{:S(2)}, u32[]{:S(2)}) collective-permute-start(f32[2,256]{1,0:T(2,128)S(1)} %get-tuple-element.152), channel_id=1, source_target_pairs={{0,3},{1,2},{2,1},{3,0},{4,7},{5,6},{6,5},{7,4},{8,11},{9,10},{10,... | collective-permute-start | bytes 6152 | tf_op jit(solution)/shard_map/ppermute | solution.py:507
  (37 other events, 345.3 us)

commit v7 on v6

--- a/solution.py
+++ b/solution.py
@@ -289,28 +289,39 @@
 PAD = 16
 
 
-def part_kernel(share, weight, bias, out, sem):
+def part_kernel(share, ahead, weight, bias, *refs):
+    if ahead:
+        out, block, sem, sems = refs[2:]
+        loads = block_copies(refs[:2], block, sems, *ahead)
+    else:
+        (out, sem), loads = refs, []
     part = weight.shape[0] // share
     start = lax.rem(lax.axis_index("dom"), share) * part
     src = weight.at[pl.ds(pl.multiple_of(start, part), part)]
     copy = pltpu.make_async_copy(src, out.at[pl.ds(0, part)], sem)
     copy.start()
+    for load in loads:
+        load.start()
     out[pl.ds(part, PAD), :] = jnp.broadcast_to(bias[...], (PAD, out.shape[1]))
     copy.wait()
-
-
-def weight_part(weight, bias, share):
+    for load in loads:
+        load.wait()
+
+
+def weight_part(weight, bias, share, vals, ahead):
     rows = weight.shape[0] // share + PAD
+    made = [block_shape(vals[0], *ahead)] if ahead else []
     return pl.pallas_call(
-        functools.partial(part_kernel, share),
-        out_shape=jax.ShapeDtypeStruct((rows, weight.shape[1]), weight.dtype),
-        in_specs=[RAW, VMEM],
-        out_specs=VMEM,
-        scratch_shapes=[pltpu.SemaphoreType.DMA],
-        compiler_params=grant(4),
+        functools.partial(part_kernel, share, ahead),
+        out_shape=[jax.ShapeDtypeStruct((rows, weight.shape[1]), weight.dtype)] + made,
+        in_specs=[RAW, VMEM] + [RAW] * (2 * len(made)),
+        out_specs=[VMEM] * (1 + len(made)),
+        scratch_shapes=[pltpu.SemaphoreType.DMA]
+        + [pltpu.SemaphoreType.DMA((2 * cols[0],)) for cols in [ahead] if ahead],
+        compiler_params=grant(8),
         cost_estimate=cost(1e8, 1 << 20),
         name="weight_part",
-    )(in_hbm(weight), bias)
+    )(in_hbm(weight), bias, *([in_hbm(v) for v in vals] * len(made)))
 
 
 def pack_kernel(*refs):
@@ -540,7 +551,10 @@
 
     share = sharers(n_dom, n_col * width)
     bias_row = out_bias.reshape(1, width)
-    mine = weight_part(weight, bias_row, share)
+    mine, *block = weight_part(
+        weight, bias_row, share, vals, ahead[1] if len(plan) > 1 else ()
+    )
+    blocks += block
     arrived = {k: along_col(mine, k) for k in order}
     parts = [pack_rows([arrived[k] for k in range(1, n_col)])]
     got = {0: parts[0]}
@@ -555,7 +569,7 @@
     for h in range(halves):
         received = assemble(far, [halo[h][k] for k in far], n_dom, peer)
         for g, (base, size) in enumerate(plan):
-            load = ahead[g + 1] if h == 0 and g + 1 < len(plan) else ()
+            load = ahead[g + 1] if h == 0 < g < len(plan) - 1 else ()
             sums, block = tile_sums(
                 index_tables, received, own_tiles[h], blocks[g], vals, per_dest, base, load
             )

time: 259 us -> 252 us (0.973)
  waiting for transfers between devices: 77.3 us -> 58.4 us
  starting transfers between devices: 122 us -> 133 us
    ppermute x42, waiting for transfers between devices: 68.6 us -> 55.4 us  [on_device(): lax.ppermute(x, 'col', [(i, partner(i, k, n_col)) for i in range(n_col)])]
    ppermute x42, starting transfers between devices: 104 us -> 114 us  [on_device(): lax.ppermute(x, 'col', [(i, partner(i, k, n_col)) for i in range(n_col)])]
    ppermute x14, waiting for transfers between devices: 8.66 us -> 2.99 us  [on_device(): lax.ppermute(x, 'dom', [(i, peer(i, k)) for i in range(n_dom)])]
  transfers between devices with their start and end apart: 63 -> 63, of which waited for: 24 -> 19; matrix products, arithmetic and copies ran while one was open for 0% -> 0% of each run, Pallas kernels for 16% -> 17%
where the time goes in v7:
time: 252 us
  starting transfers between devices  133 us (53%)
  waiting for transfers between devices  58.4 us (23%)
  Pallas kernels  50 us (20%)
  blocking collectives  9.38 us (4%)
    ppermute x42, starting transfers between devices, on_device(): lax.ppermute(x, 'col', [(i, partner(i, k, n_col)) for i in range(n_col)])  114 us
    ppermute x42, waiting for transfers between devices, on_device(): lax.ppermute(x, 'col', [(i, partner(i, k, n_col)) for i in range(n_col)])  55.4 us
    pallas_call x8, Pallas kernels, tile_sums(): pl.pallas_call(functools.partial(sum_kernel, n_col, slots, per_dest, base...  20.2 us
    ppermute x14, starting transfers between devices, on_device(): lax.ppermute(x, 'dom', [(i, peer(i, k)) for i in range(n_dom)])  14.2 us
    pallas_call x3, Pallas kernels, gather_rows(): pl.pallas_call(functools.partial(gather_kernel, peers, peer, first_row, w...  11.8 us
    pallas_call x4, Pallas kernels, mix_rows(): pl.pallas_call(functools.partial(mix_kernel, n_col, len(pieces), channels...  10.4 us
    all_gather x1, blocking collectives, on_device(): over_dom = lax.all_gather(stats, 'dom', axis=0)  9.38 us
  transfers between devices with their start and end apart: 63, of which 19 were waited for; matrix products, arithmetic and copies ran while one was open for 0% of the time, Pallas kernels for 17%

profile of v7, /device:TPU:0, one launch (start us, length us, event | category | flops | bytes accessed | tf_op | source)
XLA Modules:
  0.0 252.2 jit_solution(4291770373365812476)
XLA Ops:
  0.6 2.6 %gather_rows.3 = (bf16[512,128]{1,0:T(8,128)(2,1)S(1)}, bf16[512,128]{1,0:T(8,128)(2,1)S(1)}, bf16[512,128]{1,0:T(8,128)(2,1)S(1)}, f32[8192,128]{1,0:T(8,128)S(1)}, bf16[8192,128]{1,0:T(8,128)(2,1)S(1)}) custom-call(s32[4096]{0:T(1024)} %bitcast.58, s32[8]{0:T(128)} %bitcast.61, bf16[8192,256]{1,0:T(8,128)(2,1)} %refs_0_.3), custom_call_target="tpu_custom_call" | custom-call | flops 4000000000 | bytes 6291456 | tf_op jit(solution)/shard_map/gather_rows/pallas_call | solution.py:147
  3.3 2.9 %gather_rows.4 = (bf16[512,128]{1,0:T(8,128)(2,1)S(1)}, bf16[512,128]{1,0:T(8,128)(2,1)S(1)}, bf16[512,128]{1,0:T(8,128)(2,1)S(1)}, bf16[512,128]{1,0:T(8,128)(2,1)S(1)}, bf16[4,2,3,4,128,128]{5,4,3,2,1,0:T(8,128)(2,1)S(1)}) custom-call(s32[4096]{0:T(1024)} %bitcast.59, s32[8]{0:T(128)} %bitcast.62, f32[8192,128]{1,0:T(8,128)S(1)} %get-tuple-element.82.refs_0_, ...), custom_call_target="tpu_custom_call" | custom-call | flops 4000000000 | bytes 6291456 | tf_op jit(solution)/shard_map/gather_rows/pallas_call | solution.py:147
  6.2 3.3 %collective-permute-start.3 = (bf16[512,128]{1,0:T(8,128)(2,1)S(1)}, bf16[512,128]{1,0:T(8,128)(2,1)S(1)}, u32[]{:S(2)}, u32[]{:S(2)}) collective-permute-start(bf16[512,128]{1,0:T(8,128)(2,1)S(1)} %get-tuple-element.83), channel_id=1, source_target_pairs={{0,16},{4,20},{8,24},{12,28},{16,0},{20,4},{24,8},{28,12},{1,17},{... | collective-permute-start | bytes 393224 | tf_op jit(solution)/shard_map/ppermute | solution.py:517
  13.5 2.6 %collective-permute-start.21 = (bf16[144,256]{1,0:T(8,128)(2,1)S(1)}, bf16[144,256]{1,0:T(8,128)(2,1)S(1)}, u32[]{:S(2)}, u32[]{:S(2)}) collective-permute-start(bf16[144,256]{1,0:T(8,128)(2,1)S(1)} %get-tuple-element.106), channel_id=1, source_target_pairs={{0,2},{1,3},{2,0},{3,1},{4,6},{5,7},{6,4},{7,5},{8,10},{9,11},{10,... | collective-permute-start | bytes 221192 | tf_op jit(solution)/shard_map/ppermute | solution.py:518
  18.1 2.8 %collective-permute-done.21.refs_1_ = bf16[144,256]{1,0:T(8,128)(2,1)S(1)} collective-permute-done((bf16[144,256]{1,0:T(8,128)(2,1)S(1)}, bf16[144,256]{1,0:T(8,128)(2,1)S(1)}, u32[]{:S(2)}, u32[]{:S(2)}) %collective-permute-start.21) | collective-permute-done | bytes 73760 | tf_op jit(solution)/shard_map/ppermute | solution.py:518
  26.0 6.3 %gather_rows.5 = (bf16[512,128]{1,0:T(8,128)(2,1)S(1)}, bf16[512,128]{1,0:T(8,128)(2,1)S(1)}, bf16[512,128]{1,0:T(8,128)(2,1)S(1)}, bf16[512,128]{1,0:T(8,128)(2...) custom-call(s32[4096]{0:T(1024)} %bitcast.60, ...), custom_call_target="tpu_custom_call" | custom-call | flops 4000000000 | bytes 6291456 | tf_op jit(solution)/shard_map/gather_rows/pallas_call | solution.py:147
  45.2 2.4 collective-permute-start.44
  54.5 3.5 %tile_sums.8 = (bf16[512,128]{1,0:T(8,128)(2,1)S(1)}, bf16[512,128]{1,0:T(8,128)(2,1)S(1)}, bf16[512,128]{1,0:T(8,128)(2,1)S(1)}, bf16[512,128]{1,0:T(8,128)(2,1)S(1)}, bf16[4,2,6,4,128,128]{5,4,3,2,1,0:T(8,128)(2,1)S(1)}) custom-call(s32[4,64]{1,0:T(4,128)S(1)} %bitcast.20, s32[64]{0:T(128)S(1)} %bitcast.36, s32[4,64]{1,0:T(4,128)S(1)} %bitcast.28, ...), custom_call_target="tpu_custom_call" | custom-call | flops 2000000000 | bytes 6291456 | tf_op jit(solution)/shard_map/tile_sums/pallas_call | solution.py:269
  58.0 3.4 %tile_sums.9 = (bf16[768,128]{1,0:T(8,128)(2,1)S(1)}, bf16[768,128]{1,0:T(8,128)(2,1)S(1)}, bf16[768,128]{1,0:T(8,128)(2,1)S(1)}, bf16[768,128]{1,0:T(8,128)(2,1)S(1)}, bf16[4,2,3,4,128,128]{5,4,3,2,1,0:T(8,128)(2,1)S(1)}) custom-call(s32[4,64]{1,0:T(4,128)S(1)} %bitcast.21, s32[64]{0:T(128)S(1)} %bitcast.37, s32[4,64]{1,0:T(4,128)S(1)} %bitcast.29, ...), custom_call_target="tpu_custom_call" | custom-call | flops 2000000000 | bytes 6291456 | tf_op jit(solution)/shard_map/tile_sums/pallas_call | solution.py:269
  67.6 3.6 %collective-permute-done.45.refs_5_ = bf16[384,128]{1,0:T(8,128)(2,1)S(1)} collective-permute-done((bf16[384,128]{1,0:T(8,128)(2,1)S(1)}, bf16[384,128]{1,0:T(8,128)(2,1)S(1)}, u32[]{:S(2)}, u32[]{:S(2)}) %collective-permute-start.45) | collective-permute-done | bytes 98336 | tf_op jit(solution)/shard_map/ppermute | solution.py:518
  71.2 2.8 %collective-permute-start.15 = (bf16[384,128]{1,0:T(8,128)(2,1)S(1)}, bf16[384,128]{1,0:T(8,128)(2,1)S(1)}, u32[]{:S(2)}, u32[]{:S(2)}) collective-permute-start(bf16[384,128]{1,0:T(8,128)(2,1)S(1)} %get-tuple-element.101), channel_id=1, source_target_pairs={{0,1},{1,0},{2,3},{3,2},{4,5},{5,4},{6,7},{7,6},{8,9},{9,8},{10,11... | collective-permute-start | bytes 294920 | tf_op jit(solution)/shard_map/ppermute | solution.py:518
  75.6 2.4 tile_sums.13
  78.0 5.0 %collective-permute-start.40 = (bf16[512,128]{1,0:T(8,128)(2,1)S(1)}, bf16[512,128]{1,0:T(8,128)(2,1)S(1)}, u32[]{:S(2)}, u32[]{:S(2)}) collective-permute-start(bf16[512,128]{1,0:T(8,128)(2,1)S(1)} %get-tuple-element.123), channel_id=1, source_target_pairs={{0,3},{1,2},{2,1},{3,0},{4,7},{5,6},{6,5},{7,4},{8,11},{9,10},{10,... | collective-permute-start | bytes 393224 | tf_op jit(solution)/shard_map/ppermute | solution.py:518
  83.6 3.8 %collective-permute-done.40.refs_6_ = bf16[512,128]{1,0:T(8,128)(2,1)S(1)} collective-permute-done((bf16[512,128]{1,0:T(8,128)(2,1)S(1)}, bf16[512,128]{1,0:T(8,128)(2,1)S(1)}, u32[]{:S(2)}, u32[]{:S(2)}) %collective-permute-start.40) | collective-permute-done | bytes 131104 | tf_op jit(solution)/shard_map/ppermute | solution.py:518
  87.4 4.2 %collective-permute-done.37.refs_3_ = bf16[512,128]{1,0:T(8,128)(2,1)S(1)} collective-permute-done((bf16[512,128]{1,0:T(8,128)(2,1)S(1)}, bf16[512,128]{1,0:T(8,128)(2,1)S(1)}, u32[]{:S(2)}, u32[]{:S(2)}) %collective-permute-start.37) | collective-permute-done | bytes 131104 | tf_op jit(solution)/shard_map/ppermute | solution.py:518
  94.2 3.3 %tile_sums.12 = (bf16[768,128]{1,0:T(8,128)(2,1)S(1)}, bf16[768,128]{1,0:T(8,128)(2,1)S(1)}, bf16[768,128]{1,0:T(8,128)(2,1)S(1)}, bf16[768,128]{1,0:T(8,128)(2,1)S(1)}) custom-call(s32[4,64]{1,0:T(4,128)S(1)} %bitcast.24, s32[64]{0:T(128)S(1)} %bitcast.40, s32[4,64]{1,0:T(4,128)S(1)} %bitcast.32, s32[64]{0:T(128)S(1)} %bitcast.48, ...), custom_call_target="tpu_custom_call" | custom-call | flops 2000000000 | bytes 6291456 | tf_op jit(solution)/shard_map/tile_sums/pallas_call | solution.py:269
  104.9 5.4 %collective-permute-start.35 = (bf16[768,128]{1,0:T(8,128)(2,1)S(1)}, bf16[768,128]{1,0:T(8,128)(2,1)S(1)}, u32[]{:S(2)}, u32[]{:S(2)}) collective-permute-start(bf16[768,128]{1,0:T(8,128)(2,1)S(1)} %get-tuple-element.116), channel_id=1, source_target_pairs={{0,3},{1,2},{2,1},{3,0},{4,7},{5,6},{6,5},{7,4},{8,11},{9,10},{10,... | collective-permute-start | bytes 589832 | tf_op jit(solution)/shard_map/ppermute | solution.py:518
  110.8 3.8 %collective-permute-start.34 = (bf16[768,128]{1,0:T(8,128)(2,1)S(1)}, bf16[768,128]{1,0:T(8,128)(2,1)S(1)}, u32[]{:S(2)}, u32[]{:S(2)}) collective-permute-start(bf16[768,128]{1,0:T(8,128)(2,1)S(1)} %get-tuple-element.115), channel_id=1, source_target_pairs={{0,3},{1,2},{2,1},{3,0},{4,7},{5,6},{6,5},{7,4},{8,11},{9,10},{10,... | collective-permute-start | bytes 589832 | tf_op jit(solution)/shard_map/ppermute | solution.py:518
  117.3 2.6 %mix_rows.5 = (bf16[512,256]{1,0:T(8,128)(2,1)S(1)}, bf16[512,256]{1,0:T(8,128)(2,1)S(1)}, bf16[512,256]{1,0:T(8,128)(2,1)S(1)}, bf16[512,256]{1,0:T(8,128)(2,1)S(1)}, f32[8,256]{1,0:T(8,128)S(1)}) custom-call(bf16[512,128]{1,0:T(8,128)(2,1)S(1)} %get-tuple-element.117.refs_0_, bf16[512,128]{1,0:T(8,128)(2,1)S(1)} %get-tuple-element.118.refs_1_, ...), custom_call_target="tpu_custom_call" | custom-call | flops 1073741824 | bytes 4194304 | tf_op jit(solution)/shard_map/mix_rows/pallas_call | solution.py:421
  122.0 16.1 %collective-permute-start.14 = (bf16[384,128]{1,0:T(8,128)(2,1)S(1)}, bf16[384,128]{1,0:T(8,128)(2,1)S(1)}, u32[]{:S(2)}, u32[]{:S(2)}) collective-permute-start(bf16[384,128]{1,0:T(8,128)(2,1)S(1)} %get-tuple-element.100), channel_id=1, source_target_pairs={{0,1},{1,0},{2,3},{3,2},{4,5},{5,4},{6,7},{7,6},{8,9},{9,8},{10,11... | collective-permute-start | bytes 294920 | tf_op jit(solution)/shard_map/ppermute | solution.py:518
  140.2 2.5 collective-permute-start.18
  142.7 3.8 %mix_rows.6 = (bf16[768,256]{1,0:T(8,128)(2,1)S(1)}, bf16[768,256]{1,0:T(8,128)(2,1)S(1)}, bf16[768,256]{1,0:T(8,128)(2,1)S(1)}, bf16[768,256]{1,0:T(8,128)(2,1)S(1)}, f32[8,256]{1,0:T(8,128)S(1)}) custom-call(bf16[768,128]{1,0:T(8,128)(2,1)S(1)} %get-tuple-element.109.refs_0_, bf16[768,128]{1,0:T(8,128)(2,1)S(1)} %get-tuple-element.110.refs_1_, ...), custom_call_target="tpu_custom_call" | custom-call | flops 1610612736 | bytes 4194304 | tf_op jit(solution)/shard_map/mix_rows/pallas_call | solution.py:421
  146.5 4.2 %collective-permute-done.17.refs_5_ = bf16[384,128]{1,0:T(8,128)(2,1)S(1)} collective-permute-done((bf16[384,128]{1,0:T(8,128)(2,1)S(1)}, bf16[384,128]{1,0:T(8,128)(2,1)S(1)}, u32[]{:S(2)}, u32[]{:S(2)}) %collective-permute-start.17) | collective-permute-done | bytes 98336 | tf_op jit(solution)/shard_map/ppermute | solution.py:518
  150.7 4.0 %collective-permute-start.60 = (bf16[384,256]{1,0:T(8,128)(2,1)S(1)}, bf16[384,256]{1,0:T(8,128)(2,1)S(1)}, u32[]{:S(2)}, u32[]{:S(2)}) collective-permute-start(bf16[384,256]{1,0:T(8,128)(2,1)S(1)} %get-tuple-element.151), channel_id=1, source_target_pairs={{0,1},{1,0},{2,3},{3,2},{4,5},{5,4},{6,7},{7,6},{8,9},{9,8},{10,11... | collective-permute-start | bytes 589832 | tf_op jit(solution)/shard_map/ppermute | solution.py:518
  154.7 2.4 collective-permute-start.62
  160.2 9.4 %all-gather = f32[64,256]{1,0:T(8,128)S(1)} all-gather(f32[8,256]{1,0:T(8,128)S(1)} %get-tuple-element.141), channel_id=2, replica_groups=mesh['dom'=8,'col'=4] {'dom'}, dimensions={0}, use_global_device_ids=true | all-gather | bytes 73728 | tf_op jit(solution)/shard_map/all_gather | solution.py:588
  180.8 9.3 %collective-permute-done.58.refs_2_ = bf16[512,256]{1,0:T(8,128)(2,1)S(1)} collective-permute-done((bf16[512,256]{1,0:T(8,128)(2,1)S(1)}, bf16[512,256]{1,0:T(8,128)(2,1)S(1)}, u32[]{:S(2)}, u32[]{:S(2)}) %collective-permute-start.58) | collective-permute-done | bytes 262176 | tf_op jit(solution)/shard_map/ppermute | solution.py:518
  190.1 21.2 %collective-permute-start.48 = (bf16[384,256]{1,0:T(8,128)(2,1)S(1)}, bf16[384,256]{1,0:T(8,128)(2,1)S(1)}, u32[]{:S(2)}, u32[]{:S(2)}) collective-permute-start(bf16[384,256]{1,0:T(8,128)(2,1)S(1)} %get-tuple-element.138), channel_id=1, source_target_pairs={{0,1},{1,0},{2,3},{3,2},{4,5},{5,4},{6,7},{7,6},{8,9},{9,8},{10,11... | collective-permute-start | bytes 589832 | tf_op jit(solution)/shard_map/ppermute | solution.py:518
  211.3 13.4 %collective-permute-start.49 = (bf16[384,256]{1,0:T(8,128)(2,1)S(1)}, bf16[384,256]{1,0:T(8,128)(2,1)S(1)}, u32[]{:S(2)}, u32[]{:S(2)}) collective-permute-start(bf16[384,256]{1,0:T(8,128)(2,1)S(1)} %get-tuple-element.139), channel_id=1, source_target_pairs={{0,2},{1,3},{2,0},{3,1},{4,6},{5,7},{6,4},{7,5},{8,10},{9,11},{10,... | collective-permute-start | bytes 589832 | tf_op jit(solution)/shard_map/ppermute | solution.py:518
  227.8 7.8 %collective-permute-done.55.refs_2_ = bf16[768,256]{1,0:T(8,128)(2,1)S(1)} collective-permute-done((bf16[768,256]{1,0:T(8,128)(2,1)S(1)}, bf16[768,256]{1,0:T(8,128)(2,1)S(1)}, u32[]{:S(2)}, u32[]{:S(2)}) %collective-permute-start.55) | collective-permute-done | bytes 393248 | tf_op jit(solution)/shard_map/ppermute | solution.py:518
  235.6 2.7 %collective-permute-start.53 = (f32[2,256]{1,0:T(2,128)S(1)}, f32[2,256]{1,0:T(2,128)S(1)}, u32[]{:S(2)}, u32[]{:S(2)}) collective-permute-start(f32[2,256]{1,0:T(2,128)S(1)} %get-tuple-element.154), channel_id=1, source_target_pairs={{0,3},{1,2},{2,1},{3,0},{4,7},{5,6},{6,5},{7,4},{8,11},{9,10},{10,... | collective-permute-start | bytes 6152 | tf_op jit(solution)/shard_map/ppermute | solution.py:518
  239.4 11.1 %collective-permute-done.52.refs_6_ = f32[2,256]{1,0:T(2,128)S(1)} collective-permute-done((f32[2,256]{1,0:T(2,128)S(1)}, f32[2,256]{1,0:T(2,128)S(1)}, u32[]{:S(2)}, u32[]{:S(2)}) %collective-permute-start.52) | collective-permute-done | bytes 2080 | tf_op jit(solution)/shard_map/ppermute | solution.py:518
  (134 shorter events, 76.6 us)
Async XLA Ops:
  6.2 17.8 %collective-permute-start.3 = (bf16[512,128]{1,0:T(8,128)(2,1)S(1)}, bf16[512,128]{1,0:T(8,128)(2,1)S(1)}, u32[]{:S(2)}, u32[]{:S(2)}) collective-permute-start(bf16[512,128]{1,0:T(8,128)(2,1)S(1)} %get-tuple-element.83), channel_id=1, source_target_pairs={{0,16},{4,20},{8,24},{12,28},{16,0},{20,4},{24,8},{28,12},{1,17},{... | collective-permute-start | bytes 393224 | tf_op jit(solution)/shard_map/ppermute | solution.py:517
  9.5 16.0 %collective-permute-start.4 = (bf16[512,128]{1,0:T(8,128)(2,1)S(1)}, bf16[512,128]{1,0:T(8,128)(2,1)S(1)}, u32[]{:S(2)}, u32[]{:S(2)}) collective-permute-start(bf16[512,128]{1,0:T(8,128)(2,1)S(1)} %get-tuple-element.84), channel_id=1, source_target_pairs={{0,12},{4,8},{8,4},{12,0},{16,28},{20,24},{24,20},{28,16},{1,13},{... | collective-permute-start | bytes 393224 | tf_op jit(solution)/shard_map/ppermute | solution.py:517
  16.6 15.7 %collective-permute-start.5 = (bf16[512,128]{1,0:T(8,128)(2,1)S(1)}, bf16[512,128]{1,0:T(8,128)(2,1)S(1)}, u32[]{:S(2)}, u32[]{:S(2)}) collective-permute-start(bf16[512,128]{1,0:T(8,128)(2,1)S(1)} %get-tuple-element.85), channel_id=1, source_target_pairs={{0,8},{4,12},{8,0},{12,4},{16,24},{20,28},{24,16},{28,20},{1,9},{5... | collective-permute-start | bytes 393224 | tf_op jit(solution)/shard_map/ppermute | solution.py:517
  42.0 31.9 %collective-permute-start.26 = (bf16[432,256]{1,0:T(8,128)(2,1)S(1)}, bf16[432,256]{1,0:T(8,128)(2,1)S(1)}, u32[]{:S(2)}, u32[]{:S(2)}) collective-permute-start(bf16[432,256]{1,0:T(8,128)(2,1)S(1)} %pack_rows.1.refs_0_), channel_id=1, source_target_pairs={{0,16},{4,20},{8,24},{12,28},{16,0},{20,4},{24,8},{28,12},{1,17},{... | collective-permute-start | bytes 663560 | tf_op jit(solution)/shard_map/ppermute | solution.py:564
  43.3 18.1 %collective-permute-start.42 = (bf16[384,128]{1,0:T(8,128)(2,1)S(1)}, bf16[384,128]{1,0:T(8,128)(2,1)S(1)}, u32[]{:S(2)}, u32[]{:S(2)}) collective-permute-start(bf16[384,128]{1,0:T(8,128)(2,1)S(1)} %get-tuple-element.128), channel_id=1, source_target_pairs={{0,1},{1,0},{2,3},{3,2},{4,5},{5,4},{6,7},{7,6},{8,9},{9,8},{10,11... | collective-permute-start | bytes 294920 | tf_op jit(solution)/shard_map/ppermute | solution.py:518
  45.2 17.6 %collective-permute-start.44 = (bf16[384,128]{1,0:T(8,128)(2,1)S(1)}, bf16[384,128]{1,0:T(8,128)(2,1)S(1)}, u32[]{:S(2)}, u32[]{:S(2)}) collective-permute-start(bf16[384,128]{1,0:T(8,128)(2,1)S(1)} %get-tuple-element.130), channel_id=1, source_target_pairs={{0,2},{1,3},{2,0},{3,1},{4,6},{5,7},{6,4},{7,5},{8,10},{9,11},{10,... | collective-permute-start | bytes 294920 | tf_op jit(solution)/shard_map/ppermute | solution.py:518
  48.2 18.2 %collective-permute-start.46 = (bf16[384,128]{1,0:T(8,128)(2,1)S(1)}, bf16[384,128]{1,0:T(8,128)(2,1)S(1)}, u32[]{:S(2)}, u32[]{:S(2)}) collective-permute-start(bf16[384,128]{1,0:T(8,128)(2,1)S(1)} %get-tuple-element.132), channel_id=1, source_target_pairs={{0,3},{1,2},{2,1},{3,0},{4,7},{5,6},{6,5},{7,4},{8,11},{9,10},{10,... | collective-permute-start | bytes 294920 | tf_op jit(solution)/shard_map/ppermute | solution.py:518
  66.4 27.2 %collective-permute-start.24 = (bf16[432,256]{1,0:T(8,128)(2,1)S(1)}, bf16[432,256]{1,0:T(8,128)(2,1)S(1)}, u32[]{:S(2)}, u32[]{:S(2)}) collective-permute-start(bf16[432,256]{1,0:T(8,128)(2,1)S(1)} %pack_rows.1.refs_0_), channel_id=1, source_target_pairs={{0,8},{4,12},{8,0},{12,4},{16,24},{20,28},{24,16},{28,20},{1,9},{5... | collective-permute-start | bytes 663560 | tf_op jit(solution)/shard_map/ppermute | solution.py:564
  67.3 15.7 %collective-permute-start.36 = (bf16[512,128]{1,0:T(8,128)(2,1)S(1)}, bf16[512,128]{1,0:T(8,128)(2,1)S(1)}, u32[]{:S(2)}, u32[]{:S(2)}) collective-permute-start(bf16[512,128]{1,0:T(8,128)(2,1)S(1)} %get-tuple-element.119), channel_id=1, source_target_pairs={{0,1},{1,0},{2,3},{3,2},{4,5},{5,4},{6,7},{7,6},{8,9},{9,8},{10,11... | collective-permute-start | bytes 393224 | tf_op jit(solution)/shard_map/ppermute | solution.py:518
  73.9 20.2 %collective-permute-start.28 = (bf16[432,256]{1,0:T(8,128)(2,1)S(1)}, bf16[432,256]{1,0:T(8,128)(2,1)S(1)}, u32[]{:S(2)}, u32[]{:S(2)}) collective-permute-start(bf16[432,256]{1,0:T(8,128)(2,1)S(1)} %collective-permute-done.26.refs_4_), channel_id=1, source_target_pairs={{0,8},{4,12},{8,0},{12,4},{16,24},{20,28},{24,16},{28,20},{1,9},{5... | collective-permute-start | bytes 663560 | tf_op jit(solution)/shard_map/ppermute | solution.py:564
  93.6 16.6 %collective-permute-start.27 = (bf16[432,256]{1,0:T(8,128)(2,1)S(1)}, bf16[432,256]{1,0:T(8,128)(2,1)S(1)}, u32[]{:S(2)}, u32[]{:S(2)}) collective-permute-start(bf16[432,256]{1,0:T(8,128)(2,1)S(1)} %collective-permute-done.26.refs_4_), channel_id=1, source_target_pairs={{0,4},{4,0},{8,12},{12,8},{16,20},{20,16},{24,28},{28,24},{1,5},{5... | collective-permute-start | bytes 663560 | tf_op jit(solution)/shard_map/ppermute | solution.py:564
  93.6 16.6 %collective-permute-start.25 = (bf16[432,256]{1,0:T(8,128)(2,1)S(1)}, bf16[432,256]{1,0:T(8,128)(2,1)S(1)}, u32[]{:S(2)}, u32[]{:S(2)}) collective-permute-start(bf16[432,256]{1,0:T(8,128)(2,1)S(1)} %collective-permute-done.24.refs_2_), channel_id=1, source_target_pairs={{0,4},{4,0},{8,12},{12,8},{16,20},{20,16},{24,28},{28,24},{1,5},{5... | collective-permute-start | bytes 663560 | tf_op jit(solution)/shard_map/ppermute | solution.py:564
  94.1 16.7 %collective-permute-start.29 = (bf16[432,256]{1,0:T(8,128)(2,1)S(1)}, bf16[432,256]{1,0:T(8,128)(2,1)S(1)}, u32[]{:S(2)}, u32[]{:S(2)}) collective-permute-start(bf16[432,256]{1,0:T(8,128)(2,1)S(1)} %collective-permute-done.28.refs_6_), channel_id=1, source_target_pairs={{0,4},{4,0},{8,12},{12,8},{16,20},{20,16},{24,28},{28,24},{1,5},{5... | collective-permute-start | bytes 663560 | tf_op jit(solution)/shard_map/ppermute | solution.py:564
  102.0 17.9 %collective-permute-start.33 = (bf16[768,128]{1,0:T(8,128)(2,1)S(1)}, bf16[768,128]{1,0:T(8,128)(2,1)S(1)}, u32[]{:S(2)}, u32[]{:S(2)}) collective-permute-start(bf16[768,128]{1,0:T(8,128)(2,1)S(1)} %get-tuple-element.114), channel_id=1, source_target_pairs={{0,2},{1,3},{2,0},{3,1},{4,6},{5,7},{6,4},{7,5},{8,10},{9,11},{10,... | collective-permute-start | bytes 589832 | tf_op jit(solution)/shard_map/ppermute | solution.py:518
  110.2 29.9 %collective-permute-start.32 = (bf16[768,128]{1,0:T(8,128)(2,1)S(1)}, bf16[768,128]{1,0:T(8,128)(2,1)S(1)}, u32[]{:S(2)}, u32[]{:S(2)}) collective-permute-start(bf16[768,128]{1,0:T(8,128)(2,1)S(1)} %get-tuple-element.113), channel_id=1, source_target_pairs={{0,2},{1,3},{2,0},{3,1},{4,6},{5,7},{6,4},{7,5},{8,10},{9,11},{10,... | collective-permute-start | bytes 589832 | tf_op jit(solution)/shard_map/ppermute | solution.py:518
  110.8 29.4 %collective-permute-start.34 = (bf16[768,128]{1,0:T(8,128)(2,1)S(1)}, bf16[768,128]{1,0:T(8,128)(2,1)S(1)}, u32[]{:S(2)}, u32[]{:S(2)}) collective-permute-start(bf16[768,128]{1,0:T(8,128)(2,1)S(1)} %get-tuple-element.115), channel_id=1, source_target_pairs={{0,3},{1,2},{2,1},{3,0},{4,7},{5,6},{6,5},{7,4},{8,11},{9,10},{10,... | collective-permute-start | bytes 589832 | tf_op jit(solution)/shard_map/ppermute | solution.py:518
  119.9 30.8 %collective-permute-start.17 = (bf16[384,128]{1,0:T(8,128)(2,1)S(1)}, bf16[384,128]{1,0:T(8,128)(2,1)S(1)}, u32[]{:S(2)}, u32[]{:S(2)}) collective-permute-start(bf16[384,128]{1,0:T(8,128)(2,1)S(1)} %get-tuple-element.103), channel_id=1, source_target_pairs={{0,2},{1,3},{2,0},{3,1},{4,6},{5,7},{6,4},{7,5},{8,10},{9,11},{10,... | collective-permute-start | bytes 294920 | tf_op jit(solution)/shard_map/ppermute | solution.py:518
  120.0 34.7 %collective-permute-start.19 = (bf16[384,128]{1,0:T(8,128)(2,1)S(1)}, bf16[384,128]{1,0:T(8,128)(2,1)S(1)}, u32[]{:S(2)}, u32[]{:S(2)}) collective-permute-start(bf16[384,128]{1,0:T(8,128)(2,1)S(1)} %get-tuple-element.105), channel_id=1, source_target_pairs={{0,3},{1,2},{2,1},{3,0},{4,7},{5,6},{6,5},{7,4},{8,11},{9,10},{10,... | collective-permute-start | bytes 294920 | tf_op jit(solution)/shard_map/ppermute | solution.py:518
  122.0 32.7 %collective-permute-start.14 = (bf16[384,128]{1,0:T(8,128)(2,1)S(1)}, bf16[384,128]{1,0:T(8,128)(2,1)S(1)}, u32[]{:S(2)}, u32[]{:S(2)}) collective-permute-start(bf16[384,128]{1,0:T(8,128)(2,1)S(1)} %get-tuple-element.100), channel_id=1, source_target_pairs={{0,1},{1,0},{2,3},{3,2},{4,5},{5,4},{6,7},{7,6},{8,9},{9,8},{10,11... | collective-permute-start | bytes 294920 | tf_op jit(solution)/shard_map/ppermute | solution.py:518
  140.2 17.0 %collective-permute-start.16 = (bf16[384,128]{1,0:T(8,128)(2,1)S(1)}, bf16[384,128]{1,0:T(8,128)(2,1)S(1)}, u32[]{:S(2)}, u32[]{:S(2)}) collective-permute-start(bf16[384,128]{1,0:T(8,128)(2,1)S(1)} %get-tuple-element.102), channel_id=1, source_target_pairs={{0,2},{1,3},{2,0},{3,1},{4,6},{5,7},{6,4},{7,5},{8,10},{9,11},{10,... | collective-permute-start | bytes 294920 | tf_op jit(solution)/shard_map/ppermute | solution.py:518
  140.2 18.0 %collective-permute-start.18 = (bf16[384,128]{1,0:T(8,128)(2,1)S(1)}, bf16[384,128]{1,0:T(8,128)(2,1)S(1)}, u32[]{:S(2)}, u32[]{:S(2)}) collective-permute-start(bf16[384,128]{1,0:T(8,128)(2,1)S(1)} %get-tuple-element.104), channel_id=1, source_target_pairs={{0,3},{1,2},{2,1},{3,0},{4,7},{5,6},{6,5},{7,4},{8,11},{9,10},{10,... | collective-permute-start | bytes 294920 | tf_op jit(solution)/shard_map/ppermute | solution.py:518
  150.7 24.2 %collective-permute-start.60 = (bf16[384,256]{1,0:T(8,128)(2,1)S(1)}, bf16[384,256]{1,0:T(8,128)(2,1)S(1)}, u32[]{:S(2)}, u32[]{:S(2)}) collective-permute-start(bf16[384,256]{1,0:T(8,128)(2,1)S(1)} %get-tuple-element.151), channel_id=1, source_target_pairs={{0,1},{1,0},{2,3},{3,2},{4,5},{5,4},{6,7},{7,6},{8,9},{9,8},{10,11... | collective-permute-start | bytes 589832 | tf_op jit(solution)/shard_map/ppermute | solution.py:518
  154.7 21.4 %collective-permute-start.61 = (bf16[384,256]{1,0:T(8,128)(2,1)S(1)}, bf16[384,256]{1,0:T(8,128)(2,1)S(1)}, u32[]{:S(2)}, u32[]{:S(2)}) collective-permute-start(bf16[384,256]{1,0:T(8,128)(2,1)S(1)} %get-tuple-element.152), channel_id=1, source_target_pairs={{0,2},{1,3},{2,0},{3,1},{4,6},{5,7},{6,4},{7,5},{8,10},{9,11},{10,... | collective-permute-start | bytes 589832 | tf_op jit(solution)/shard_map/ppermute | solution.py:518
  154.7 22.9 %collective-permute-start.62 = (bf16[384,256]{1,0:T(8,128)(2,1)S(1)}, bf16[384,256]{1,0:T(8,128)(2,1)S(1)}, u32[]{:S(2)}, u32[]{:S(2)}) collective-permute-start(bf16[384,256]{1,0:T(8,128)(2,1)S(1)} %get-tuple-element.153), channel_id=1, source_target_pairs={{0,3},{1,2},{2,1},{3,0},{4,7},{5,6},{6,5},{7,4},{8,11},{9,10},{10,... | collective-permute-start | bytes 589832 | tf_op jit(solution)/shard_map/ppermute | solution.py:518
  157.2 22.4 %collective-permute-start.57 = (bf16[512,256]{1,0:T(8,128)(2,1)S(1)}, bf16[512,256]{1,0:T(8,128)(2,1)S(1)}, u32[]{:S(2)}, u32[]{:S(2)}) collective-permute-start(bf16[512,256]{1,0:T(8,128)(2,1)S(1)} %get-tuple-element.147), channel_id=1, source_target_pairs={{0,1},{1,0},{2,3},{3,2},{4,5},{5,4},{6,7},{7,6},{8,9},{9,8},{10,11... | collective-permute-start | bytes 786440 | tf_op jit(solution)/shard_map/ppermute | solution.py:518
  173.2 51.5 %collective-permute-start.54 = (bf16[768,256]{1,0:T(8,128)(2,1)S(1)}, bf16[768,256]{1,0:T(8,128)(2,1)S(1)}, u32[]{:S(2)}, u32[]{:S(2)}) collective-permute-start(bf16[768,256]{1,0:T(8,128)(2,1)S(1)} %get-tuple-element.143), channel_id=1, source_target_pairs={{0,1},{1,0},{2,3},{3,2},{4,5},{5,4},{6,7},{7,6},{8,9},{9,8},{10,11... | collective-permute-start | bytes 1179656 | tf_op jit(solution)/shard_map/ppermute | solution.py:518
  176.1 35.2 %collective-permute-start.59 = (bf16[512,256]{1,0:T(8,128)(2,1)S(1)}, bf16[512,256]{1,0:T(8,128)(2,1)S(1)}, u32[]{:S(2)}, u32[]{:S(2)}) collective-permute-start(bf16[512,256]{1,0:T(8,128)(2,1)S(1)} %get-tuple-element.149), channel_id=1, source_target_pairs={{0,3},{1,2},{2,1},{3,0},{4,7},{5,6},{6,5},{7,4},{8,11},{9,10},{10,... | collective-permute-start | bytes 786440 | tf_op jit(solution)/shard_map/ppermute | solution.py:518
  177.6 58.0 %collective-permute-start.55 = (bf16[768,256]{1,0:T(8,128)(2,1)S(1)}, bf16[768,256]{1,0:T(8,128)(2,1)S(1)}, u32[]{:S(2)}, u32[]{:S(2)}) collective-permute-start(bf16[768,256]{1,0:T(8,128)(2,1)S(1)} %get-tuple-element.144), channel_id=1, source_target_pairs={{0,2},{1,3},{2,0},{3,1},{4,6},{5,7},{6,4},{7,5},{8,10},{9,11},{10,... | collective-permute-start | bytes 1179656 | tf_op jit(solution)/shard_map/ppermute | solution.py:518
  179.6 56.0 %collective-permute-start.56 = (bf16[768,256]{1,0:T(8,128)(2,1)S(1)}, bf16[768,256]{1,0:T(8,128)(2,1)S(1)}, u32[]{:S(2)}, u32[]{:S(2)}) collective-permute-start(bf16[768,256]{1,0:T(8,128)(2,1)S(1)} %get-tuple-element.145), channel_id=1, source_target_pairs={{0,3},{1,2},{2,1},{3,0},{4,7},{5,6},{6,5},{7,4},{8,11},{9,10},{10,... | collective-permute-start | bytes 1179656 | tf_op jit(solution)/shard_map/ppermute | solution.py:518
  190.1 60.5 %collective-permute-start.48 = (bf16[384,256]{1,0:T(8,128)(2,1)S(1)}, bf16[384,256]{1,0:T(8,128)(2,1)S(1)}, u32[]{:S(2)}, u32[]{:S(2)}) collective-permute-start(bf16[384,256]{1,0:T(8,128)(2,1)S(1)} %get-tuple-element.138), channel_id=1, source_target_pairs={{0,1},{1,0},{2,3},{3,2},{4,5},{5,4},{6,7},{7,6},{8,9},{9,8},{10,11... | collective-permute-start | bytes 589832 | tf_op jit(solution)/shard_map/ppermute | solution.py:518
  211.3 39.3 %collective-permute-start.49 = (bf16[384,256]{1,0:T(8,128)(2,1)S(1)}, bf16[384,256]{1,0:T(8,128)(2,1)S(1)}, u32[]{:S(2)}, u32[]{:S(2)}) collective-permute-start(bf16[384,256]{1,0:T(8,128)(2,1)S(1)} %get-tuple-element.139), channel_id=1, source_target_pairs={{0,2},{1,3},{2,0},{3,1},{4,6},{5,7},{6,4},{7,5},{8,10},{9,11},{10,... | collective-permute-start | bytes 589832 | tf_op jit(solution)/shard_map/ppermute | solution.py:518
  224.7 25.9 %collective-permute-start.50 = (bf16[384,256]{1,0:T(8,128)(2,1)S(1)}, bf16[384,256]{1,0:T(8,128)(2,1)S(1)}, u32[]{:S(2)}, u32[]{:S(2)}) collective-permute-start(bf16[384,256]{1,0:T(8,128)(2,1)S(1)} %get-tuple-element.140), channel_id=1, source_target_pairs={{0,3},{1,2},{2,1},{3,0},{4,7},{5,6},{6,5},{7,4},{8,11},{9,10},{10,... | collective-permute-start | bytes 589832 | tf_op jit(solution)/shard_map/ppermute | solution.py:518
  (37 other events, 360.7 us)

commit v8 on v6

--- a/solution.py
+++ b/solution.py
@@ -94,9 +94,11 @@
         feat, table, raw = source, refs.pop(0), refs.pop(0)
     else:
         table = source
-    block = refs.pop(0) if ahead else None
+    blocks = [refs.pop(0) for _ in ahead]
     rows, counts, index_sems, stage = refs[:4]
-    loads = block_copies(vals, block, refs[-1], *ahead) if ahead else []
+    loads = []
+    for spec, block, sem in zip(ahead, blocks, refs[len(refs) - len(ahead) :]):
+        loads += block_copies(vals, block, sem, *spec)
     for load in loads:
         load.start()
     load_rows = pltpu.make_async_copy(rows_in, rows, index_sems.at[0])
@@ -143,11 +145,11 @@
         jax.ShapeDtypeStruct((n_rows, LANES), jnp.float32),
         jax.ShapeDtypeStruct((n_rows, LANES), features.dtype),
     ]
-    block = [block_shape(vals[0], *ahead)] if ahead else []
+    block = [block_shape(vals[0], *spec) for spec in ahead]
     out = pl.pallas_call(
         functools.partial(gather_kernel, peers, peer, first_row, within, half, build, ahead),
         out_shape=[piece] * len(peers) + made * build + block,
-        in_specs=[RAW, RAW, RAW if build else VMEM] + [RAW] * (2 * len(block)),
+        in_specs=[RAW, RAW, RAW if build else VMEM] + [RAW] * (2 * bool(ahead)),
         out_specs=[VMEM] * (len(peers) + 2 * build + len(block)),
         scratch_shapes=[
             pltpu.SMEM(rows.shape, jnp.int32),
@@ -156,13 +158,13 @@
             pltpu.VMEM((slots, LANES), jnp.float32),
         ]
         + [pltpu.SemaphoreType.DMA((parts,))] * build
-        + [pltpu.SemaphoreType.DMA((2 * cols[0],)) for cols in [ahead] if ahead],
+        + [pltpu.SemaphoreType.DMA((2 * spec[0],)) for spec in ahead],
         compiler_params=grant(10 + len(peers) if build else 8),
         cost_estimate=cost(4e9, 6 << 20),
         name="gather_rows",
     )(
         in_hbm(rows), in_hbm(send_count), in_hbm(features) if build else table,
-        *([in_hbm(v) for v in vals] * len(block)),
+        *([in_hbm(v) for v in vals] * bool(ahead)),
     )
     n_out = len(peers)
     return out[:n_out], out[n_out : n_out + 2 * build], out[n_out + 2 * build :]
@@ -510,8 +512,8 @@
     order = list(reversed(range(1, n_col)))
 
     far = list(reversed(range(1, n_dom)))
-    lead = far[:3]
-    rest = [k for k in far if k not in lead]
+    lead, rest = far[:2], far[2:]
+    rest = rest[0::2] + rest[1::2]
     rows, first_row, within = storage_order(send_rows[0])
     slots = send_rows.shape[2]
     halves = width // LANES
@@ -524,13 +526,13 @@
         pieces, table = {}, None
         groups = [g for g in (lead, rest) if g] if h == 0 else [lead + rest]
         for peers in groups:
-            load = ahead[0] if h == 0 and peers is groups[-1] else ()
+            load = ahead[:2] if h == 0 and peers is groups[-1] else []
             outgoing, made, block = gather_rows(
                 rows, first_row, within, send_count[0], features, h, table, peers, peer,
                 slots, vals, load,
             )
             if load:
-                blocks = [block[0]]
+                blocks = list(block)
             if made:
                 table, tiles = made
             for k, piece in zip(peers, outgoing):
@@ -555,7 +557,7 @@
     for h in range(halves):
         received = assemble(far, [halo[h][k] for k in far], n_dom, peer)
         for g, (base, size) in enumerate(plan):
-            load = ahead[g + 1] if h == 0 and g + 1 < len(plan) else ()
+            load = ahead[g + 1] if h == 0 < g < len(plan) - 1 else ()
             sums, block = tile_sums(
                 index_tables, received, own_tiles[h], blocks[g], vals, per_dest, base, load
             )

time: 259 us -> 248 us (0.958)
  waiting for transfers between devices: 77.3 us -> 61.9 us
  starting transfers between devices: 122 us -> 126 us
    ppermute x42, waiting for transfers between devices: 68.6 us -> 57.5 us  [on_device(): lax.ppermute(x, 'col', [(i, partner(i, k, n_col)) for i in range(n_col)])]
    ppermute x42, starting transfers between devices: 104 us -> 110 us  [on_device(): lax.ppermute(x, 'col', [(i, partner(i, k, n_col)) for i in range(n_col)])]
    ppermute x14, waiting for transfers between devices: 8.66 us -> 4.43 us  [on_device(): lax.ppermute(x, 'dom', [(i, peer(i, k)) for i in range(n_dom)])]
  transfers between devices with their start and end apart: 63 -> 63, of which waited for: 24 -> 17; matrix products, arithmetic and copies ran while one was open for 0% -> 0% of each run, Pallas kernels for 16% -> 19%
where the time goes in v8:
time: 248 us
  starting transfers between devices  126 us (51%)
  waiting for transfers between devices  61.9 us (25%)
  Pallas kernels  48.8 us (20%)
  blocking collectives  8.57 us (3%)
    ppermute x42, starting transfers between devices, on_device(): lax.ppermute(x, 'col', [(i, partner(i, k, n_col)) for i in range(n_col)])  110 us
    ppermute x42, waiting for transfers between devices, on_device(): lax.ppermute(x, 'col', [(i, partner(i, k, n_col)) for i in range(n_col)])  57.5 us
    pallas_call x8, Pallas kernels, tile_sums(): pl.pallas_call(functools.partial(sum_kernel, n_col, slots, per_dest, base...  20.2 us
    ppermute x14, starting transfers between devices, on_device(): lax.ppermute(x, 'dom', [(i, peer(i, k)) for i in range(n_dom)])  13.2 us
    pallas_call x3, Pallas kernels, gather_rows(): pl.pallas_call(functools.partial(gather_kernel, peers, peer, first_row, w...  11.8 us
    pallas_call x4, Pallas kernels, mix_rows(): pl.pallas_call(functools.partial(mix_kernel, n_col, len(pieces), channels...  10.4 us
    all_gather x1, blocking collectives, on_device(): over_dom = lax.all_gather(stats, 'dom', axis=0)  8.57 us
  transfers between devices with their start and end apart: 63, of which 17 were waited for; matrix products, arithmetic and copies ran while one was open for 0% of the time, Pallas kernels for 19%

profile of v8, /device:TPU:0, one launch (start us, length us, event | category | flops | bytes accessed | tf_op | source)
XLA Modules:
  0.0 247.6 jit_solution(1413283868226462209)
XLA Ops:
  2.2 5.1 %collective-permute-start.22 = (bf16[144,256]{1,0:T(8,128)(2,1)S(1)}, bf16[144,256]{1,0:T(8,128)(2,1)S(1)}, u32[]{:S(2)}, u32[]{:S(2)}) collective-permute-start(bf16[144,256]{1,0:T(8,128)(2,1)S(1)} %weight_part.1), channel_id=1, source_target_pairs={{0,3},{1,2},{2,1},{3,0},{4,7},{5,6},{6,5},{7,4},{8,11},{9,10},{10,... | collective-permute-start | bytes 221192 | tf_op jit(solution)/shard_map/ppermute | solution.py:509
  7.9 6.3 %gather_rows.5 = (bf16[512,128]{1,0:T(8,128)(2,1)S(1)}, bf16[512,128]{1,0:T(8,128)(2,1)S(1)}, bf16[512,128]{1,0:T(8,128)(2,1)S(1)}, bf16[512,128]{1,0:T(8,128)(2...) custom-call(s32[4096]{0:T(1024)} %bitcast.56, ...), custom_call_target="tpu_custom_call" | custom-call | flops 4000000000 | bytes 6291456 | tf_op jit(solution)/shard_map/gather_rows/pallas_call | solution.py:149
  23.9 3.5 %gather_rows.4 = (bf16[512,128]{1,0:T(8,128)(2,1)S(1)}, bf16[512,128]{1,0:T(8,128)(2,1)S(1)}, bf16[512,128]{1,0:T(8,128)(2,1)S(1)}, bf16[512,128]{1,0:T(8,128)(2...) custom-call(s32[4096]{0:T(1024)} %bitcast.58, ...), custom_call_target="tpu_custom_call" | custom-call | flops 4000000000 | bytes 6291456 | tf_op jit(solution)/shard_map/gather_rows/pallas_call | solution.py:149
  44.7 3.5 %tile_sums.8 = (bf16[512,128]{1,0:T(8,128)(2,1)S(1)}, bf16[512,128]{1,0:T(8,128)(2,1)S(1)}, bf16[512,128]{1,0:T(8,128)(2,1)S(1)}, bf16[512,128]{1,0:T(8,128)(2,1)S(1)}, bf16[4,2,6,4,128,128]{5,4,3,2,1,0:T(8,128)(2,1)S(1)}) custom-call(s32[4,64]{1,0:T(4,128)S(1)} %bitcast.21, s32[64]{0:T(128)S(1)} %bitcast.37, s32[4,64]{1,0:T(4,128)S(1)} %bitcast.29, ...), custom_call_target="tpu_custom_call" | custom-call | flops 2000000000 | bytes 6291456 | tf_op jit(solution)/shard_map/tile_sums/pallas_call | solution.py:271
  49.6 2.9 %collective-permute-start.44 = (bf16[384,128]{1,0:T(8,128)(2,1)S(1)}, bf16[384,128]{1,0:T(8,128)(2,1)S(1)}, u32[]{:S(2)}, u32[]{:S(2)}) collective-permute-start(bf16[384,128]{1,0:T(8,128)(2,1)S(1)} %get-tuple-element.128), channel_id=1, source_target_pairs={{0,2},{1,3},{2,0},{3,1},{4,6},{5,7},{6,4},{7,5},{8,10},{9,11},{10,... | collective-permute-start | bytes 294920 | tf_op jit(solution)/shard_map/ppermute | solution.py:509
  53.1 3.4 %tile_sums.9 = (bf16[768,128]{1,0:T(8,128)(2,1)S(1)}, bf16[768,128]{1,0:T(8,128)(2,1)S(1)}, bf16[768,128]{1,0:T(8,128)(2,1)S(1)}, bf16[768,128]{1,0:T(8,128)(2,1)S(1)}, bf16[4,2,3,4,128,128]{5,4,3,2,1,0:T(8,128)(2,1)S(1)}) custom-call(s32[4,64]{1,0:T(4,128)S(1)} %bitcast.22, s32[64]{0:T(128)S(1)} %bitcast.38, s32[4,64]{1,0:T(4,128)S(1)} %bitcast.30, ...), custom_call_target="tpu_custom_call" | custom-call | flops 2000000000 | bytes 6291456 | tf_op jit(solution)/shard_map/tile_sums/pallas_call | solution.py:271
  56.5 3.9 %collective-permute-start.45 = (bf16[384,128]{1,0:T(8,128)(2,1)S(1)}, bf16[384,128]{1,0:T(8,128)(2,1)S(1)}, u32[]{:S(2)}, u32[]{:S(2)}) collective-permute-start(bf16[384,128]{1,0:T(8,128)(2,1)S(1)} %get-tuple-element.129), channel_id=1, source_target_pairs={{0,2},{1,3},{2,0},{3,1},{4,6},{5,7},{6,4},{7,5},{8,10},{9,11},{10,... | collective-permute-start | bytes 294920 | tf_op jit(solution)/shard_map/ppermute | solution.py:509
  60.4 2.5 %collective-permute-start.47 = (bf16[384,128]{1,0:T(8,128)(2,1)S(1)}, bf16[384,128]{1,0:T(8,128)(2,1)S(1)}, u32[]{:S(2)}, u32[]{:S(2)}) collective-permute-start(bf16[384,128]{1,0:T(8,128)(2,1)S(1)} %get-tuple-element.131), channel_id=1, source_target_pairs={{0,3},{1,2},{2,1},{3,0},{4,7},{5,6},{6,5},{7,4},{8,11},{9,10},{10,... | collective-permute-start | bytes 294920 | tf_op jit(solution)/shard_map/ppermute | solution.py:509
  62.9 3.4 %collective-permute-start.37 = (bf16[512,128]{1,0:T(8,128)(2,1)S(1)}, bf16[512,128]{1,0:T(8,128)(2,1)S(1)}, u32[]{:S(2)}, u32[]{:S(2)}) collective-permute-start(bf16[512,128]{1,0:T(8,128)(2,1)S(1)} %get-tuple-element.118), channel_id=1, source_target_pairs={{0,1},{1,0},{2,3},{3,2},{4,5},{5,4},{6,7},{7,6},{8,9},{9,8},{10,11... | collective-permute-start | bytes 393224 | tf_op jit(solution)/shard_map/ppermute | solution.py:509
  73.3 5.2 %collective-permute-done.15.refs_3_ = bf16[384,128]{1,0:T(8,128)(2,1)S(1)} collective-permute-done((bf16[384,128]{1,0:T(8,128)(2,1)S(1)}, bf16[384,128]{1,0:T(8,128)(2,1)S(1)}, u32[]{:S(2)}, u32[]{:S(2)}) %collective-permute-start.15) | collective-permute-done | bytes 98336 | tf_op jit(solution)/shard_map/ppermute | solution.py:509
  78.6 3.9 %collective-permute-start.41 = (bf16[512,128]{1,0:T(8,128)(2,1)S(1)}, bf16[512,128]{1,0:T(8,128)(2,1)S(1)}, u32[]{:S(2)}, u32[]{:S(2)}) collective-permute-start(bf16[512,128]{1,0:T(8,128)(2,1)S(1)} %get-tuple-element.122), channel_id=1, source_target_pairs={{0,3},{1,2},{2,1},{3,0},{4,7},{5,6},{6,5},{7,4},{8,11},{9,10},{10,... | collective-permute-start | bytes 393224 | tf_op jit(solution)/shard_map/ppermute | solution.py:509
  85.4 2.6 %collective-permute-done.36.refs_2_ = bf16[512,128]{1,0:T(8,128)(2,1)S(1)} collective-permute-done((bf16[512,128]{1,0:T(8,128)(2,1)S(1)}, bf16[512,128]{1,0:T(8,128)(2,1)S(1)}, u32[]{:S(2)}, u32[]{:S(2)}) %collective-permute-start.36) | collective-permute-done | bytes 131104 | tf_op jit(solution)/shard_map/ppermute | solution.py:509
  89.3 3.2 %collective-permute-done.38.refs_4_ = bf16[512,128]{1,0:T(8,128)(2,1)S(1)} collective-permute-done((bf16[512,128]{1,0:T(8,128)(2,1)S(1)}, bf16[512,128]{1,0:T(8,128)(2,1)S(1)}, u32[]{:S(2)}, u32[]{:S(2)}) %collective-permute-start.38) | collective-permute-done | bytes 131104 | tf_op jit(solution)/shard_map/ppermute | solution.py:509
  93.1 3.3 %tile_sums.12 = (bf16[768,128]{1,0:T(8,128)(2,1)S(1)}, bf16[768,128]{1,0:T(8,128)(2,1)S(1)}, bf16[768,128]{1,0:T(8,128)(2,1)S(1)}, bf16[768,128]{1,0:T(8,128)(2,1)S(1)}) custom-call(s32[4,64]{1,0:T(4,128)S(1)} %bitcast.24, s32[64]{0:T(128)S(1)} %bitcast.40, s32[4,64]{1,0:T(4,128)S(1)} %bitcast.32, s32[64]{0:T(128)S(1)} %bitcast.48, ...), custom_call_target="tpu_custom_call" | custom-call | flops 2000000000 | bytes 6291456 | tf_op jit(solution)/shard_map/tile_sums/pallas_call | solution.py:271
  99.7 5.2 %collective-permute-done.31.refs_3_ = bf16[768,128]{1,0:T(8,128)(2,1)S(1)} collective-permute-done((bf16[768,128]{1,0:T(8,128)(2,1)S(1)}, bf16[768,128]{1,0:T(8,128)(2,1)S(1)}, u32[]{:S(2)}, u32[]{:S(2)}) %collective-permute-start.31) | collective-permute-done | bytes 196640 | tf_op jit(solution)/shard_map/ppermute | solution.py:509
  106.4 3.0 %collective-permute-start.32 = (bf16[768,128]{1,0:T(8,128)(2,1)S(1)}, bf16[768,128]{1,0:T(8,128)(2,1)S(1)}, u32[]{:S(2)}, u32[]{:S(2)}) collective-permute-start(bf16[768,128]{1,0:T(8,128)(2,1)S(1)} %get-tuple-element.111), channel_id=1, source_target_pairs={{0,2},{1,3},{2,0},{3,1},{4,6},{5,7},{6,4},{7,5},{8,10},{9,11},{10,... | collective-permute-start | bytes 589832 | tf_op jit(solution)/shard_map/ppermute | solution.py:509
  113.4 2.6 %mix_rows.5 = (bf16[512,256]{1,0:T(8,128)(2,1)S(1)}, bf16[512,256]{1,0:T(8,128)(2,1)S(1)}, bf16[512,256]{1,0:T(8,128)(2,1)S(1)}, bf16[512,256]{1,0:T(8,128)(2,1)S(1)}, f32[8,256]{1,0:T(8,128)S(1)}) custom-call(bf16[512,128]{1,0:T(8,128)(2,1)S(1)} %get-tuple-element.115.refs_0_, bf16[512,128]{1,0:T(8,128)(2,1)S(1)} %get-tuple-element.116.refs_1_, ...), custom_call_target="tpu_custom_call" | custom-call | flops 1073741824 | bytes 4194304 | tf_op jit(solution)/shard_map/mix_rows/pallas_call | solution.py:412
  118.6 15.4 %collective-permute-start.14 = (bf16[384,128]{1,0:T(8,128)(2,1)S(1)}, bf16[384,128]{1,0:T(8,128)(2,1)S(1)}, u32[]{:S(2)}, u32[]{:S(2)}) collective-permute-start(bf16[384,128]{1,0:T(8,128)(2,1)S(1)} %get-tuple-element.99), channel_id=1, source_target_pairs={{0,1},{1,0},{2,3},{3,2},{4,5},{5,4},{6,7},{7,6},{8,9},{9,8},{10,11... | collective-permute-start | bytes 294920 | tf_op jit(solution)/shard_map/ppermute | solution.py:509
  134.0 2.8 %collective-permute-done.32.refs_4_ = bf16[768,128]{1,0:T(8,128)(2,1)S(1)} collective-permute-done((bf16[768,128]{1,0:T(8,128)(2,1)S(1)}, bf16[768,128]{1,0:T(8,128)(2,1)S(1)}, u32[]{:S(2)}, u32[]{:S(2)}) %collective-permute-start.32) | collective-permute-done | bytes 196640 | tf_op jit(solution)/shard_map/ppermute | solution.py:509
  138.5 3.9 %mix_rows.6 = (bf16[768,256]{1,0:T(8,128)(2,1)S(1)}, bf16[768,256]{1,0:T(8,128)(2,1)S(1)}, bf16[768,256]{1,0:T(8,128)(2,1)S(1)}, bf16[768,256]{1,0:T(8,128)(2,1)S(1)}, f32[8,256]{1,0:T(8,128)S(1)}) custom-call(bf16[768,128]{1,0:T(8,128)(2,1)S(1)} %get-tuple-element.107.refs_0_, bf16[768,128]{1,0:T(8,128)(2,1)S(1)} %get-tuple-element.108.refs_1_, ...), custom_call_target="tpu_custom_call" | custom-call | flops 1610612736 | bytes 4194304 | tf_op jit(solution)/shard_map/mix_rows/pallas_call | solution.py:412
  142.4 4.9 %collective-permute-done.17.refs_5_ = bf16[384,128]{1,0:T(8,128)(2,1)S(1)} collective-permute-done((bf16[384,128]{1,0:T(8,128)(2,1)S(1)}, bf16[384,128]{1,0:T(8,128)(2,1)S(1)}, u32[]{:S(2)}, u32[]{:S(2)}) %collective-permute-start.17) | collective-permute-done | bytes 98336 | tf_op jit(solution)/shard_map/ppermute | solution.py:509
  147.3 3.2 %collective-permute-start.60 = (bf16[384,256]{1,0:T(8,128)(2,1)S(1)}, bf16[384,256]{1,0:T(8,128)(2,1)S(1)}, u32[]{:S(2)}, u32[]{:S(2)}) collective-permute-start(bf16[384,256]{1,0:T(8,128)(2,1)S(1)} %get-tuple-element.149), channel_id=1, source_target_pairs={{0,1},{1,0},{2,3},{3,2},{4,5},{5,4},{6,7},{7,6},{8,9},{9,8},{10,11... | collective-permute-start | bytes 589832 | tf_op jit(solution)/shard_map/ppermute | solution.py:509
  156.0 8.6 %all-gather = f32[64,256]{1,0:T(8,128)S(1)} all-gather(f32[8,256]{1,0:T(8,128)S(1)} %get-tuple-element.139), channel_id=2, replica_groups=mesh['dom'=8,'col'=4] {'dom'}, dimensions={0}, use_global_device_ids=true | all-gather | bytes 73728 | tf_op jit(solution)/shard_map/all_gather | solution.py:576
  166.8 3.5 %collective-permute-done.53.refs_7_ = f32[2,256]{1,0:T(2,128)S(1)} collective-permute-done((f32[2,256]{1,0:T(2,128)S(1)}, f32[2,256]{1,0:T(2,128)S(1)}, u32[]{:S(2)}, u32[]{:S(2)}) %collective-permute-start.53) | collective-permute-done | bytes 2080 | tf_op jit(solution)/shard_map/ppermute | solution.py:509
  176.7 9.1 %collective-permute-done.58.refs_2_ = bf16[512,256]{1,0:T(8,128)(2,1)S(1)} collective-permute-done((bf16[512,256]{1,0:T(8,128)(2,1)S(1)}, bf16[512,256]{1,0:T(8,128)(2,1)S(1)}, u32[]{:S(2)}, u32[]{:S(2)}) %collective-permute-start.58) | collective-permute-done | bytes 262176 | tf_op jit(solution)/shard_map/ppermute | solution.py:509
  185.8 2.7 %collective-permute-start.48 = (bf16[384,256]{1,0:T(8,128)(2,1)S(1)}, bf16[384,256]{1,0:T(8,128)(2,1)S(1)}, u32[]{:S(2)}, u32[]{:S(2)}) collective-permute-start(bf16[384,256]{1,0:T(8,128)(2,1)S(1)} %get-tuple-element.136), channel_id=1, source_target_pairs={{0,1},{1,0},{2,3},{3,2},{4,5},{5,4},{6,7},{7,6},{8,9},{9,8},{10,11... | collective-permute-start | bytes 589832 | tf_op jit(solution)/shard_map/ppermute | solution.py:509
  188.4 5.1 %collective-permute-done.59.refs_3_ = bf16[512,256]{1,0:T(8,128)(2,1)S(1)} collective-permute-done((bf16[512,256]{1,0:T(8,128)(2,1)S(1)}, bf16[512,256]{1,0:T(8,128)(2,1)S(1)}, u32[]{:S(2)}, u32[]{:S(2)}) %collective-permute-start.59) | collective-permute-done | bytes 262176 | tf_op jit(solution)/shard_map/ppermute | solution.py:509
  193.5 24.5 %collective-permute-start.49 = (bf16[384,256]{1,0:T(8,128)(2,1)S(1)}, bf16[384,256]{1,0:T(8,128)(2,1)S(1)}, u32[]{:S(2)}, u32[]{:S(2)}) collective-permute-start(bf16[384,256]{1,0:T(8,128)(2,1)S(1)} %get-tuple-element.137), channel_id=1, source_target_pairs={{0,2},{1,3},{2,0},{3,1},{4,6},{5,7},{6,4},{7,5},{8,10},{9,11},{10,... | collective-permute-start | bytes 589832 | tf_op jit(solution)/shard_map/ppermute | solution.py:509
  218.0 3.5 %collective-permute-start.50 = (bf16[384,256]{1,0:T(8,128)(2,1)S(1)}, bf16[384,256]{1,0:T(8,128)(2,1)S(1)}, u32[]{:S(2)}, u32[]{:S(2)}) collective-permute-start(bf16[384,256]{1,0:T(8,128)(2,1)S(1)} %get-tuple-element.138), channel_id=1, source_target_pairs={{0,3},{1,2},{2,1},{3,0},{4,7},{5,6},{6,5},{7,4},{8,11},{9,10},{10,... | collective-permute-start | bytes 589832 | tf_op jit(solution)/shard_map/ppermute | solution.py:509
  223.5 7.8 %collective-permute-done.55.refs_2_ = bf16[768,256]{1,0:T(8,128)(2,1)S(1)} collective-permute-done((bf16[768,256]{1,0:T(8,128)(2,1)S(1)}, bf16[768,256]{1,0:T(8,128)(2,1)S(1)}, u32[]{:S(2)}, u32[]{:S(2)}) %collective-permute-start.55) | collective-permute-done | bytes 393248 | tf_op jit(solution)/shard_map/ppermute | solution.py:509
  231.3 9.0 %collective-permute-start.51 = (f32[2,256]{1,0:T(2,128)S(1)}, f32[2,256]{1,0:T(2,128)S(1)}, u32[]{:S(2)}, u32[]{:S(2)}) collective-permute-start(f32[2,256]{1,0:T(2,128)S(1)} %get-tuple-element.154), channel_id=1, source_target_pairs={{0,1},{1,0},{2,3},{3,2},{4,5},{5,4},{6,7},{7,6},{8,9},{9,8},{10,11... | collective-permute-start | bytes 6152 | tf_op jit(solution)/shard_map/ppermute | solution.py:509
  241.4 4.5 %collective-permute-done.52.refs_6_ = f32[2,256]{1,0:T(2,128)S(1)} collective-permute-done((f32[2,256]{1,0:T(2,128)S(1)}, f32[2,256]{1,0:T(2,128)S(1)}, u32[]{:S(2)}, u32[]{:S(2)}) %collective-permute-start.52) | collective-permute-done | bytes 2080 | tf_op jit(solution)/shard_map/ppermute | solution.py:509
  (132 shorter events, 74.6 us)
Async XLA Ops:
  2.2 17.1 %collective-permute-start.22 = (bf16[144,256]{1,0:T(8,128)(2,1)S(1)}, bf16[144,256]{1,0:T(8,128)(2,1)S(1)}, u32[]{:S(2)}, u32[]{:S(2)}) collective-permute-start(bf16[144,256]{1,0:T(8,128)(2,1)S(1)} %weight_part.1), channel_id=1, source_target_pairs={{0,3},{1,2},{2,1},{3,0},{4,7},{5,6},{6,5},{7,4},{8,11},{9,10},{10,... | collective-permute-start | bytes 221192 | tf_op jit(solution)/shard_map/ppermute | solution.py:509
  7.3 14.1 %collective-permute-start.20 = (bf16[144,256]{1,0:T(8,128)(2,1)S(1)}, bf16[144,256]{1,0:T(8,128)(2,1)S(1)}, u32[]{:S(2)}, u32[]{:S(2)}) collective-permute-start(bf16[144,256]{1,0:T(8,128)(2,1)S(1)} %weight_part.1), channel_id=1, source_target_pairs={{0,1},{1,0},{2,3},{3,2},{4,5},{5,4},{6,7},{7,6},{8,9},{9,8},{10,11... | collective-permute-start | bytes 221192 | tf_op jit(solution)/shard_map/ppermute | solution.py:509
  39.9 32.2 %collective-permute-start.26 = (bf16[432,256]{1,0:T(8,128)(2,1)S(1)}, bf16[432,256]{1,0:T(8,128)(2,1)S(1)}, u32[]{:S(2)}, u32[]{:S(2)}) collective-permute-start(bf16[432,256]{1,0:T(8,128)(2,1)S(1)} %pack_rows.1.refs_0_), channel_id=1, source_target_pairs={{0,16},{4,20},{8,24},{12,28},{16,0},{20,4},{24,8},{28,12},{1,17},{... | collective-permute-start | bytes 663560 | tf_op jit(solution)/shard_map/ppermute | solution.py:552
  62.9 19.6 %collective-permute-start.37 = (bf16[512,128]{1,0:T(8,128)(2,1)S(1)}, bf16[512,128]{1,0:T(8,128)(2,1)S(1)}, u32[]{:S(2)}, u32[]{:S(2)}) collective-permute-start(bf16[512,128]{1,0:T(8,128)(2,1)S(1)} %get-tuple-element.118), channel_id=1, source_target_pairs={{0,1},{1,0},{2,3},{3,2},{4,5},{5,4},{6,7},{7,6},{8,9},{9,8},{10,11... | collective-permute-start | bytes 393224 | tf_op jit(solution)/shard_map/ppermute | solution.py:509
  66.3 16.2 %collective-permute-start.39 = (bf16[512,128]{1,0:T(8,128)(2,1)S(1)}, bf16[512,128]{1,0:T(8,128)(2,1)S(1)}, u32[]{:S(2)}, u32[]{:S(2)}) collective-permute-start(bf16[512,128]{1,0:T(8,128)(2,1)S(1)} %get-tuple-element.120), channel_id=1, source_target_pairs={{0,2},{1,3},{2,0},{3,1},{4,6},{5,7},{6,4},{7,5},{8,10},{9,11},{10,... | collective-permute-start | bytes 393224 | tf_op jit(solution)/shard_map/ppermute | solution.py:509
  71.3 21.2 %collective-permute-start.24 = (bf16[432,256]{1,0:T(8,128)(2,1)S(1)}, bf16[432,256]{1,0:T(8,128)(2,1)S(1)}, u32[]{:S(2)}, u32[]{:S(2)}) collective-permute-start(bf16[432,256]{1,0:T(8,128)(2,1)S(1)} %pack_rows.1.refs_0_), channel_id=1, source_target_pairs={{0,8},{4,12},{8,0},{12,4},{16,24},{20,28},{24,16},{28,20},{1,9},{5... | collective-permute-start | bytes 663560 | tf_op jit(solution)/shard_map/ppermute | solution.py:552
  72.1 20.9 %collective-permute-start.28 = (bf16[432,256]{1,0:T(8,128)(2,1)S(1)}, bf16[432,256]{1,0:T(8,128)(2,1)S(1)}, u32[]{:S(2)}, u32[]{:S(2)}) collective-permute-start(bf16[432,256]{1,0:T(8,128)(2,1)S(1)} %collective-permute-done.26.refs_4_), channel_id=1, source_target_pairs={{0,8},{4,12},{8,0},{12,4},{16,24},{20,28},{24,16},{28,20},{1,9},{5... | collective-permute-start | bytes 663560 | tf_op jit(solution)/shard_map/ppermute | solution.py:552
  92.5 13.8 %collective-permute-start.27 = (bf16[432,256]{1,0:T(8,128)(2,1)S(1)}, bf16[432,256]{1,0:T(8,128)(2,1)S(1)}, u32[]{:S(2)}, u32[]{:S(2)}) collective-permute-start(bf16[432,256]{1,0:T(8,128)(2,1)S(1)} %collective-permute-done.26.refs_4_), channel_id=1, source_target_pairs={{0,4},{4,0},{8,12},{12,8},{16,20},{20,16},{24,28},{28,24},{1,5},{5... | collective-permute-start | bytes 663560 | tf_op jit(solution)/shard_map/ppermute | solution.py:552
  92.5 13.8 %collective-permute-start.25 = (bf16[432,256]{1,0:T(8,128)(2,1)S(1)}, bf16[432,256]{1,0:T(8,128)(2,1)S(1)}, u32[]{:S(2)}, u32[]{:S(2)}) collective-permute-start(bf16[432,256]{1,0:T(8,128)(2,1)S(1)} %collective-permute-done.24.refs_2_), channel_id=1, source_target_pairs={{0,4},{4,0},{8,12},{12,8},{16,20},{20,16},{24,28},{28,24},{1,5},{5... | collective-permute-start | bytes 663560 | tf_op jit(solution)/shard_map/ppermute | solution.py:552
  93.0 16.3 %collective-permute-start.29 = (bf16[432,256]{1,0:T(8,128)(2,1)S(1)}, bf16[432,256]{1,0:T(8,128)(2,1)S(1)}, u32[]{:S(2)}, u32[]{:S(2)}) collective-permute-start(bf16[432,256]{1,0:T(8,128)(2,1)S(1)} %collective-permute-done.28.refs_6_), channel_id=1, source_target_pairs={{0,4},{4,0},{8,12},{12,8},{16,20},{20,16},{24,28},{28,24},{1,5},{5... | collective-permute-start | bytes 663560 | tf_op jit(solution)/shard_map/ppermute | solution.py:552
  98.4 17.6 %collective-permute-start.33 = (bf16[768,128]{1,0:T(8,128)(2,1)S(1)}, bf16[768,128]{1,0:T(8,128)(2,1)S(1)}, u32[]{:S(2)}, u32[]{:S(2)}) collective-permute-start(bf16[768,128]{1,0:T(8,128)(2,1)S(1)} %get-tuple-element.112), channel_id=1, source_target_pairs={{0,2},{1,3},{2,0},{3,1},{4,6},{5,7},{6,4},{7,5},{8,10},{9,11},{10,... | collective-permute-start | bytes 589832 | tf_op jit(solution)/shard_map/ppermute | solution.py:509
  106.4 30.4 %collective-permute-start.32 = (bf16[768,128]{1,0:T(8,128)(2,1)S(1)}, bf16[768,128]{1,0:T(8,128)(2,1)S(1)}, u32[]{:S(2)}, u32[]{:S(2)}) collective-permute-start(bf16[768,128]{1,0:T(8,128)(2,1)S(1)} %get-tuple-element.111), channel_id=1, source_target_pairs={{0,2},{1,3},{2,0},{3,1},{4,6},{5,7},{6,4},{7,5},{8,10},{9,11},{10,... | collective-permute-start | bytes 589832 | tf_op jit(solution)/shard_map/ppermute | solution.py:509
  109.3 27.5 %collective-permute-start.34 = (bf16[768,128]{1,0:T(8,128)(2,1)S(1)}, bf16[768,128]{1,0:T(8,128)(2,1)S(1)}, u32[]{:S(2)}, u32[]{:S(2)}) collective-permute-start(bf16[768,128]{1,0:T(8,128)(2,1)S(1)} %get-tuple-element.113), channel_id=1, source_target_pairs={{0,3},{1,2},{2,1},{3,0},{4,7},{5,6},{6,5},{7,4},{8,11},{9,10},{10,... | collective-permute-start | bytes 589832 | tf_op jit(solution)/shard_map/ppermute | solution.py:509
  116.0 31.3 %collective-permute-start.17 = (bf16[384,128]{1,0:T(8,128)(2,1)S(1)}, bf16[384,128]{1,0:T(8,128)(2,1)S(1)}, u32[]{:S(2)}, u32[]{:S(2)}) collective-permute-start(bf16[384,128]{1,0:T(8,128)(2,1)S(1)} %get-tuple-element.102), channel_id=1, source_target_pairs={{0,2},{1,3},{2,0},{3,1},{4,6},{5,7},{6,4},{7,5},{8,10},{9,11},{10,... | collective-permute-start | bytes 294920 | tf_op jit(solution)/shard_map/ppermute | solution.py:509
  116.2 34.4 %collective-permute-start.19 = (bf16[384,128]{1,0:T(8,128)(2,1)S(1)}, bf16[384,128]{1,0:T(8,128)(2,1)S(1)}, u32[]{:S(2)}, u32[]{:S(2)}) collective-permute-start(bf16[384,128]{1,0:T(8,128)(2,1)S(1)} %get-tuple-element.104), channel_id=1, source_target_pairs={{0,3},{1,2},{2,1},{3,0},{4,7},{5,6},{6,5},{7,4},{8,11},{9,10},{10,... | collective-permute-start | bytes 294920 | tf_op jit(solution)/shard_map/ppermute | solution.py:509
  118.6 32.8 %collective-permute-start.14 = (bf16[384,128]{1,0:T(8,128)(2,1)S(1)}, bf16[384,128]{1,0:T(8,128)(2,1)S(1)}, u32[]{:S(2)}, u32[]{:S(2)}) collective-permute-start(bf16[384,128]{1,0:T(8,128)(2,1)S(1)} %get-tuple-element.99), channel_id=1, source_target_pairs={{0,1},{1,0},{2,3},{3,2},{4,5},{5,4},{6,7},{7,6},{8,9},{9,8},{10,11... | collective-permute-start | bytes 294920 | tf_op jit(solution)/shard_map/ppermute | solution.py:509
  136.8 16.2 %collective-permute-start.16 = (bf16[384,128]{1,0:T(8,128)(2,1)S(1)}, bf16[384,128]{1,0:T(8,128)(2,1)S(1)}, u32[]{:S(2)}, u32[]{:S(2)}) collective-permute-start(bf16[384,128]{1,0:T(8,128)(2,1)S(1)} %get-tuple-element.101), channel_id=1, source_target_pairs={{0,2},{1,3},{2,0},{3,1},{4,6},{5,7},{6,4},{7,5},{8,10},{9,11},{10,... | collective-permute-start | bytes 294920 | tf_op jit(solution)/shard_map/ppermute | solution.py:509
  136.8 17.3 %collective-permute-start.18 = (bf16[384,128]{1,0:T(8,128)(2,1)S(1)}, bf16[384,128]{1,0:T(8,128)(2,1)S(1)}, u32[]{:S(2)}, u32[]{:S(2)}) collective-permute-start(bf16[384,128]{1,0:T(8,128)(2,1)S(1)} %get-tuple-element.103), channel_id=1, source_target_pairs={{0,3},{1,2},{2,1},{3,0},{4,7},{5,6},{6,5},{7,4},{8,11},{9,10},{10,... | collective-permute-start | bytes 294920 | tf_op jit(solution)/shard_map/ppermute | solution.py:509
  147.3 23.3 %collective-permute-start.60 = (bf16[384,256]{1,0:T(8,128)(2,1)S(1)}, bf16[384,256]{1,0:T(8,128)(2,1)S(1)}, u32[]{:S(2)}, u32[]{:S(2)}) collective-permute-start(bf16[384,256]{1,0:T(8,128)(2,1)S(1)} %get-tuple-element.149), channel_id=1, source_target_pairs={{0,1},{1,0},{2,3},{3,2},{4,5},{5,4},{6,7},{7,6},{8,9},{9,8},{10,11... | collective-permute-start | bytes 589832 | tf_op jit(solution)/shard_map/ppermute | solution.py:509
  150.6 22.2 %collective-permute-start.61 = (bf16[384,256]{1,0:T(8,128)(2,1)S(1)}, bf16[384,256]{1,0:T(8,128)(2,1)S(1)}, u32[]{:S(2)}, u32[]{:S(2)}) collective-permute-start(bf16[384,256]{1,0:T(8,128)(2,1)S(1)} %get-tuple-element.150), channel_id=1, source_target_pairs={{0,2},{1,3},{2,0},{3,1},{4,6},{5,7},{6,4},{7,5},{8,10},{9,11},{10,... | collective-permute-start | bytes 589832 | tf_op jit(solution)/shard_map/ppermute | solution.py:509
  151.3 23.4 %collective-permute-start.62 = (bf16[384,256]{1,0:T(8,128)(2,1)S(1)}, bf16[384,256]{1,0:T(8,128)(2,1)S(1)}, u32[]{:S(2)}, u32[]{:S(2)}) collective-permute-start(bf16[384,256]{1,0:T(8,128)(2,1)S(1)} %get-tuple-element.151), channel_id=1, source_target_pairs={{0,3},{1,2},{2,1},{3,0},{4,7},{5,6},{6,5},{7,4},{8,11},{9,10},{10,... | collective-permute-start | bytes 589832 | tf_op jit(solution)/shard_map/ppermute | solution.py:509
  153.0 21.7 %collective-permute-start.57 = (bf16[512,256]{1,0:T(8,128)(2,1)S(1)}, bf16[512,256]{1,0:T(8,128)(2,1)S(1)}, u32[]{:S(2)}, u32[]{:S(2)}) collective-permute-start(bf16[512,256]{1,0:T(8,128)(2,1)S(1)} %get-tuple-element.145), channel_id=1, source_target_pairs={{0,1},{1,0},{2,3},{3,2},{4,5},{5,4},{6,7},{7,6},{8,9},{9,8},{10,11... | collective-permute-start | bytes 786440 | tf_op jit(solution)/shard_map/ppermute | solution.py:509
  170.3 47.7 %collective-permute-start.54 = (bf16[768,256]{1,0:T(8,128)(2,1)S(1)}, bf16[768,256]{1,0:T(8,128)(2,1)S(1)}, u32[]{:S(2)}, u32[]{:S(2)}) collective-permute-start(bf16[768,256]{1,0:T(8,128)(2,1)S(1)} %get-tuple-element.141), channel_id=1, source_target_pairs={{0,1},{1,0},{2,3},{3,2},{4,5},{5,4},{6,7},{7,6},{8,9},{9,8},{10,11... | collective-permute-start | bytes 1179656 | tf_op jit(solution)/shard_map/ppermute | solution.py:509
  170.6 15.2 %collective-permute-start.58 = (bf16[512,256]{1,0:T(8,128)(2,1)S(1)}, bf16[512,256]{1,0:T(8,128)(2,1)S(1)}, u32[]{:S(2)}, u32[]{:S(2)}) collective-permute-start(bf16[512,256]{1,0:T(8,128)(2,1)S(1)} %get-tuple-element.146), channel_id=1, source_target_pairs={{0,2},{1,3},{2,0},{3,1},{4,6},{5,7},{6,4},{7,5},{8,10},{9,11},{10,... | collective-permute-start | bytes 786440 | tf_op jit(solution)/shard_map/ppermute | solution.py:509
  172.8 20.8 %collective-permute-start.59 = (bf16[512,256]{1,0:T(8,128)(2,1)S(1)}, bf16[512,256]{1,0:T(8,128)(2,1)S(1)}, u32[]{:S(2)}, u32[]{:S(2)}) collective-permute-start(bf16[512,256]{1,0:T(8,128)(2,1)S(1)} %get-tuple-element.147), channel_id=1, source_target_pairs={{0,3},{1,2},{2,1},{3,0},{4,7},{5,6},{6,5},{7,4},{8,11},{9,10},{10,... | collective-permute-start | bytes 786440 | tf_op jit(solution)/shard_map/ppermute | solution.py:509
  174.7 56.6 %collective-permute-start.55 = (bf16[768,256]{1,0:T(8,128)(2,1)S(1)}, bf16[768,256]{1,0:T(8,128)(2,1)S(1)}, u32[]{:S(2)}, u32[]{:S(2)}) collective-permute-start(bf16[768,256]{1,0:T(8,128)(2,1)S(1)} %get-tuple-element.142), channel_id=1, source_target_pairs={{0,2},{1,3},{2,0},{3,1},{4,6},{5,7},{6,4},{7,5},{8,10},{9,11},{10,... | collective-permute-start | bytes 1179656 | tf_op jit(solution)/shard_map/ppermute | solution.py:509
  174.7 56.6 %collective-permute-start.56 = (bf16[768,256]{1,0:T(8,128)(2,1)S(1)}, bf16[768,256]{1,0:T(8,128)(2,1)S(1)}, u32[]{:S(2)}, u32[]{:S(2)}) collective-permute-start(bf16[768,256]{1,0:T(8,128)(2,1)S(1)} %get-tuple-element.143), channel_id=1, source_target_pairs={{0,3},{1,2},{2,1},{3,0},{4,7},{5,6},{6,5},{7,4},{8,11},{9,10},{10,... | collective-permute-start | bytes 1179656 | tf_op jit(solution)/shard_map/ppermute | solution.py:509
  185.8 60.2 %collective-permute-start.48 = (bf16[384,256]{1,0:T(8,128)(2,1)S(1)}, bf16[384,256]{1,0:T(8,128)(2,1)S(1)}, u32[]{:S(2)}, u32[]{:S(2)}) collective-permute-start(bf16[384,256]{1,0:T(8,128)(2,1)S(1)} %get-tuple-element.136), channel_id=1, source_target_pairs={{0,1},{1,0},{2,3},{3,2},{4,5},{5,4},{6,7},{7,6},{8,9},{9,8},{10,11... | collective-permute-start | bytes 589832 | tf_op jit(solution)/shard_map/ppermute | solution.py:509
  193.5 52.4 %collective-permute-start.49 = (bf16[384,256]{1,0:T(8,128)(2,1)S(1)}, bf16[384,256]{1,0:T(8,128)(2,1)S(1)}, u32[]{:S(2)}, u32[]{:S(2)}) collective-permute-start(bf16[384,256]{1,0:T(8,128)(2,1)S(1)} %get-tuple-element.137), channel_id=1, source_target_pairs={{0,2},{1,3},{2,0},{3,1},{4,6},{5,7},{6,4},{7,5},{8,10},{9,11},{10,... | collective-permute-start | bytes 589832 | tf_op jit(solution)/shard_map/ppermute | solution.py:509
  218.0 28.0 %collective-permute-start.50 = (bf16[384,256]{1,0:T(8,128)(2,1)S(1)}, bf16[384,256]{1,0:T(8,128)(2,1)S(1)}, u32[]{:S(2)}, u32[]{:S(2)}) collective-permute-start(bf16[384,256]{1,0:T(8,128)(2,1)S(1)} %get-tuple-element.138), channel_id=1, source_target_pairs={{0,3},{1,2},{2,1},{3,0},{4,7},{5,6},{6,5},{7,4},{8,11},{9,10},{10,... | collective-permute-start | bytes 589832 | tf_op jit(solution)/shard_map/ppermute | solution.py:509
  231.3 14.7 %collective-permute-start.52 = (f32[2,256]{1,0:T(2,128)S(1)}, f32[2,256]{1,0:T(2,128)S(1)}, u32[]{:S(2)}, u32[]{:S(2)}) collective-permute-start(f32[2,256]{1,0:T(2,128)S(1)} %get-tuple-element.153), channel_id=1, source_target_pairs={{0,2},{1,3},{2,0},{3,1},{4,6},{5,7},{6,4},{7,5},{8,10},{9,11},{10,... | collective-permute-start | bytes 6152 | tf_op jit(solution)/shard_map/ppermute | solution.py:509
  231.3 14.7 %collective-permute-start.51 = (f32[2,256]{1,0:T(2,128)S(1)}, f32[2,256]{1,0:T(2,128)S(1)}, u32[]{:S(2)}, u32[]{:S(2)}) collective-permute-start(f32[2,256]{1,0:T(2,128)S(1)} %get-tuple-element.154), channel_id=1, source_target_pairs={{0,1},{1,0},{2,3},{3,2},{4,5},{5,4},{6,7},{7,6},{8,9},{9,8},{10,11... | collective-permute-start | bytes 6152 | tf_op jit(solution)/shard_map/ppermute | solution.py:509
  (36 other events, 329.5 us)

commit v9 on v8

--- a/solution.py
+++ b/solution.py
@@ -236,26 +236,26 @@
     )(*pieces)
 
 
-def sum_kernel(n_col, slots, per_dest, base, ahead, *refs):
+def sum_kernel(ks, n_col, slots, per_dest, base, ahead, *refs):
     own_index, own_counts, halo_index, halo_counts, feat, halo, block = refs[:7]
     refs = refs[7:]
     loads = []
     if ahead:
-        loads = block_copies(refs[:2], refs[2 + n_col], refs[-1], *ahead)
+        loads = block_copies(refs[:2], refs[2 + len(ks)], refs[-1], *ahead)
         refs = refs[2:]
-    outs = refs[:n_col]
+    outs = refs[: len(ks)]
     for load in loads:
         load.start()
 
     def one(t, carry):
-        for k in range(n_col):
+        for out, k in zip(outs, ks):
             row_tile = row_tile_of(k, n_col, per_dest, base + t)
             left = masked(block.at[k, 0, t], own_counts[row_tile])
             left += masked(block.at[k, 1, t], halo_counts[row_tile])
             right = tiles_of(feat, own_index, row_tile, slots)
             right += tiles_of(halo, halo_index, row_tile, slots)
             at = pl.ds(pl.multiple_of(t * TILE, TILE), TILE)
-            outs[k][at, :] = product(left, right).astype(outs[k].dtype)
+            out[at, :] = product(left, right).astype(out.dtype)
         return carry
 
     lax.fori_loop(0, block.shape[2], one, 0)
@@ -263,19 +263,19 @@
         load.wait()
 
 
-def tile_sums(tables, halo, features, block, vals, per_dest, base, ahead):
+def tile_sums(tables, halo, features, block, vals, per_dest, base, ahead, ks):
     n_col, _, size, slots = block.shape[:4]
     width = features.shape[1]
     made = [block_shape(vals[0], *ahead)] if ahead else []
     smem = pl.BlockSpec(memory_space=pltpu.SMEM)
     out = pl.pallas_call(
-        functools.partial(sum_kernel, n_col, slots, per_dest, base, ahead),
-        out_shape=[jax.ShapeDtypeStruct((size * TILE, width), jnp.bfloat16)] * n_col + made,
+        functools.partial(sum_kernel, ks, n_col, slots, per_dest, base, ahead),
+        out_shape=[jax.ShapeDtypeStruct((size * TILE, width), jnp.bfloat16)] * len(ks) + made,
         grid_spec=pltpu.PrefetchScalarGridSpec(
             num_scalar_prefetch=4,
             grid=(1,),
             in_specs=[VMEM] * 3 + [RAW] * (2 * len(made)),
-            out_specs=[VMEM] * (n_col + len(made)),
+            out_specs=[VMEM] * (len(ks) + len(made)),
             scratch_shapes=[pltpu.SemaphoreType.DMA((2 * n_col,))] * len(made),
         ),
         compiler_params=grant(8),
@@ -285,7 +285,7 @@
         *tables, in_vmem(features), in_vmem(halo), in_vmem(block),
         *([in_hbm(v) for v in vals] * len(made)),
     )
-    return out[:n_col], out[n_col:]
+    return dict(zip(ks, out)), out[len(ks) :]
 
 
 PAD = 16
@@ -473,7 +473,7 @@
 def chunk_plan(per_dest):
     if per_dest < 16:
         return [(0, per_dest)]
-    cuts = [per_dest * c // 16 for c in (0, 3, 7, 13, 16)]
+    cuts = [per_dest * c // 16 for c in (0, 3, 7, 14, 16)]
     return [(a, b - a) for a, b in zip(cuts, cuts[1:])]
 
 
@@ -558,11 +558,18 @@
         received = assemble(far, [halo[h][k] for k in far], n_dom, peer)
         for g, (base, size) in enumerate(plan):
             load = ahead[g + 1] if h == 0 < g < len(plan) - 1 else ()
-            sums, block = tile_sums(
-                index_tables, received, own_tiles[h], blocks[g], vals, per_dest, base, load
-            )
-            blocks += block
-            moved = {k: along_col(sums[k], k) for k in order}
+            groups = [order + [0]]
+            if g == h == 0 and n_col > 2:
+                groups = [order[:1], order[1:] + [0]]
+            sums, moved = {}, {}
+            for ks in groups:
+                made, block = tile_sums(
+                    index_tables, received, own_tiles[h], blocks[g], vals, per_dest, base,
+                    load, ks,
+                )
+                sums.update(made)
+                blocks += block
+                moved.update({k: along_col(made[k], k) for k in ks if k})
             for k in range(n_col):
                 incoming[g][k].append(moved[k] if k else sums[0])
 

time: 248 us -> 254 us (1.024)
  waiting for transfers between devices: 61.9 us -> 86.8 us
  starting transfers between devices: 126 us -> 106 us
    ppermute x42, waiting for transfers between devices: 57.5 us -> 86.8 us  [on_device(): lax.ppermute(x, 'col', [(i, partner(i, k, n_col)) for i in range(n_col)])]
    ppermute x42, starting transfers between devices: 110 us -> 87.6 us  [on_device(): lax.ppermute(x, 'col', [(i, partner(i, k, n_col)) for i in range(n_col)])]
    ppermute x14, waiting for transfers between devices: 4.43 us -> 0.04 us  [on_device(): lax.ppermute(x, 'dom', [(i, peer(i, k)) for i in range(n_dom)])]
    pallas_call x8 -> x9, Pallas kernels: 20.2 us -> 21.7 us  [tile_sums(): pl.pallas_call(functools.partial(sum_kernel, ks, n_col, slots, per_dest,...]
  transfers between devices with their start and end apart: 63 -> 63, of which waited for: 17 -> 12; matrix products, arithmetic and copies ran while one was open for 0% -> 0% of each run, Pallas kernels for 19% -> 19%
where the time goes in v9:
time: 254 us
  starting transfers between devices  106 us (42%)
  waiting for transfers between devices  86.8 us (34%)
  Pallas kernels  50.3 us (20%)
  blocking collectives  9.08 us (4%)
    ppermute x42, starting transfers between devices, on_device(): lax.ppermute(x, 'col', [(i, partner(i, k, n_col)) for i in range(n_col)])  87.6 us
    ppermute x42, waiting for transfers between devices, on_device(): lax.ppermute(x, 'col', [(i, partner(i, k, n_col)) for i in range(n_col)])  86.8 us
    pallas_call x9, Pallas kernels, tile_sums(): pl.pallas_call(functools.partial(sum_kernel, ks, n_col, slots, per_dest,...  21.7 us
    ppermute x14, starting transfers between devices, on_device(): lax.ppermute(x, 'dom', [(i, peer(i, k)) for i in range(n_dom)])  13.4 us
    pallas_call x3, Pallas kernels, gather_rows(): pl.pallas_call(functools.partial(gather_kernel, peers, peer, first_row, w...  11.8 us
    pallas_call x4, Pallas kernels, mix_rows(): pl.pallas_call(functools.partial(mix_kernel, n_col, len(pieces), channels...  10.5 us
    all_gather x1, blocking collectives, on_device(): over_dom = lax.all_gather(stats, 'dom', axis=0)  9.08 us
  transfers between devices with their start and end apart: 63, of which 12 were waited for; matrix products, arithmetic and copies ran while one was open for 0% of the time, Pallas kernels for 19%

profile of v9, /device:TPU:0, one launch (start us, length us, event | category | flops | bytes accessed | tf_op | source)
XLA Modules:
  0.0 253.8 jit_solution(5237551503075930317)
XLA Ops:
  2.2 5.1 %collective-permute-start.22 = (bf16[144,256]{1,0:T(8,128)(2,1)S(1)}, bf16[144,256]{1,0:T(8,128)(2,1)S(1)}, u32[]{:S(2)}, u32[]{:S(2)}) collective-permute-start(bf16[144,256]{1,0:T(8,128)(2,1)S(1)} %weight_part.1), channel_id=1, source_target_pairs={{0,3},{1,2},{2,1},{3,0},{4,7},{5,6},{6,5},{7,4},{8,11},{9,10},{10,... | collective-permute-start | bytes 221192 | tf_op jit(solution)/shard_map/ppermute | solution.py:509
  13.2 3.5 %gather_rows.4 = (bf16[512,128]{1,0:T(8,128)(2,1)S(1)}, bf16[512,128]{1,0:T(8,128)(2,1)S(1)}, bf16[512,128]{1,0:T(8,128)(2,1)S(1)}, bf16[512,128]{1,0:T(8,128)(2...) custom-call(s32[4096]{0:T(1024)} %bitcast.61, ...), custom_call_target="tpu_custom_call" | custom-call | flops 4000000000 | bytes 6291456 | tf_op jit(solution)/shard_map/gather_rows/pallas_call | solution.py:149
  20.3 6.3 %gather_rows.5 = (bf16[512,128]{1,0:T(8,128)(2,1)S(1)}, bf16[512,128]{1,0:T(8,128)(2,1)S(1)}, bf16[512,128]{1,0:T(8,128)(2,1)S(1)}, bf16[512,128]{1,0:T(8,128)(2...) custom-call(s32[4096]{0:T(1024)} %bitcast.62, ...), custom_call_target="tpu_custom_call" | custom-call | flops 4000000000 | bytes 6291456 | tf_op jit(solution)/shard_map/gather_rows/pallas_call | solution.py:149
  35.3 3.8 %tile_sums.9 = (bf16[512,128]{1,0:T(8,128)(2,1)S(1)}, bf16[512,128]{1,0:T(8,128)(2,1)S(1)}, bf16[512,128]{1,0:T(8,128)(2,1)S(1)}, bf16[512,128]{1,0:T(8,128)(2,1)S(1)}, bf16[4,2,7,4,128,128]{5,4,3,2,1,0:T(8,128)(2,1)S(1)}) custom-call(s32[4,64]{1,0:T(4,128)S(1)} %bitcast.20, s32[64]{0:T(128)S(1)} %bitcast.38, s32[4,64]{1,0:T(4,128)S(1)} %bitcast.29, ...), custom_call_target="tpu_custom_call" | custom-call | flops 2000000000 | bytes 6291456 | tf_op jit(solution)/shard_map/tile_sums/pallas_call | solution.py:271
  40.3 3.8 %tile_sums.10 = (bf16[896,128]{1,0:T(8,128)(2,1)S(1)}, bf16[896,128]{1,0:T(8,128)(2,1)S(1)}, bf16[896,128]{1,0:T(8,128)(2,1)S(1)}, bf16[896,128]{1,0:T(8,128)(2,1)S(1)}, bf16[4,2,2,4,128,128]{5,4,3,2,1,0:T(8,128)(2,1)S(1)}) custom-call(s32[4,64]{1,0:T(4,128)S(1)} %bitcast.21, s32[64]{0:T(128)S(1)} %bitcast.39, s32[4,64]{1,0:T(4,128)S(1)} %bitcast.30, ...), custom_call_target="tpu_custom_call" | custom-call | flops 2000000000 | bytes 6291456 | tf_op jit(solution)/shard_map/tile_sums/pallas_call | solution.py:271
  45.7 3.6 %collective-permute-start.46 = (bf16[384,128]{1,0:T(8,128)(2,1)S(1)}, bf16[384,128]{1,0:T(8,128)(2,1)S(1)}, u32[]{:S(2)}, u32[]{:S(2)}) collective-permute-start(bf16[384,128]{1,0:T(8,128)(2,1)S(1)} %tile_sums.17), channel_id=1, source_target_pairs={{0,3},{1,2},{2,1},{3,0},{4,7},{5,6},{6,5},{7,4},{8,11},{9,10},{10,... | collective-permute-start | bytes 294920 | tf_op jit(solution)/shard_map/ppermute | solution.py:509
  55.9 2.2 collective-permute-start.45
  58.1 2.4 tile_sums.14
  65.3 2.3 collective-permute-done.45.refs_5_
  67.7 7.2 %collective-permute-done.47.refs_7_ = bf16[384,128]{1,0:T(8,128)(2,1)S(1)} collective-permute-done((bf16[384,128]{1,0:T(8,128)(2,1)S(1)}, bf16[384,128]{1,0:T(8,128)(2,1)S(1)}, u32[]{:S(2)}, u32[]{:S(2)}) %collective-permute-start.47) | collective-permute-done | bytes 98336 | tf_op jit(solution)/shard_map/ppermute | solution.py:509
  76.9 7.0 %collective-permute-start.36 = (bf16[512,128]{1,0:T(8,128)(2,1)S(1)}, bf16[512,128]{1,0:T(8,128)(2,1)S(1)}, u32[]{:S(2)}, u32[]{:S(2)}) collective-permute-start(bf16[512,128]{1,0:T(8,128)(2,1)S(1)} %get-tuple-element.116), channel_id=1, source_target_pairs={{0,1},{1,0},{2,3},{3,2},{4,5},{5,4},{6,7},{7,6},{8,9},{9,8},{10,11... | collective-permute-start | bytes 393224 | tf_op jit(solution)/shard_map/ppermute | solution.py:509
  83.9 2.4 collective-permute-start.40
  86.4 3.7 %tile_sums.13 = (bf16[896,128]{1,0:T(8,128)(2,1)S(1)}, bf16[896,128]{1,0:T(8,128)(2,1)S(1)}, bf16[896,128]{1,0:T(8,128)(2,1)S(1)}, bf16[896,128]{1,0:T(8,128)(2,1)S(1)}) custom-call(s32[4,64]{1,0:T(4,128)S(1)} %bitcast.25, s32[64]{0:T(128)S(1)} %bitcast.43, s32[4,64]{1,0:T(4,128)S(1)} %bitcast.34, s32[64]{0:T(128)S(1)} %bitcast.52, ...), custom_call_target="tpu_custom_call" | custom-call | flops 2000000000 | bytes 6291456 | tf_op jit(solution)/shard_map/tile_sums/pallas_call | solution.py:271
  91.2 3.9 %collective-permute-done.38.refs_4_ = bf16[512,128]{1,0:T(8,128)(2,1)S(1)} collective-permute-done((bf16[512,128]{1,0:T(8,128)(2,1)S(1)}, bf16[512,128]{1,0:T(8,128)(2,1)S(1)}, u32[]{:S(2)}, u32[]{:S(2)}) %collective-permute-start.38) | collective-permute-done | bytes 131104 | tf_op jit(solution)/shard_map/ppermute | solution.py:509
  99.6 2.2 collective-permute-start.35
  104.0 2.2 collective-permute-start.34
  108.9 2.6 %mix_rows.5 = (bf16[512,256]{1,0:T(8,128)(2,1)S(1)}, bf16[512,256]{1,0:T(8,128)(2,1)S(1)}, bf16[512,256]{1,0:T(8,128)(2,1)S(1)}, bf16[512,256]{1,0:T(8,128)(2,1)S(1)}, f32[8,256]{1,0:T(8,128)S(1)}) custom-call(bf16[512,128]{1,0:T(8,128)(2,1)S(1)} %get-tuple-element.114.refs_0_, bf16[512,128]{1,0:T(8,128)(2,1)S(1)} %get-tuple-element.115.refs_1_, ...), custom_call_target="tpu_custom_call" | custom-call | flops 1073741824 | bytes 4194304 | tf_op jit(solution)/shard_map/mix_rows/pallas_call | solution.py:412
  111.5 5.4 %collective-permute-done.33.refs_5_ = bf16[896,128]{1,0:T(8,128)(2,1)S(1)} collective-permute-done((bf16[896,128]{1,0:T(8,128)(2,1)S(1)}, bf16[896,128]{1,0:T(8,128)(2,1)S(1)}, u32[]{:S(2)}, u32[]{:S(2)}) %collective-permute-start.33) | collective-permute-done | bytes 229408 | tf_op jit(solution)/shard_map/ppermute | solution.py:509
  118.6 17.2 %collective-permute-start.14 = (bf16[256,128]{1,0:T(8,128)(2,1)S(1)}, bf16[256,128]{1,0:T(8,128)(2,1)S(1)}, u32[]{:S(2)}, u32[]{:S(2)}) collective-permute-start(bf16[256,128]{1,0:T(8,128)(2,1)S(1)} %get-tuple-element.98), channel_id=1, source_target_pairs={{0,1},{1,0},{2,3},{3,2},{4,5},{5,4},{6,7},{7,6},{8,9},{9,8},{10,11... | collective-permute-start | bytes 196616 | tf_op jit(solution)/shard_map/ppermute | solution.py:509
  135.8 3.6 %collective-permute-done.32.refs_4_ = bf16[896,128]{1,0:T(8,128)(2,1)S(1)} collective-permute-done((bf16[896,128]{1,0:T(8,128)(2,1)S(1)}, bf16[896,128]{1,0:T(8,128)(2,1)S(1)}, u32[]{:S(2)}, u32[]{:S(2)}) %collective-permute-start.32) | collective-permute-done | bytes 229408 | tf_op jit(solution)/shard_map/ppermute | solution.py:509
  141.1 4.6 %mix_rows.6 = (bf16[896,256]{1,0:T(8,128)(2,1)S(1)}, bf16[896,256]{1,0:T(8,128)(2,1)S(1)}, bf16[896,256]{1,0:T(8,128)(2,1)S(1)}, bf16[896,256]{1,0:T(8,128)(2,1)S(1)}, f32[8,256]{1,0:T(8,128)S(1)}) custom-call(bf16[896,128]{1,0:T(8,128)(2,1)S(1)} %get-tuple-element.106.refs_0_, bf16[896,128]{1,0:T(8,128)(2,1)S(1)} %get-tuple-element.107.refs_1_, ...), custom_call_target="tpu_custom_call" | custom-call | flops 1879048192 | bytes 4194304 | tf_op jit(solution)/shard_map/mix_rows/pallas_call | solution.py:412
  145.7 2.9 %collective-permute-done.17.refs_5_ = bf16[256,128]{1,0:T(8,128)(2,1)S(1)} collective-permute-done((bf16[256,128]{1,0:T(8,128)(2,1)S(1)}, bf16[256,128]{1,0:T(8,128)(2,1)S(1)}, u32[]{:S(2)}, u32[]{:S(2)}) %collective-permute-start.17) | collective-permute-done | bytes 65568 | tf_op jit(solution)/shard_map/ppermute | solution.py:509
  148.5 4.6 %collective-permute-start.60 = (bf16[384,256]{1,0:T(8,128)(2,1)S(1)}, bf16[384,256]{1,0:T(8,128)(2,1)S(1)}, u32[]{:S(2)}, u32[]{:S(2)}) collective-permute-start(bf16[384,256]{1,0:T(8,128)(2,1)S(1)} %get-tuple-element.147), channel_id=1, source_target_pairs={{0,1},{1,0},{2,3},{3,2},{4,5},{5,4},{6,7},{7,6},{8,9},{9,8},{10,11... | collective-permute-start | bytes 589832 | tf_op jit(solution)/shard_map/ppermute | solution.py:509
  157.2 9.1 %all-gather = f32[64,256]{1,0:T(8,128)S(1)} all-gather(f32[8,256]{1,0:T(8,128)S(1)} %get-tuple-element.137), channel_id=2, replica_groups=mesh['dom'=8,'col'=4] {'dom'}, dimensions={0}, use_global_device_ids=true | all-gather | bytes 73728 | tf_op jit(solution)/shard_map/all_gather | solution.py:583
  168.0 2.2 collective-permute-start.62
  171.8 2.2 collective-permute-start.55
  174.0 2.2 collective-permute-start.56
  177.6 2.3 collective-permute-start.58
  181.5 53.2 %collective-permute-done.58.refs_2_ = bf16[512,256]{1,0:T(8,128)(2,1)S(1)} collective-permute-done((bf16[512,256]{1,0:T(8,128)(2,1)S(1)}, bf16[512,256]{1,0:T(8,128)(2,1)S(1)}, u32[]{:S(2)}, u32[]{:S(2)}) %collective-permute-start.58) | collective-permute-done | bytes 262176 | tf_op jit(solution)/shard_map/ppermute | solution.py:509
  234.8 6.0 %collective-permute-start.49 = (bf16[256,256]{1,0:T(8,128)(2,1)S(1)}, bf16[256,256]{1,0:T(8,128)(2,1)S(1)}, u32[]{:S(2)}, u32[]{:S(2)}) collective-permute-start(bf16[256,256]{1,0:T(8,128)(2,1)S(1)} %get-tuple-element.135), channel_id=1, source_target_pairs={{0,2},{1,3},{2,0},{3,1},{4,6},{5,7},{6,4},{7,5},{8,10},{9,11},{10,... | collective-permute-start | bytes 393224 | tf_op jit(solution)/shard_map/ppermute | solution.py:509
  244.5 2.7 %collective-permute-start.51 = (f32[2,256]{1,0:T(2,128)S(1)}, f32[2,256]{1,0:T(2,128)S(1)}, u32[]{:S(2)}, u32[]{:S(2)}) collective-permute-start(f32[2,256]{1,0:T(2,128)S(1)} %get-tuple-element.152), channel_id=1, source_target_pairs={{0,1},{1,0},{2,3},{3,2},{4,5},{5,4},{6,7},{7,6},{8,9},{9,8},{10,11... | collective-permute-start | bytes 6152 | tf_op jit(solution)/shard_map/ppermute | solution.py:509
  248.5 3.7 %collective-permute-done.52.refs_6_ = f32[2,256]{1,0:T(2,128)S(1)} collective-permute-done((f32[2,256]{1,0:T(2,128)S(1)}, f32[2,256]{1,0:T(2,128)S(1)}, u32[]{:S(2)}, u32[]{:S(2)}) %collective-permute-start.52) | collective-permute-done | bytes 2080 | tf_op jit(solution)/shard_map/ppermute | solution.py:509
  (133 shorter events, 66.4 us)
Async XLA Ops:
  2.2 14.6 %collective-permute-start.22 = (bf16[144,256]{1,0:T(8,128)(2,1)S(1)}, bf16[144,256]{1,0:T(8,128)(2,1)S(1)}, u32[]{:S(2)}, u32[]{:S(2)}) collective-permute-start(bf16[144,256]{1,0:T(8,128)(2,1)S(1)} %weight_part.1), channel_id=1, source_target_pairs={{0,3},{1,2},{2,1},{3,0},{4,7},{5,6},{6,5},{7,4},{8,11},{9,10},{10,... | collective-permute-start | bytes 221192 | tf_op jit(solution)/shard_map/ppermute | solution.py:509
  26.6 12.5 %collective-permute-start.7 = (bf16[512,128]{1,0:T(8,128)(2,1)S(1)}, bf16[512,128]{1,0:T(8,128)(2,1)S(1)}, u32[]{:S(2)}, u32[]{:S(2)}) collective-permute-start(bf16[512,128]{1,0:T(8,128)(2,1)S(1)} %get-tuple-element.90), channel_id=1, source_target_pairs={{0,28},{4,24},{8,20},{12,16},{16,12},{20,8},{24,4},{28,0},{1,29},{... | collective-permute-start | bytes 393224 | tf_op jit(solution)/shard_map/ppermute | solution.py:508
  29.7 14.4 %collective-permute-start.9 = (bf16[512,128]{1,0:T(8,128)(2,1)S(1)}, bf16[512,128]{1,0:T(8,128)(2,1)S(1)}, u32[]{:S(2)}, u32[]{:S(2)}) collective-permute-start(bf16[512,128]{1,0:T(8,128)(2,1)S(1)} %get-tuple-element.92), channel_id=1, source_target_pairs={{0,20},{4,16},{8,28},{12,24},{16,4},{20,0},{24,12},{28,8},{1,21},{... | collective-permute-start | bytes 393224 | tf_op jit(solution)/shard_map/ppermute | solution.py:508
  30.9 14.9 %collective-permute-start.10 = (bf16[512,128]{1,0:T(8,128)(2,1)S(1)}, bf16[512,128]{1,0:T(8,128)(2,1)S(1)}, u32[]{:S(2)}, u32[]{:S(2)}) collective-permute-start(bf16[512,128]{1,0:T(8,128)(2,1)S(1)} %get-tuple-element.93), channel_id=1, source_target_pairs={{0,16},{4,20},{8,24},{12,28},{16,0},{20,4},{24,8},{28,12},{1,17},{... | collective-permute-start | bytes 393224 | tf_op jit(solution)/shard_map/ppermute | solution.py:508
  31.2 18.2 %collective-permute-start.11 = (bf16[512,128]{1,0:T(8,128)(2,1)S(1)}, bf16[512,128]{1,0:T(8,128)(2,1)S(1)}, u32[]{:S(2)}, u32[]{:S(2)}) collective-permute-start(bf16[512,128]{1,0:T(8,128)(2,1)S(1)} %get-tuple-element.94), channel_id=1, source_target_pairs={{0,12},{4,8},{8,4},{12,0},{16,28},{20,24},{24,20},{28,16},{1,13},{... | collective-permute-start | bytes 393224 | tf_op jit(solution)/shard_map/ppermute | solution.py:508
  44.1 32.2 %collective-permute-start.26 = (bf16[432,256]{1,0:T(8,128)(2,1)S(1)}, bf16[432,256]{1,0:T(8,128)(2,1)S(1)}, u32[]{:S(2)}, u32[]{:S(2)}) collective-permute-start(bf16[432,256]{1,0:T(8,128)(2,1)S(1)} %pack_rows.1.refs_0_), channel_id=1, source_target_pairs={{0,16},{4,20},{8,24},{12,28},{16,0},{20,4},{24,8},{28,12},{1,17},{... | collective-permute-start | bytes 663560 | tf_op jit(solution)/shard_map/ppermute | solution.py:552
  60.5 16.4 %collective-permute-start.37 = (bf16[512,128]{1,0:T(8,128)(2,1)S(1)}, bf16[512,128]{1,0:T(8,128)(2,1)S(1)}, u32[]{:S(2)}, u32[]{:S(2)}) collective-permute-start(bf16[512,128]{1,0:T(8,128)(2,1)S(1)} %get-tuple-element.117), channel_id=1, source_target_pairs={{0,1},{1,0},{2,3},{3,2},{4,5},{5,4},{6,7},{7,6},{8,9},{9,8},{10,11... | collective-permute-start | bytes 393224 | tf_op jit(solution)/shard_map/ppermute | solution.py:509
  63.8 20.1 %collective-permute-start.39 = (bf16[512,128]{1,0:T(8,128)(2,1)S(1)}, bf16[512,128]{1,0:T(8,128)(2,1)S(1)}, u32[]{:S(2)}, u32[]{:S(2)}) collective-permute-start(bf16[512,128]{1,0:T(8,128)(2,1)S(1)} %get-tuple-element.119), channel_id=1, source_target_pairs={{0,2},{1,3},{2,0},{3,1},{4,6},{5,7},{6,4},{7,5},{8,10},{9,11},{10,... | collective-permute-start | bytes 393224 | tf_op jit(solution)/shard_map/ppermute | solution.py:509
  63.9 20.0 %collective-permute-start.41 = (bf16[512,128]{1,0:T(8,128)(2,1)S(1)}, bf16[512,128]{1,0:T(8,128)(2,1)S(1)}, u32[]{:S(2)}, u32[]{:S(2)}) collective-permute-start(bf16[512,128]{1,0:T(8,128)(2,1)S(1)} %get-tuple-element.121), channel_id=1, source_target_pairs={{0,3},{1,2},{2,1},{3,0},{4,7},{5,6},{6,5},{7,4},{8,11},{9,10},{10,... | collective-permute-start | bytes 393224 | tf_op jit(solution)/shard_map/ppermute | solution.py:509
  74.9 20.7 %collective-permute-start.24 = (bf16[432,256]{1,0:T(8,128)(2,1)S(1)}, bf16[432,256]{1,0:T(8,128)(2,1)S(1)}, u32[]{:S(2)}, u32[]{:S(2)}) collective-permute-start(bf16[432,256]{1,0:T(8,128)(2,1)S(1)} %pack_rows.1.refs_0_), channel_id=1, source_target_pairs={{0,8},{4,12},{8,0},{12,4},{16,24},{20,28},{24,16},{28,20},{1,9},{5... | collective-permute-start | bytes 663560 | tf_op jit(solution)/shard_map/ppermute | solution.py:552
  76.3 19.3 %collective-permute-start.28 = (bf16[432,256]{1,0:T(8,128)(2,1)S(1)}, bf16[432,256]{1,0:T(8,128)(2,1)S(1)}, u32[]{:S(2)}, u32[]{:S(2)}) collective-permute-start(bf16[432,256]{1,0:T(8,128)(2,1)S(1)} %collective-permute-done.26.refs_4_), channel_id=1, source_target_pairs={{0,8},{4,12},{8,0},{12,4},{16,24},{20,28},{24,16},{28,20},{1,9},{5... | collective-permute-start | bytes 663560 | tf_op jit(solution)/shard_map/ppermute | solution.py:552
  76.9 13.1 %collective-permute-start.36 = (bf16[512,128]{1,0:T(8,128)(2,1)S(1)}, bf16[512,128]{1,0:T(8,128)(2,1)S(1)}, u32[]{:S(2)}, u32[]{:S(2)}) collective-permute-start(bf16[512,128]{1,0:T(8,128)(2,1)S(1)} %get-tuple-element.116), channel_id=1, source_target_pairs={{0,1},{1,0},{2,3},{3,2},{4,5},{5,4},{6,7},{7,6},{8,9},{9,8},{10,11... | collective-permute-start | bytes 393224 | tf_op jit(solution)/shard_map/ppermute | solution.py:509
  97.6 19.3 %collective-permute-start.33 = (bf16[896,128]{1,0:T(8,128)(2,1)S(1)}, bf16[896,128]{1,0:T(8,128)(2,1)S(1)}, u32[]{:S(2)}, u32[]{:S(2)}) collective-permute-start(bf16[896,128]{1,0:T(8,128)(2,1)S(1)} %get-tuple-element.111), channel_id=1, source_target_pairs={{0,2},{1,3},{2,0},{3,1},{4,6},{5,7},{6,4},{7,5},{8,10},{9,11},{10,... | collective-permute-start | bytes 688136 | tf_op jit(solution)/shard_map/ppermute | solution.py:509
  99.6 17.3 %collective-permute-start.35 = (bf16[896,128]{1,0:T(8,128)(2,1)S(1)}, bf16[896,128]{1,0:T(8,128)(2,1)S(1)}, u32[]{:S(2)}, u32[]{:S(2)}) collective-permute-start(bf16[896,128]{1,0:T(8,128)(2,1)S(1)} %get-tuple-element.113), channel_id=1, source_target_pairs={{0,3},{1,2},{2,1},{3,0},{4,7},{5,6},{6,5},{7,4},{8,11},{9,10},{10,... | collective-permute-start | bytes 688136 | tf_op jit(solution)/shard_map/ppermute | solution.py:509
  101.8 16.8 %collective-permute-start.30 = (bf16[896,128]{1,0:T(8,128)(2,1)S(1)}, bf16[896,128]{1,0:T(8,128)(2,1)S(1)}, u32[]{:S(2)}, u32[]{:S(2)}) collective-permute-start(bf16[896,128]{1,0:T(8,128)(2,1)S(1)} %get-tuple-element.108), channel_id=1, source_target_pairs={{0,1},{1,0},{2,3},{3,2},{4,5},{5,4},{6,7},{7,6},{8,9},{9,8},{10,11... | collective-permute-start | bytes 688136 | tf_op jit(solution)/shard_map/ppermute | solution.py:509
  101.8 37.6 %collective-permute-start.32 = (bf16[896,128]{1,0:T(8,128)(2,1)S(1)}, bf16[896,128]{1,0:T(8,128)(2,1)S(1)}, u32[]{:S(2)}, u32[]{:S(2)}) collective-permute-start(bf16[896,128]{1,0:T(8,128)(2,1)S(1)} %get-tuple-element.110), channel_id=1, source_target_pairs={{0,2},{1,3},{2,0},{3,1},{4,6},{5,7},{6,4},{7,5},{8,10},{9,11},{10,... | collective-permute-start | bytes 688136 | tf_op jit(solution)/shard_map/ppermute | solution.py:509
  104.0 35.4 %collective-permute-start.34 = (bf16[896,128]{1,0:T(8,128)(2,1)S(1)}, bf16[896,128]{1,0:T(8,128)(2,1)S(1)}, u32[]{:S(2)}, u32[]{:S(2)}) collective-permute-start(bf16[896,128]{1,0:T(8,128)(2,1)S(1)} %get-tuple-element.112), channel_id=1, source_target_pairs={{0,3},{1,2},{2,1},{3,0},{4,7},{5,6},{6,5},{7,4},{8,11},{9,10},{10,... | collective-permute-start | bytes 688136 | tf_op jit(solution)/shard_map/ppermute | solution.py:509
  116.9 31.6 %collective-permute-start.17 = (bf16[256,128]{1,0:T(8,128)(2,1)S(1)}, bf16[256,128]{1,0:T(8,128)(2,1)S(1)}, u32[]{:S(2)}, u32[]{:S(2)}) collective-permute-start(bf16[256,128]{1,0:T(8,128)(2,1)S(1)} %get-tuple-element.101), channel_id=1, source_target_pairs={{0,2},{1,3},{2,0},{3,1},{4,6},{5,7},{6,4},{7,5},{8,10},{9,11},{10,... | collective-permute-start | bytes 196616 | tf_op jit(solution)/shard_map/ppermute | solution.py:509
  116.9 36.2 %collective-permute-start.19 = (bf16[256,128]{1,0:T(8,128)(2,1)S(1)}, bf16[256,128]{1,0:T(8,128)(2,1)S(1)}, u32[]{:S(2)}, u32[]{:S(2)}) collective-permute-start(bf16[256,128]{1,0:T(8,128)(2,1)S(1)} %get-tuple-element.103), channel_id=1, source_target_pairs={{0,3},{1,2},{2,1},{3,0},{4,7},{5,6},{6,5},{7,4},{8,11},{9,10},{10,... | collective-permute-start | bytes 196616 | tf_op jit(solution)/shard_map/ppermute | solution.py:509
  118.6 35.3 %collective-permute-start.14 = (bf16[256,128]{1,0:T(8,128)(2,1)S(1)}, bf16[256,128]{1,0:T(8,128)(2,1)S(1)}, u32[]{:S(2)}, u32[]{:S(2)}) collective-permute-start(bf16[256,128]{1,0:T(8,128)(2,1)S(1)} %get-tuple-element.98), channel_id=1, source_target_pairs={{0,1},{1,0},{2,3},{3,2},{4,5},{5,4},{6,7},{7,6},{8,9},{9,8},{10,11... | collective-permute-start | bytes 196616 | tf_op jit(solution)/shard_map/ppermute | solution.py:509
  139.4 16.4 %collective-permute-start.16 = (bf16[256,128]{1,0:T(8,128)(2,1)S(1)}, bf16[256,128]{1,0:T(8,128)(2,1)S(1)}, u32[]{:S(2)}, u32[]{:S(2)}) collective-permute-start(bf16[256,128]{1,0:T(8,128)(2,1)S(1)} %get-tuple-element.100), channel_id=1, source_target_pairs={{0,2},{1,3},{2,0},{3,1},{4,6},{5,7},{6,4},{7,5},{8,10},{9,11},{10,... | collective-permute-start | bytes 196616 | tf_op jit(solution)/shard_map/ppermute | solution.py:509
  139.4 16.4 %collective-permute-start.18 = (bf16[256,128]{1,0:T(8,128)(2,1)S(1)}, bf16[256,128]{1,0:T(8,128)(2,1)S(1)}, u32[]{:S(2)}, u32[]{:S(2)}) collective-permute-start(bf16[256,128]{1,0:T(8,128)(2,1)S(1)} %get-tuple-element.102), channel_id=1, source_target_pairs={{0,3},{1,2},{2,1},{3,0},{4,7},{5,6},{6,5},{7,4},{8,11},{9,10},{10,... | collective-permute-start | bytes 196616 | tf_op jit(solution)/shard_map/ppermute | solution.py:509
  148.5 23.3 %collective-permute-start.60 = (bf16[384,256]{1,0:T(8,128)(2,1)S(1)}, bf16[384,256]{1,0:T(8,128)(2,1)S(1)}, u32[]{:S(2)}, u32[]{:S(2)}) collective-permute-start(bf16[384,256]{1,0:T(8,128)(2,1)S(1)} %get-tuple-element.147), channel_id=1, source_target_pairs={{0,1},{1,0},{2,3},{3,2},{4,5},{5,4},{6,7},{7,6},{8,9},{9,8},{10,11... | collective-permute-start | bytes 589832 | tf_op jit(solution)/shard_map/ppermute | solution.py:509
  153.1 20.9 %collective-permute-start.61 = (bf16[384,256]{1,0:T(8,128)(2,1)S(1)}, bf16[384,256]{1,0:T(8,128)(2,1)S(1)}, u32[]{:S(2)}, u32[]{:S(2)}) collective-permute-start(bf16[384,256]{1,0:T(8,128)(2,1)S(1)} %get-tuple-element.148), channel_id=1, source_target_pairs={{0,2},{1,3},{2,0},{3,1},{4,6},{5,7},{6,4},{7,5},{8,10},{9,11},{10,... | collective-permute-start | bytes 589832 | tf_op jit(solution)/shard_map/ppermute | solution.py:509
  153.9 26.0 %collective-permute-start.57 = (bf16[512,256]{1,0:T(8,128)(2,1)S(1)}, bf16[512,256]{1,0:T(8,128)(2,1)S(1)}, u32[]{:S(2)}, u32[]{:S(2)}) collective-permute-start(bf16[512,256]{1,0:T(8,128)(2,1)S(1)} %get-tuple-element.143), channel_id=1, source_target_pairs={{0,1},{1,0},{2,3},{3,2},{4,5},{5,4},{6,7},{7,6},{8,9},{9,8},{10,11... | collective-permute-start | bytes 786440 | tf_op jit(solution)/shard_map/ppermute | solution.py:509
  171.8 69.0 %collective-permute-start.54 = (bf16[896,256]{1,0:T(8,128)(2,1)S(1)}, bf16[896,256]{1,0:T(8,128)(2,1)S(1)}, u32[]{:S(2)}, u32[]{:S(2)}) collective-permute-start(bf16[896,256]{1,0:T(8,128)(2,1)S(1)} %get-tuple-element.139), channel_id=1, source_target_pairs={{0,1},{1,0},{2,3},{3,2},{4,5},{5,4},{6,7},{7,6},{8,9},{9,8},{10,11... | collective-permute-start | bytes 1376264 | tf_op jit(solution)/shard_map/ppermute | solution.py:509
  171.8 72.5 %collective-permute-start.55 = (bf16[896,256]{1,0:T(8,128)(2,1)S(1)}, bf16[896,256]{1,0:T(8,128)(2,1)S(1)}, u32[]{:S(2)}, u32[]{:S(2)}) collective-permute-start(bf16[896,256]{1,0:T(8,128)(2,1)S(1)} %get-tuple-element.140), channel_id=1, source_target_pairs={{0,2},{1,3},{2,0},{3,1},{4,6},{5,7},{6,4},{7,5},{8,10},{9,11},{10,... | collective-permute-start | bytes 1376264 | tf_op jit(solution)/shard_map/ppermute | solution.py:509
  174.0 70.5 %collective-permute-start.56 = (bf16[896,256]{1,0:T(8,128)(2,1)S(1)}, bf16[896,256]{1,0:T(8,128)(2,1)S(1)}, u32[]{:S(2)}, u32[]{:S(2)}) collective-permute-start(bf16[896,256]{1,0:T(8,128)(2,1)S(1)} %get-tuple-element.141), channel_id=1, source_target_pairs={{0,3},{1,2},{2,1},{3,0},{4,7},{5,6},{6,5},{7,4},{8,11},{9,10},{10,... | collective-permute-start | bytes 1376264 | tf_op jit(solution)/shard_map/ppermute | solution.py:509
  177.6 57.2 %collective-permute-start.58 = (bf16[512,256]{1,0:T(8,128)(2,1)S(1)}, bf16[512,256]{1,0:T(8,128)(2,1)S(1)}, u32[]{:S(2)}, u32[]{:S(2)}) collective-permute-start(bf16[512,256]{1,0:T(8,128)(2,1)S(1)} %get-tuple-element.144), channel_id=1, source_target_pairs={{0,2},{1,3},{2,0},{3,1},{4,6},{5,7},{6,4},{7,5},{8,10},{9,11},{10,... | collective-permute-start | bytes 786440 | tf_op jit(solution)/shard_map/ppermute | solution.py:509
  179.9 54.9 %collective-permute-start.59 = (bf16[512,256]{1,0:T(8,128)(2,1)S(1)}, bf16[512,256]{1,0:T(8,128)(2,1)S(1)}, u32[]{:S(2)}, u32[]{:S(2)}) collective-permute-start(bf16[512,256]{1,0:T(8,128)(2,1)S(1)} %get-tuple-element.145), channel_id=1, source_target_pairs={{0,3},{1,2},{2,1},{3,0},{4,7},{5,6},{6,5},{7,4},{8,11},{9,10},{10,... | collective-permute-start | bytes 786440 | tf_op jit(solution)/shard_map/ppermute | solution.py:509
  234.8 17.4 %collective-permute-start.48 = (bf16[256,256]{1,0:T(8,128)(2,1)S(1)}, bf16[256,256]{1,0:T(8,128)(2,1)S(1)}, u32[]{:S(2)}, u32[]{:S(2)}) collective-permute-start(bf16[256,256]{1,0:T(8,128)(2,1)S(1)} %get-tuple-element.134), channel_id=1, source_target_pairs={{0,1},{1,0},{2,3},{3,2},{4,5},{5,4},{6,7},{7,6},{8,9},{9,8},{10,11... | collective-permute-start | bytes 393224 | tf_op jit(solution)/shard_map/ppermute | solution.py:509
  234.8 17.4 %collective-permute-start.49 = (bf16[256,256]{1,0:T(8,128)(2,1)S(1)}, bf16[256,256]{1,0:T(8,128)(2,1)S(1)}, u32[]{:S(2)}, u32[]{:S(2)}) collective-permute-start(bf16[256,256]{1,0:T(8,128)(2,1)S(1)} %get-tuple-element.135), channel_id=1, source_target_pairs={{0,2},{1,3},{2,0},{3,1},{4,6},{5,7},{6,4},{7,5},{8,10},{9,11},{10,... | collective-permute-start | bytes 393224 | tf_op jit(solution)/shard_map/ppermute | solution.py:509
  (36 other events, 319.7 us)
